TPU v7x, 32 devices: a whole 2x2x4 slice. The times are simulated.
32 devices in a mesh: row: 8 (over z, y), col: 4 (over x, core).
Axes of the slice: x: 2, y: 2, z: 4, core: 2. Of those that a mesh axis runs over, the one named last changes fastest.
Arguments:
- spectra: bfloat16 [600, 32, 512], P(None, 'row', 'col'), may hold values from 0.0099487305 to 1
- wind: float32 [2, 32, 512], P(None, 'row', 'col'), may hold values from -18 to 18
- wave_current: float32 [3, 32, 512], P(None, 'row', 'col'), may hold values from -3 to 3
- wave_wet: int32 [32, 512], P('row', 'col'), may hold values 0 or 1
- interaction: bfloat16 [600, 600], replicated, may hold values from -0.25 to 0.25
- input_rate: float32 [25], replicated, may hold values from 0.002 to 0.03
- eta_gain: float32 [25], replicated, may hold values from -0.5 to 0.5
- stress_map: float32 [2, 600], replicated, may hold values from -0.25 to 0.25
- stokes_map: float32 [6, 600], replicated, may hold values from -0.25 to 0.25
- ocean_vel: float32 [2, 30, 64, 512], P(None, None, 'row', 'col'), may hold values from -3 to 3
- ocean_eta: float32 [64, 512], P('row', 'col'), may hold values from -3 to 3
- ocean_wet: int32 [64, 512], P('row', 'col'), may hold values 0 or 1
- coriolis: float32 [64, 512], P('row', 'col'), may hold values from -1.5 to 1.5
- tau_profile: float32 [30], replicated, may hold values from 0.05 to 1
- stokes_profile: float32 [3, 30], replicated, may hold values from 0.05 to 1
- thickness: float32 [30], replicated, may hold values from 0.02 to 0.1
- mix_inverse: float32 [30, 30], replicated
- fold_index: int32 [512], P('col'), may hold values from 0 to 511, as said below
- wave_send: int32 [8, 4, 3, 64], P('row', 'col'), may hold values from 0 to 511
- ocean_recv: bfloat16 [8, 4, 3, 64, 1024], P('row', 'col'), may hold values from -0.4375 to 0.4375
- ocean_send: int32 [8, 4, 3, 64], P('row', 'col'), may hold values from 0 to 1023
- wave_recv: bfloat16 [8, 4, 3, 64, 512], P('row', 'col'), may hold values from -0.4375 to 0.4375
Outputs:
- spectra_out: bfloat16 [600, 32, 512], P(None, 'row', 'col')
- ocean_vel_out: float32 [2, 30, 64, 512], P(None, None, 'row', 'col')
- ocean_eta_out: float32 [64, 512], P('row', 'col')
- current_out: float32 [3, 32, 512], P(None, 'row', 'col')
Inputs may be any that keep to these rules, and one draw needn't show every extreme that they name: `wave_send`: entries name cells of the sending wave tile numbered y * 128 + x. `ocean_send`: entries name cells of the sending ocean tile numbered y * 128 + x. `fold_index`: each entry names a column of the whole top line; columns of any block may be named from any block.
All inputs are finite; a program needn't handle non-finite values. No bound on the sum of `wave_wet` or of `ocean_wet` on one device may be relied on, other than what follows from the above.
Results may differ from a plain program's by a relative error of at most 0.006.
Values may be sent and summed in bfloat16 or wider, within the bound.
No kernel may reach another device: no remote copies, remote signals or barrier semaphores. Data moves between devices by JAX's collectives and lax.ppermute only.
A program may use at most 64 MiB of HBM per device.

v0:
```python
import math

import jax
import jax.numpy as jnp
from jax import lax
from jax.sharding import PartitionSpec as P

NDIR = 24
NBAND = 3
STEPS = 2


viscous = 0.2
surface_rate = 0.5
highest = lax.Precision.HIGHEST


def padded_2(array, sides, width):
    for axis, dim in sides:
        peers, length = (lax.axis_size(axis), array.shape[dim])
        up = [(i, (i + 1) % peers) for i in range(peers)]
        down = [(j, i) for i, j in up]
        last = lax.slice_in_dim(array, length - width, length, axis=dim)
        initial = lax.slice_in_dim(array, 0, width, axis=dim)
        before = lax.ppermute(last, axis, up)
        after = lax.ppermute(initial, axis, down)
        array = jnp.concatenate([before, array, after], axis=dim)
    return array


def from_behind(array, axis, by):
    peers = lax.axis_size(axis)
    pairs = [(i, i + by) for i in range(peers) if 0 <= i + by < peers]
    return lax.ppermute(array, axis, pairs)


def wave_cells(
    energy,
    wind_cells,
    current,
    wet_cells,
    interaction,
    input_rate,
    eta_gain,
    stress_map,
    stokes_map,
):
    spectrum_len = energy.shape[0]
    heading = ((jnp.arange(spectrum_len) % NDIR).astype(jnp.float32) + 0.5) * (2.0 * math.pi / NDIR)
    cosine = jnp.cos(heading)[:, None]
    sine_dir = jnp.sin(heading)[:, None]
    relative = (wind_cells[0] - current[0]) * cosine + (wind_cells[1] - current[1]) * sine_dir
    growth = jnp.repeat(input_rate, NDIR)[:, None] * jax.nn.softplus(relative)
    energy_wide = energy.astype(jnp.float32)
    transfer_term = jnp.dot(interaction, energy, preferred_element_type=jnp.float32)
    level_term = jnp.repeat(eta_gain, NDIR)[:, None] * current[2]
    updated = (
        wet_cells.astype(jnp.float32)
        * (energy_wide + (growth + level_term) * energy_wide + transfer_term)
    ).astype(jnp.bfloat16)
    stress = jnp.dot(stress_map, growth * energy_wide, precision=highest)
    stokes = jnp.dot(stokes_map, updated.astype(jnp.float32), precision=highest)
    return (updated, jnp.concatenate([stress, stokes], 0).astype(jnp.bfloat16))


def ocean_force(velocity, forcing, ocean_wet, coriolis, tau_profile, stokes_profile):
    wet_mask = ocean_wet.astype(jnp.float32)
    along_u = tau_profile[:, None, None] * forcing[0]
    along_v = tau_profile[:, None, None] * forcing[1]
    for band_index in range(NBAND):
        profile = stokes_profile[band_index][:, None, None]
        along_u = along_u + coriolis * profile * forcing[3 + 2 * band_index]
        along_v = along_v - coriolis * profile * forcing[2 + 2 * band_index]
    return wet_mask * (velocity + jnp.stack([along_u, along_v]))


def ocean_finish(forced, padded, elevation, ocean_wet, thickness, mix_inverse):
    wet_mask = ocean_wet.astype(jnp.float32)
    laplacian = (
        padded[:, :, 2:, 1:-1]
        + padded[:, :, :-2, 1:-1]
        + padded[:, :, 1:-1, 2:]
        + padded[:, :, 1:-1, :-2]
        - 4.0 * forced
    )
    smoothed = wet_mask * (forced + viscous * laplacian)
    transport = jnp.einsum("l,clyx->cyx", thickness, padded, precision=highest)
    divergence = 0.5 * (transport[0, 1:-1, 2:] - transport[0, 1:-1, :-2]) + 0.5 * (
        transport[1, 2:, 1:-1] - transport[1, :-2, 1:-1]
    )
    eta_next = wet_mask * (elevation - surface_rate * divergence)
    vel_next = jnp.einsum("lm,cmyx->clyx", mix_inverse, smoothed, precision=highest)
    return (vel_next, eta_next)


def edge_cells(forced, fold_index):
    padded = padded_2(forced.astype(jnp.bfloat16), (("row", 2), ("col", 3)), 1).astype(forced.dtype)
    row_count = lax.axis_size("row")
    row_here = lax.axis_index("row")
    top_line = forced[:, :, -1, :]
    piece = lax.all_gather(top_line, "col", axis=2, tiled=True)
    width = piece.shape[2]
    inside = (fold_index >= 0) & (fold_index < width)
    picked = jnp.take(piece, jnp.clip(fold_index, 0, width - 1), axis=2)
    across = -jnp.where(inside[None, None, :], picked, 0.0)
    north_row = jnp.where(row_here == row_count - 1, across, padded[:, :, -1, 1:-1])
    south_row = jnp.where(row_here == 0, 0.0, padded[:, :, 0, 1:-1])
    return padded.at[:, :, -1, 1:-1].set(north_row).at[:, :, 0, 1:-1].set(south_row)


def route_fields(fields, send_rows, weights, toward_ocean):
    slot_rows = jnp.moveaxis(jnp.take(fields, send_rows, axis=1), 1, 0)
    if toward_ocean:
        from_north = from_behind(slot_rows[0], "row", -1)
        from_south = from_behind(slot_rows[2], "row", 1)
    else:
        from_north = from_behind(slot_rows[0], "row", -1)
        from_south = from_behind(slot_rows[2], "row", 1)
    received = jnp.stack([from_north, slot_rows[1], from_south])
    return jnp.einsum("jfs,jsn->fn", received, weights, preferred_element_type=jnp.float32)


def shards(
    spectra,
    wind,
    wave_current,
    wave_wet,
    interaction,
    input_rate,
    eta_gain,
    stress_map,
    stokes_map,
    ocean_vel,
    ocean_eta,
    ocean_wet,
    coriolis,
    tau_profile,
    stokes_profile,
    thickness,
    mix_inverse,
    fold_index,
    wave_send,
    ocean_recv,
    ocean_send,
    wave_recv,
):
    spectrum_len, wave_rows, wave_cols = spectra.shape
    cell_count = wave_rows * wave_cols
    ocean_rows, ocean_cols = ocean_eta.shape
    energy = spectra.reshape(spectrum_len, cell_count)
    wind_cells = wind.reshape(2, cell_count)
    current = wave_current.reshape(3, cell_count)
    wet_cells = wave_wet.reshape(cell_count)
    velocity = ocean_vel
    elevation = ocean_eta
    for step_index in range(STEPS):
        energy, fields = wave_cells(
            energy,
            wind_cells,
            current,
            wet_cells,
            interaction,
            input_rate,
            eta_gain,
            stress_map,
            stokes_map,
        )
        forcing = route_fields(fields, wave_send[0, 0], ocean_recv[0, 0], True).reshape(
            -1, ocean_rows, ocean_cols
        )
        forced = ocean_force(velocity, forcing, ocean_wet, coriolis, tau_profile, stokes_profile)
        padded = edge_cells(forced, fold_index)
        velocity, elevation = ocean_finish(
            forced, padded, elevation, ocean_wet, thickness, mix_inverse
        )
        back = (
            jnp.stack([velocity[0, 0], velocity[1, 0], elevation])
            .reshape(3, ocean_rows * ocean_cols)
            .astype(jnp.bfloat16)
        )
        current = route_fields(back, ocean_send[0, 0], wave_recv[0, 0], False)
    return (
        energy.reshape(spectrum_len, wave_rows, wave_cols),
        velocity,
        elevation,
        current.reshape(3, wave_rows, wave_cols),
    )


def solution(mesh):
    in_specs = (
        P(None, "row", "col"),
        P(None, "row", "col"),
        P(None, "row", "col"),
        P("row", "col"),
        P(),
        P(),
        P(),
        P(),
        P(),
        P(None, None, "row", "col"),
        P("row", "col"),
        P("row", "col"),
        P("row", "col"),
        P(),
        P(),
        P(),
        P(),
        P("col"),
        P("row", "col", None, None),
        P("row", "col", None, None, None),
        P("row", "col", None, None),
        P("row", "col", None, None, None),
    )
    out_specs = (
        P(None, "row", "col"),
        P(None, None, "row", "col"),
        P("row", "col"),
        P(None, "row", "col"),
    )
    return jax.shard_map(shards, mesh=mesh, in_specs=in_specs, out_specs=out_specs, check_vma=False)
```

profile of v0, /device:TPU:0, one launch (start us, length us, event | category | flops | bytes accessed | tf_op | source)
XLA Modules:
  0.0 97.8 jit_solution(12859148233236759224)
XLA Ops:
  5.2 2.8 %fusion.13 = bf16[2,512]{1,0:T(2,128)(2,1)S(1)} fusion(f32[2,600]{1,0:T(2,128)} %param.43, f32[600]{0:T(1024)S(1)} %get-tuple-element.137, f32[512]{0:T(512)S(1)} %get-tuple-element.104, f32[600]{0:T(1024)S(1)} %get-tuple-element.138, f32[512]{0:T(512)S(1)} %get-tuple-element.103, f32[600]{0:T(1024)S(1)} %mul.659, bf16[75,8,4,128]{3,2,1,0:T(4,128)(2,1)} %bitcast.291), kind=kOutput, calls=%fused_computation.35 | convolution fusion | flops 11060224 | bytes 632544 | tf_op jit(solution)/shard_map/dot_general | solution.py:61
  8.1 1.4 %fusion.4 = bf16[600,512]{1,0:T(8,128)(2,1)S(1)} fusion(bf16[600,600]{1,0:T(8,128)(2,1)S(1)} %copy-done, f32[512]{0:T(512)S(1)} %get-tuple-element.118, f32[600]{0:T(1024)S(1)} %mul.669, f32[600]{0:T(1024)S(1)} %get-tuple-element.137, f32[512]{0:T(512)S(1)} %get-tuple-element.104, f32[600]{0:T(1024)S(1)} %get-tuple-element.138, ...), kind=kOutput, calls=%fused_computation.18 | convolution fusion | flops 374169600 | bytes 1966592 | tf_op jit(solution)/shard_map/dot_general | solution.py:55
  10.2 0.8 gather_fusion
  11.1 1.3 %collective-permute-start = (bf16[8,64]{1,0:T(8,128)(2,1)S(1)}, bf16[8,64]{1,0:T(8,128)(2,1)S(1)}, u32[]{:S(2)}, u32[]{:S(2)}) collective-permute-start(bf16[8,64]{1,0:T(8,128)(2,1)S(1)} %get-tuple-element.115), channel_id=1, source_target_pairs={{4,0},{8,4},{12,8},{16,12},{20,16},{24,20},{28,24},{5,1},{9,5},{13... | collective-permute-start | bytes 3080 | tf_op jit(solution)/shard_map/ppermute | solution.py:34
  12.4 5.5 %collective-permute-start.1 = (bf16[8,64]{1,0:T(8,128)(2,1)S(1)}, bf16[8,64]{1,0:T(8,128)(2,1)S(1)}, u32[]{:S(2)}, u32[]{:S(2)}) collective-permute-start(bf16[8,64]{1,0:T(8,128)(2,1)S(1)} %get-tuple-element.116), channel_id=1, source_target_pairs={{0,4},{4,8},{8,12},{12,16},{16,20},{20,24},{24,28},{1,5},{5,9},{9,... | collective-permute-start | bytes 3080 | tf_op jit(solution)/shard_map/ppermute | solution.py:34
  19.8 3.0 %collective-permute-start.2 = (bf16[2,30,1,128]{3,1,2,0:T(8,128)(2,1)S(1)}, bf16[2,30,1,128]{3,1,2,0:T(8,128)(2,1)S(1)}, u32[]{:S(2)}, u32[]{:S(2)}) collective-permute-start(bf16[2,30,1,128]{3,1,2,0:T(8,128)(2,1)S(1)} %get-tuple-element.85), channel_id=1, source_target_pairs={{0,4},{4,8},{8,12},{12,16},{16,20},{20,24},{24,28},{28,0},{1,5},{5... | collective-permute-start | bytes 46088 | tf_op jit(solution)/shard_map/ppermute | solution.py:25
  22.8 3.0 %collective-permute-start.3 = (bf16[2,30,1,128]{3,1,2,0:T(8,128)(2,1)S(1)}, bf16[2,30,1,128]{3,1,2,0:T(8,128)(2,1)S(1)}, u32[]{:S(2)}, u32[]{:S(2)}) collective-permute-start(bf16[2,30,1,128]{3,1,2,0:T(8,128)(2,1)S(1)} %get-tuple-element.86), channel_id=1, source_target_pairs={{4,0},{8,4},{12,8},{16,12},{20,16},{24,20},{28,24},{0,28},{5,1},{9... | collective-permute-start | bytes 46088 | tf_op jit(solution)/shard_map/ppermute | solution.py:26
  25.7 1.6 %collective-permute-done.2 = bf16[2,30,1,128]{3,1,2,0:T(8,128)(2,1)S(1)} collective-permute-done((bf16[2,30,1,128]{3,1,2,0:T(8,128)(2,1)S(1)}, bf16[2,30,1,128]{3,1,2,0:T(8,128)(2,1)S(1)}, u32[]{:S(2)}, u32[]{:S(2)}) %collective-permute-start.2) | collective-permute-done | bytes 15392 | tf_op jit(solution)/shard_map/ppermute | solution.py:25
  27.9 1.7 %collective-permute-start.5 = (bf16[2,30,10,1]{3,1,2,0:T(8,128)(2,1)S(1)}, bf16[2,30,10,1]{3,1,2,0:T(8,128)(2,1)S(1)}, u32[]{:S(2)}, u32[]{:S(2)}) collective-permute-start(bf16[2,30,10,1]{3,1,2,0:T(8,128)(2,1)S(1)} %get-tuple-element.78), channel_id=1, source_target_pairs={{1,0},{2,1},{3,2},{0,3},{5,4},{6,5},{7,6},{4,7},{9,8},{10,9},{11,1... | collective-permute-start | bytes 3608 | tf_op jit(solution)/shard_map/ppermute | solution.py:26
  29.6 6.3 %all-gather = f32[2,30,1,512]{3,1,2,0:T(8,128)S(1)} all-gather(f32[2,30,1,128]{3,1,2,0:T(8,128)S(1)} %slice.474), channel_id=2, replica_groups=mesh['row'=8,'col'=4] {'col'}, dimensions={3}, use_global_device_ids=true | all-gather | bytes 153600 | tf_op jit(solution)/shard_map/all_gather | solution.py:101
  38.0 1.9 %scatter.15 = f32[2,30,10,130]{3,1,2,0:T(8,128)S(1)} dynamic-update-slice(f32[2,30,10,130]{3,1,2,0:T(8,128)S(1)} %scatter.14, f32[2,30,1,128]{3,1,2,0:T(8,128)S(1)} %slice_select_fusion.1, s32[]{:T(128)} %constant.164.clone.1, s32[]{:T(128)} %constant.164.clone.1, s32[]{:T(128)} %bitcast.34, s32[]{:T(128)} %bitcast.35) | dynamic-update-slice | bytes 61444 | tf_op jit(solution)/shard_map/scatter | solution.py:108
  41.5 0.8 gather_fusion.2
  42.5 1.3 %collective-permute-start.6 = (bf16[3,64]{1,0:T(4,128)(2,1)S(1)}, bf16[3,64]{1,0:T(4,128)(2,1)S(1)}, u32[]{:S(2)}, u32[]{:S(2)}) collective-permute-start(bf16[3,64]{1,0:T(4,128)(2,1)S(1)} %get-tuple-element.124), channel_id=1, source_target_pairs={{4,0},{8,4},{12,8},{16,12},{20,16},{24,20},{28,24},{5,1},{9,5},{13... | collective-permute-start | bytes 1160 | tf_op jit(solution)/shard_map/ppermute | solution.py:34
  43.8 5.4 %collective-permute-start.7 = (bf16[3,64]{1,0:T(4,128)(2,1)S(1)}, bf16[3,64]{1,0:T(4,128)(2,1)S(1)}, u32[]{:S(2)}, u32[]{:S(2)}) collective-permute-start(bf16[3,64]{1,0:T(4,128)(2,1)S(1)} %get-tuple-element.125), channel_id=1, source_target_pairs={{0,4},{4,8},{8,12},{12,16},{16,20},{20,24},{24,28},{1,5},{5,9},{9,... | collective-permute-start | bytes 1160 | tf_op jit(solution)/shard_map/ppermute | solution.py:34
  49.2 1.3 %collective-permute-done.7 = bf16[3,64]{1,0:T(4,128)(2,1)S(1)} collective-permute-done((bf16[3,64]{1,0:T(4,128)(2,1)S(1)}, bf16[3,64]{1,0:T(4,128)(2,1)S(1)}, u32[]{:S(2)}, u32[]{:S(2)}) %collective-permute-start.7) | collective-permute-done | bytes 416 | tf_op jit(solution)/shard_map/ppermute | solution.py:34
  50.7 1.7 %fusion.14 = bf16[2,512]{1,0:T(2,128)(2,1)S(1)} fusion(f32[2,600]{1,0:T(2,128)S(1)} %copy-done.18, bf16[600,512]{1,0:T(8,128)(2,1)S(1)} %copy-done.3, f32[512]{0:T(512)S(1)} %bitcast.287, f32[512]{0:T(512)S(1)} %bitcast.284, f32[600]{0:T(1024)S(1)} %get-tuple-element.137, f32[600]{0:T(1024)S(1)} %get-tuple-element.138, f32[600]{0:T(1024)S(1)} %mul.659), kind=kOutput, calls=%fused_computation.36 | convolution fusion | flops 11060224 | bytes 632544 | tf_op jit(solution)/shard_map/dot_general | solution.py:61
  52.4 1.4 %fusion.3 = bf16[600,512]{1,0:T(8,128)(2,1)S(1)} fusion(bf16[600,512]{1,0:T(8,128)(2,1)S(1)} %copy-done.4, bf16[600,600]{1,0:T(8,128)(2,1)S(1)} %copy-done, f32[512]{0:T(512)S(1)} %bitcast.286, f32[512]{0:T(512)S(1)} %bitcast.288, f32[512]{0:T(512)S(1)} %bitcast.285, f32[600]{0:T(1024)S(1)} %mul.669, f32[600]{0:T(1024)S(1)} %get-tuple-element.137, ...), kind=kOutput, calls=%fused_computation.17 | convolution fusion | flops 374169600 | bytes 1966592 | tf_op jit(solution)/shard_map/dot_general | solution.py:55
  54.4 0.8 gather_fusion.3
  55.3 1.3 %collective-permute-start.8 = (bf16[8,64]{1,0:T(8,128)(2,1)S(1)}, bf16[8,64]{1,0:T(8,128)(2,1)S(1)}, u32[]{:S(2)}, u32[]{:S(2)}) collective-permute-start(bf16[8,64]{1,0:T(8,128)(2,1)S(1)} %get-tuple-element.110), channel_id=1, source_target_pairs={{4,0},{8,4},{12,8},{16,12},{20,16},{24,20},{28,24},{5,1},{9,5},{13... | collective-permute-start | bytes 3080 | tf_op jit(solution)/shard_map/ppermute | solution.py:34
  56.6 5.4 %collective-permute-start.9 = (bf16[8,64]{1,0:T(8,128)(2,1)S(1)}, bf16[8,64]{1,0:T(8,128)(2,1)S(1)}, u32[]{:S(2)}, u32[]{:S(2)}) collective-permute-start(bf16[8,64]{1,0:T(8,128)(2,1)S(1)} %get-tuple-element.111), channel_id=1, source_target_pairs={{0,4},{4,8},{8,12},{12,16},{16,20},{20,24},{24,28},{1,5},{5,9},{9,... | collective-permute-start | bytes 3080 | tf_op jit(solution)/shard_map/ppermute | solution.py:34
  62.0 1.3 %collective-permute-done.9 = bf16[8,64]{1,0:T(8,128)(2,1)S(1)} collective-permute-done((bf16[8,64]{1,0:T(8,128)(2,1)S(1)}, bf16[8,64]{1,0:T(8,128)(2,1)S(1)}, u32[]{:S(2)}, u32[]{:S(2)}) %collective-permute-start.9) | collective-permute-done | bytes 1056 | tf_op jit(solution)/shard_map/ppermute | solution.py:34
  63.8 3.4 %collective-permute-start.10 = (bf16[2,30,1,128]{3,1,0,2:T(8,128)(2,1)S(1)}, bf16[2,30,1,128]{3,1,0,2:T(8,128)(2,1)S(1)}, u32[]{:S(2)}, u32[]{:S(2)}) collective-permute-start(bf16[2,30,1,128]{3,1,0,2:T(8,128)(2,1)S(1)} %get-tuple-element.81), channel_id=1, source_target_pairs={{0,4},{4,8},{8,12},{12,16},{16,20},{20,24},{24,28},{28,0},{1,5},{5... | collective-permute-start | bytes 46088 | tf_op jit(solution)/shard_map/ppermute | solution.py:25
  67.2 4.4 %collective-permute-start.11 = (bf16[2,30,1,128]{3,1,0,2:T(8,128)(2,1)S(1)}, bf16[2,30,1,128]{3,1,0,2:T(8,128)(2,1)S(1)}, u32[]{:S(2)}, u32[]{:S(2)}) collective-permute-start(bf16[2,30,1,128]{3,1,0,2:T(8,128)(2,1)S(1)} %get-tuple-element.82), channel_id=1, source_target_pairs={{4,0},{8,4},{12,8},{16,12},{20,16},{24,20},{28,24},{0,28},{5,1},{9... | collective-permute-start | bytes 46088 | tf_op jit(solution)/shard_map/ppermute | solution.py:26
  71.6 1.6 %collective-permute-done.10 = bf16[2,30,1,128]{3,1,0,2:T(8,128)(2,1)S(1)} collective-permute-done((bf16[2,30,1,128]{3,1,0,2:T(8,128)(2,1)S(1)}, bf16[2,30,1,128]{3,1,0,2:T(8,128)(2,1)S(1)}, u32[]{:S(2)}, u32[]{:S(2)}) %collective-permute-start.10) | collective-permute-done | bytes 15392 | tf_op jit(solution)/shard_map/ppermute | solution.py:25
  74.0 1.7 %collective-permute-start.13 = (bf16[2,30,10,1]{3,1,0,2:T(8,128)(2,1)}, bf16[2,30,10,1]{3,1,0,2:T(8,128)(2,1)S(1)}, u32[]{:S(2)}, u32[]{:S(2)}) collective-permute-start(bf16[2,30,10,1]{3,1,0,2:T(8,128)(2,1)} %get-tuple-element.76), channel_id=1, source_target_pairs={{1,0},{2,1},{3,2},{0,3},{5,4},{6,5},{7,6},{4,7},{9,8},{10,9},{11,1... | collective-permute-start | bytes 3608 | tf_op jit(solution)/shard_map/ppermute | solution.py:26
  75.8 6.5 %all-gather.1 = f32[2,30,1,512]{3,1,2,0:T(8,128)S(1)} all-gather(f32[2,30,1,128]{3,1,2,0:T(8,128)S(1)} %slice.508), channel_id=3, replica_groups=mesh['row'=8,'col'=4] {'col'}, dimensions={3}, use_global_device_ids=true | all-gather | bytes 153600 | tf_op jit(solution)/shard_map/all_gather | solution.py:101
  84.4 1.9 %scatter.19 = f32[2,30,10,130]{3,1,0,2:T(8,128)S(1)} dynamic-update-slice(f32[2,30,10,130]{3,1,0,2:T(8,128)S(1)} %scatter.16, f32[2,30,1,128]{3,1,0,2:T(8,128)S(1)} %slice_select_fusion, s32[]{:T(128)} %constant.164.clone.1, s32[]{:T(128)} %constant.164.clone.1, s32[]{:T(128)} %bitcast.34, s32[]{:T(128)} %bitcast.35) | dynamic-update-slice | bytes 61444 | tf_op jit(solution)/shard_map/scatter | solution.py:108
  88.4 0.8 gather_fusion.5
  89.4 1.3 %collective-permute-start.14 = (bf16[3,64]{1,0:T(4,128)(2,1)S(1)}, bf16[3,64]{1,0:T(4,128)(2,1)S(1)}, u32[]{:S(2)}, u32[]{:S(2)}) collective-permute-start(bf16[3,64]{1,0:T(4,128)(2,1)S(1)} %get-tuple-element.121), channel_id=1, source_target_pairs={{4,0},{8,4},{12,8},{16,12},{20,16},{24,20},{28,24},{5,1},{9,5},{13... | collective-permute-start | bytes 1160 | tf_op jit(solution)/shard_map/ppermute | solution.py:34
  90.7 4.5 %collective-permute-start.15 = (bf16[3,64]{1,0:T(4,128)(2,1)S(1)}, bf16[3,64]{1,0:T(4,128)(2,1)S(1)}, u32[]{:S(2)}, u32[]{:S(2)}) collective-permute-start(bf16[3,64]{1,0:T(4,128)(2,1)S(1)} %get-tuple-element.122), channel_id=1, source_target_pairs={{0,4},{4,8},{8,12},{12,16},{16,20},{20,24},{24,28},{1,5},{5,9},{9,... | collective-permute-start | bytes 1160 | tf_op jit(solution)/shard_map/ppermute | solution.py:34
  95.2 1.0 reshape.413
  96.2 0.8 copy.93
  (141 shorter events, 18.4 us)
Async XLA Ops:
  0.6 7.4 %copy-start = (bf16[600,600]{1,0:T(8,128)(2,1)S(1)}, bf16[600,600]{1,0:T(8,128)(2,1)}, u32[]{:S(2)}) copy-start(bf16[600,600]{1,0:T(8,128)(2,1)} %param.40) | copy-start | bytes 2160004
  5.2 2.8 %copy-start.17 = (bf16[600,4,128]{2,1,0:T(4,128)(2,1)S(1)}, bf16[600,4,128]{2,1,0:T(4,128)(2,1)}, u32[]{:S(2)}) copy-start(bf16[600,4,128]{2,1,0:T(4,128)(2,1)} %param.36) | copy-start | bytes 1843204
  9.5 10.0 %copy-start.2 = (bf16[600,512]{1,0:T(8,128)(2,1)}, bf16[600,512]{1,0:T(8,128)(2,1)S(1)}, u32[]{:S(2)}) copy-start(bf16[600,512]{1,0:T(8,128)(2,1)S(1)} %fusion.4) | copy-start | bytes 1843204
  9.5 8.5 %copy-start.11 = (s32[1,1,3,64]{3,1,2,0:T(1,128)S(1)}, s32[1,1,3,64]{3,1,2,0:T(1,128)}, u32[]{:S(2)}) copy-start(s32[1,1,3,64]{3,1,2,0:T(1,128)} %param.56) | copy-start | bytes 2308
  9.5 8.5 %copy-start.15 = (f32[3,30]{1,0:T(4,128)S(1)}, f32[3,30]{1,0:T(4,128)}, u32[]{:S(2)}) copy-start(f32[3,30]{1,0:T(4,128)} %param.50) | copy-start | bytes 1084
  9.5 8.5 %copy-start.16 = (s32[128]{0:T(128)S(1)}, s32[128]{0:T(128)}, u32[]{:S(2)}) copy-start(s32[128]{0:T(128)} %param.53) | copy-start | bytes 1540
  9.5 9.1 %copy-start.9 = (s32[8,128]{1,0:T(8,128)S(1)}, s32[8,128]{1,0:T(8,128)}, u32[]{:S(2)}) copy-start(s32[8,128]{1,0:T(8,128)} %param.47) | copy-start | bytes 12292
  9.5 9.7 %copy-start.1 = (bf16[1,1,3,64,1024]{4,3,2,1,0:T(8,128)(2,1)S(1)}, bf16[1,1,3,64,1024]{4,3,2,1,0:T(8,128)(2,1)}, u32[]{:S(2)}) copy-start(bf16[1,1,3,64,1024]{4,3,2,1,0:T(8,128)(2,1)} %param.55) | copy-start | bytes 1179652
  9.6 9.9 %copy-start.10 = (f32[8,128]{1,0:T(8,128)S(1)}, f32[8,128]{1,0:T(8,128)}, u32[]{:S(2)}) copy-start(f32[8,128]{1,0:T(8,128)} %param.48) | copy-start | bytes 12292
  9.6 9.9 %copy-start.13 = (f32[30]{0:T(128)S(1)}, f32[30]{0:T(128)}, u32[]{:S(2)}) copy-start(f32[30]{0:T(128)} %param.49) | copy-start | bytes 364
  9.6 10.1 %copy-start.5 = (f32[2,30,8,128]{3,2,1,0:T(8,128)S(1)}, f32[2,30,8,128]{3,2,1,0:T(8,128)}, u32[]{:S(2)}) copy-start(f32[2,30,8,128]{3,2,1,0:T(8,128)} %param.45) | copy-start | bytes 737284
  11.1 7.6 %collective-permute-start = (bf16[8,64]{1,0:T(8,128)(2,1)S(1)}, bf16[8,64]{1,0:T(8,128)(2,1)S(1)}, u32[]{:S(2)}, u32[]{:S(2)}) collective-permute-start(bf16[8,64]{1,0:T(8,128)(2,1)S(1)} %get-tuple-element.115), channel_id=1, source_target_pairs={{4,0},{8,4},{12,8},{16,12},{20,16},{24,20},{28,24},{5,1},{9,5},{13... | collective-permute-start | bytes 3080 | tf_op jit(solution)/shard_map/ppermute | solution.py:34
  12.4 6.8 %collective-permute-start.1 = (bf16[8,64]{1,0:T(8,128)(2,1)S(1)}, bf16[8,64]{1,0:T(8,128)(2,1)S(1)}, u32[]{:S(2)}, u32[]{:S(2)}) collective-permute-start(bf16[8,64]{1,0:T(8,128)(2,1)S(1)} %get-tuple-element.116), channel_id=1, source_target_pairs={{0,4},{4,8},{8,12},{12,16},{16,20},{20,24},{24,28},{1,5},{5,9},{9,... | collective-permute-start | bytes 3080 | tf_op jit(solution)/shard_map/ppermute | solution.py:34
  19.8 7.6 %collective-permute-start.2 = (bf16[2,30,1,128]{3,1,2,0:T(8,128)(2,1)S(1)}, bf16[2,30,1,128]{3,1,2,0:T(8,128)(2,1)S(1)}, u32[]{:S(2)}, u32[]{:S(2)}) collective-permute-start(bf16[2,30,1,128]{3,1,2,0:T(8,128)(2,1)S(1)} %get-tuple-element.85), channel_id=1, source_target_pairs={{0,4},{4,8},{8,12},{12,16},{16,20},{20,24},{24,28},{28,0},{1,5},{5... | collective-permute-start | bytes 46088 | tf_op jit(solution)/shard_map/ppermute | solution.py:25
  22.8 4.9 %collective-permute-start.3 = (bf16[2,30,1,128]{3,1,2,0:T(8,128)(2,1)S(1)}, bf16[2,30,1,128]{3,1,2,0:T(8,128)(2,1)S(1)}, u32[]{:S(2)}, u32[]{:S(2)}) collective-permute-start(bf16[2,30,1,128]{3,1,2,0:T(8,128)(2,1)S(1)} %get-tuple-element.86), channel_id=1, source_target_pairs={{4,0},{8,4},{12,8},{16,12},{20,16},{24,20},{28,24},{0,28},{5,1},{9... | collective-permute-start | bytes 46088 | tf_op jit(solution)/shard_map/ppermute | solution.py:26
  27.8 9.2 %collective-permute-start.4 = (bf16[2,30,10,1]{3,1,2,0:T(8,128)(2,1)S(1)}, bf16[2,30,10,1]{3,1,2,0:T(8,128)(2,1)S(1)}, u32[]{:S(2)}, u32[]{:S(2)}) collective-permute-start(bf16[2,30,10,1]{3,1,2,0:T(8,128)(2,1)S(1)} %get-tuple-element.77), channel_id=1, source_target_pairs={{0,1},{1,2},{2,3},{3,0},{4,5},{5,6},{6,7},{7,4},{8,9},{9,10},{10,1... | collective-permute-start | bytes 3608 | tf_op jit(solution)/shard_map/ppermute | solution.py:25
  27.9 9.2 %collective-permute-start.5 = (bf16[2,30,10,1]{3,1,2,0:T(8,128)(2,1)S(1)}, bf16[2,30,10,1]{3,1,2,0:T(8,128)(2,1)S(1)}, u32[]{:S(2)}, u32[]{:S(2)}) collective-permute-start(bf16[2,30,10,1]{3,1,2,0:T(8,128)(2,1)S(1)} %get-tuple-element.78), channel_id=1, source_target_pairs={{1,0},{2,1},{3,2},{0,3},{5,4},{6,5},{7,6},{4,7},{9,8},{10,9},{11,1... | collective-permute-start | bytes 3608 | tf_op jit(solution)/shard_map/ppermute | solution.py:26
  37.0 3.0 %copy-start.8 = (f32[30,30]{1,0:T(8,128)S(1)}, f32[30,30]{1,0:T(8,128)}, u32[]{:S(2)}) copy-start(f32[30,30]{1,0:T(8,128)} %param.52) | copy-start | bytes 10804
  37.3 3.4 %copy-start.14 = (f32[30]{0:T(128)S(1)}, f32[30]{0:T(128)}, u32[]{:S(2)}) copy-start(f32[30]{0:T(128)} %param.51) | copy-start | bytes 364
  40.6 9.9 %copy-start.6 = (bf16[1,1,3,64,512]{4,3,2,1,0:T(8,128)(2,1)S(1)}, bf16[1,1,3,64,512]{4,3,2,1,0:T(8,128)(2,1)}, u32[]{:S(2)}) copy-start(bf16[1,1,3,64,512]{4,3,2,1,0:T(8,128)(2,1)} %param.57) | copy-start | bytes 589828
  40.6 10.1 %copy-start.3 = (bf16[600,512]{1,0:T(8,128)(2,1)S(1)}, bf16[600,512]{1,0:T(8,128)(2,1)}, u32[]{:S(2)}) copy-start(bf16[600,512]{1,0:T(8,128)(2,1)} %copy-done.2) | copy-start | bytes 1843204
  40.7 10.1 %copy-start.18 = (f32[2,600]{1,0:T(2,128)S(1)}, f32[2,600]{1,0:T(2,128)}, u32[]{:S(2)}) copy-start(f32[2,600]{1,0:T(2,128)} %param.43) | copy-start | bytes 14404
  42.5 6.8 %collective-permute-start.6 = (bf16[3,64]{1,0:T(4,128)(2,1)S(1)}, bf16[3,64]{1,0:T(4,128)(2,1)S(1)}, u32[]{:S(2)}, u32[]{:S(2)}) collective-permute-start(bf16[3,64]{1,0:T(4,128)(2,1)S(1)} %get-tuple-element.124), channel_id=1, source_target_pairs={{4,0},{8,4},{12,8},{16,12},{20,16},{24,20},{28,24},{5,1},{9,5},{13... | collective-permute-start | bytes 1160 | tf_op jit(solution)/shard_map/ppermute | solution.py:34
  43.8 6.7 %collective-permute-start.7 = (bf16[3,64]{1,0:T(4,128)(2,1)S(1)}, bf16[3,64]{1,0:T(4,128)(2,1)S(1)}, u32[]{:S(2)}, u32[]{:S(2)}) collective-permute-start(bf16[3,64]{1,0:T(4,128)(2,1)S(1)} %get-tuple-element.125), channel_id=1, source_target_pairs={{0,4},{4,8},{8,12},{12,16},{16,20},{20,24},{24,28},{1,5},{5,9},{9,... | collective-permute-start | bytes 1160 | tf_op jit(solution)/shard_map/ppermute | solution.py:34
  55.3 6.8 %collective-permute-start.8 = (bf16[8,64]{1,0:T(8,128)(2,1)S(1)}, bf16[8,64]{1,0:T(8,128)(2,1)S(1)}, u32[]{:S(2)}, u32[]{:S(2)}) collective-permute-start(bf16[8,64]{1,0:T(8,128)(2,1)S(1)} %get-tuple-element.110), channel_id=1, source_target_pairs={{4,0},{8,4},{12,8},{16,12},{20,16},{24,20},{28,24},{5,1},{9,5},{13... | collective-permute-start | bytes 3080 | tf_op jit(solution)/shard_map/ppermute | solution.py:34
  56.6 6.7 %collective-permute-start.9 = (bf16[8,64]{1,0:T(8,128)(2,1)S(1)}, bf16[8,64]{1,0:T(8,128)(2,1)S(1)}, u32[]{:S(2)}, u32[]{:S(2)}) collective-permute-start(bf16[8,64]{1,0:T(8,128)(2,1)S(1)} %get-tuple-element.111), channel_id=1, source_target_pairs={{0,4},{4,8},{8,12},{12,16},{16,20},{20,24},{24,28},{1,5},{5,9},{9,... | collective-permute-start | bytes 3080 | tf_op jit(solution)/shard_map/ppermute | solution.py:34
  63.8 9.4 %collective-permute-start.10 = (bf16[2,30,1,128]{3,1,0,2:T(8,128)(2,1)S(1)}, bf16[2,30,1,128]{3,1,0,2:T(8,128)(2,1)S(1)}, u32[]{:S(2)}, u32[]{:S(2)}) collective-permute-start(bf16[2,30,1,128]{3,1,0,2:T(8,128)(2,1)S(1)} %get-tuple-element.81), channel_id=1, source_target_pairs={{0,4},{4,8},{8,12},{12,16},{16,20},{20,24},{24,28},{28,0},{1,5},{5... | collective-permute-start | bytes 46088 | tf_op jit(solution)/shard_map/ppermute | solution.py:25
  67.2 6.0 %collective-permute-start.11 = (bf16[2,30,1,128]{3,1,0,2:T(8,128)(2,1)S(1)}, bf16[2,30,1,128]{3,1,0,2:T(8,128)(2,1)S(1)}, u32[]{:S(2)}, u32[]{:S(2)}) collective-permute-start(bf16[2,30,1,128]{3,1,0,2:T(8,128)(2,1)S(1)} %get-tuple-element.82), channel_id=1, source_target_pairs={{4,0},{8,4},{12,8},{16,12},{20,16},{24,20},{28,24},{0,28},{5,1},{9... | collective-permute-start | bytes 46088 | tf_op jit(solution)/shard_map/ppermute | solution.py:26
  74.0 9.3 %collective-permute-start.12 = (bf16[2,30,10,1]{3,1,0,2:T(8,128)(2,1)}, bf16[2,30,10,1]{3,1,0,2:T(8,128)(2,1)S(1)}, u32[]{:S(2)}, u32[]{:S(2)}) collective-permute-start(bf16[2,30,10,1]{3,1,0,2:T(8,128)(2,1)} %get-tuple-element.75), channel_id=1, source_target_pairs={{0,1},{1,2},{2,3},{3,0},{4,5},{5,6},{6,7},{7,4},{8,9},{9,10},{10,1... | collective-permute-start | bytes 3608 | tf_op jit(solution)/shard_map/ppermute | solution.py:25
  74.0 9.3 %collective-permute-start.13 = (bf16[2,30,10,1]{3,1,0,2:T(8,128)(2,1)}, bf16[2,30,10,1]{3,1,0,2:T(8,128)(2,1)S(1)}, u32[]{:S(2)}, u32[]{:S(2)}) collective-permute-start(bf16[2,30,10,1]{3,1,0,2:T(8,128)(2,1)} %get-tuple-element.76), channel_id=1, source_target_pairs={{1,0},{2,1},{3,2},{0,3},{5,4},{6,5},{7,6},{4,7},{9,8},{10,9},{11,1... | collective-permute-start | bytes 3608 | tf_op jit(solution)/shard_map/ppermute | solution.py:26
  89.4 7.7 %collective-permute-start.14 = (bf16[3,64]{1,0:T(4,128)(2,1)S(1)}, bf16[3,64]{1,0:T(4,128)(2,1)S(1)}, u32[]{:S(2)}, u32[]{:S(2)}) collective-permute-start(bf16[3,64]{1,0:T(4,128)(2,1)S(1)} %get-tuple-element.121), channel_id=1, source_target_pairs={{4,0},{8,4},{12,8},{16,12},{20,16},{24,20},{28,24},{5,1},{9,5},{13... | collective-permute-start | bytes 1160 | tf_op jit(solution)/shard_map/ppermute | solution.py:34
  90.7 6.4 %collective-permute-start.15 = (bf16[3,64]{1,0:T(4,128)(2,1)S(1)}, bf16[3,64]{1,0:T(4,128)(2,1)S(1)}, u32[]{:S(2)}, u32[]{:S(2)}) collective-permute-start(bf16[3,64]{1,0:T(4,128)(2,1)S(1)} %get-tuple-element.122), channel_id=1, source_target_pairs={{0,4},{4,8},{8,12},{12,16},{16,20},{20,24},{24,28},{1,5},{5,9},{9,... | collective-permute-start | bytes 1160 | tf_op jit(solution)/shard_map/ppermute | solution.py:34
  (3 other events, 4.4 us)
where the time goes:
time: 99.1 us; the launch traced here: 97.8 us
  starting transfers between devices  43.4 us (44%)
  local copies, waits for them, and re-layouts  17.4 us (18%)
  blocking collectives  12.8 us (13%)
  matrix products  11.1 us (11%)
  waiting for transfers between devices  6.6 us (7%)
  other arithmetic  5.19 us (5%)
  between operations  1.39 us (1%)
    ppermute x8, starting transfers between devices, from_behind(): return lax.ppermute(array, axis, pairs)  26.1 us
    all_gather x2, blocking collectives, edge_cells(): piece = lax.all_gather(top_line, 'col', axis=2, tiled=True)  12.8 us
    ppermute x4, starting transfers between devices, padded_2(): after = lax.ppermute(initial, axis, down)  10.8 us
    ppermute x4, starting transfers between devices, padded_2(): before = lax.ppermute(last, axis, up)  6.43 us
    scatter x4, local copies, waits for them, and re-layouts, edge_cells(): padded.at[:, :, -1, 1:-1].set(north_row).at[:, :, 0, 1:-1].set(south_row)  5.03 us
    dot_general x2, matrix products, wave_cells(): stress = jnp.dot(stress_map, growth * energy_wide, precision=highest)  4.51 us
    gather x8, local copies, waits for them, and re-layouts, route_fields(): slot_rows = jnp.moveaxis(jnp.take(fields, send_rows, axis=1), 1, 0)  3.52 us
    ppermute x4, waiting for transfers between devices, padded_2(): before = lax.ppermute(last, axis, up)  3.24 us
  transfers between devices with their start and end apart: 16, of which 6 were waited for; matrix products, arithmetic and copies ran while one was open for 5% of the time, Pallas kernels for 0%

commit v1 on v0

v1 whole, which is shorter than its diff:
```python
import functools
import math

import jax
import jax.numpy as jnp
import numpy as np
from jax import lax
from jax.experimental import pallas as pl
from jax.experimental.pallas import tpu as pltpu
from jax.sharding import PartitionSpec as P

NDIR = 24
NBAND = 3
STEPS = 2
viscous = 0.2
surface_rate = 0.5

f32, bf16 = jnp.float32, jnp.bfloat16
VMEM = pl.BlockSpec(memory_space=pltpu.VMEM)
SMEM = pl.BlockSpec(memory_space=pltpu.SMEM)


def call(kernel, outs, specs, scratch=(), name=None):
    out_shape = tuple(jax.ShapeDtypeStruct(s, d) for s, d in outs)
    return pl.pallas_call(
        kernel,
        out_shape=out_shape,
        in_specs=list(specs),
        out_specs=tuple(VMEM for _ in outs),
        scratch_shapes=list(scratch),
        name=name,
    )


def dot(a, b):
    return jnp.dot(a, b, preferred_element_type=f32)


def split2(w):
    high = w.astype(bf16)
    low = (w - high.astype(f32)).astype(bf16)
    return high, low


def is_even(index):
    return lax.rem(index, 2) == 0


def stress_rows(smap, rate_ref, nfreq):
    spec = smap.shape[1]
    col = lax.broadcasted_iota(jnp.int32, (1, spec), 1)
    band = jnp.zeros((1, spec), jnp.int32)
    rate = jnp.full((1, spec), rate_ref[0], f32)
    for f in range(1, nfreq):
        past = col >= NDIR * f
        band = band + jnp.where(past, 1, 0)
        rate = jnp.where(past, rate_ref[f], rate)
    direction = col - NDIR * band
    row = lax.broadcasted_iota(jnp.int32, (NDIR, spec), 0)
    keep = row == direction
    weights = [jnp.where(keep, smap[i : i + 1] * rate, 0.0) for i in range(2)]
    weights = jnp.concatenate(weights, axis=0)
    high, low = split2(weights)
    return jnp.concatenate([high.astype(f32), low.astype(f32)], axis=0).astype(bf16)


def transfer(inter, smap, rate_ref, eb, t_ref, q_ref, nfreq):
    t_ref[...] = dot(inter, eb)
    q = dot(stress_rows(smap, rate_ref, nfreq), eb)
    half = 2 * NDIR
    q_ref[...] = q[:half] + q[half:]


def wave_finish(
    e_of, t_ref, q_ref, wind_ref, current_of, wet_ref, rate_ref, gain_ref, kmap, trig_ref, upd_ref, nfreq
):
    rows, lanes = wet_ref.shape
    cosine, sine = trig_ref[:NDIR], trig_ref[NDIR:]
    stress = []
    for y in range(rows):
        cells = slice(y * lanes, (y + 1) * lanes)
        dx = wind_ref[0, y : y + 1, :] - current_of(0, y)
        dy = wind_ref[1, y : y + 1, :] - current_of(1, y)
        level = current_of(2, y)
        wet = wet_ref[y : y + 1, :].astype(f32)
        relative = dx * cosine + dy * sine
        soft = jnp.maximum(relative, 0.0) + jnp.log1p(jnp.exp(-jnp.abs(relative)))
        stress.append(
            [
                jnp.sum(soft * q_ref[i * NDIR : (i + 1) * NDIR, cells], axis=0, keepdims=True)
                for i in range(2)
            ]
        )
        rate = jnp.concatenate(
            [rate_ref[f] * soft + gain_ref[f] * level for f in range(nfreq)], axis=0
        )
        e = e_of(y)
        upd_ref[:, cells] = (wet * (e + rate * e + t_ref[:, cells])).astype(bf16)
    high, low = split2(kmap)
    pair = jnp.concatenate([high.astype(f32), low.astype(f32)], axis=0).astype(bf16)
    stokes = dot(pair, upd_ref[...])
    bands = 2 * NBAND
    stokes = stokes[:bands] + stokes[bands:]
    stress = jnp.concatenate(
        [jnp.concatenate([stress[y][i] for y in range(rows)], axis=1) for i in range(2)], axis=0
    )
    return jnp.concatenate([stress, stokes], axis=0)


def pick(fields, send, outs):
    to_even, to_odd, own = outs
    slot = send.shape[1]
    index = jnp.concatenate([send[j : j + 1] for j in range(3)], axis=1)
    cell = lax.broadcasted_iota(jnp.int32, (fields.shape[1], 3 * slot), 0)
    hot = jnp.where(cell == index, 1.0, 0.0).astype(bf16)
    slots = dot(fields.astype(bf16), hot)
    even = is_even(lax.axis_index("row"))
    south, north = slots[:, :slot], slots[:, 2 * slot :]
    to_even[...] = jnp.where(even, north, south).astype(bf16)
    to_odd[...] = jnp.where(even, south, north).astype(bf16)
    own[...] = slots[:, slot : 2 * slot].astype(bf16)


def gather_slots(got_even, got_odd, own, rows):
    row = lax.axis_index("row")
    even = is_even(row)
    a, b = got_even[...].astype(f32), got_odd[...].astype(f32)
    north = jnp.where(row == rows - 1, 0.0, jnp.where(even, a, b))
    south = jnp.where(row == 0, 0.0, jnp.where(even, b, a))
    return jnp.concatenate([north, own[...].astype(f32), south], axis=1).astype(bf16)


def k_wave_first(
    nfreq,
    spec_ref, wind_ref, cur_ref, wet_ref, inter_ref, rate_ref, gain_ref, smap_ref, kmap_ref, trig_ref, send_ref,
    upd_ref, to_even, to_odd, own,
    ef, eb, t, q,
):
    rows, lanes = wet_ref.shape
    spec = inter_ref.shape[0]
    ef[...] = spec_ref[...].astype(f32)
    for y in range(rows):
        eb[:, y * lanes : (y + 1) * lanes] = ef[pl.ds(y, spec, stride=rows), :].astype(bf16)
    transfer(inter_ref[...], smap_ref[...], rate_ref, eb[...], t, q, nfreq)
    fields = wave_finish(
        lambda y: ef[pl.ds(y, spec, stride=rows), :],
        t, q, wind_ref,
        lambda i, y: cur_ref[i, y : y + 1, :],
        wet_ref, rate_ref, gain_ref, kmap_ref[...], trig_ref, upd_ref, nfreq,
    )
    pick(fields, send_ref[...], (to_even, to_odd, own))


def k_transfer(nfreq, upd_ref, inter_ref, smap_ref, rate_ref, t_ref, q_ref):
    transfer(inter_ref[...], smap_ref[...], rate_ref, upd_ref[...], t_ref, q_ref, nfreq)


def k_wave_next(
    nfreq, n_row,
    got_even, got_odd, got_own, recv_ref, old_ref, t_ref, q_ref, wind_ref, wet_ref, rate_ref, gain_ref, kmap_ref, trig_ref, send_ref,
    upd_ref, to_even, to_odd, own,
    cur,
):
    lanes = wet_ref.shape[1]
    slots = gather_slots(got_even, got_odd, got_own, n_row)
    cur[...] = dot(slots, recv_ref[...])
    fields = wave_finish(
        lambda y: old_ref[:, y * lanes : (y + 1) * lanes].astype(f32),
        t_ref, q_ref, wind_ref,
        lambda i, y: cur[i : i + 1, y * lanes : (y + 1) * lanes],
        wet_ref, rate_ref, gain_ref, kmap_ref[...], trig_ref, upd_ref, nfreq,
    )
    pick(fields, send_ref[...], (to_even, to_odd, own))


def k_spectra_out(rows, upd_ref, out_ref, wide):
    spec = upd_ref.shape[0]
    lanes = out_ref.shape[1]
    for y in range(rows):
        wide[pl.ds(y, spec, stride=rows), :] = upd_ref[:, y * lanes : (y + 1) * lanes].astype(f32)
    out_ref[...] = wide[...].astype(bf16)


def k_current_out(n_row, got_even, got_odd, own, recv_ref, out_ref):
    rows, lanes = out_ref.shape[1:]
    cur = dot(gather_slots(got_even, got_odd, own, n_row), recv_ref[...])
    for i in range(3):
        for y in range(rows):
            out_ref[i, y : y + 1, :] = cur[i : i + 1, y * lanes : (y + 1) * lanes]


def k_force(
    n_row, lev, pad,
    got_even, got_odd, own, recv_ref, vel_ref, wet_ref, cor_ref, tau_ref, prof_ref,
    forced_ref, row_even, row_odd, col_even, col_odd,
    fs,
):
    oy, ox = wet_ref.shape
    planes = 2 * lev
    forcing = dot(gather_slots(got_even, got_odd, own, n_row), recv_ref[...])
    nf = forcing.shape[0]
    for y in range(oy):
        fs[y * nf : (y + 1) * nf, :] = forcing[:, y * ox : (y + 1) * ox]
    field = [fs[pl.ds(i, oy, stride=nf), :] for i in range(nf)]
    wet = wet_ref[...].astype(f32)
    cor = cor_ref[...]
    along = [cor * field[i] for i in range(2, nf)]
    lane = lax.broadcasted_iota(jnp.int32, (oy, ox), 1)
    east = jnp.zeros((oy, ox), f32)
    west = jnp.zeros((oy, ox), f32)
    for i in range(planes):
        c, l = divmod(i, lev)
        accel = tau_ref[l] * field[c]
        for b in range(NBAND):
            term = prof_ref[b, l] * along[2 * b + 1 - c]
            accel = accel + term if c == 0 else accel - term
        value = wet * (vel_ref[i * oy : (i + 1) * oy, :] + accel)
        forced_ref[i * oy : (i + 1) * oy, :] = value
        here = lane == i
        west = jnp.where(here, pltpu.roll(value, i, 1) if i else value, west)
        east = jnp.where(here, pltpu.roll(value, (i + 1) % ox, 1), east)
    bottom = forced_ref[pl.ds(0, planes, stride=oy), :]
    top = forced_ref[pl.ds(oy - 1, planes, stride=oy), :]
    even = is_even(lax.axis_index("row"))
    row_even[...] = jnp.where(even, top, bottom).astype(bf16)
    row_odd[...] = jnp.where(even, bottom, top).astype(bf16)
    even = is_even(lax.axis_index("col"))
    col_even[:planes, :] = top.astype(bf16)
    col_odd[:planes, :] = top.astype(bf16)
    filler = jnp.zeros((16 - oy, ox), f32)
    col_even[pad:, :] = jnp.concatenate([jnp.where(even, east, west), filler], 0).astype(bf16)
    col_odd[pad:, :] = jnp.concatenate([jnp.where(even, west, east), filler], 0).astype(bf16)


def k_smooth(
    n_row, n_col, lev, pad, whole,
    forced_ref, got_row_even, got_row_odd, got_col_even, got_col_odd, line_ref, fold_ref, eta_ref, wet_ref, thick_ref, mix_ref, send_ref,
    smooth_ref, eta_out, to_even, to_odd, own,
    north, south, bs,
):
    oy, ox = wet_ref.shape
    planes = 2 * lev
    row, col = lax.axis_index("row"), lax.axis_index("col")
    even = is_even(row)
    a, b = got_row_even[...].astype(f32), got_row_odd[...].astype(f32)
    if whole:
        pieces = [(line_ref[t * planes : (t + 1) * planes, :], t) for t in range(n_col)]
    else:
        top = forced_ref[pl.ds(oy - 1, planes, stride=oy), :].astype(bf16)
        pair_even = jnp.where(is_even(col), col + 1, col - 1)
        pair_odd = lax.rem(jnp.where(is_even(col), col - 1, col + 1) + n_col, n_col)
        pieces = [
            (top, col),
            (got_col_even[:planes, :], pair_even),
            (got_col_odd[:planes, :], pair_odd),
            (got_row_odd[...], lax.rem(col + n_col // 2, n_col)),
        ]
    cell = lax.broadcasted_iota(jnp.int32, (ox, ox), 0)
    across = None
    for piece, tile in pieces:
        hot = jnp.where(cell == fold_ref[...] - tile * ox, 1.0, 0.0).astype(bf16)
        part = dot(piece, hot)
        across = part if across is None else across + part
    north[...] = jnp.where(row == n_row - 1, -across, jnp.where(even, a, b))
    south[...] = jnp.where(row == 0, 0.0, jnp.where(even, b, a))
    even = is_even(col)
    a = got_col_even[pad:, :].astype(f32)[:oy]
    b = got_col_odd[pad:, :].astype(f32)[:oy]
    east_col = jnp.where(even, a, b)
    west_col = jnp.where(even, b, a)
    wet = wet_ref[...].astype(f32)
    lane = lax.broadcasted_iota(jnp.int32, (oy, ox), 1)
    line = lax.broadcasted_iota(jnp.int32, (oy, ox), 0)
    is_top, is_bottom = line == oy - 1, line == 0
    is_east, is_west = lane == ox - 1, lane == 0
    across_u = jnp.zeros((oy, ox), f32)
    across_v = jnp.zeros((oy, ox), f32)
    surface = []
    for i in range(planes):
        c, l = divmod(i, lev)
        here = forced_ref[i * oy : (i + 1) * oy, :]
        up = jnp.where(is_top, north[i : i + 1, :], pltpu.roll(here, oy - 1, 0))
        down = jnp.where(is_bottom, south[i : i + 1, :], pltpu.roll(here, 1, 0))
        right = jnp.where(is_east, pltpu.roll(east_col, (ox - 1 - i) % ox, 1), pltpu.roll(here, ox - 1, 1))
        left = jnp.where(is_west, pltpu.roll(west_col, (ox - i) % ox, 1), pltpu.roll(here, 1, 1))
        smooth = wet * (here + viscous * (up + down + right + left - 4.0 * here))
        smooth_ref[i * oy : (i + 1) * oy, :] = smooth
        if l == 0:
            surface.append(mix_ref[0, 0] * smooth)
        else:
            surface[c] = surface[c] + mix_ref[0, l] * smooth
        if c == 0:
            across_u = across_u + thick_ref[l] * (right - left)
        else:
            across_v = across_v + thick_ref[l] * (up - down)
    eta = wet * (eta_ref[...] - surface_rate * (0.5 * across_u + 0.5 * across_v))
    eta_out[...] = eta
    bs[: oy, :] = surface[0]
    bs[oy : 2 * oy, :] = surface[1]
    bs[2 * oy : 3 * oy, :] = eta
    bs[3 * oy :, :] = jnp.zeros((5 * oy, ox), f32)
    back = jnp.concatenate([bs[pl.ds(y, 8, stride=oy), :] for y in range(oy)], axis=1)
    pick(back, send_ref[...], (to_even, to_odd, own))


def k_mix(lev, oy, smooth_ref, mix_ref, vel_ref):
    group = 6
    for first in range(0, lev, group):
        levels = range(first, min(first + group, lev))
        total = {}
        for m in range(lev):
            u = smooth_ref[m * oy : (m + 1) * oy, :]
            v = smooth_ref[(lev + m) * oy : (lev + m + 1) * oy, :]
            for l in levels:
                w = mix_ref[l, m]
                total[l, 0] = w * u if m == 0 else total[l, 0] + w * u
                total[l, 1] = w * v if m == 0 else total[l, 1] + w * v
        for l in levels:
            vel_ref[l * oy : (l + 1) * oy, :] = total[l, 0]
            vel_ref[(lev + l) * oy : (lev + l + 1) * oy, :] = total[l, 1]


def pairings(n_row, n_col):
    def place(r, c):
        return r * n_col + c

    row_even = [(place(r, c), place(r ^ 1, c)) for r in range(n_row) for c in range(n_col)]
    row_odd = []
    for r in range(n_row):
        other = r + 1 if r % 2 else r - 1
        for c in range(n_col):
            if 0 <= other < n_row:
                row_odd.append((place(r, c), place(other, c)))
            else:
                row_odd.append((place(r, c), place(r, (c + n_col // 2) % n_col)))
    col_even = [(c, c ^ 1) for c in range(n_col)]
    col_odd = [(c, (c + 1 if c % 2 else c - 1) % n_col) for c in range(n_col)]
    return row_even, row_odd, col_even, col_odd


def shards(
    n_row,
    n_col,
    spectra,
    wind,
    wave_current,
    wave_wet,
    interaction,
    input_rate,
    eta_gain,
    stress_map,
    stokes_map,
    ocean_vel,
    ocean_eta,
    ocean_wet,
    coriolis,
    tau_profile,
    stokes_profile,
    thickness,
    mix_inverse,
    fold_index,
    wave_send,
    ocean_recv,
    ocean_send,
    wave_recv,
):
    spec, rows, lanes = spectra.shape
    cells = rows * lanes
    oy, ox = ocean_eta.shape
    lev = ocean_vel.shape[1]
    planes = 2 * lev
    nfreq = input_rate.shape[0]
    slot = wave_send.shape[-1]
    pad = -(-planes // 16) * 16
    heading = ((np.arange(NDIR)).astype(np.float32) + 0.5) * np.float32(2.0 * math.pi / NDIR)
    trig = np.concatenate([np.cos(heading), np.sin(heading)]).astype(np.float32)
    trig = jnp.asarray(np.repeat(trig[:, None], lanes, axis=1))
    pairs = pairings(n_row, n_col)
    both = ("row", "col")
    ocean_w = ocean_recv.reshape(3 * slot, oy * ox)
    wave_w = wave_recv.reshape(3 * slot, cells)
    wsend, osend = wave_send.reshape(3, slot), ocean_send.reshape(3, slot)
    fold = fold_index.reshape(1, ox)
    velocity = ocean_vel.reshape(planes * oy, ox)
    eta = ocean_eta
    whole = n_col != 4

    def trade_rows(to_even, to_odd):
        return lax.ppermute(to_odd, both, pairs[1]), lax.ppermute(to_even, both, pairs[0])

    slots_out = [((8, slot), bf16)] * 3
    wave_outs = [((spec, cells), bf16)] + slots_out
    for step in range(STEPS):
        if step == 0:
            updated, to_even, to_odd, own = call(
                functools.partial(k_wave_first, nfreq),
                wave_outs,
                [VMEM] * 5 + [SMEM] * 2 + [VMEM] * 4,
                [
                    pltpu.VMEM((spec * rows, lanes), f32),
                    pltpu.VMEM((spec, cells), bf16),
                    pltpu.VMEM((spec, cells), f32),
                    pltpu.VMEM((2 * NDIR, cells), f32),
                ],
                "wave_first",
            )(
                spectra.reshape(spec * rows, lanes), wind, wave_current, wave_wet, interaction,
                input_rate, eta_gain, stress_map, stokes_map, trig, wsend,
            )
        else:
            updated, to_even, to_odd, own = call(
                functools.partial(k_wave_next, nfreq, n_row),
                wave_outs,
                [VMEM] * 9 + [SMEM] * 2 + [VMEM] * 3,
                [pltpu.VMEM((8, cells), f32)],
                "wave_next",
            )(
                got_even, got_odd, own, wave_w, updated, moved, q, wind, wave_wet,
                input_rate, eta_gain, stokes_map, trig, wsend,
            )
        got_odd, got_even = trade_rows(to_even, to_odd)
        if step + 1 < STEPS:
            moved, q = call(
                functools.partial(k_transfer, nfreq),
                [((spec, cells), f32), ((2 * NDIR, cells), f32)],
                [VMEM] * 3 + [SMEM],
                name="transfer",
            )(updated, interaction, stress_map, input_rate)
        else:
            (spectra_out,) = call(
                functools.partial(k_spectra_out, rows),
                [((spec * rows, lanes), bf16)],
                [VMEM],
                [pltpu.VMEM((spec * rows, lanes), f32)],
                "spectra_out",
            )(updated)
        forced, row_even, row_odd, col_even, col_odd = call(
            functools.partial(k_force, n_row, lev, pad),
            [((planes * oy, ox), f32)] + [((planes, ox), bf16)] * 2 + [((pad + 16, ox), bf16)] * 2,
            [VMEM] * 7 + [SMEM] * 2,
            [pltpu.VMEM((8 * oy, ox), f32)],
            "force",
        )(got_even, got_odd, own, ocean_w, velocity, ocean_wet, coriolis, tau_profile, stokes_profile)
        got_row_odd, got_row_even = trade_rows(row_even, row_odd)
        got_col_odd = lax.ppermute(col_odd, "col", pairs[3])
        got_col_even = lax.ppermute(col_even, "col", pairs[2])
        if whole:
            top_line = lax.all_gather(col_even[:planes], "col", axis=0, tiled=True)
        else:
            top_line = fold
        smooth, eta, to_even, to_odd, own = call(
            functools.partial(k_smooth, n_row, n_col, lev, pad, whole),
            [((planes * oy, ox), f32), ((oy, ox), f32)] + slots_out,
            [VMEM] * 9 + [SMEM] * 2 + [VMEM],
            [
                pltpu.VMEM((planes, ox), f32),
                pltpu.VMEM((planes, ox), f32),
                pltpu.VMEM((8 * oy, ox), f32),
            ],
            "smooth",
        )(
            forced, got_row_even, got_row_odd, got_col_even, got_col_odd, top_line, fold, eta, ocean_wet,
            thickness, mix_inverse, osend,
        )
        got_odd, got_even = trade_rows(to_even, to_odd)
        (velocity,) = call(
            functools.partial(k_mix, lev, oy), [((planes * oy, ox), f32)], [VMEM, SMEM], name="mix"
        )(smooth, mix_inverse)
    (current,) = call(
        functools.partial(k_current_out, n_row), [((3, rows, lanes), f32)], [VMEM] * 4, name="current_out"
    )(got_even, got_odd, own, wave_w)
    return (
        spectra_out.reshape(spec, rows, lanes),
        velocity.reshape(2, lev, oy, ox),
        eta,
        current,
    )


def solution(mesh):
    n_row, n_col = mesh.shape["row"], mesh.shape["col"]
    in_specs = (
        P(None, "row", "col"),
        P(None, "row", "col"),
        P(None, "row", "col"),
        P("row", "col"),
        P(),
        P(),
        P(),
        P(),
        P(),
        P(None, None, "row", "col"),
        P("row", "col"),
        P("row", "col"),
        P("row", "col"),
        P(),
        P(),
        P(),
        P(),
        P("col"),
        P("row", "col", None, None),
        P("row", "col", None, None, None),
        P("row", "col", None, None),
        P("row", "col", None, None, None),
    )
    out_specs = (
        P(None, "row", "col"),
        P(None, None, "row", "col"),
        P("row", "col"),
        P(None, "row", "col"),
    )
    body = functools.partial(shards, n_row, n_col)
    return jax.shard_map(body, mesh=mesh, in_specs=in_specs, out_specs=out_specs, check_vma=False)
```

time: 99.1 us -> 62.7 us (0.63)
  Pallas kernels: 0 us -> 27.1 us
  starting transfers between devices: 43.4 us -> 20 us
  blocking collectives: 12.8 us -> 0 us
  local copies, waits for them, and re-layouts: 17.4 us -> 5.37 us
  matrix products: 11.1 us -> 0 us
  other arithmetic: 5.19 us -> 0 us
  waiting for transfers between devices: 6.6 us -> 9.04 us
    pallas_call x0 -> x11, Pallas kernels: none -> 27.1 us  [the longest x2 4.88 us: shards(): call(functools.partial(k_mix, lev, oy), [((planes * oy, ox), f32)], [VMEM...]
    ppermute x16, starting transfers between devices: 43.4 us -> 20 us  [the longest x6 12 us: trade_rows(): lax.ppermute(to_even, both, pairs[0])]
    all_gather x2 -> x0, blocking collectives: 12.8 us -> none  [edge_cells(): piece = lax.all_gather(top_line, 'col', axis=2, tiled=True)]
    dot_general x14 -> x0, matrix products: 11.1 us -> none  [the longest x2 4.51 us: wave_cells(): stress = jnp.dot(stress_map, growth * energy_wide, precision=highest)]
    gather x12 -> x0, local copies, waits for them, and re-layouts: 5.17 us -> none  [the longest x8 3.52 us: route_fields(): slot_rows = jnp.moveaxis(jnp.take(fields, send_rows, axis=1), 1, 0)]
    scatter x4 -> x0, local copies, waits for them, and re-layouts: 5.03 us -> none  [edge_cells(): padded.at[:, :, -1, 1:-1].set(north_row).at[:, :, 0, 1:-1].set(south_row)]
    unnamed x42 -> x36, local copies, waits for them, and re-layouts: 1.57 us -> 5.37 us
    ppermute x16, waiting for transfers between devices: 6.6 us -> 9.04 us  [the longest x6 6.02 us: trade_rows(): lax.ppermute(to_odd, both, pairs[1])]
  transfers between devices with their start and end apart: 16 -> 16, of which waited for: 6 -> 8; matrix products, arithmetic and copies ran while one was open for 5% -> 1% of each run, Pallas kernels for 0% -> 16%
where the time goes in v1:
time: 62.7 us; the launch traced here: 62.2 us
  Pallas kernels  27.1 us (43%)
  starting transfers between devices  20 us (32%)
  waiting for transfers between devices  9.04 us (14%)
  local copies, waits for them, and re-layouts  5.37 us (9%)
  between operations  0.74 us (1%)
    ppermute x6, starting transfers between devices, trade_rows(): lax.ppermute(to_even, both, pairs[0])  12 us
    ppermute x6, waiting for transfers between devices, trade_rows(): lax.ppermute(to_odd, both, pairs[1])  6.02 us
    ppermute x6, starting transfers between devices, trade_rows(): lax.ppermute(to_odd, both, pairs[1])  5.54 us
    unnamed x36, local copies, waits for them, and re-layouts  5.37 us
    pallas_call x2, Pallas kernels, shards(): call(functools.partial(k_mix, lev, oy), [((planes * oy, ox), f32)], [VMEM...  4.88 us
    pallas_call x2, Pallas kernels, shards(): call(functools.partial(k_smooth, n_row, n_col, lev, pad, whole), [((plane...  4.65 us
    pallas_call x2, Pallas kernels, shards(): call(functools.partial(k_force, n_row, lev, pad), [((planes * oy, ox), f3...  4.28 us
    pallas_call x1, Pallas kernels, shards(): call(functools.partial(k_wave_first, nfreq), wave_outs, [VMEM] * 5 + [SME...  3.23 us
  transfers between devices with their start and end apart: 16, of which 8 were waited for; matrix products, arithmetic and copies ran while one was open for 1% of the time, Pallas kernels for 16%

profile of v1, /device:TPU:0, one launch (start us, length us, event | category | flops | bytes accessed | tf_op | source)
XLA Modules:
  0.0 62.2 jit_solution(1936318824019283478)
XLA Ops:
  0.6 1.3 %copy.32 = s32[1,1,3,64]{3,2,1,0:T(4,128)} copy(s32[1,1,3,64]{3,1,2,0:T(1,128)} %param.41) | data formatting | bytes 1536
  1.9 3.2 %wave_first.1 = (bf16[600,512]{1,0:T(8,128)(2,1)}, bf16[8,64]{1,0:T(8,128)(2,1)}, bf16[8,64]{1,0:T(8,128)(2,1)}, bf16[8,64]{1,0:T(8,128)(2,1)}) custom-call(bf16[2400,128]{1,0:T(8,128)(2,1)} %bitcast.17, f32[2,4,128]{2,1,0:T(4,128)} %wind_ref.3, f32[3,4,128]{2,1,0:T(4,128)} %cur_ref.1, s32[4,128]{1,0:T(4,128)} %wet_ref.9, bf16[600,600]{1,0:T(8,128)(2,1)} %inter_ref.3, ...), custom_call_target="tpu_custom_call" | custom-call | tf_op jit(solution)/shard_map/wave_first/pallas_call | solution.py:395
  5.1 3.0 %collective-permute-start = (bf16[8,64]{1,0:T(8,128)(2,1)}, bf16[8,64]{1,0:T(8,128)(2,1)S(1)}, u32[]{:S(2)}, u32[]{:S(2)}) collective-permute-start(bf16[8,64]{1,0:T(8,128)(2,1)} %get-tuple-element.34), channel_id=1, source_target_pairs={{0,4},{1,5},{2,6},{3,7},{4,0},{5,1},{6,2},{7,3},{8,12},{9,13},{10,... | collective-permute-start | bytes 3080 | tf_op jit(solution)/shard_map/ppermute | solution.py:389
  8.1 1.5 %collective-permute-start.1 = (bf16[8,64]{1,0:T(8,128)(2,1)}, bf16[8,64]{1,0:T(8,128)(2,1)S(1)}, u32[]{:S(2)}, u32[]{:S(2)}) collective-permute-start(bf16[8,64]{1,0:T(8,128)(2,1)} %get-tuple-element.35), channel_id=1, source_target_pairs={{0,2},{1,3},{2,0},{3,1},{4,8},{5,9},{6,10},{7,11},{8,4},{9,5},{10,... | collective-permute-start | bytes 3080 | tf_op jit(solution)/shard_map/ppermute | solution.py:389
  9.9 2.0 %collective-permute-done.1.got_odd = bf16[8,64]{1,0:T(8,128)(2,1)S(1)} collective-permute-done((bf16[8,64]{1,0:T(8,128)(2,1)}, bf16[8,64]{1,0:T(8,128)(2,1)S(1)}, u32[]{:S(2)}, u32[]{:S(2)}) %collective-permute-start.1) | collective-permute-done | bytes 1056 | tf_op jit(solution)/shard_map/ppermute | solution.py:389
  11.9 0.6 copy-done.14
  12.5 2.1 %force.2 = (f32[480,128]{1,0:T(8,128)}, bf16[60,128]{1,0:T(8,128)(2,1)}, bf16[60,128]{1,0:T(8,128)(2,1)}, bf16[80,128]{1,0:T(8,128)(2,1)}, bf16[80,128]{1,0:T(8,128)(2,1)}) custom-call(bf16[8,64]{1,0:T(8,128)(2,1)} %copy-done.11, bf16[8,64]{1,0:T(8,128)(2,1)} %copy-done.14, bf16[8,64]{1,0:T(8,128)(2,1)} %get-tuple-element.36.own, ...), custom_call_target="tpu_custom_call" | custom-call | tf_op jit(solution)/shard_map/force/pallas_call | solution.py:437
  14.7 1.6 %collective-permute-start.5 = (bf16[80,128]{1,0:T(8,128)(2,1)}, bf16[80,128]{1,0:T(8,128)(2,1)S(1)}, u32[]{:S(2)}, u32[]{:S(2)}) collective-permute-start(bf16[80,128]{1,0:T(8,128)(2,1)} %get-tuple-element.41), channel_id=1, source_target_pairs={{0,3},{1,2},{2,1},{3,0},{4,7},{5,6},{6,5},{7,4},{8,11},{9,10},{10,... | collective-permute-start | bytes 61448 | tf_op jit(solution)/shard_map/ppermute | solution.py:445
  16.3 1.4 %collective-permute-start.2 = (bf16[60,128]{1,0:T(8,128)(2,1)}, bf16[60,128]{1,0:T(8,128)(2,1)S(1)}, u32[]{:S(2)}, u32[]{:S(2)}) collective-permute-start(bf16[60,128]{1,0:T(8,128)(2,1)} %get-tuple-element.38), channel_id=1, source_target_pairs={{0,4},{1,5},{2,6},{3,7},{4,0},{5,1},{6,2},{7,3},{8,12},{9,13},{10,... | collective-permute-start | bytes 46088 | tf_op jit(solution)/shard_map/ppermute | solution.py:389
  17.8 0.6 copy.31
  18.4 1.8 %collective-permute-done.2.got_row_even = bf16[60,128]{1,0:T(8,128)(2,1)S(1)} collective-permute-done((bf16[60,128]{1,0:T(8,128)(2,1)}, bf16[60,128]{1,0:T(8,128)(2,1)S(1)}, u32[]{:S(2)}, u32[]{:S(2)}) %collective-permute-start.2) | collective-permute-done | bytes 15392 | tf_op jit(solution)/shard_map/ppermute | solution.py:389
  20.2 1.4 %collective-permute-done.3.got_row_odd = bf16[60,128]{1,0:T(8,128)(2,1)S(1)} collective-permute-done((bf16[60,128]{1,0:T(8,128)(2,1)}, bf16[60,128]{1,0:T(8,128)(2,1)S(1)}, u32[]{:S(2)}, u32[]{:S(2)}) %collective-permute-start.3) | collective-permute-done | bytes 15392 | tf_op jit(solution)/shard_map/ppermute | solution.py:389
  22.2 2.3 %smooth.2 = (f32[480,128]{1,0:T(8,128)}, f32[8,128]{1,0:T(8,128)}, bf16[8,64]{1,0:T(8,128)(2,1)}, bf16[8,64]{1,0:T(8,128)(2,1)}, bf16[8,64]{1,0:T(8,128)(2,1)}) custom-call(f32[480,128]{1,0:T(8,128)} %get-tuple-element.37.forced_ref, bf16[60,128]{1,0:T(8,128)(2,1)} %copy-done.5, bf16[60,128]{1,0:T(8,128)(2,1)} %copy-done.7, bf16[80,128]{1,0:T(8,128)(2,1)} %copy-done.1, ...), custom_call_target="tpu_custom_call" | custom-call | tf_op jit(solution)/shard_map/smooth/pallas_call | solution.py:451
  24.6 1.5 %collective-permute-start.6 = (bf16[8,64]{1,0:T(8,128)(2,1)}, bf16[8,64]{1,0:T(8,128)(2,1)S(1)}, u32[]{:S(2)}, u32[]{:S(2)}) collective-permute-start(bf16[8,64]{1,0:T(8,128)(2,1)} %get-tuple-element.42), channel_id=1, source_target_pairs={{0,4},{1,5},{2,6},{3,7},{4,0},{5,1},{6,2},{7,3},{8,12},{9,13},{10,... | collective-permute-start | bytes 3080 | tf_op jit(solution)/shard_map/ppermute | solution.py:389
  26.6 3.0 %transfer.1 = (f32[600,512]{1,0:T(8,128)}, f32[48,512]{1,0:T(8,128)}) custom-call(bf16[600,512]{1,0:T(8,128)(2,1)} %get-tuple-element.45.upd_ref.old_ref, bf16[600,600]{1,0:T(8,128)(2,1)} %inter_ref.3, f32[2,600]{1,0:T(2,128)} %smap_ref.3, f32[25]{0:T(128)} %rate_ref.5), custom_call_target="tpu_custom_call" | custom-call | tf_op jit(solution)/shard_map/transfer/pallas_call | solution.py:423
  30.5 3.2 %wave_next.1 = (bf16[600,512]{1,0:T(8,128)(2,1)}, bf16[8,64]{1,0:T(8,128)(2,1)}, bf16[8,64]{1,0:T(8,128)(2,1)}, bf16[8,64]{1,0:T(8,128)(2,1)}) custom-call(bf16[8,64]{1,0:T(8,128)(2,1)} %copy-done.8, bf16[8,64]{1,0:T(8,128)(2,1)} %copy-done.9, bf16[8,64]{1,0:T(8,128)(2,1)} %get-tuple-element.44.got_own, bf16[192,512]{1,0:T(8,128)(2,1)} %bitcast.15, ...), custom_call_target="tpu_custom_call" | custom-call | tf_op jit(solution)/shard_map/wave_next/pallas_call | solution.py:411
  33.7 3.2 %collective-permute-start.8 = (bf16[8,64]{1,0:T(8,128)(2,1)}, bf16[8,64]{1,0:T(8,128)(2,1)S(1)}, u32[]{:S(2)}, u32[]{:S(2)}) collective-permute-start(bf16[8,64]{1,0:T(8,128)(2,1)} %get-tuple-element.49), channel_id=1, source_target_pairs={{0,4},{1,5},{2,6},{3,7},{4,0},{5,1},{6,2},{7,3},{8,12},{9,13},{10,... | collective-permute-start | bytes 3080 | tf_op jit(solution)/shard_map/ppermute | solution.py:389
  37.4 2.4 %mix.2.vel_ref = f32[480,128]{1,0:T(8,128)} custom-call(f32[480,128]{1,0:T(8,128)} %get-tuple-element.52.smooth_ref, f32[30,30]{1,0:T(8,128)} %mix_ref.7), custom_call_target="tpu_custom_call" | custom-call | tf_op jit(solution)/shard_map/mix/pallas_call | solution.py:466
  39.8 0.8 %collective-permute-done.9.got_odd = bf16[8,64]{1,0:T(8,128)(2,1)S(1)} collective-permute-done((bf16[8,64]{1,0:T(8,128)(2,1)}, bf16[8,64]{1,0:T(8,128)(2,1)S(1)}, u32[]{:S(2)}, u32[]{:S(2)}) %collective-permute-start.9) | collective-permute-done | bytes 1056 | tf_op jit(solution)/shard_map/ppermute | solution.py:389
  40.7 0.6 copy-done.13
  41.3 2.1 %force.3 = (f32[480,128]{1,0:T(8,128)}, bf16[60,128]{1,0:T(8,128)(2,1)}, bf16[60,128]{1,0:T(8,128)(2,1)}, bf16[80,128]{1,0:T(8,128)(2,1)}, bf16[80,128]{1,0:T(8,128)(2,1)}) custom-call(bf16[8,64]{1,0:T(8,128)(2,1)} %copy-done.10, bf16[8,64]{1,0:T(8,128)(2,1)} %copy-done.13, bf16[8,64]{1,0:T(8,128)(2,1)} %get-tuple-element.51.own, ...), custom_call_target="tpu_custom_call" | custom-call | tf_op jit(solution)/shard_map/force/pallas_call | solution.py:437
  43.4 0.8 %collective-permute-start.13 = (bf16[80,128]{1,0:T(8,128)(2,1)}, bf16[80,128]{1,0:T(8,128)(2,1)S(1)}, u32[]{:S(2)}, u32[]{:S(2)}) collective-permute-start(bf16[80,128]{1,0:T(8,128)(2,1)} %get-tuple-element.57), channel_id=1, source_target_pairs={{0,3},{1,2},{2,1},{3,0},{4,7},{5,6},{6,5},{7,4},{8,11},{9,10},{10,... | collective-permute-start | bytes 61448 | tf_op jit(solution)/shard_map/ppermute | solution.py:445
  44.2 1.5 %collective-permute-start.10 = (bf16[60,128]{1,0:T(8,128)(2,1)}, bf16[60,128]{1,0:T(8,128)(2,1)S(1)}, u32[]{:S(2)}, u32[]{:S(2)}) collective-permute-start(bf16[60,128]{1,0:T(8,128)(2,1)} %get-tuple-element.54), channel_id=1, source_target_pairs={{0,4},{1,5},{2,6},{3,7},{4,0},{5,1},{6,2},{7,3},{8,12},{9,13},{10,... | collective-permute-start | bytes 46088 | tf_op jit(solution)/shard_map/ppermute | solution.py:389
  45.7 1.5 %collective-permute-start.11 = (bf16[60,128]{1,0:T(8,128)(2,1)}, bf16[60,128]{1,0:T(8,128)(2,1)S(1)}, u32[]{:S(2)}, u32[]{:S(2)}) collective-permute-start(bf16[60,128]{1,0:T(8,128)(2,1)} %get-tuple-element.55), channel_id=1, source_target_pairs={{0,2},{1,3},{2,0},{3,1},{4,8},{5,9},{6,10},{7,11},{8,4},{9,5},{10,... | collective-permute-start | bytes 46088 | tf_op jit(solution)/shard_map/ppermute | solution.py:389
  47.2 0.9 %collective-permute-done.10.got_row_even = bf16[60,128]{1,0:T(8,128)(2,1)S(1)} collective-permute-done((bf16[60,128]{1,0:T(8,128)(2,1)}, bf16[60,128]{1,0:T(8,128)(2,1)S(1)}, u32[]{:S(2)}, u32[]{:S(2)}) %collective-permute-start.10) | collective-permute-done | bytes 15392 | tf_op jit(solution)/shard_map/ppermute | solution.py:389
  48.1 1.5 %collective-permute-done.11.got_row_odd = bf16[60,128]{1,0:T(8,128)(2,1)S(1)} collective-permute-done((bf16[60,128]{1,0:T(8,128)(2,1)}, bf16[60,128]{1,0:T(8,128)(2,1)S(1)}, u32[]{:S(2)}, u32[]{:S(2)}) %collective-permute-start.11) | collective-permute-done | bytes 15392 | tf_op jit(solution)/shard_map/ppermute | solution.py:389
  50.3 2.3 %smooth.3 = (f32[480,128]{1,0:T(8,128)}, f32[8,128]{1,0:T(8,128)}, bf16[8,64]{1,0:T(8,128)(2,1)}, bf16[8,64]{1,0:T(8,128)(2,1)}, bf16[8,64]{1,0:T(8,128)(2,1)}) custom-call(f32[480,128]{1,0:T(8,128)} %get-tuple-element.53.forced_ref, bf16[60,128]{1,0:T(8,128)(2,1)} %copy-done.4, bf16[60,128]{1,0:T(8,128)(2,1)} %copy-done.6, bf16[80,128]{1,0:T(8,128)(2,1)} %copy-done, ...), custom_call_target="tpu_custom_call" | custom-call | tf_op jit(solution)/shard_map/smooth/pallas_call | solution.py:451
  52.6 1.4 %collective-permute-start.14 = (bf16[8,64]{1,0:T(8,128)(2,1)}, bf16[8,64]{1,0:T(8,128)(2,1)S(1)}, u32[]{:S(2)}, u32[]{:S(2)}) collective-permute-start(bf16[8,64]{1,0:T(8,128)(2,1)} %get-tuple-element.61), channel_id=1, source_target_pairs={{0,4},{1,5},{2,6},{3,7},{4,0},{5,1},{6,2},{7,3},{8,12},{9,13},{10,... | collective-permute-start | bytes 3080 | tf_op jit(solution)/shard_map/ppermute | solution.py:389
  54.0 1.3 %collective-permute-start.15 = (bf16[8,64]{1,0:T(8,128)(2,1)}, bf16[8,64]{1,0:T(8,128)(2,1)S(1)}, u32[]{:S(2)}, u32[]{:S(2)}) collective-permute-start(bf16[8,64]{1,0:T(8,128)(2,1)} %get-tuple-element.62), channel_id=1, source_target_pairs={{0,2},{1,3},{2,0},{3,1},{4,8},{5,9},{6,10},{7,11},{8,4},{9,5},{10,... | collective-permute-start | bytes 3080 | tf_op jit(solution)/shard_map/ppermute | solution.py:389
  55.4 2.1 %spectra_out.1 = bf16[2400,128]{1,0:T(8,128)(2,1)} custom-call(bf16[600,512]{1,0:T(8,128)(2,1)} %get-tuple-element.48.upd_ref), custom_call_target="tpu_custom_call" | custom-call | tf_op jit(solution)/shard_map/spectra_out/pallas_call | solution.py:430
  57.5 2.4 %mix.3 = f32[480,128]{1,0:T(8,128)} custom-call(f32[480,128]{1,0:T(8,128)} %get-tuple-element.59.smooth_ref, f32[30,30]{1,0:T(8,128)} %mix_ref.7), custom_call_target="tpu_custom_call" | custom-call | tf_op jit(solution)/shard_map/mix/pallas_call | solution.py:466
  60.5 1.7 %current_out.1 = f32[3,4,128]{2,1,0:T(4,128)} custom-call(bf16[8,64]{1,0:T(8,128)(2,1)} %copy-done.12, bf16[8,64]{1,0:T(8,128)(2,1)} %copy-done.15, bf16[8,64]{1,0:T(8,128)(2,1)} %get-tuple-element.63.own, bf16[192,512]{1,0:T(8,128)(2,1)} %bitcast.16), custom_call_target="tpu_custom_call" | custom-call | tf_op jit(solution)/shard_map/current_out/pallas_call | solution.py:469
  (47 shorter events, 4.1 us)
Async XLA Ops:
  0.6 17.2 %copy-start.16 = (s32[1,1,3,64]{3,1,2,0:T(1,128)S(1)}, s32[1,1,3,64]{3,1,2,0:T(1,128)}, u32[]{:S(2)}) copy-start(s32[1,1,3,64]{3,1,2,0:T(1,128)} %param.43) | copy-start | bytes 2308
  5.1 4.8 %collective-permute-start = (bf16[8,64]{1,0:T(8,128)(2,1)}, bf16[8,64]{1,0:T(8,128)(2,1)S(1)}, u32[]{:S(2)}, u32[]{:S(2)}) collective-permute-start(bf16[8,64]{1,0:T(8,128)(2,1)} %get-tuple-element.34), channel_id=1, source_target_pairs={{0,4},{1,5},{2,6},{3,7},{4,0},{5,1},{6,2},{7,3},{8,12},{9,13},{10,... | collective-permute-start | bytes 3080 | tf_op jit(solution)/shard_map/ppermute | solution.py:389
  8.1 3.8 %collective-permute-start.1 = (bf16[8,64]{1,0:T(8,128)(2,1)}, bf16[8,64]{1,0:T(8,128)(2,1)S(1)}, u32[]{:S(2)}, u32[]{:S(2)}) collective-permute-start(bf16[8,64]{1,0:T(8,128)(2,1)} %get-tuple-element.35), channel_id=1, source_target_pairs={{0,2},{1,3},{2,0},{3,1},{4,8},{5,9},{6,10},{7,11},{8,4},{9,5},{10,... | collective-permute-start | bytes 3080 | tf_op jit(solution)/shard_map/ppermute | solution.py:389
  9.9 2.0 %copy-start.11 = (bf16[8,64]{1,0:T(8,128)(2,1)}, bf16[8,64]{1,0:T(8,128)(2,1)S(1)}, u32[]{:S(2)}) copy-start(bf16[8,64]{1,0:T(8,128)(2,1)S(1)} %collective-permute-done.got_even) | copy-start | bytes 3076
  11.9 0.6 copy-start.14
  14.7 7.0 %collective-permute-start.4 = (bf16[80,128]{1,0:T(8,128)(2,1)}, bf16[80,128]{1,0:T(8,128)(2,1)S(1)}, u32[]{:S(2)}, u32[]{:S(2)}) collective-permute-start(bf16[80,128]{1,0:T(8,128)(2,1)} %get-tuple-element.40), channel_id=1, source_target_pairs={{0,1},{1,0},{2,3},{3,2},{4,5},{5,4},{6,7},{7,6},{8,9},{9,8},{10,11... | collective-permute-start | bytes 61448 | tf_op jit(solution)/shard_map/ppermute | solution.py:446
  14.7 7.0 %collective-permute-start.5 = (bf16[80,128]{1,0:T(8,128)(2,1)}, bf16[80,128]{1,0:T(8,128)(2,1)S(1)}, u32[]{:S(2)}, u32[]{:S(2)}) collective-permute-start(bf16[80,128]{1,0:T(8,128)(2,1)} %get-tuple-element.41), channel_id=1, source_target_pairs={{0,3},{1,2},{2,1},{3,0},{4,7},{5,6},{6,5},{7,4},{8,11},{9,10},{10,... | collective-permute-start | bytes 61448 | tf_op jit(solution)/shard_map/ppermute | solution.py:445
  16.3 3.9 %collective-permute-start.2 = (bf16[60,128]{1,0:T(8,128)(2,1)}, bf16[60,128]{1,0:T(8,128)(2,1)S(1)}, u32[]{:S(2)}, u32[]{:S(2)}) collective-permute-start(bf16[60,128]{1,0:T(8,128)(2,1)} %get-tuple-element.38), channel_id=1, source_target_pairs={{0,4},{1,5},{2,6},{3,7},{4,0},{5,1},{6,2},{7,3},{8,12},{9,13},{10,... | collective-permute-start | bytes 46088 | tf_op jit(solution)/shard_map/ppermute | solution.py:389
  17.7 3.9 %collective-permute-start.3 = (bf16[60,128]{1,0:T(8,128)(2,1)}, bf16[60,128]{1,0:T(8,128)(2,1)S(1)}, u32[]{:S(2)}, u32[]{:S(2)}) collective-permute-start(bf16[60,128]{1,0:T(8,128)(2,1)} %get-tuple-element.39), channel_id=1, source_target_pairs={{0,2},{1,3},{2,0},{3,1},{4,8},{5,9},{6,10},{7,11},{8,4},{9,5},{10,... | collective-permute-start | bytes 46088 | tf_op jit(solution)/shard_map/ppermute | solution.py:389
  20.2 1.4 %copy-start.5 = (bf16[60,128]{1,0:T(8,128)(2,1)}, bf16[60,128]{1,0:T(8,128)(2,1)S(1)}, u32[]{:S(2)}) copy-start(bf16[60,128]{1,0:T(8,128)(2,1)S(1)} %collective-permute-done.2.got_row_even) | copy-start | bytes 46084
  21.6 0.6 copy-start.7
  21.6 0.6 copy-start.1
  21.6 0.6 copy-start.3
  24.6 5.1 %collective-permute-start.6 = (bf16[8,64]{1,0:T(8,128)(2,1)}, bf16[8,64]{1,0:T(8,128)(2,1)S(1)}, u32[]{:S(2)}, u32[]{:S(2)}) collective-permute-start(bf16[8,64]{1,0:T(8,128)(2,1)} %get-tuple-element.42), channel_id=1, source_target_pairs={{0,4},{1,5},{2,6},{3,7},{4,0},{5,1},{6,2},{7,3},{8,12},{9,13},{10,... | collective-permute-start | bytes 3080 | tf_op jit(solution)/shard_map/ppermute | solution.py:389
  26.1 3.8 %collective-permute-start.7 = (bf16[8,64]{1,0:T(8,128)(2,1)}, bf16[8,64]{1,0:T(8,128)(2,1)S(1)}, u32[]{:S(2)}, u32[]{:S(2)}) collective-permute-start(bf16[8,64]{1,0:T(8,128)(2,1)} %get-tuple-element.43), channel_id=1, source_target_pairs={{0,2},{1,3},{2,0},{3,1},{4,8},{5,9},{6,10},{7,11},{8,4},{9,5},{10,... | collective-permute-start | bytes 3080 | tf_op jit(solution)/shard_map/ppermute | solution.py:389
  29.6 0.6 copy-start.8
  29.9 0.6 copy-start.9
  33.7 6.2 %collective-permute-start.8 = (bf16[8,64]{1,0:T(8,128)(2,1)}, bf16[8,64]{1,0:T(8,128)(2,1)S(1)}, u32[]{:S(2)}, u32[]{:S(2)}) collective-permute-start(bf16[8,64]{1,0:T(8,128)(2,1)} %get-tuple-element.49), channel_id=1, source_target_pairs={{0,4},{1,5},{2,6},{3,7},{4,0},{5,1},{6,2},{7,3},{8,12},{9,13},{10,... | collective-permute-start | bytes 3080 | tf_op jit(solution)/shard_map/ppermute | solution.py:389
  36.9 3.8 %collective-permute-start.9 = (bf16[8,64]{1,0:T(8,128)(2,1)}, bf16[8,64]{1,0:T(8,128)(2,1)S(1)}, u32[]{:S(2)}, u32[]{:S(2)}) collective-permute-start(bf16[8,64]{1,0:T(8,128)(2,1)} %get-tuple-element.50), channel_id=1, source_target_pairs={{0,2},{1,3},{2,0},{3,1},{4,8},{5,9},{6,10},{7,11},{8,4},{9,5},{10,... | collective-permute-start | bytes 3080 | tf_op jit(solution)/shard_map/ppermute | solution.py:389
  39.8 0.8 %copy-start.10 = (bf16[8,64]{1,0:T(8,128)(2,1)}, bf16[8,64]{1,0:T(8,128)(2,1)S(1)}, u32[]{:S(2)}) copy-start(bf16[8,64]{1,0:T(8,128)(2,1)S(1)} %collective-permute-done.8.got_even) | copy-start | bytes 3076
  40.7 0.6 copy-start.13
  43.4 6.3 %collective-permute-start.12 = (bf16[80,128]{1,0:T(8,128)(2,1)}, bf16[80,128]{1,0:T(8,128)(2,1)S(1)}, u32[]{:S(2)}, u32[]{:S(2)}) collective-permute-start(bf16[80,128]{1,0:T(8,128)(2,1)} %get-tuple-element.56), channel_id=1, source_target_pairs={{0,1},{1,0},{2,3},{3,2},{4,5},{5,4},{6,7},{7,6},{8,9},{9,8},{10,11... | collective-permute-start | bytes 61448 | tf_op jit(solution)/shard_map/ppermute | solution.py:446
  43.4 6.3 %collective-permute-start.13 = (bf16[80,128]{1,0:T(8,128)(2,1)}, bf16[80,128]{1,0:T(8,128)(2,1)S(1)}, u32[]{:S(2)}, u32[]{:S(2)}) collective-permute-start(bf16[80,128]{1,0:T(8,128)(2,1)} %get-tuple-element.57), channel_id=1, source_target_pairs={{0,3},{1,2},{2,1},{3,0},{4,7},{5,6},{6,5},{7,4},{8,11},{9,10},{10,... | collective-permute-start | bytes 61448 | tf_op jit(solution)/shard_map/ppermute | solution.py:445
  44.2 3.9 %collective-permute-start.10 = (bf16[60,128]{1,0:T(8,128)(2,1)}, bf16[60,128]{1,0:T(8,128)(2,1)S(1)}, u32[]{:S(2)}, u32[]{:S(2)}) collective-permute-start(bf16[60,128]{1,0:T(8,128)(2,1)} %get-tuple-element.54), channel_id=1, source_target_pairs={{0,4},{1,5},{2,6},{3,7},{4,0},{5,1},{6,2},{7,3},{8,12},{9,13},{10,... | collective-permute-start | bytes 46088 | tf_op jit(solution)/shard_map/ppermute | solution.py:389
  45.7 3.9 %collective-permute-start.11 = (bf16[60,128]{1,0:T(8,128)(2,1)}, bf16[60,128]{1,0:T(8,128)(2,1)S(1)}, u32[]{:S(2)}, u32[]{:S(2)}) collective-permute-start(bf16[60,128]{1,0:T(8,128)(2,1)} %get-tuple-element.55), channel_id=1, source_target_pairs={{0,2},{1,3},{2,0},{3,1},{4,8},{5,9},{6,10},{7,11},{8,4},{9,5},{10,... | collective-permute-start | bytes 46088 | tf_op jit(solution)/shard_map/ppermute | solution.py:389
  48.1 1.6 %copy-start.4 = (bf16[60,128]{1,0:T(8,128)(2,1)}, bf16[60,128]{1,0:T(8,128)(2,1)S(1)}, u32[]{:S(2)}) copy-start(bf16[60,128]{1,0:T(8,128)(2,1)S(1)} %collective-permute-done.10.got_row_even) | copy-start | bytes 46084
  49.7 0.6 copy-start.6
  49.7 0.6 copy-start
  49.7 0.6 copy-start.2
  52.6 7.3 %collective-permute-start.14 = (bf16[8,64]{1,0:T(8,128)(2,1)}, bf16[8,64]{1,0:T(8,128)(2,1)S(1)}, u32[]{:S(2)}, u32[]{:S(2)}) collective-permute-start(bf16[8,64]{1,0:T(8,128)(2,1)} %get-tuple-element.61), channel_id=1, source_target_pairs={{0,4},{1,5},{2,6},{3,7},{4,0},{5,1},{6,2},{7,3},{8,12},{9,13},{10,... | collective-permute-start | bytes 3080 | tf_op jit(solution)/shard_map/ppermute | solution.py:389
  54.0 5.9 %collective-permute-start.15 = (bf16[8,64]{1,0:T(8,128)(2,1)}, bf16[8,64]{1,0:T(8,128)(2,1)S(1)}, u32[]{:S(2)}, u32[]{:S(2)}) collective-permute-start(bf16[8,64]{1,0:T(8,128)(2,1)} %get-tuple-element.62), channel_id=1, source_target_pairs={{0,2},{1,3},{2,0},{3,1},{4,8},{5,9},{6,10},{7,11},{8,4},{9,5},{10,... | collective-permute-start | bytes 3080 | tf_op jit(solution)/shard_map/ppermute | solution.py:389
  59.9 0.6 copy-start.15
  (1 other events, 0.5 us)

commit v2 on v1

--- a/solution.py
+++ b/solution.py
@@ -3,11 +3,11 @@
 
 import jax
 import jax.numpy as jnp
-import numpy as np
 from jax import lax
 from jax.experimental import pallas as pl
 from jax.experimental.pallas import tpu as pltpu
 from jax.sharding import PartitionSpec as P
+
 
 NDIR = 24
 NBAND = 3
@@ -18,9 +18,10 @@
 f32, bf16 = jnp.float32, jnp.bfloat16
 VMEM = pl.BlockSpec(memory_space=pltpu.VMEM)
 SMEM = pl.BlockSpec(memory_space=pltpu.SMEM)
-
-
-def call(kernel, outs, specs, scratch=(), name=None):
+HBM = pl.BlockSpec(memory_space=pltpu.HBM)
+
+
+def call(kernel, outs, specs, scratch=()):
     out_shape = tuple(jax.ShapeDtypeStruct(s, d) for s, d in outs)
     return pl.pallas_call(
         kernel,
@@ -28,7 +29,7 @@
         in_specs=list(specs),
         out_specs=tuple(VMEM for _ in outs),
         scratch_shapes=list(scratch),
-        name=name,
+        compiler_params=pltpu.CompilerParams(vmem_limit_bytes=12 << 20),
     )
 
 
@@ -72,10 +73,12 @@
 
 
 def wave_finish(
-    e_of, t_ref, q_ref, wind_ref, current_of, wet_ref, rate_ref, gain_ref, kmap, trig_ref, upd_ref, nfreq
+    e_of, t_ref, q_ref, wind_ref, current_of, wet_ref, rate_ref, gain_ref, kmap, upd_ref, nfreq
 ):
     rows, lanes = wet_ref.shape
-    cosine, sine = trig_ref[:NDIR], trig_ref[NDIR:]
+    heading = lax.broadcasted_iota(jnp.int32, (NDIR, lanes), 0).astype(f32)
+    heading = (heading + 0.5) * (2.0 * math.pi / NDIR)
+    cosine, sine = jnp.cos(heading), jnp.sin(heading)
     stress = []
     for y in range(rows):
         cells = slice(y * lanes, (y + 1) * lanes)
@@ -109,8 +112,8 @@
 
 def pick(fields, send, outs):
     to_even, to_odd, own = outs
-    slot = send.shape[1]
-    index = jnp.concatenate([send[j : j + 1] for j in range(3)], axis=1)
+    slot = send.shape[2]
+    index = jnp.concatenate([send[j] for j in range(3)], axis=1)
     cell = lax.broadcasted_iota(jnp.int32, (fields.shape[1], 3 * slot), 0)
     hot = jnp.where(cell == index, 1.0, 0.0).astype(bf16)
     slots = dot(fields.astype(bf16), hot)
@@ -132,23 +135,32 @@
 
 def k_wave_first(
     nfreq,
-    spec_ref, wind_ref, cur_ref, wet_ref, inter_ref, rate_ref, gain_ref, smap_ref, kmap_ref, trig_ref, send_ref,
+    spec_hbm, inter_hbm, smap_hbm, rate_hbm, wind_hbm, cur_hbm, wet_hbm, gain_hbm, kmap_hbm, send_hbm,
     upd_ref, to_even, to_odd, own,
-    ef, eb, t, q,
+    spec_ref, inter_ref, smap_ref, rate_ref, wind_ref, cur_ref, wet_ref, gain_ref, kmap_ref, send_ref,
+    ef, eb, t, q, sems,
 ):
+    sources = (spec_hbm, inter_hbm, smap_hbm, rate_hbm, wind_hbm, cur_hbm, wet_hbm, gain_hbm, kmap_hbm, send_hbm)
+    held = (spec_ref, inter_ref, smap_ref, rate_ref, wind_ref, cur_ref, wet_ref, gain_ref, kmap_ref, send_ref)
+    copies = [pltpu.make_async_copy(a, b, sems.at[i]) for i, (a, b) in enumerate(zip(sources, held))]
+    for copy in copies:
+        copy.start()
     rows, lanes = wet_ref.shape
     spec = inter_ref.shape[0]
+    copies[0].wait()
     ef[...] = spec_ref[...].astype(f32)
     for y in range(rows):
         eb[:, y * lanes : (y + 1) * lanes] = ef[pl.ds(y, spec, stride=rows), :].astype(bf16)
+    for copy in copies[1:]:
+        copy.wait()
     transfer(inter_ref[...], smap_ref[...], rate_ref, eb[...], t, q, nfreq)
     fields = wave_finish(
         lambda y: ef[pl.ds(y, spec, stride=rows), :],
         t, q, wind_ref,
         lambda i, y: cur_ref[i, y : y + 1, :],
-        wet_ref, rate_ref, gain_ref, kmap_ref[...], trig_ref, upd_ref, nfreq,
-    )
-    pick(fields, send_ref[...], (to_even, to_odd, own))
+        wet_ref, rate_ref, gain_ref, kmap_ref[...], upd_ref, nfreq,
+    )
+    pick(fields, send_ref, (to_even, to_odd, own))
 
 
 def k_transfer(nfreq, upd_ref, inter_ref, smap_ref, rate_ref, t_ref, q_ref):
@@ -157,7 +169,7 @@
 
 def k_wave_next(
     nfreq, n_row,
-    got_even, got_odd, got_own, recv_ref, old_ref, t_ref, q_ref, wind_ref, wet_ref, rate_ref, gain_ref, kmap_ref, trig_ref, send_ref,
+    got_even, got_odd, got_own, recv_ref, old_ref, t_ref, q_ref, wind_ref, wet_ref, rate_ref, gain_ref, kmap_ref, send_ref,
     upd_ref, to_even, to_odd, own,
     cur,
 ):
@@ -168,9 +180,9 @@
         lambda y: old_ref[:, y * lanes : (y + 1) * lanes].astype(f32),
         t_ref, q_ref, wind_ref,
         lambda i, y: cur[i : i + 1, y * lanes : (y + 1) * lanes],
-        wet_ref, rate_ref, gain_ref, kmap_ref[...], trig_ref, upd_ref, nfreq,
-    )
-    pick(fields, send_ref[...], (to_even, to_odd, own))
+        wet_ref, rate_ref, gain_ref, kmap_ref[...], upd_ref, nfreq,
+    )
+    pick(fields, send_ref, (to_even, to_odd, own))
 
 
 def k_spectra_out(rows, upd_ref, out_ref, wide):
@@ -300,7 +312,7 @@
     bs[2 * oy : 3 * oy, :] = eta
     bs[3 * oy :, :] = jnp.zeros((5 * oy, ox), f32)
     back = jnp.concatenate([bs[pl.ds(y, 8, stride=oy), :] for y in range(oy)], axis=1)
-    pick(back, send_ref[...], (to_even, to_odd, own))
+    pick(back, send_ref, (to_even, to_odd, own))
 
 
 def k_mix(lev, oy, smooth_ref, mix_ref, vel_ref):
@@ -335,7 +347,7 @@
                 row_odd.append((place(r, c), place(r, (c + n_col // 2) % n_col)))
     col_even = [(c, c ^ 1) for c in range(n_col)]
     col_odd = [(c, (c + 1 if c % 2 else c - 1) % n_col) for c in range(n_col)]
-    return row_even, row_odd, col_even, col_odd
+    return dict(row_even=row_even, row_odd=row_odd, col_even=col_even, col_odd=col_odd)
 
 
 def shards(
@@ -372,78 +384,74 @@
     nfreq = input_rate.shape[0]
     slot = wave_send.shape[-1]
     pad = -(-planes // 16) * 16
-    heading = ((np.arange(NDIR)).astype(np.float32) + 0.5) * np.float32(2.0 * math.pi / NDIR)
-    trig = np.concatenate([np.cos(heading), np.sin(heading)]).astype(np.float32)
-    trig = jnp.asarray(np.repeat(trig[:, None], lanes, axis=1))
     pairs = pairings(n_row, n_col)
     both = ("row", "col")
     ocean_w = ocean_recv.reshape(3 * slot, oy * ox)
     wave_w = wave_recv.reshape(3 * slot, cells)
-    wsend, osend = wave_send.reshape(3, slot), ocean_send.reshape(3, slot)
+    wsend, osend = wave_send.reshape(3, 1, slot), ocean_send.reshape(3, 1, slot)
     fold = fold_index.reshape(1, ox)
     velocity = ocean_vel.reshape(planes * oy, ox)
     eta = ocean_eta
     whole = n_col != 4
 
-    def trade_rows(to_even, to_odd):
-        return lax.ppermute(to_odd, both, pairs[1]), lax.ppermute(to_even, both, pairs[0])
+    def trade(label, array):
+        axis = both if label.startswith("row") else "col"
+        return lax.ppermute(array, axis, pairs[label])
 
     slots_out = [((8, slot), bf16)] * 3
     wave_outs = [((spec, cells), bf16)] + slots_out
     for step in range(STEPS):
         if step == 0:
+            inputs = (
+                spectra.reshape(spec * rows, lanes), interaction, stress_map, input_rate, wind, wave_current,
+                wave_wet, eta_gain, stokes_map, wsend,
+            )
+            held = [(pltpu.SMEM if x.ndim == 1 else pltpu.VMEM)(x.shape, x.dtype) for x in inputs]
             updated, to_even, to_odd, own = call(
                 functools.partial(k_wave_first, nfreq),
                 wave_outs,
-                [VMEM] * 5 + [SMEM] * 2 + [VMEM] * 4,
-                [
+                [HBM] * len(inputs),
+                held
+                + [
                     pltpu.VMEM((spec * rows, lanes), f32),
                     pltpu.VMEM((spec, cells), bf16),
                     pltpu.VMEM((spec, cells), f32),
                     pltpu.VMEM((2 * NDIR, cells), f32),
+                    pltpu.SemaphoreType.DMA((len(inputs),)),
                 ],
-                "wave_first",
-            )(
-                spectra.reshape(spec * rows, lanes), wind, wave_current, wave_wet, interaction,
-                input_rate, eta_gain, stress_map, stokes_map, trig, wsend,
-            )
+            )(*(pltpu.with_memory_space_constraint(x, pltpu.HBM) for x in inputs))
         else:
             updated, to_even, to_odd, own = call(
                 functools.partial(k_wave_next, nfreq, n_row),
                 wave_outs,
-                [VMEM] * 9 + [SMEM] * 2 + [VMEM] * 3,
+                [VMEM] * 9 + [SMEM] * 2 + [VMEM] * 2,
                 [pltpu.VMEM((8, cells), f32)],
-                "wave_next",
             )(
                 got_even, got_odd, own, wave_w, updated, moved, q, wind, wave_wet,
-                input_rate, eta_gain, stokes_map, trig, wsend,
+                input_rate, eta_gain, stokes_map, wsend,
             )
-        got_odd, got_even = trade_rows(to_even, to_odd)
+        got_odd, got_even = trade("row_odd", to_odd), trade("row_even", to_even)
         if step + 1 < STEPS:
             moved, q = call(
                 functools.partial(k_transfer, nfreq),
                 [((spec, cells), f32), ((2 * NDIR, cells), f32)],
                 [VMEM] * 3 + [SMEM],
-                name="transfer",
             )(updated, interaction, stress_map, input_rate)
-        else:
+        forced, row_even, row_odd, col_even, col_odd = call(
+            functools.partial(k_force, n_row, lev, pad),
+            [((planes * oy, ox), f32)] + [((planes, ox), bf16)] * 2 + [((pad + 16, ox), bf16)] * 2,
+            [VMEM] * 7 + [SMEM] * 2,
+            [pltpu.VMEM((8 * oy, ox), f32)],
+        )(got_even, got_odd, own, ocean_w, velocity, ocean_wet, coriolis, tau_profile, stokes_profile)
+        got_row_odd, got_row_even = trade("row_odd", row_odd), trade("row_even", row_even)
+        got_col_odd, got_col_even = trade("col_odd", col_odd), trade("col_even", col_even)
+        if step + 1 == STEPS:
             (spectra_out,) = call(
                 functools.partial(k_spectra_out, rows),
                 [((spec * rows, lanes), bf16)],
                 [VMEM],
                 [pltpu.VMEM((spec * rows, lanes), f32)],
-                "spectra_out",
             )(updated)
-        forced, row_even, row_odd, col_even, col_odd = call(
-            functools.partial(k_force, n_row, lev, pad),
-            [((planes * oy, ox), f32)] + [((planes, ox), bf16)] * 2 + [((pad + 16, ox), bf16)] * 2,
-            [VMEM] * 7 + [SMEM] * 2,
-            [pltpu.VMEM((8 * oy, ox), f32)],
-            "force",
-        )(got_even, got_odd, own, ocean_w, velocity, ocean_wet, coriolis, tau_profile, stokes_profile)
-        got_row_odd, got_row_even = trade_rows(row_even, row_odd)
-        got_col_odd = lax.ppermute(col_odd, "col", pairs[3])
-        got_col_even = lax.ppermute(col_even, "col", pairs[2])
         if whole:
             top_line = lax.all_gather(col_even[:planes], "col", axis=0, tiled=True)
         else:
@@ -457,17 +465,16 @@
                 pltpu.VMEM((planes, ox), f32),
                 pltpu.VMEM((8 * oy, ox), f32),
             ],
-            "smooth",
         )(
             forced, got_row_even, got_row_odd, got_col_even, got_col_odd, top_line, fold, eta, ocean_wet,
             thickness, mix_inverse, osend,
         )
-        got_odd, got_even = trade_rows(to_even, to_odd)
+        got_odd, got_even = trade("row_odd", to_odd), trade("row_even", to_even)
         (velocity,) = call(
-            functools.partial(k_mix, lev, oy), [((planes * oy, ox), f32)], [VMEM, SMEM], name="mix"
+            functools.partial(k_mix, lev, oy), [((planes * oy, ox), f32)], [VMEM, SMEM]
         )(smooth, mix_inverse)
     (current,) = call(
-        functools.partial(k_current_out, n_row), [((3, rows, lanes), f32)], [VMEM] * 4, name="current_out"
+        functools.partial(k_current_out, n_row), [((3, rows, lanes), f32)], [VMEM] * 4
     )(got_even, got_odd, own, wave_w)
     return (
         spectra_out.reshape(spec, rows, lanes),

time: 62.7 us -> 48.5 us (0.77)
  Pallas kernels: 27.1 us -> 16.2 us
  local copies, waits for them, and re-layouts: 5.37 us -> 0.1 us
  waiting for transfers between devices: 9.04 us -> 11.2 us
    unnamed x36 -> x40, local copies, waits for them, and re-layouts: 5.37 us -> 0.1 us
    pallas_call x2, Pallas kernels: 4.28 us -> 1.97 us  [shards(): call(functools.partial(k_force, n_row, lev, pad), [((planes * oy, ox), f3...]
    ppermute x16, waiting for transfers between devices: 9.04 us -> 11.2 us  [trade(): return lax.ppermute(array, axis, pairs[label])]
    pallas_call x1, Pallas kernels: 3.02 us -> 1.28 us  [shards(): call(functools.partial(k_transfer, nfreq), [((spec, cells), f32), ((2 * N...]
    pallas_call x1, Pallas kernels: 3.21 us -> 1.56 us  [shards(): call(functools.partial(k_wave_next, nfreq, n_row), wave_outs, [VMEM] * 9...]
    pallas_call x2, Pallas kernels: 4.65 us -> 3.23 us  [shards(): call(functools.partial(k_smooth, n_row, n_col, lev, pad, whole), [((plane...]
    pallas_call x2, Pallas kernels: 4.88 us -> 3.69 us  [shards(): call(functools.partial(k_mix, lev, oy), [((planes * oy, ox), f32)], [VMEM...]
    pallas_call x1, Pallas kernels: 2.12 us -> 1.05 us  [shards(): call(functools.partial(k_spectra_out, rows), [((spec * rows, lanes), bf16...]
  transfers between devices with their start and end apart: 16 -> 16, of which waited for: 8 -> 9; matrix products, arithmetic and copies ran while one was open for 1% -> 0% of each run, Pallas kernels for 16% -> 12%
where the time goes in v2:
time: 48.5 us; the launch traced here: 48.3 us
  starting transfers between devices  19.8 us (41%)
  Pallas kernels  16.2 us (33%)
  waiting for transfers between devices  11.2 us (23%)
  between operations  0.94 us (2%)
    ppermute x16, starting transfers between devices, trade(): return lax.ppermute(array, axis, pairs[label])  19.8 us
    ppermute x16, waiting for transfers between devices, trade(): return lax.ppermute(array, axis, pairs[label])  11.2 us
    pallas_call x2, Pallas kernels, shards(): call(functools.partial(k_mix, lev, oy), [((planes * oy, ox), f32)], [VMEM...  3.69 us
    pallas_call x2, Pallas kernels, shards(): call(functools.partial(k_smooth, n_row, n_col, lev, pad, whole), [((plane...  3.23 us
    pallas_call x1, Pallas kernels, shards(): call(functools.partial(k_wave_first, nfreq), wave_outs, [HBM] * len(input...  2.66 us
    pallas_call x2, Pallas kernels, shards(): call(functools.partial(k_force, n_row, lev, pad), [((planes * oy, ox), f3...  1.97 us
    pallas_call x1, Pallas kernels, shards(): call(functools.partial(k_wave_next, nfreq, n_row), wave_outs, [VMEM] * 9...  1.56 us
    pallas_call x1, Pallas kernels, shards(): call(functools.partial(k_transfer, nfreq), [((spec, cells), f32), ((2 * N...  1.28 us
  transfers between devices with their start and end apart: 16, of which 9 were waited for; matrix products, arithmetic and copies ran while one was open for 0% of the time, Pallas kernels for 12%

profile of v2, /device:TPU:0, one launch (start us, length us, event | category | flops | bytes accessed | tf_op | source)
XLA Modules:
  0.0 48.3 jit_solution(12890701481463093144)
XLA Ops:
  0.8 2.7 %shard_map.237 = (bf16[600,512]{1,0:T(8,128)(2,1)S(1)}, bf16[8,64]{1,0:T(8,128)(2,1)S(1)}, bf16[8,64]{1,0:T(8,128)(2,1)S(1)}, bf16[8,64]{1,0:T(8,128)(2,1)S(1)}) custom-call(bf16[2400,128]{1,0:T(8,128)(2,1)} %bitcast.22, bf16[600,600]{1,0:T(8,128)(2,1)} %inter_ref.1, f32[2,600]{1,0:T(2,128)} %smap_ref.1, f32[25]{0:T(128)} %rate_ref.3, ...), custom_call_target="tpu_custom_call" | custom-call | tf_op jit(solution)/shard_map/pallas_call | solution.py:410
  3.5 3.1 %collective-permute-start = (bf16[8,64]{1,0:T(8,128)(2,1)S(1)}, bf16[8,64]{1,0:T(8,128)(2,1)S(1)}, u32[]{:S(2)}, u32[]{:S(2)}) collective-permute-start(bf16[8,64]{1,0:T(8,128)(2,1)S(1)} %get-tuple-element.34), channel_id=1, source_target_pairs={{0,4},{1,5},{2,6},{3,7},{4,0},{5,1},{6,2},{7,3},{8,12},{9,13},{10,... | collective-permute-start | bytes 3080 | tf_op jit(solution)/shard_map/ppermute | solution.py:399
  6.6 1.5 %collective-permute-start.1 = (bf16[8,64]{1,0:T(8,128)(2,1)S(1)}, bf16[8,64]{1,0:T(8,128)(2,1)S(1)}, u32[]{:S(2)}, u32[]{:S(2)}) collective-permute-start(bf16[8,64]{1,0:T(8,128)(2,1)S(1)} %get-tuple-element.35), channel_id=1, source_target_pairs={{0,2},{1,3},{2,0},{3,1},{4,8},{5,9},{6,10},{7,11},{8,4},{9,5},{10,... | collective-permute-start | bytes 3080 | tf_op jit(solution)/shard_map/ppermute | solution.py:399
  8.1 2.0 %collective-permute-done.1.got_odd = bf16[8,64]{1,0:T(8,128)(2,1)S(1)} collective-permute-done((bf16[8,64]{1,0:T(8,128)(2,1)S(1)}, bf16[8,64]{1,0:T(8,128)(2,1)S(1)}, u32[]{:S(2)}, u32[]{:S(2)}) %collective-permute-start.1) | collective-permute-done | bytes 1056 | tf_op jit(solution)/shard_map/ppermute | solution.py:399
  10.2 1.0 %shard_map.238 = (f32[480,128]{1,0:T(8,128)S(1)}, bf16[60,128]{1,0:T(8,128)(2,1)S(1)}, bf16[60,128]{1,0:T(8,128)(2,1)S(1)}, bf16[80,128]{1,0:T(8,128)(2,1)S(1)}, bf16[80,128]{1,0:T(8,128)(2,1)S(1)}) custom-call(bf16[8,64]{1,0:T(8,128)(2,1)S(1)} %collective-permute-done.got_even, bf16[8,64]{1,0:T(8,128)(2,1)S(1)} %collective-permute-done.1.got_odd, ...), custom_call_target="tpu_custom_call" | custom-call | tf_op jit(solution)/shard_map/pallas_call | solution.py:440
  11.3 1.6 %collective-permute-start.5 = (bf16[80,128]{1,0:T(8,128)(2,1)S(1)}, bf16[80,128]{1,0:T(8,128)(2,1)S(1)}, u32[]{:S(2)}, u32[]{:S(2)}) collective-permute-start(bf16[80,128]{1,0:T(8,128)(2,1)S(1)} %get-tuple-element.41), channel_id=1, source_target_pairs={{0,3},{1,2},{2,1},{3,0},{4,7},{5,6},{6,5},{7,4},{8,11},{9,10},{10,... | collective-permute-start | bytes 61448 | tf_op jit(solution)/shard_map/ppermute | solution.py:399
  12.9 1.4 %collective-permute-start.2 = (bf16[60,128]{1,0:T(8,128)(2,1)S(1)}, bf16[60,128]{1,0:T(8,128)(2,1)S(1)}, u32[]{:S(2)}, u32[]{:S(2)}) collective-permute-start(bf16[60,128]{1,0:T(8,128)(2,1)S(1)} %get-tuple-element.38), channel_id=1, source_target_pairs={{0,4},{1,5},{2,6},{3,7},{4,0},{5,1},{6,2},{7,3},{8,12},{9,13},{10,... | collective-permute-start | bytes 46088 | tf_op jit(solution)/shard_map/ppermute | solution.py:399
  14.4 2.2 %collective-permute-done.2.got_row_even = bf16[60,128]{1,0:T(8,128)(2,1)S(1)} collective-permute-done((bf16[60,128]{1,0:T(8,128)(2,1)S(1)}, bf16[60,128]{1,0:T(8,128)(2,1)S(1)}, u32[]{:S(2)}, u32[]{:S(2)}) %collective-permute-start.2) | collective-permute-done | bytes 15392 | tf_op jit(solution)/shard_map/ppermute | solution.py:399
  16.6 1.4 %collective-permute-done.3.got_row_odd = bf16[60,128]{1,0:T(8,128)(2,1)S(1)} collective-permute-done((bf16[60,128]{1,0:T(8,128)(2,1)S(1)}, bf16[60,128]{1,0:T(8,128)(2,1)S(1)}, u32[]{:S(2)}, u32[]{:S(2)}) %collective-permute-start.3) | collective-permute-done | bytes 15392 | tf_op jit(solution)/shard_map/ppermute | solution.py:399
  18.1 1.4 %shard_map.239 = (f32[480,128]{1,0:T(8,128)S(1)}, f32[8,128]{1,0:T(8,128)S(1)}, bf16[8,64]{1,0:T(8,128)(2,1)S(1)}, bf16[8,64]{1,0:T(8,128)(2,1)S(1)}, bf16[8,64]{1,0:T(8,128)(2,1)S(1)}) custom-call(f32[480,128]{1,0:T(8,128)S(1)} %get-tuple-element.37.forced_ref, bf16[60,128]{1,0:T(8,128)(2,1)S(1)} %collective-permute-done.2.got_row_even, ...), custom_call_target="tpu_custom_call" | custom-call | tf_op jit(solution)/shard_map/pallas_call | solution.py:459
  19.5 1.6 %collective-permute-start.6 = (bf16[8,64]{1,0:T(8,128)(2,1)S(1)}, bf16[8,64]{1,0:T(8,128)(2,1)S(1)}, u32[]{:S(2)}, u32[]{:S(2)}) collective-permute-start(bf16[8,64]{1,0:T(8,128)(2,1)S(1)} %get-tuple-element.42), channel_id=1, source_target_pairs={{0,4},{1,5},{2,6},{3,7},{4,0},{5,1},{6,2},{7,3},{8,12},{9,13},{10,... | collective-permute-start | bytes 3080 | tf_op jit(solution)/shard_map/ppermute | solution.py:399
  21.1 0.5 %collective-permute-start.7 = (bf16[8,64]{1,0:T(8,128)(2,1)S(1)}, bf16[8,64]{1,0:T(8,128)(2,1)S(1)}, u32[]{:S(2)}, u32[]{:S(2)}) collective-permute-start(bf16[8,64]{1,0:T(8,128)(2,1)S(1)} %get-tuple-element.43), channel_id=1, source_target_pairs={{0,2},{1,3},{2,0},{3,1},{4,8},{5,9},{6,10},{7,11},{8,4},{9,5},{10,... | collective-permute-start | bytes 3080 | tf_op jit(solution)/shard_map/ppermute | solution.py:399
  21.6 1.3 %shard_map.240 = (f32[600,512]{1,0:T(8,128)S(1)}, f32[48,512]{1,0:T(8,128)S(1)}) custom-call(bf16[600,512]{1,0:T(8,128)(2,1)S(1)} %get-tuple-element.45.upd_ref.old_ref, bf16[600,600]{1,0:T(8,128)(2,1)S(1)} %copy-done, f32[2,600]{1,0:T(2,128)S(1)} %copy-done.7, f32[25]{0:T(128)S(1)} %copy-done.15), custom_call_target="tpu_custom_call" | custom-call | tf_op jit(solution)/shard_map/pallas_call | solution.py:435
  22.9 0.2 collective-permute-done.6.got_even
  23.1 1.5 %collective-permute-done.7.got_odd = bf16[8,64]{1,0:T(8,128)(2,1)S(1)} collective-permute-done((bf16[8,64]{1,0:T(8,128)(2,1)S(1)}, bf16[8,64]{1,0:T(8,128)(2,1)S(1)}, u32[]{:S(2)}, u32[]{:S(2)}) %collective-permute-start.7) | collective-permute-done | bytes 1056 | tf_op jit(solution)/shard_map/ppermute | solution.py:399
  24.7 1.6 %shard_map.241 = (bf16[600,512]{1,0:T(8,128)(2,1)S(1)}, bf16[8,64]{1,0:T(8,128)(2,1)S(1)}, bf16[8,64]{1,0:T(8,128)(2,1)S(1)}, bf16[8,64]{1,0:T(8,128)(2,1)S(1)}) custom-call(bf16[8,64]{1,0:T(8,128)(2,1)S(1)} %collective-permute-done.6.got_even, bf16[8,64]{1,0:T(8,128)(2,1)S(1)} %collective-permute-done.7.got_odd, ...), custom_call_target="tpu_custom_call" | custom-call | tf_op jit(solution)/shard_map/pallas_call | solution.py:424
  26.2 1.9 %collective-permute-start.8 = (bf16[8,64]{1,0:T(8,128)(2,1)S(1)}, bf16[8,64]{1,0:T(8,128)(2,1)S(1)}, u32[]{:S(2)}, u32[]{:S(2)}) collective-permute-start(bf16[8,64]{1,0:T(8,128)(2,1)S(1)} %get-tuple-element.49), channel_id=1, source_target_pairs={{0,4},{1,5},{2,6},{3,7},{4,0},{5,1},{6,2},{7,3},{8,12},{9,13},{10,... | collective-permute-start | bytes 3080 | tf_op jit(solution)/shard_map/ppermute | solution.py:399
  28.2 0.5 %collective-permute-start.9 = (bf16[8,64]{1,0:T(8,128)(2,1)S(1)}, bf16[8,64]{1,0:T(8,128)(2,1)S(1)}, u32[]{:S(2)}, u32[]{:S(2)}) collective-permute-start(bf16[8,64]{1,0:T(8,128)(2,1)S(1)} %get-tuple-element.50), channel_id=1, source_target_pairs={{0,2},{1,3},{2,0},{3,1},{4,8},{5,9},{6,10},{7,11},{8,4},{9,5},{10,... | collective-permute-start | bytes 3080 | tf_op jit(solution)/shard_map/ppermute | solution.py:399
  28.7 1.5 %shard_map.243.vel_ref = f32[480,128]{1,0:T(8,128)S(1)} custom-call(f32[480,128]{1,0:T(8,128)S(1)} %get-tuple-element.52.smooth_ref, f32[30,30]{1,0:T(8,128)S(1)} %copy-done.3), custom_call_target="tpu_custom_call" | custom-call | tf_op jit(solution)/shard_map/pallas_call | solution.py:473
  30.2 1.5 %collective-permute-done.9.got_odd = bf16[8,64]{1,0:T(8,128)(2,1)S(1)} collective-permute-done((bf16[8,64]{1,0:T(8,128)(2,1)S(1)}, bf16[8,64]{1,0:T(8,128)(2,1)S(1)}, u32[]{:S(2)}, u32[]{:S(2)}) %collective-permute-start.9) | collective-permute-done | bytes 1056 | tf_op jit(solution)/shard_map/ppermute | solution.py:399
  31.7 1.0 %shard_map.244 = (f32[480,128]{1,0:T(8,128)S(1)}, bf16[60,128]{1,0:T(8,128)(2,1)S(1)}, bf16[60,128]{1,0:T(8,128)(2,1)S(1)}, bf16[80,128]{1,0:T(8,128)(2,1)S(1)}, bf16[80,128]{1,0:T(8,128)(2,1)S(1)}) custom-call(bf16[8,64]{1,0:T(8,128)(2,1)S(1)} %collective-permute-done.8.got_even, bf16[8,64]{1,0:T(8,128)(2,1)S(1)} %collective-permute-done.9.got_odd, ...), custom_call_target="tpu_custom_call" | custom-call | tf_op jit(solution)/shard_map/pallas_call | solution.py:440
  32.8 0.6 %collective-permute-start.13 = (bf16[80,128]{1,0:T(8,128)(2,1)S(1)}, bf16[80,128]{1,0:T(8,128)(2,1)S(1)}, u32[]{:S(2)}, u32[]{:S(2)}) collective-permute-start(bf16[80,128]{1,0:T(8,128)(2,1)S(1)} %get-tuple-element.57), channel_id=1, source_target_pairs={{0,3},{1,2},{2,1},{3,0},{4,7},{5,6},{6,5},{7,4},{8,11},{9,10},{10,... | collective-permute-start | bytes 61448 | tf_op jit(solution)/shard_map/ppermute | solution.py:399
  33.4 1.4 %collective-permute-start.10 = (bf16[60,128]{1,0:T(8,128)(2,1)S(1)}, bf16[60,128]{1,0:T(8,128)(2,1)S(1)}, u32[]{:S(2)}, u32[]{:S(2)}) collective-permute-start(bf16[60,128]{1,0:T(8,128)(2,1)S(1)} %get-tuple-element.54), channel_id=1, source_target_pairs={{0,4},{1,5},{2,6},{3,7},{4,0},{5,1},{6,2},{7,3},{8,12},{9,13},{10,... | collective-permute-start | bytes 46088 | tf_op jit(solution)/shard_map/ppermute | solution.py:399
  34.9 1.5 %collective-permute-start.11 = (bf16[60,128]{1,0:T(8,128)(2,1)S(1)}, bf16[60,128]{1,0:T(8,128)(2,1)S(1)}, u32[]{:S(2)}, u32[]{:S(2)}) collective-permute-start(bf16[60,128]{1,0:T(8,128)(2,1)S(1)} %get-tuple-element.55), channel_id=1, source_target_pairs={{0,2},{1,3},{2,0},{3,1},{4,8},{5,9},{6,10},{7,11},{8,4},{9,5},{10,... | collective-permute-start | bytes 46088 | tf_op jit(solution)/shard_map/ppermute | solution.py:399
  36.3 0.8 %collective-permute-done.10.got_row_even = bf16[60,128]{1,0:T(8,128)(2,1)S(1)} collective-permute-done((bf16[60,128]{1,0:T(8,128)(2,1)S(1)}, bf16[60,128]{1,0:T(8,128)(2,1)S(1)}, u32[]{:S(2)}, u32[]{:S(2)}) %collective-permute-start.10) | collective-permute-done | bytes 15392 | tf_op jit(solution)/shard_map/ppermute | solution.py:399
  37.2 1.4 %collective-permute-done.11.got_row_odd = bf16[60,128]{1,0:T(8,128)(2,1)S(1)} collective-permute-done((bf16[60,128]{1,0:T(8,128)(2,1)S(1)}, bf16[60,128]{1,0:T(8,128)(2,1)S(1)}, u32[]{:S(2)}, u32[]{:S(2)}) %collective-permute-start.11) | collective-permute-done | bytes 15392 | tf_op jit(solution)/shard_map/ppermute | solution.py:399
  38.6 1.8 %shard_map.245 = (f32[480,128]{1,0:T(8,128)S(1)}, f32[8,128]{1,0:T(8,128)}, bf16[8,64]{1,0:T(8,128)(2,1)S(1)}, bf16[8,64]{1,0:T(8,128)(2,1)S(1)}, bf16[8,64]{1,0:T(8,128)(2,1)S(1)}) custom-call(f32[480,128]{1,0:T(8,128)S(1)} %get-tuple-element.53.forced_ref, bf16[60,128]{1,0:T(8,128)(2,1)S(1)} %collective-permute-done.10.got_row_even, ...), custom_call_target="tpu_custom_call" | custom-call | tf_op jit(solution)/shard_map/pallas_call | solution.py:459
  40.4 2.4 %collective-permute-start.14 = (bf16[8,64]{1,0:T(8,128)(2,1)S(1)}, bf16[8,64]{1,0:T(8,128)(2,1)S(1)}, u32[]{:S(2)}, u32[]{:S(2)}) collective-permute-start(bf16[8,64]{1,0:T(8,128)(2,1)S(1)} %get-tuple-element.61), channel_id=1, source_target_pairs={{0,4},{1,5},{2,6},{3,7},{4,0},{5,1},{6,2},{7,3},{8,12},{9,13},{10,... | collective-permute-start | bytes 3080 | tf_op jit(solution)/shard_map/ppermute | solution.py:399
  42.8 1.5 %collective-permute-start.15 = (bf16[8,64]{1,0:T(8,128)(2,1)S(1)}, bf16[8,64]{1,0:T(8,128)(2,1)S(1)}, u32[]{:S(2)}, u32[]{:S(2)}) collective-permute-start(bf16[8,64]{1,0:T(8,128)(2,1)S(1)} %get-tuple-element.62), channel_id=1, source_target_pairs={{0,2},{1,3},{2,0},{3,1},{4,8},{5,9},{6,10},{7,11},{8,4},{9,5},{10,... | collective-permute-start | bytes 3080 | tf_op jit(solution)/shard_map/ppermute | solution.py:399
  44.3 1.1 %shard_map.242 = bf16[2400,128]{1,0:T(8,128)(2,1)} custom-call(bf16[600,512]{1,0:T(8,128)(2,1)S(1)} %get-tuple-element.48.upd_ref), custom_call_target="tpu_custom_call" | custom-call | tf_op jit(solution)/shard_map/pallas_call | solution.py:449
  45.4 2.2 %shard_map.246 = f32[480,128]{1,0:T(8,128)} custom-call(f32[480,128]{1,0:T(8,128)S(1)} %get-tuple-element.59.smooth_ref, f32[30,30]{1,0:T(8,128)S(1)} %copy-done.3), custom_call_target="tpu_custom_call" | custom-call | tf_op jit(solution)/shard_map/pallas_call | solution.py:473
  47.6 0.8 %shard_map.247 = f32[3,4,128]{2,1,0:T(4,128)} custom-call(bf16[8,64]{1,0:T(8,128)(2,1)S(1)} %collective-permute-done.14.got_even, bf16[8,64]{1,0:T(8,128)(2,1)S(1)} %collective-permute-done.15.got_odd, bf16[8,64]{1,0:T(8,128)(2,1)S(1)} %get-tuple-element.63.own, bf16[192,512]{1,0:T(8,128)(2,1)S(1)} %bitcast.12), custom_call_target="tpu_custom_call" | custom-call | tf_op jit(solution)/shard_map/pallas_call | solution.py:476
  (51 shorter events, 0.5 us)
Async XLA Ops:
  0.6 9.5 %copy-start.6 = (s32[8,128]{1,0:T(8,128)S(1)}, s32[8,128]{1,0:T(8,128)}, u32[]{:S(2)}) copy-start(s32[8,128]{1,0:T(8,128)} %wet_ref.9) | copy-start | bytes 12292
  0.6 9.5 %copy-start.10 = (f32[3,30]{1,0:T(4,128)S(1)}, f32[3,30]{1,0:T(4,128)}, u32[]{:S(2)}) copy-start(f32[3,30]{1,0:T(4,128)} %prof_ref.3) | copy-start | bytes 1084
  0.7 17.3 %copy-start.3 = (f32[30,30]{1,0:T(8,128)S(1)}, f32[30,30]{1,0:T(8,128)}, u32[]{:S(2)}) copy-start(f32[30,30]{1,0:T(8,128)} %mix_ref.7) | copy-start | bytes 10804
  0.7 17.3 %copy-start.17 = (f32[30]{0:T(128)S(1)}, f32[30]{0:T(128)}, u32[]{:S(2)}) copy-start(f32[30]{0:T(128)} %thick_ref.3) | copy-start | bytes 364
  0.7 17.3 %copy-start.14 = (s32[1,1,3,64]{3,1,2,0:T(1,128)S(1)}, s32[1,1,3,64]{3,1,2,0:T(1,128)}, u32[]{:S(2)}) copy-start(s32[1,1,3,64]{3,1,2,0:T(1,128)} %param.42) | copy-start | bytes 2308
  0.7 17.3 %copy-start.11 = (s32[128]{0:T(128)S(1)}, s32[128]{0:T(128)}, u32[]{:S(2)}) copy-start(s32[128]{0:T(128)} %param.39) | copy-start | bytes 1540
  0.7 17.3 %copy-start.16 = (f32[8,128]{1,0:T(8,128)S(1)}, f32[8,128]{1,0:T(8,128)}, u32[]{:S(2)}) copy-start(f32[8,128]{1,0:T(8,128)} %eta_ref.1) | copy-start | bytes 12292
  0.7 20.9 %copy-start = (bf16[600,600]{1,0:T(8,128)(2,1)S(1)}, bf16[600,600]{1,0:T(8,128)(2,1)}, u32[]{:S(2)}) copy-start(bf16[600,600]{1,0:T(8,128)(2,1)} %inter_ref.1) | copy-start | bytes 2160004
  0.8 20.8 %copy-start.7 = (f32[2,600]{1,0:T(2,128)S(1)}, f32[2,600]{1,0:T(2,128)}, u32[]{:S(2)}) copy-start(f32[2,600]{1,0:T(2,128)} %smap_ref.1) | copy-start | bytes 14404
  0.8 20.8 %copy-start.15 = (f32[25]{0:T(128)S(1)}, f32[25]{0:T(128)}, u32[]{:S(2)}) copy-start(f32[25]{0:T(128)} %rate_ref.3) | copy-start | bytes 304
  3.4 21.2 %copy-start.2 = (bf16[1,1,3,64,512]{4,3,2,1,0:T(8,128)(2,1)S(1)}, bf16[1,1,3,64,512]{4,3,2,1,0:T(8,128)(2,1)}, u32[]{:S(2)}) copy-start(bf16[1,1,3,64,512]{4,3,2,1,0:T(8,128)(2,1)} %param.43) | copy-start | bytes 589828
  3.5 21.2 %copy-start.5 = (f32[6,600]{1,0:T(8,128)S(1)}, f32[6,600]{1,0:T(8,128)}, u32[]{:S(2)}) copy-start(f32[6,600]{1,0:T(8,128)} %kmap_ref.1) | copy-start | bytes 43204
  3.5 21.2 %copy-start.8 = (f32[2,4,128]{2,1,0:T(4,128)S(1)}, f32[2,4,128]{2,1,0:T(4,128)}, u32[]{:S(2)}) copy-start(f32[2,4,128]{2,1,0:T(4,128)} %wind_ref.1) | copy-start | bytes 12292
  3.5 21.2 %copy-start.12 = (s32[4,128]{1,0:T(4,128)S(1)}, s32[4,128]{1,0:T(4,128)}, u32[]{:S(2)}) copy-start(s32[4,128]{1,0:T(4,128)} %wet_ref.7) | copy-start | bytes 6148
  3.5 21.2 %copy-start.13 = (s32[1,1,3,64]{3,1,2,0:T(1,128)S(1)}, s32[1,1,3,64]{3,1,2,0:T(1,128)}, u32[]{:S(2)}) copy-start(s32[1,1,3,64]{3,1,2,0:T(1,128)} %param.40) | copy-start | bytes 2308
  3.5 21.2 %copy-start.19 = (f32[25]{0:T(128)S(1)}, f32[25]{0:T(128)}, u32[]{:S(2)}) copy-start(f32[25]{0:T(128)} %gain_ref.1) | copy-start | bytes 304
  3.5 4.6 %collective-permute-start = (bf16[8,64]{1,0:T(8,128)(2,1)S(1)}, bf16[8,64]{1,0:T(8,128)(2,1)S(1)}, u32[]{:S(2)}, u32[]{:S(2)}) collective-permute-start(bf16[8,64]{1,0:T(8,128)(2,1)S(1)} %get-tuple-element.34), channel_id=1, source_target_pairs={{0,4},{1,5},{2,6},{3,7},{4,0},{5,1},{6,2},{7,3},{8,12},{9,13},{10,... | collective-permute-start | bytes 3080 | tf_op jit(solution)/shard_map/ppermute | solution.py:399
  6.6 3.6 %collective-permute-start.1 = (bf16[8,64]{1,0:T(8,128)(2,1)S(1)}, bf16[8,64]{1,0:T(8,128)(2,1)S(1)}, u32[]{:S(2)}, u32[]{:S(2)}) collective-permute-start(bf16[8,64]{1,0:T(8,128)(2,1)S(1)} %get-tuple-element.35), channel_id=1, source_target_pairs={{0,2},{1,3},{2,0},{3,1},{4,8},{5,9},{6,10},{7,11},{8,4},{9,5},{10,... | collective-permute-start | bytes 3080 | tf_op jit(solution)/shard_map/ppermute | solution.py:399
  11.2 6.8 %collective-permute-start.4 = (bf16[80,128]{1,0:T(8,128)(2,1)S(1)}, bf16[80,128]{1,0:T(8,128)(2,1)S(1)}, u32[]{:S(2)}, u32[]{:S(2)}) collective-permute-start(bf16[80,128]{1,0:T(8,128)(2,1)S(1)} %get-tuple-element.40), channel_id=1, source_target_pairs={{0,1},{1,0},{2,3},{3,2},{4,5},{5,4},{6,7},{7,6},{8,9},{9,8},{10,11... | collective-permute-start | bytes 61448 | tf_op jit(solution)/shard_map/ppermute | solution.py:399
  11.3 6.7 %collective-permute-start.5 = (bf16[80,128]{1,0:T(8,128)(2,1)S(1)}, bf16[80,128]{1,0:T(8,128)(2,1)S(1)}, u32[]{:S(2)}, u32[]{:S(2)}) collective-permute-start(bf16[80,128]{1,0:T(8,128)(2,1)S(1)} %get-tuple-element.41), channel_id=1, source_target_pairs={{0,3},{1,2},{2,1},{3,0},{4,7},{5,6},{6,5},{7,4},{8,11},{9,10},{10,... | collective-permute-start | bytes 61448 | tf_op jit(solution)/shard_map/ppermute | solution.py:399
  12.9 3.7 %collective-permute-start.2 = (bf16[60,128]{1,0:T(8,128)(2,1)S(1)}, bf16[60,128]{1,0:T(8,128)(2,1)S(1)}, u32[]{:S(2)}, u32[]{:S(2)}) collective-permute-start(bf16[60,128]{1,0:T(8,128)(2,1)S(1)} %get-tuple-element.38), channel_id=1, source_target_pairs={{0,4},{1,5},{2,6},{3,7},{4,0},{5,1},{6,2},{7,3},{8,12},{9,13},{10,... | collective-permute-start | bytes 46088 | tf_op jit(solution)/shard_map/ppermute | solution.py:399
  14.3 3.7 %collective-permute-start.3 = (bf16[60,128]{1,0:T(8,128)(2,1)S(1)}, bf16[60,128]{1,0:T(8,128)(2,1)S(1)}, u32[]{:S(2)}, u32[]{:S(2)}) collective-permute-start(bf16[60,128]{1,0:T(8,128)(2,1)S(1)} %get-tuple-element.39), channel_id=1, source_target_pairs={{0,2},{1,3},{2,0},{3,1},{4,8},{5,9},{6,10},{7,11},{8,4},{9,5},{10,... | collective-permute-start | bytes 46088 | tf_op jit(solution)/shard_map/ppermute | solution.py:399
  19.5 3.6 %collective-permute-start.6 = (bf16[8,64]{1,0:T(8,128)(2,1)S(1)}, bf16[8,64]{1,0:T(8,128)(2,1)S(1)}, u32[]{:S(2)}, u32[]{:S(2)}) collective-permute-start(bf16[8,64]{1,0:T(8,128)(2,1)S(1)} %get-tuple-element.42), channel_id=1, source_target_pairs={{0,4},{1,5},{2,6},{3,7},{4,0},{5,1},{6,2},{7,3},{8,12},{9,13},{10,... | collective-permute-start | bytes 3080 | tf_op jit(solution)/shard_map/ppermute | solution.py:399
  21.1 3.6 %collective-permute-start.7 = (bf16[8,64]{1,0:T(8,128)(2,1)S(1)}, bf16[8,64]{1,0:T(8,128)(2,1)S(1)}, u32[]{:S(2)}, u32[]{:S(2)}) collective-permute-start(bf16[8,64]{1,0:T(8,128)(2,1)S(1)} %get-tuple-element.43), channel_id=1, source_target_pairs={{0,2},{1,3},{2,0},{3,1},{4,8},{5,9},{6,10},{7,11},{8,4},{9,5},{10,... | collective-permute-start | bytes 3080 | tf_op jit(solution)/shard_map/ppermute | solution.py:399
  26.2 4.0 %collective-permute-start.8 = (bf16[8,64]{1,0:T(8,128)(2,1)S(1)}, bf16[8,64]{1,0:T(8,128)(2,1)S(1)}, u32[]{:S(2)}, u32[]{:S(2)}) collective-permute-start(bf16[8,64]{1,0:T(8,128)(2,1)S(1)} %get-tuple-element.49), channel_id=1, source_target_pairs={{0,4},{1,5},{2,6},{3,7},{4,0},{5,1},{6,2},{7,3},{8,12},{9,13},{10,... | collective-permute-start | bytes 3080 | tf_op jit(solution)/shard_map/ppermute | solution.py:399
  28.2 3.6 %collective-permute-start.9 = (bf16[8,64]{1,0:T(8,128)(2,1)S(1)}, bf16[8,64]{1,0:T(8,128)(2,1)S(1)}, u32[]{:S(2)}, u32[]{:S(2)}) collective-permute-start(bf16[8,64]{1,0:T(8,128)(2,1)S(1)} %get-tuple-element.50), channel_id=1, source_target_pairs={{0,2},{1,3},{2,0},{3,1},{4,8},{5,9},{6,10},{7,11},{8,4},{9,5},{10,... | collective-permute-start | bytes 3080 | tf_op jit(solution)/shard_map/ppermute | solution.py:399
  32.7 5.9 %collective-permute-start.12 = (bf16[80,128]{1,0:T(8,128)(2,1)S(1)}, bf16[80,128]{1,0:T(8,128)(2,1)S(1)}, u32[]{:S(2)}, u32[]{:S(2)}) collective-permute-start(bf16[80,128]{1,0:T(8,128)(2,1)S(1)} %get-tuple-element.56), channel_id=1, source_target_pairs={{0,1},{1,0},{2,3},{3,2},{4,5},{5,4},{6,7},{7,6},{8,9},{9,8},{10,11... | collective-permute-start | bytes 61448 | tf_op jit(solution)/shard_map/ppermute | solution.py:399
  32.8 5.8 %collective-permute-start.13 = (bf16[80,128]{1,0:T(8,128)(2,1)S(1)}, bf16[80,128]{1,0:T(8,128)(2,1)S(1)}, u32[]{:S(2)}, u32[]{:S(2)}) collective-permute-start(bf16[80,128]{1,0:T(8,128)(2,1)S(1)} %get-tuple-element.57), channel_id=1, source_target_pairs={{0,3},{1,2},{2,1},{3,0},{4,7},{5,6},{6,5},{7,4},{8,11},{9,10},{10,... | collective-permute-start | bytes 61448 | tf_op jit(solution)/shard_map/ppermute | solution.py:399
  33.4 3.7 %collective-permute-start.10 = (bf16[60,128]{1,0:T(8,128)(2,1)S(1)}, bf16[60,128]{1,0:T(8,128)(2,1)S(1)}, u32[]{:S(2)}, u32[]{:S(2)}) collective-permute-start(bf16[60,128]{1,0:T(8,128)(2,1)S(1)} %get-tuple-element.54), channel_id=1, source_target_pairs={{0,4},{1,5},{2,6},{3,7},{4,0},{5,1},{6,2},{7,3},{8,12},{9,13},{10,... | collective-permute-start | bytes 46088 | tf_op jit(solution)/shard_map/ppermute | solution.py:399
  34.9 3.7 %collective-permute-start.11 = (bf16[60,128]{1,0:T(8,128)(2,1)S(1)}, bf16[60,128]{1,0:T(8,128)(2,1)S(1)}, u32[]{:S(2)}, u32[]{:S(2)}) collective-permute-start(bf16[60,128]{1,0:T(8,128)(2,1)S(1)} %get-tuple-element.55), channel_id=1, source_target_pairs={{0,2},{1,3},{2,0},{3,1},{4,8},{5,9},{6,10},{7,11},{8,4},{9,5},{10,... | collective-permute-start | bytes 46088 | tf_op jit(solution)/shard_map/ppermute | solution.py:399
  40.4 7.2 %collective-permute-start.14 = (bf16[8,64]{1,0:T(8,128)(2,1)S(1)}, bf16[8,64]{1,0:T(8,128)(2,1)S(1)}, u32[]{:S(2)}, u32[]{:S(2)}) collective-permute-start(bf16[8,64]{1,0:T(8,128)(2,1)S(1)} %get-tuple-element.61), channel_id=1, source_target_pairs={{0,4},{1,5},{2,6},{3,7},{4,0},{5,1},{6,2},{7,3},{8,12},{9,13},{10,... | collective-permute-start | bytes 3080 | tf_op jit(solution)/shard_map/ppermute | solution.py:399
  42.8 4.7 %collective-permute-start.15 = (bf16[8,64]{1,0:T(8,128)(2,1)S(1)}, bf16[8,64]{1,0:T(8,128)(2,1)S(1)}, u32[]{:S(2)}, u32[]{:S(2)}) collective-permute-start(bf16[8,64]{1,0:T(8,128)(2,1)S(1)} %get-tuple-element.62), channel_id=1, source_target_pairs={{0,2},{1,3},{2,0},{3,1},{4,8},{5,9},{6,10},{7,11},{8,4},{9,5},{10,... | collective-permute-start | bytes 3080 | tf_op jit(solution)/shard_map/ppermute | solution.py:399
  (4 other events, 38.0 us)

commit v3 on v2

--- a/solution.py
+++ b/solution.py
@@ -65,15 +65,15 @@
     return jnp.concatenate([high.astype(f32), low.astype(f32)], axis=0).astype(bf16)
 
 
-def transfer(inter, smap, rate_ref, eb, t_ref, q_ref, nfreq):
+def transfer(inter, weights, eb, t_ref, q_ref):
     t_ref[...] = dot(inter, eb)
-    q = dot(stress_rows(smap, rate_ref, nfreq), eb)
+    q = dot(weights, eb)
     half = 2 * NDIR
     q_ref[...] = q[:half] + q[half:]
 
 
 def wave_finish(
-    e_of, t_ref, q_ref, wind_ref, current_of, wet_ref, rate_ref, gain_ref, kmap, upd_ref, nfreq
+    e_of, t_ref, q_ref, wind_ref, current_of, wet_ref, rate_of, gain_of, kmap, upd_ref, nfreq
 ):
     rows, lanes = wet_ref.shape
     heading = lax.broadcasted_iota(jnp.int32, (NDIR, lanes), 0).astype(f32)
@@ -95,7 +95,7 @@
             ]
         )
         rate = jnp.concatenate(
-            [rate_ref[f] * soft + gain_ref[f] * level for f in range(nfreq)], axis=0
+            [rate_of(f) * soft + gain_of(f) * level for f in range(nfreq)], axis=0
         )
         e = e_of(y)
         upd_ref[:, cells] = (wet * (e + rate * e + t_ref[:, cells])).astype(bf16)
@@ -136,7 +136,7 @@
 def k_wave_first(
     nfreq,
     spec_hbm, inter_hbm, smap_hbm, rate_hbm, wind_hbm, cur_hbm, wet_hbm, gain_hbm, kmap_hbm, send_hbm,
-    upd_ref, to_even, to_odd, own,
+    upd_ref, to_even, to_odd, own, weight_ref,
     spec_ref, inter_ref, smap_ref, rate_ref, wind_ref, cur_ref, wet_ref, gain_ref, kmap_ref, send_ref,
     ef, eb, t, q, sems,
 ):
@@ -153,23 +153,24 @@
         eb[:, y * lanes : (y + 1) * lanes] = ef[pl.ds(y, spec, stride=rows), :].astype(bf16)
     for copy in copies[1:]:
         copy.wait()
-    transfer(inter_ref[...], smap_ref[...], rate_ref, eb[...], t, q, nfreq)
+    weight_ref[...] = stress_rows(smap_ref[...], rate_ref, nfreq)
+    transfer(inter_ref[...], weight_ref[...], eb[...], t, q)
     fields = wave_finish(
         lambda y: ef[pl.ds(y, spec, stride=rows), :],
         t, q, wind_ref,
         lambda i, y: cur_ref[i, y : y + 1, :],
-        wet_ref, rate_ref, gain_ref, kmap_ref[...], upd_ref, nfreq,
+        wet_ref, lambda f: rate_ref[f], lambda f: gain_ref[f], kmap_ref[...], upd_ref, nfreq,
     )
     pick(fields, send_ref, (to_even, to_odd, own))
 
 
-def k_transfer(nfreq, upd_ref, inter_ref, smap_ref, rate_ref, t_ref, q_ref):
-    transfer(inter_ref[...], smap_ref[...], rate_ref, upd_ref[...], t_ref, q_ref, nfreq)
+def k_transfer(upd_ref, inter_ref, weight_ref, t_ref, q_ref):
+    transfer(inter_ref[...], weight_ref[...], upd_ref[...], t_ref, q_ref)
 
 
 def k_wave_next(
     nfreq, n_row,
-    got_even, got_odd, got_own, recv_ref, old_ref, t_ref, q_ref, wind_ref, wet_ref, rate_ref, gain_ref, kmap_ref, send_ref,
+    got_even, got_odd, got_own, recv_ref, old_ref, t_ref, q_ref, wind_ref, wet_ref, coef_ref, kmap_ref, send_ref,
     upd_ref, to_even, to_odd, own,
     cur,
 ):
@@ -180,7 +181,7 @@
         lambda y: old_ref[:, y * lanes : (y + 1) * lanes].astype(f32),
         t_ref, q_ref, wind_ref,
         lambda i, y: cur[i : i + 1, y * lanes : (y + 1) * lanes],
-        wet_ref, rate_ref, gain_ref, kmap_ref[...], upd_ref, nfreq,
+        wet_ref, row_of(coef_ref, RATE), row_of(coef_ref, GAIN), kmap_ref[...], upd_ref, nfreq,
     )
     pick(fields, send_ref, (to_even, to_odd, own))
 
@@ -201,9 +202,45 @@
             out_ref[i, y : y + 1, :] = cur[i : i + 1, y * lanes : (y + 1) * lanes]
 
 
+TAU, PROF, THICK, SURF, RATE, GAIN = 0, 1, 1 + NBAND, 2 + NBAND, 3 + NBAND, 4 + NBAND
+
+
+def row_of(coef_ref, which):
+    return lambda l: coef_ref[which * 32 + l : which * 32 + l + 1, :]
+
+
+def column(vector, first, count):
+    row = lax.broadcasted_iota(jnp.int32, (count, vector.shape[1]), 0)
+    lane = lax.broadcasted_iota(jnp.int32, (count, vector.shape[1]), 1)
+    picked = jnp.sum(jnp.where(row - first == lane, vector, 0.0), axis=1, keepdims=True)
+    return jnp.broadcast_to(picked, (count, 128))
+
+
+def spread(vector, first):
+    lev = vector.shape[1]
+    parts = [vector, jnp.zeros((1, 128 - lev - first), f32)]
+    if first:
+        parts = [jnp.zeros((1, first), f32)] + parts
+    return jnp.concatenate(parts, axis=1)
+
+
+def k_prepare(lev, tau_ref, prof_ref, thick_ref, mix_ref, rate_ref, gain_ref, coef_ref, side_ref, lane_ref):
+    surf = mix_ref[0:1, :]
+    vectors = [tau_ref[...]] + [prof_ref[b : b + 1, :] for b in range(NBAND)]
+    vectors += [thick_ref[...], surf, rate_ref[...], gain_ref[...]]
+    for i, vector in enumerate(vectors):
+        coef_ref[i * 32 : (i + 1) * 32, :] = column(vector, 0, 32)
+    side_ref[0] = column(surf, 0, 2 * lev)
+    side_ref[1] = column(surf, lev, 2 * lev)
+    side_ref[2] = column(thick_ref[...], lev, 2 * lev)
+    lane_ref[0:1, :] = spread(surf, 0)
+    lane_ref[1:2, :] = spread(surf, lev)
+    lane_ref[2:3, :] = spread(thick_ref[...], 0)
+
+
 def k_force(
     n_row, lev, pad,
-    got_even, got_odd, own, recv_ref, vel_ref, wet_ref, cor_ref, tau_ref, prof_ref,
+    got_even, got_odd, own, recv_ref, vel_ref, wet_ref, cor_ref, coef_ref,
     forced_ref, row_even, row_odd, col_even, col_odd,
     fs,
 ):
@@ -217,14 +254,16 @@
     wet = wet_ref[...].astype(f32)
     cor = cor_ref[...]
     along = [cor * field[i] for i in range(2, nf)]
+    tau = row_of(coef_ref, TAU)
+    prof = [row_of(coef_ref, PROF + b) for b in range(NBAND)]
     lane = lax.broadcasted_iota(jnp.int32, (oy, ox), 1)
     east = jnp.zeros((oy, ox), f32)
     west = jnp.zeros((oy, ox), f32)
     for i in range(planes):
         c, l = divmod(i, lev)
-        accel = tau_ref[l] * field[c]
+        accel = tau(l) * field[c]
         for b in range(NBAND):
-            term = prof_ref[b, l] * along[2 * b + 1 - c]
+            term = prof[b](l) * along[2 * b + 1 - c]
             accel = accel + term if c == 0 else accel - term
         value = wet * (vel_ref[i * oy : (i + 1) * oy, :] + accel)
         forced_ref[i * oy : (i + 1) * oy, :] = value
@@ -244,25 +283,53 @@
     col_odd[pad:, :] = jnp.concatenate([jnp.where(even, west, east), filler], 0).astype(bf16)
 
 
-def k_smooth(
-    n_row, n_col, lev, pad, whole,
-    forced_ref, got_row_even, got_row_odd, got_col_even, got_col_odd, line_ref, fold_ref, eta_ref, wet_ref, thick_ref, mix_ref, send_ref,
-    smooth_ref, eta_out, to_even, to_odd, own,
-    north, south, bs,
+def borders(oy, ox):
+    lane = lax.broadcasted_iota(jnp.int32, (oy, ox), 1)
+    line = lax.broadcasted_iota(jnp.int32, (oy, ox), 0)
+    return line == oy - 1, line == 0, lane == ox - 1, lane == 0
+
+
+def k_interior(lev, forced_ref, eta_ref, wet_ref, coef_ref, part_ref, sums_ref):
+    oy, ox = wet_ref.shape
+    wet = wet_ref[...].astype(f32)
+    is_top, is_bottom, is_east, is_west = borders(oy, ox)
+    thick, surf = row_of(coef_ref, THICK), row_of(coef_ref, SURF)
+    across = jnp.zeros((oy, ox), f32)
+    surface = [jnp.zeros((oy, ox), f32), jnp.zeros((oy, ox), f32)]
+    for i in range(2 * lev):
+        c, l = divmod(i, lev)
+        here = forced_ref[i * oy : (i + 1) * oy, :]
+        up = jnp.where(is_top, 0.0, pltpu.roll(here, oy - 1, 0))
+        down = jnp.where(is_bottom, 0.0, pltpu.roll(here, 1, 0))
+        right = jnp.where(is_east, 0.0, pltpu.roll(here, ox - 1, 1))
+        left = jnp.where(is_west, 0.0, pltpu.roll(here, 1, 1))
+        part = wet * (here + viscous * (up + down + right + left - 4.0 * here))
+        part_ref[i * oy : (i + 1) * oy, :] = part
+        surface[c] = surface[c] + surf(l) * part
+        across = across + thick(l) * (right - left if c == 0 else up - down)
+    sums_ref[:oy, :] = surface[0]
+    sums_ref[oy : 2 * oy, :] = surface[1]
+    sums_ref[2 * oy :, :] = wet * (eta_ref[...] - surface_rate * 0.5 * across)
+
+
+def k_back(
+    n_row, n_col, pad, whole,
+    got_row_even, got_row_odd, got_col_even, got_col_odd, sent_col, line_ref, fold_ref, sums_ref, wet_ref, side_ref, lane_ref, send_ref,
+    eta_out, to_even, to_odd, own, north_ref, south_ref, ends_ref,
+    bs,
 ):
     oy, ox = wet_ref.shape
-    planes = 2 * lev
+    planes = got_row_even.shape[0]
     row, col = lax.axis_index("row"), lax.axis_index("col")
     even = is_even(row)
     a, b = got_row_even[...].astype(f32), got_row_odd[...].astype(f32)
     if whole:
         pieces = [(line_ref[t * planes : (t + 1) * planes, :], t) for t in range(n_col)]
     else:
-        top = forced_ref[pl.ds(oy - 1, planes, stride=oy), :].astype(bf16)
         pair_even = jnp.where(is_even(col), col + 1, col - 1)
         pair_odd = lax.rem(jnp.where(is_even(col), col - 1, col + 1) + n_col, n_col)
         pieces = [
-            (top, col),
+            (sent_col[:planes, :], col),
             (got_col_even[:planes, :], pair_even),
             (got_col_odd[:planes, :], pair_odd),
             (got_row_odd[...], lax.rem(col + n_col // 2, n_col)),
@@ -273,63 +340,70 @@
         hot = jnp.where(cell == fold_ref[...] - tile * ox, 1.0, 0.0).astype(bf16)
         part = dot(piece, hot)
         across = part if across is None else across + part
-    north[...] = jnp.where(row == n_row - 1, -across, jnp.where(even, a, b))
-    south[...] = jnp.where(row == 0, 0.0, jnp.where(even, b, a))
+    north = jnp.where(row == n_row - 1, -across, jnp.where(even, a, b))
+    south = jnp.where(row == 0, 0.0, jnp.where(even, b, a))
     even = is_even(col)
     a = got_col_even[pad:, :].astype(f32)[:oy]
     b = got_col_odd[pad:, :].astype(f32)[:oy]
-    east_col = jnp.where(even, a, b)
-    west_col = jnp.where(even, b, a)
+    east, west = jnp.where(even, a, b), jnp.where(even, b, a)
+    north_ref[...] = north
+    south_ref[...] = south
+    ends_ref[:oy, :] = east
+    ends_ref[oy:, :] = west
     wet = wet_ref[...].astype(f32)
-    lane = lax.broadcasted_iota(jnp.int32, (oy, ox), 1)
-    line = lax.broadcasted_iota(jnp.int32, (oy, ox), 0)
-    is_top, is_bottom = line == oy - 1, line == 0
-    is_east, is_west = lane == ox - 1, lane == 0
-    across_u = jnp.zeros((oy, ox), f32)
-    across_v = jnp.zeros((oy, ox), f32)
-    surface = []
-    for i in range(planes):
-        c, l = divmod(i, lev)
-        here = forced_ref[i * oy : (i + 1) * oy, :]
-        up = jnp.where(is_top, north[i : i + 1, :], pltpu.roll(here, oy - 1, 0))
-        down = jnp.where(is_bottom, south[i : i + 1, :], pltpu.roll(here, 1, 0))
-        right = jnp.where(is_east, pltpu.roll(east_col, (ox - 1 - i) % ox, 1), pltpu.roll(here, ox - 1, 1))
-        left = jnp.where(is_west, pltpu.roll(west_col, (ox - i) % ox, 1), pltpu.roll(here, 1, 1))
-        smooth = wet * (here + viscous * (up + down + right + left - 4.0 * here))
-        smooth_ref[i * oy : (i + 1) * oy, :] = smooth
-        if l == 0:
-            surface.append(mix_ref[0, 0] * smooth)
-        else:
-            surface[c] = surface[c] + mix_ref[0, l] * smooth
-        if c == 0:
-            across_u = across_u + thick_ref[l] * (right - left)
-        else:
-            across_v = across_v + thick_ref[l] * (up - down)
-    eta = wet * (eta_ref[...] - surface_rate * (0.5 * across_u + 0.5 * across_v))
+    is_top, is_bottom, is_east, is_west = borders(oy, ox)
+
+    def over_rows(x, i):
+        return jnp.sum(x * side_ref[i], axis=0, keepdims=True)
+
+    def over_lanes(x, i):
+        return jnp.sum(x * lane_ref[i : i + 1, :], axis=1, keepdims=True)
+
+    for c in range(2):
+        edge = jnp.where(is_top, over_rows(north, c), 0.0) + jnp.where(is_bottom, over_rows(south, c), 0.0)
+        edge = edge + jnp.where(is_east, over_lanes(east, c), 0.0)
+        edge = edge + jnp.where(is_west, over_lanes(west, c), 0.0)
+        bs[c * oy : (c + 1) * oy, :] = sums_ref[c * oy : (c + 1) * oy, :] + viscous * wet * edge
+    flow = jnp.where(is_east, over_lanes(east, 2), 0.0) - jnp.where(is_west, over_lanes(west, 2), 0.0)
+    flow = flow + jnp.where(is_top, over_rows(north, 2), 0.0) - jnp.where(is_bottom, over_rows(south, 2), 0.0)
+    eta = sums_ref[2 * oy :, :] - surface_rate * 0.5 * wet * flow
     eta_out[...] = eta
-    bs[: oy, :] = surface[0]
-    bs[oy : 2 * oy, :] = surface[1]
     bs[2 * oy : 3 * oy, :] = eta
     bs[3 * oy :, :] = jnp.zeros((5 * oy, ox), f32)
     back = jnp.concatenate([bs[pl.ds(y, 8, stride=oy), :] for y in range(oy)], axis=1)
     pick(back, send_ref, (to_even, to_odd, own))
 
 
-def k_mix(lev, oy, smooth_ref, mix_ref, vel_ref):
-    group = 6
-    for first in range(0, lev, group):
-        levels = range(first, min(first + group, lev))
-        total = {}
-        for m in range(lev):
-            u = smooth_ref[m * oy : (m + 1) * oy, :]
-            v = smooth_ref[(lev + m) * oy : (lev + m + 1) * oy, :]
-            for l in levels:
-                w = mix_ref[l, m]
-                total[l, 0] = w * u if m == 0 else total[l, 0] + w * u
-                total[l, 1] = w * v if m == 0 else total[l, 1] + w * v
-        for l in levels:
-            vel_ref[l * oy : (l + 1) * oy, :] = total[l, 0]
-            vel_ref[(lev + l) * oy : (lev + l + 1) * oy, :] = total[l, 1]
+def k_mix(lev, part_ref, north_ref, south_ref, ends_ref, wet_ref, mix_ref, eta_ref, vel_ref, eta_out, smooth, wide):
+    oy, ox = wet_ref.shape
+    planes = 2 * lev
+    eta_out[...] = eta_ref[...]
+    wet = viscous * wet_ref[...].astype(f32)
+    is_top, is_bottom, is_east, is_west = borders(oy, ox)
+    east, west = ends_ref[:oy, :], ends_ref[oy:, :]
+    for i in range(planes):
+        edge = jnp.where(is_top, north_ref[i : i + 1, :], 0.0)
+        edge = edge + jnp.where(is_bottom, south_ref[i : i + 1, :], 0.0)
+        edge = edge + jnp.where(is_east, pltpu.roll(east, (ox - 1 - i) % ox, 1), 0.0)
+        edge = edge + jnp.where(is_west, pltpu.roll(west, (ox - i) % ox, 1), 0.0)
+        smooth[i * oy : (i + 1) * oy, :] = part_ref[i * oy : (i + 1) * oy, :] + wet * edge
+    step = wide.shape[0] // 3
+    blocks = [(c, y) for c in range(2) for y in range(oy)]
+    for n, (c, y) in enumerate(blocks):
+        column_block = smooth[pl.ds(c * lev * oy + y, lev, stride=oy), :]
+        column_block = jnp.concatenate([column_block, jnp.zeros((step - lev, ox), f32)], axis=0)
+        high, low = split2(column_block)
+        cells = slice(n * ox, (n + 1) * ox)
+        wide[:step, cells] = high
+        wide[step : 2 * step, cells] = low
+        wide[2 * step :, cells] = high
+    high, low = split2(mix_ref[...])
+    filler = jnp.zeros((lev, step - lev), f32)
+    high, low = high.astype(f32), low.astype(f32)
+    left = jnp.concatenate([high, filler, high, filler, low, filler], axis=1).astype(bf16)
+    mixed = dot(left, wide[...])
+    for n, (c, y) in enumerate(blocks):
+        vel_ref[pl.ds(c * lev * oy + y, lev, stride=oy), :] = mixed[:, n * ox : (n + 1) * ox]
 
 
 def pairings(n_row, n_col):
@@ -400,16 +474,18 @@
 
     slots_out = [((8, slot), bf16)] * 3
     wave_outs = [((spec, cells), bf16)] + slots_out
+    full = (planes * oy, ox)
     for step in range(STEPS):
+        last = step + 1 == STEPS
         if step == 0:
             inputs = (
                 spectra.reshape(spec * rows, lanes), interaction, stress_map, input_rate, wind, wave_current,
                 wave_wet, eta_gain, stokes_map, wsend,
             )
             held = [(pltpu.SMEM if x.ndim == 1 else pltpu.VMEM)(x.shape, x.dtype) for x in inputs]
-            updated, to_even, to_odd, own = call(
+            updated, to_even, to_odd, own, weights = call(
                 functools.partial(k_wave_first, nfreq),
-                wave_outs,
+                wave_outs + [((4 * NDIR, spec), bf16)],
                 [HBM] * len(inputs),
                 held
                 + [
@@ -422,57 +498,63 @@
             )(*(pltpu.with_memory_space_constraint(x, pltpu.HBM) for x in inputs))
         else:
             updated, to_even, to_odd, own = call(
-                functools.partial(k_wave_next, nfreq, n_row),
-                wave_outs,
-                [VMEM] * 9 + [SMEM] * 2 + [VMEM] * 2,
-                [pltpu.VMEM((8, cells), f32)],
+                functools.partial(k_wave_next, nfreq, n_row), wave_outs, [VMEM] * 12, [pltpu.VMEM((8, cells), f32)]
             )(
                 got_even, got_odd, own, wave_w, updated, moved, q, wind, wave_wet,
-                input_rate, eta_gain, stokes_map, wsend,
+                coef, stokes_map, wsend,
             )
         got_odd, got_even = trade("row_odd", to_odd), trade("row_even", to_even)
-        if step + 1 < STEPS:
-            moved, q = call(
-                functools.partial(k_transfer, nfreq),
-                [((spec, cells), f32), ((2 * NDIR, cells), f32)],
-                [VMEM] * 3 + [SMEM],
-            )(updated, interaction, stress_map, input_rate)
-        forced, row_even, row_odd, col_even, col_odd = call(
-            functools.partial(k_force, n_row, lev, pad),
-            [((planes * oy, ox), f32)] + [((planes, ox), bf16)] * 2 + [((pad + 16, ox), bf16)] * 2,
-            [VMEM] * 7 + [SMEM] * 2,
-            [pltpu.VMEM((8 * oy, ox), f32)],
-        )(got_even, got_odd, own, ocean_w, velocity, ocean_wet, coriolis, tau_profile, stokes_profile)
-        got_row_odd, got_row_even = trade("row_odd", row_odd), trade("row_even", row_even)
-        got_col_odd, got_col_even = trade("col_odd", col_odd), trade("col_even", col_even)
-        if step + 1 == STEPS:
+        if step == 0:
+            coef, side, lane_rows = call(
+                functools.partial(k_prepare, lev),
+                [((8 * 32, 128), f32), ((3, planes, 128), f32), ((8, 128), f32)],
+                [VMEM] * 6,
+            )(
+                tau_profile.reshape(1, lev), stokes_profile, thickness.reshape(1, lev), mix_inverse,
+                input_rate.reshape(1, nfreq), eta_gain.reshape(1, nfreq),
+            )
+        if last:
             (spectra_out,) = call(
                 functools.partial(k_spectra_out, rows),
                 [((spec * rows, lanes), bf16)],
                 [VMEM],
                 [pltpu.VMEM((spec * rows, lanes), f32)],
             )(updated)
+        forced, row_even, row_odd, col_even, col_odd = call(
+            functools.partial(k_force, n_row, lev, pad),
+            [(full, f32)] + [((planes, ox), bf16)] * 2 + [((pad + 16, ox), bf16)] * 2,
+            [VMEM] * 8,
+            [pltpu.VMEM((8 * oy, ox), f32)],
+        )(got_even, got_odd, own, ocean_w, velocity, ocean_wet, coriolis, coef)
+        got_row_odd, got_row_even = trade("row_odd", row_odd), trade("row_even", row_even)
+        got_col_odd, got_col_even = trade("col_odd", col_odd), trade("col_even", col_even)
+        part, sums = call(
+            functools.partial(k_interior, lev), [(full, f32), ((3 * oy, ox), f32)], [VMEM] * 4
+        )(forced, eta, ocean_wet, coef)
         if whole:
             top_line = lax.all_gather(col_even[:planes], "col", axis=0, tiled=True)
         else:
             top_line = fold
-        smooth, eta, to_even, to_odd, own = call(
-            functools.partial(k_smooth, n_row, n_col, lev, pad, whole),
-            [((planes * oy, ox), f32), ((oy, ox), f32)] + slots_out,
-            [VMEM] * 9 + [SMEM] * 2 + [VMEM],
-            [
-                pltpu.VMEM((planes, ox), f32),
-                pltpu.VMEM((planes, ox), f32),
-                pltpu.VMEM((8 * oy, ox), f32),
-            ],
+        eta, to_even, to_odd, own, north, south, ends = call(
+            functools.partial(k_back, n_row, n_col, pad, whole),
+            [((oy, ox), f32)] + slots_out + [((planes, ox), f32)] * 2 + [((2 * oy, ox), f32)],
+            [VMEM] * 12,
+            [pltpu.VMEM((8 * oy, ox), f32)],
         )(
-            forced, got_row_even, got_row_odd, got_col_even, got_col_odd, top_line, fold, eta, ocean_wet,
-            thickness, mix_inverse, osend,
+            got_row_even, got_row_odd, got_col_even, got_col_odd, col_even, top_line, fold, sums, ocean_wet,
+            side, lane_rows, osend,
         )
         got_odd, got_even = trade("row_odd", to_odd), trade("row_even", to_even)
-        (velocity,) = call(
-            functools.partial(k_mix, lev, oy), [((planes * oy, ox), f32)], [VMEM, SMEM]
-        )(smooth, mix_inverse)
+        if not last:
+            moved, q = call(
+                k_transfer, [((spec, cells), f32), ((2 * NDIR, cells), f32)], [VMEM] * 3
+            )(updated, interaction, weights)
+        velocity, eta = call(
+            functools.partial(k_mix, lev),
+            [(full, f32), ((oy, ox), f32)],
+            [VMEM] * 7,
+            [pltpu.VMEM(full, f32), pltpu.VMEM((96, 2 * oy * ox), bf16)],
+        )(part, north, south, ends, ocean_wet, mix_inverse, eta)
     (current,) = call(
         functools.partial(k_current_out, n_row), [((3, rows, lanes), f32)], [VMEM] * 4
     )(got_even, got_odd, own, wave_w)

time: 48.5 us -> 43.3 us (0.89)
  Pallas kernels: 16.2 us -> 9.96 us
  waiting for transfers between devices: 11.2 us -> 12.2 us
    pallas_call x9 -> x12, Pallas kernels: 14.4 us -> 8.13 us  [the longest x1 2.68 us: shards(): call(functools.partial(k_wave_first, nfreq), wave_outs + [((4 * NDIR, spe...]
    ppermute x16, waiting for transfers between devices: 11.2 us -> 12.2 us  [trade(): return lax.ppermute(array, axis, pairs[label])]
  transfers between devices with their start and end apart: 16 -> 16, of which waited for: 9 -> 9; matrix products, arithmetic and copies ran while one was open for 0% -> 0% of each run, Pallas kernels for 12% -> 9%
where the time goes in v3:
time: 43.3 us; the launch traced here: 43.1 us
  starting transfers between devices  19.9 us (46%)
  waiting for transfers between devices  12.2 us (28%)
  Pallas kernels  9.96 us (23%)
  between operations  0.94 us (2%)
    ppermute x16, starting transfers between devices, trade(): return lax.ppermute(array, axis, pairs[label])  19.9 us
    ppermute x16, waiting for transfers between devices, trade(): return lax.ppermute(array, axis, pairs[label])  12.2 us
    pallas_call x1, Pallas kernels, shards(): call(functools.partial(k_wave_first, nfreq), wave_outs + [((4 * NDIR, spe...  2.68 us
    pallas_call x2, Pallas kernels, shards(): call(functools.partial(k_mix, lev), [(full, f32), ((oy, ox), f32)], [VMEM...  1.53 us
    pallas_call x1, Pallas kernels, shards(): call(functools.partial(k_spectra_out, rows), [((spec * rows, lanes), bf16...  1.05 us
    pallas_call x1, Pallas kernels, shards(): call(functools.partial(k_wave_next, nfreq, n_row), wave_outs, [VMEM] * 12...  1 us
  transfers between devices with their start and end apart: 16, of which 9 were waited for; matrix products, arithmetic and copies ran while one was open for 0% of the time, Pallas kernels for 9%

profile of v3, /device:TPU:0, one launch (start us, length us, event | category | flops | bytes accessed | tf_op | source)
XLA Modules:
  0.0 43.1 jit_solution(14371491305974173314)
XLA Ops:
  0.8 2.7 %shard_map.237 = (bf16[600,512]{1,0:T(8,128)(2,1)S(1)}, bf16[8,64]{1,0:T(8,128)(2,1)S(1)}, bf16[8,64]{1,0:T(8,128)(2,1)S(1)}, bf16[8,64]{1,0:T(8,128)(2,1)S(1)}, bf16[96,600]{1,0:T(8,128)(2,1)S(1)}) custom-call(bf16[2400,128]{1,0:T(8,128)(2,1)} %bitcast.30, bf16[600,600]{1,0:T(8,128)(2,1)} %inter_ref.1, f32[2,600]{1,0:T(2,128)} %smap_hbm.1, f32[25]{0:T(128)} %rate_hbm.1, ...), custom_call_target="tpu_custom_call" | custom-call | tf_op jit(solution)/shard_map/pallas_call | solution.py:486
  3.5 3.1 %collective-permute-start = (bf16[8,64]{1,0:T(8,128)(2,1)S(1)}, bf16[8,64]{1,0:T(8,128)(2,1)S(1)}, u32[]{:S(2)}, u32[]{:S(2)}) collective-permute-start(bf16[8,64]{1,0:T(8,128)(2,1)S(1)} %get-tuple-element.50), channel_id=1, source_target_pairs={{0,4},{1,5},{2,6},{3,7},{4,0},{5,1},{6,2},{7,3},{8,12},{9,13},{10,... | collective-permute-start | bytes 3080 | tf_op jit(solution)/shard_map/ppermute | solution.py:473
  6.5 1.5 %collective-permute-start.1 = (bf16[8,64]{1,0:T(8,128)(2,1)S(1)}, bf16[8,64]{1,0:T(8,128)(2,1)S(1)}, u32[]{:S(2)}, u32[]{:S(2)}) collective-permute-start(bf16[8,64]{1,0:T(8,128)(2,1)S(1)} %get-tuple-element.51), channel_id=1, source_target_pairs={{0,2},{1,3},{2,0},{3,1},{4,8},{5,9},{6,10},{7,11},{8,4},{9,5},{10,... | collective-permute-start | bytes 3080 | tf_op jit(solution)/shard_map/ppermute | solution.py:473
  8.2 1.9 %collective-permute-done.1.got_odd = bf16[8,64]{1,0:T(8,128)(2,1)S(1)} collective-permute-done((bf16[8,64]{1,0:T(8,128)(2,1)S(1)}, bf16[8,64]{1,0:T(8,128)(2,1)S(1)}, u32[]{:S(2)}, u32[]{:S(2)}) %collective-permute-start.1) | collective-permute-done | bytes 1056 | tf_op jit(solution)/shard_map/ppermute | solution.py:473
  10.7 1.6 %collective-permute-start.4 = (bf16[80,128]{1,0:T(8,128)(2,1)S(1)}, bf16[80,128]{1,0:T(8,128)(2,1)S(1)}, u32[]{:S(2)}, u32[]{:S(2)}) collective-permute-start(bf16[80,128]{1,0:T(8,128)(2,1)S(1)} %get-tuple-element.56.sent_col), channel_id=1, source_target_pairs={{0,1},{1,0},{2,3},{3,2},{4,5},{5,4},{6,7},{7,6},{8,9},{9,8},{10,11... | collective-permute-start | bytes 61448 | tf_op jit(solution)/shard_map/ppermute | solution.py:473
  12.2 1.4 %collective-permute-start.2 = (bf16[60,128]{1,0:T(8,128)(2,1)S(1)}, bf16[60,128]{1,0:T(8,128)(2,1)S(1)}, u32[]{:S(2)}, u32[]{:S(2)}) collective-permute-start(bf16[60,128]{1,0:T(8,128)(2,1)S(1)} %get-tuple-element.54), channel_id=1, source_target_pairs={{0,4},{1,5},{2,6},{3,7},{4,0},{5,1},{6,2},{7,3},{8,12},{9,13},{10,... | collective-permute-start | bytes 46088 | tf_op jit(solution)/shard_map/ppermute | solution.py:473
  14.0 2.0 %collective-permute-done.2.got_row_even = bf16[60,128]{1,0:T(8,128)(2,1)S(1)} collective-permute-done((bf16[60,128]{1,0:T(8,128)(2,1)S(1)}, bf16[60,128]{1,0:T(8,128)(2,1)S(1)}, u32[]{:S(2)}, u32[]{:S(2)}) %collective-permute-start.2) | collective-permute-done | bytes 15392 | tf_op jit(solution)/shard_map/ppermute | solution.py:473
  16.0 1.4 %collective-permute-done.3.got_row_odd = bf16[60,128]{1,0:T(8,128)(2,1)S(1)} collective-permute-done((bf16[60,128]{1,0:T(8,128)(2,1)S(1)}, bf16[60,128]{1,0:T(8,128)(2,1)S(1)}, u32[]{:S(2)}, u32[]{:S(2)}) %collective-permute-start.3) | collective-permute-done | bytes 15392 | tf_op jit(solution)/shard_map/ppermute | solution.py:473
  17.4 0.4 %shard_map.241 = (f32[8,128]{1,0:T(8,128)S(1)}, bf16[8,64]{1,0:T(8,128)(2,1)S(1)}, bf16[8,64]{1,0:T(8,128)(2,1)S(1)}, bf16[8,64]{1,0:T(8,128)(2,1)S(1)}, f32[60,...) custom-call(bf16[60,128]{1,0:T(8,128)(2,1)S(1)} %collective-permute-done.2.got_row_even, ...), custom_call_target="tpu_custom_call" | custom-call | tf_op jit(solution)/shard_map/pallas_call | solution.py:538
  17.8 1.6 %collective-permute-start.6 = (bf16[8,64]{1,0:T(8,128)(2,1)S(1)}, bf16[8,64]{1,0:T(8,128)(2,1)S(1)}, u32[]{:S(2)}, u32[]{:S(2)}) collective-permute-start(bf16[8,64]{1,0:T(8,128)(2,1)S(1)} %get-tuple-element.62), channel_id=1, source_target_pairs={{0,4},{1,5},{2,6},{3,7},{4,0},{5,1},{6,2},{7,3},{8,12},{9,13},{10,... | collective-permute-start | bytes 3080 | tf_op jit(solution)/shard_map/ppermute | solution.py:473
  19.4 0.5 %collective-permute-start.7 = (bf16[8,64]{1,0:T(8,128)(2,1)S(1)}, bf16[8,64]{1,0:T(8,128)(2,1)S(1)}, u32[]{:S(2)}, u32[]{:S(2)}) collective-permute-start(bf16[8,64]{1,0:T(8,128)(2,1)S(1)} %get-tuple-element.63), channel_id=1, source_target_pairs={{0,2},{1,3},{2,0},{3,1},{4,8},{5,9},{6,10},{7,11},{8,4},{9,5},{10,... | collective-permute-start | bytes 3080 | tf_op jit(solution)/shard_map/ppermute | solution.py:473
  20.0 0.7 %shard_map.242 = (f32[600,512]{1,0:T(8,128)S(1)}, f32[48,512]{1,0:T(8,128)S(1)}) custom-call(bf16[600,512]{1,0:T(8,128)(2,1)S(1)} %get-tuple-element.65.upd_ref.old_ref, bf16[600,600]{1,0:T(8,128)(2,1)S(1)} %copy-done, bf16[96,600]{1,0:T(8,128)(2,1)S(1)} %get-tuple-element.66.weight_ref), custom_call_target="tpu_custom_call" | custom-call | tf_op jit(solution)/shard_map/pallas_call | solution.py:549
  20.7 0.8 %collective-permute-done.6.got_even = bf16[8,64]{1,0:T(8,128)(2,1)S(1)} collective-permute-done((bf16[8,64]{1,0:T(8,128)(2,1)S(1)}, bf16[8,64]{1,0:T(8,128)(2,1)S(1)}, u32[]{:S(2)}, u32[]{:S(2)}) %collective-permute-start.6) | collective-permute-done | bytes 1056 | tf_op jit(solution)/shard_map/ppermute | solution.py:473
  21.5 1.5 %collective-permute-done.7.got_odd = bf16[8,64]{1,0:T(8,128)(2,1)S(1)} collective-permute-done((bf16[8,64]{1,0:T(8,128)(2,1)S(1)}, bf16[8,64]{1,0:T(8,128)(2,1)S(1)}, u32[]{:S(2)}, u32[]{:S(2)}) %collective-permute-start.7) | collective-permute-done | bytes 1056 | tf_op jit(solution)/shard_map/ppermute | solution.py:473
  23.0 1.0 %shard_map.243 = (bf16[600,512]{1,0:T(8,128)(2,1)S(1)}, bf16[8,64]{1,0:T(8,128)(2,1)S(1)}, bf16[8,64]{1,0:T(8,128)(2,1)S(1)}, bf16[8,64]{1,0:T(8,128)(2,1)S(1)}) custom-call(bf16[8,64]{1,0:T(8,128)(2,1)S(1)} %collective-permute-done.6.got_even, bf16[8,64]{1,0:T(8,128)(2,1)S(1)} %collective-permute-done.7.got_odd, ...), custom_call_target="tpu_custom_call" | custom-call | tf_op jit(solution)/shard_map/pallas_call | solution.py:500
  24.0 1.9 %collective-permute-start.8 = (bf16[8,64]{1,0:T(8,128)(2,1)S(1)}, bf16[8,64]{1,0:T(8,128)(2,1)S(1)}, u32[]{:S(2)}, u32[]{:S(2)}) collective-permute-start(bf16[8,64]{1,0:T(8,128)(2,1)S(1)} %get-tuple-element.70), channel_id=1, source_target_pairs={{0,4},{1,5},{2,6},{3,7},{4,0},{5,1},{6,2},{7,3},{8,12},{9,13},{10,... | collective-permute-start | bytes 3080 | tf_op jit(solution)/shard_map/ppermute | solution.py:473
  26.0 0.5 %collective-permute-start.9 = (bf16[8,64]{1,0:T(8,128)(2,1)S(1)}, bf16[8,64]{1,0:T(8,128)(2,1)S(1)}, u32[]{:S(2)}, u32[]{:S(2)}) collective-permute-start(bf16[8,64]{1,0:T(8,128)(2,1)S(1)} %get-tuple-element.71), channel_id=1, source_target_pairs={{0,2},{1,3},{2,0},{3,1},{4,8},{5,9},{6,10},{7,11},{8,4},{9,5},{10,... | collective-permute-start | bytes 3080 | tf_op jit(solution)/shard_map/ppermute | solution.py:473
  26.5 0.4 shard_map.245
  26.9 0.7 %collective-permute-done.8.got_even = bf16[8,64]{1,0:T(8,128)(2,1)S(1)} collective-permute-done((bf16[8,64]{1,0:T(8,128)(2,1)S(1)}, bf16[8,64]{1,0:T(8,128)(2,1)S(1)}, u32[]{:S(2)}, u32[]{:S(2)}) %collective-permute-start.8) | collective-permute-done | bytes 1056 | tf_op jit(solution)/shard_map/ppermute | solution.py:473
  27.6 1.9 %collective-permute-done.9.got_odd = bf16[8,64]{1,0:T(8,128)(2,1)S(1)} collective-permute-done((bf16[8,64]{1,0:T(8,128)(2,1)S(1)}, bf16[8,64]{1,0:T(8,128)(2,1)S(1)}, u32[]{:S(2)}, u32[]{:S(2)}) %collective-permute-start.9) | collective-permute-done | bytes 1056 | tf_op jit(solution)/shard_map/ppermute | solution.py:473
  29.5 0.4 shard_map.246
  30.0 0.6 %collective-permute-start.12 = (bf16[80,128]{1,0:T(8,128)(2,1)S(1)}, bf16[80,128]{1,0:T(8,128)(2,1)S(1)}, u32[]{:S(2)}, u32[]{:S(2)}) collective-permute-start(bf16[80,128]{1,0:T(8,128)(2,1)S(1)} %get-tuple-element.84.sent_col), channel_id=1, source_target_pairs={{0,1},{1,0},{2,3},{3,2},{4,5},{5,4},{6,7},{7,6},{8,9},{9,8},{10,11... | collective-permute-start | bytes 61448 | tf_op jit(solution)/shard_map/ppermute | solution.py:473
  30.6 1.4 %collective-permute-start.10 = (bf16[60,128]{1,0:T(8,128)(2,1)S(1)}, bf16[60,128]{1,0:T(8,128)(2,1)S(1)}, u32[]{:S(2)}, u32[]{:S(2)}) collective-permute-start(bf16[60,128]{1,0:T(8,128)(2,1)S(1)} %get-tuple-element.82), channel_id=1, source_target_pairs={{0,4},{1,5},{2,6},{3,7},{4,0},{5,1},{6,2},{7,3},{8,12},{9,13},{10,... | collective-permute-start | bytes 46088 | tf_op jit(solution)/shard_map/ppermute | solution.py:473
  32.1 1.5 %collective-permute-start.11 = (bf16[60,128]{1,0:T(8,128)(2,1)S(1)}, bf16[60,128]{1,0:T(8,128)(2,1)S(1)}, u32[]{:S(2)}, u32[]{:S(2)}) collective-permute-start(bf16[60,128]{1,0:T(8,128)(2,1)S(1)} %get-tuple-element.83), channel_id=1, source_target_pairs={{0,2},{1,3},{2,0},{3,1},{4,8},{5,9},{6,10},{7,11},{8,4},{9,5},{10,... | collective-permute-start | bytes 46088 | tf_op jit(solution)/shard_map/ppermute | solution.py:473
  33.8 0.6 %collective-permute-done.10.got_row_even = bf16[60,128]{1,0:T(8,128)(2,1)S(1)} collective-permute-done((bf16[60,128]{1,0:T(8,128)(2,1)S(1)}, bf16[60,128]{1,0:T(8,128)(2,1)S(1)}, u32[]{:S(2)}, u32[]{:S(2)}) %collective-permute-start.10) | collective-permute-done | bytes 15392 | tf_op jit(solution)/shard_map/ppermute | solution.py:473
  34.4 1.4 %collective-permute-done.11.got_row_odd = bf16[60,128]{1,0:T(8,128)(2,1)S(1)} collective-permute-done((bf16[60,128]{1,0:T(8,128)(2,1)S(1)}, bf16[60,128]{1,0:T(8,128)(2,1)S(1)}, u32[]{:S(2)}, u32[]{:S(2)}) %collective-permute-start.11) | collective-permute-done | bytes 15392 | tf_op jit(solution)/shard_map/ppermute | solution.py:473
  35.8 0.4 shard_map.248
  36.2 2.5 %collective-permute-start.14 = (bf16[8,64]{1,0:T(8,128)(2,1)S(1)}, bf16[8,64]{1,0:T(8,128)(2,1)S(1)}, u32[]{:S(2)}, u32[]{:S(2)}) collective-permute-start(bf16[8,64]{1,0:T(8,128)(2,1)S(1)} %get-tuple-element.93), channel_id=1, source_target_pairs={{0,4},{1,5},{2,6},{3,7},{4,0},{5,1},{6,2},{7,3},{8,12},{9,13},{10,... | collective-permute-start | bytes 3080 | tf_op jit(solution)/shard_map/ppermute | solution.py:473
  38.7 1.5 %collective-permute-start.15 = (bf16[8,64]{1,0:T(8,128)(2,1)S(1)}, bf16[8,64]{1,0:T(8,128)(2,1)S(1)}, u32[]{:S(2)}, u32[]{:S(2)}) collective-permute-start(bf16[8,64]{1,0:T(8,128)(2,1)S(1)} %get-tuple-element.94), channel_id=1, source_target_pairs={{0,2},{1,3},{2,0},{3,1},{4,8},{5,9},{6,10},{7,11},{8,4},{9,5},{10,... | collective-permute-start | bytes 3080 | tf_op jit(solution)/shard_map/ppermute | solution.py:473
  40.2 1.0 %shard_map.244 = bf16[2400,128]{1,0:T(8,128)(2,1)} custom-call(bf16[600,512]{1,0:T(8,128)(2,1)S(1)} %get-tuple-element.69.upd_ref), custom_call_target="tpu_custom_call" | custom-call | tf_op jit(solution)/shard_map/pallas_call | solution.py:517
  41.2 1.1 %shard_map.249 = (f32[480,128]{1,0:T(8,128)}, f32[8,128]{1,0:T(8,128)}) custom-call(f32[480,128]{1,0:T(8,128)S(1)} %get-tuple-element.81.part_ref, f32[60,128]{1,0:T(8,128)S(1)} %get-tuple-element.87.north_ref, f32[60,128]{1,0:T(8,128)S(1)} %get-tuple-element.88.south_ref, f32[16,128]{1,0:T(8,128)S(1)} %get-tuple-element.89.ends_ref, ...), custom_call_target="tpu_custom_call" | custom-call | tf_op jit(solution)/shard_map/pallas_call | solution.py:552
  42.4 0.8 %shard_map.250 = f32[3,4,128]{2,1,0:T(4,128)} custom-call(bf16[8,64]{1,0:T(8,128)(2,1)S(1)} %collective-permute-done.14.got_even, bf16[8,64]{1,0:T(8,128)(2,1)S(1)} %collective-permute-done.15.got_odd, bf16[8,64]{1,0:T(8,128)(2,1)S(1)} %get-tuple-element.95.own, bf16[192,512]{1,0:T(8,128)(2,1)S(1)} %bitcast.16), custom_call_target="tpu_custom_call" | custom-call | tf_op jit(solution)/shard_map/pallas_call | solution.py:558
  (52 shorter events, 1.3 us)
Async XLA Ops:
  0.6 7.4 %copy-start.15 = (f32[25]{0:T(128)S(1)}, f32[25]{0:T(128)}, u32[]{:S(2)}) copy-start(f32[25]{0:T(128)} %gain_hbm.1) | copy-start | bytes 304
  0.6 7.4 %copy-start.14 = (f32[25]{0:T(128)S(1)}, f32[25]{0:T(128)}, u32[]{:S(2)}) copy-start(f32[25]{0:T(128)} %rate_hbm.1) | copy-start | bytes 304
  0.7 7.4 %copy-start.5 = (f32[30,30]{1,0:T(8,128)S(1)}, f32[30,30]{1,0:T(8,128)}, u32[]{:S(2)}) copy-start(f32[30,30]{1,0:T(8,128)} %mix_ref.5) | copy-start | bytes 10804
  0.7 9.4 %copy-start.3 = (s32[8,128]{1,0:T(8,128)S(1)}, s32[8,128]{1,0:T(8,128)}, u32[]{:S(2)}) copy-start(s32[8,128]{1,0:T(8,128)} %wet_ref.17) | copy-start | bytes 12292
  0.7 9.4 %copy-start.8 = (f32[8,128]{1,0:T(8,128)S(1)}, f32[8,128]{1,0:T(8,128)}, u32[]{:S(2)}) copy-start(f32[8,128]{1,0:T(8,128)} %cor_ref.3) | copy-start | bytes 12292
  0.7 9.4 %copy-start.1 = (bf16[1,1,3,64,1024]{4,3,2,1,0:T(8,128)(2,1)S(1)}, bf16[1,1,3,64,1024]{4,3,2,1,0:T(8,128)(2,1)}, u32[]{:S(2)}) copy-start(bf16[1,1,3,64,1024]{4,3,2,1,0:T(8,128)(2,1)} %param.41) | copy-start | bytes 1179652
  0.7 9.4 %copy-start.4 = (f32[2,30,8,128]{3,2,1,0:T(8,128)S(1)}, f32[2,30,8,128]{3,2,1,0:T(8,128)}, u32[]{:S(2)}) copy-start(f32[2,30,8,128]{3,2,1,0:T(8,128)} %param.31) | copy-start | bytes 737284
  0.7 13.1 %copy-start.13 = (f32[8,128]{1,0:T(8,128)S(1)}, f32[8,128]{1,0:T(8,128)}, u32[]{:S(2)}) copy-start(f32[8,128]{1,0:T(8,128)} %eta_ref.1) | copy-start | bytes 12292
  0.7 16.7 %copy-start.10 = (s32[128]{0:T(128)S(1)}, s32[128]{0:T(128)}, u32[]{:S(2)}) copy-start(s32[128]{0:T(128)} %param.39) | copy-start | bytes 1540
  0.8 16.6 %copy-start.12 = (s32[1,1,3,64]{3,1,2,0:T(1,128)S(1)}, s32[1,1,3,64]{3,1,2,0:T(1,128)}, u32[]{:S(2)}) copy-start(s32[1,1,3,64]{3,1,2,0:T(1,128)} %param.42) | copy-start | bytes 2308
  0.8 19.2 %copy-start = (bf16[600,600]{1,0:T(8,128)(2,1)S(1)}, bf16[600,600]{1,0:T(8,128)(2,1)}, u32[]{:S(2)}) copy-start(bf16[600,600]{1,0:T(8,128)(2,1)} %inter_ref.1) | copy-start | bytes 2160004
  3.5 4.7 %collective-permute-start = (bf16[8,64]{1,0:T(8,128)(2,1)S(1)}, bf16[8,64]{1,0:T(8,128)(2,1)S(1)}, u32[]{:S(2)}, u32[]{:S(2)}) collective-permute-start(bf16[8,64]{1,0:T(8,128)(2,1)S(1)} %get-tuple-element.50), channel_id=1, source_target_pairs={{0,4},{1,5},{2,6},{3,7},{4,0},{5,1},{6,2},{7,3},{8,12},{9,13},{10,... | collective-permute-start | bytes 3080 | tf_op jit(solution)/shard_map/ppermute | solution.py:473
  6.5 3.6 %collective-permute-start.1 = (bf16[8,64]{1,0:T(8,128)(2,1)S(1)}, bf16[8,64]{1,0:T(8,128)(2,1)S(1)}, u32[]{:S(2)}, u32[]{:S(2)}) collective-permute-start(bf16[8,64]{1,0:T(8,128)(2,1)S(1)} %get-tuple-element.51), channel_id=1, source_target_pairs={{0,2},{1,3},{2,0},{3,1},{4,8},{5,9},{6,10},{7,11},{8,4},{9,5},{10,... | collective-permute-start | bytes 3080 | tf_op jit(solution)/shard_map/ppermute | solution.py:473
  10.5 12.5 %copy-start.2 = (bf16[1,1,3,64,512]{4,3,2,1,0:T(8,128)(2,1)S(1)}, bf16[1,1,3,64,512]{4,3,2,1,0:T(8,128)(2,1)}, u32[]{:S(2)}) copy-start(bf16[1,1,3,64,512]{4,3,2,1,0:T(8,128)(2,1)} %param.43) | copy-start | bytes 589828
  10.5 12.5 %copy-start.6 = (f32[6,600]{1,0:T(8,128)S(1)}, f32[6,600]{1,0:T(8,128)}, u32[]{:S(2)}) copy-start(f32[6,600]{1,0:T(8,128)} %kmap_ref.1) | copy-start | bytes 43204
  10.5 12.5 %copy-start.7 = (f32[2,4,128]{2,1,0:T(4,128)S(1)}, f32[2,4,128]{2,1,0:T(4,128)}, u32[]{:S(2)}) copy-start(f32[2,4,128]{2,1,0:T(4,128)} %wind_ref.1) | copy-start | bytes 12292
  10.6 12.5 %copy-start.9 = (s32[4,128]{1,0:T(4,128)S(1)}, s32[4,128]{1,0:T(4,128)}, u32[]{:S(2)}) copy-start(s32[4,128]{1,0:T(4,128)} %wet_ref.12) | copy-start | bytes 6148
  10.6 12.5 %copy-start.11 = (s32[1,1,3,64]{3,1,2,0:T(1,128)S(1)}, s32[1,1,3,64]{3,1,2,0:T(1,128)}, u32[]{:S(2)}) copy-start(s32[1,1,3,64]{3,1,2,0:T(1,128)} %param.40) | copy-start | bytes 2308
  10.6 6.8 %collective-permute-start.5 = (bf16[80,128]{1,0:T(8,128)(2,1)S(1)}, bf16[80,128]{1,0:T(8,128)(2,1)S(1)}, u32[]{:S(2)}, u32[]{:S(2)}) collective-permute-start(bf16[80,128]{1,0:T(8,128)(2,1)S(1)} %get-tuple-element.57), channel_id=1, source_target_pairs={{0,3},{1,2},{2,1},{3,0},{4,7},{5,6},{6,5},{7,4},{8,11},{9,10},{10,... | collective-permute-start | bytes 61448 | tf_op jit(solution)/shard_map/ppermute | solution.py:473
  10.7 6.7 %collective-permute-start.4 = (bf16[80,128]{1,0:T(8,128)(2,1)S(1)}, bf16[80,128]{1,0:T(8,128)(2,1)S(1)}, u32[]{:S(2)}, u32[]{:S(2)}) collective-permute-start(bf16[80,128]{1,0:T(8,128)(2,1)S(1)} %get-tuple-element.56.sent_col), channel_id=1, source_target_pairs={{0,1},{1,0},{2,3},{3,2},{4,5},{5,4},{6,7},{7,6},{8,9},{9,8},{10,11... | collective-permute-start | bytes 61448 | tf_op jit(solution)/shard_map/ppermute | solution.py:473
  12.2 3.7 %collective-permute-start.2 = (bf16[60,128]{1,0:T(8,128)(2,1)S(1)}, bf16[60,128]{1,0:T(8,128)(2,1)S(1)}, u32[]{:S(2)}, u32[]{:S(2)}) collective-permute-start(bf16[60,128]{1,0:T(8,128)(2,1)S(1)} %get-tuple-element.54), channel_id=1, source_target_pairs={{0,4},{1,5},{2,6},{3,7},{4,0},{5,1},{6,2},{7,3},{8,12},{9,13},{10,... | collective-permute-start | bytes 46088 | tf_op jit(solution)/shard_map/ppermute | solution.py:473
  13.7 3.7 %collective-permute-start.3 = (bf16[60,128]{1,0:T(8,128)(2,1)S(1)}, bf16[60,128]{1,0:T(8,128)(2,1)S(1)}, u32[]{:S(2)}, u32[]{:S(2)}) collective-permute-start(bf16[60,128]{1,0:T(8,128)(2,1)S(1)} %get-tuple-element.55), channel_id=1, source_target_pairs={{0,2},{1,3},{2,0},{3,1},{4,8},{5,9},{6,10},{7,11},{8,4},{9,5},{10,... | collective-permute-start | bytes 46088 | tf_op jit(solution)/shard_map/ppermute | solution.py:473
  17.8 3.6 %collective-permute-start.6 = (bf16[8,64]{1,0:T(8,128)(2,1)S(1)}, bf16[8,64]{1,0:T(8,128)(2,1)S(1)}, u32[]{:S(2)}, u32[]{:S(2)}) collective-permute-start(bf16[8,64]{1,0:T(8,128)(2,1)S(1)} %get-tuple-element.62), channel_id=1, source_target_pairs={{0,4},{1,5},{2,6},{3,7},{4,0},{5,1},{6,2},{7,3},{8,12},{9,13},{10,... | collective-permute-start | bytes 3080 | tf_op jit(solution)/shard_map/ppermute | solution.py:473
  19.4 3.6 %collective-permute-start.7 = (bf16[8,64]{1,0:T(8,128)(2,1)S(1)}, bf16[8,64]{1,0:T(8,128)(2,1)S(1)}, u32[]{:S(2)}, u32[]{:S(2)}) collective-permute-start(bf16[8,64]{1,0:T(8,128)(2,1)S(1)} %get-tuple-element.63), channel_id=1, source_target_pairs={{0,2},{1,3},{2,0},{3,1},{4,8},{5,9},{6,10},{7,11},{8,4},{9,5},{10,... | collective-permute-start | bytes 3080 | tf_op jit(solution)/shard_map/ppermute | solution.py:473
  24.0 3.6 %collective-permute-start.8 = (bf16[8,64]{1,0:T(8,128)(2,1)S(1)}, bf16[8,64]{1,0:T(8,128)(2,1)S(1)}, u32[]{:S(2)}, u32[]{:S(2)}) collective-permute-start(bf16[8,64]{1,0:T(8,128)(2,1)S(1)} %get-tuple-element.70), channel_id=1, source_target_pairs={{0,4},{1,5},{2,6},{3,7},{4,0},{5,1},{6,2},{7,3},{8,12},{9,13},{10,... | collective-permute-start | bytes 3080 | tf_op jit(solution)/shard_map/ppermute | solution.py:473
  26.0 3.6 %collective-permute-start.9 = (bf16[8,64]{1,0:T(8,128)(2,1)S(1)}, bf16[8,64]{1,0:T(8,128)(2,1)S(1)}, u32[]{:S(2)}, u32[]{:S(2)}) collective-permute-start(bf16[8,64]{1,0:T(8,128)(2,1)S(1)} %get-tuple-element.71), channel_id=1, source_target_pairs={{0,2},{1,3},{2,0},{3,1},{4,8},{5,9},{6,10},{7,11},{8,4},{9,5},{10,... | collective-permute-start | bytes 3080 | tf_op jit(solution)/shard_map/ppermute | solution.py:473
  29.9 5.9 %collective-permute-start.13 = (bf16[80,128]{1,0:T(8,128)(2,1)S(1)}, bf16[80,128]{1,0:T(8,128)(2,1)S(1)}, u32[]{:S(2)}, u32[]{:S(2)}) collective-permute-start(bf16[80,128]{1,0:T(8,128)(2,1)S(1)} %get-tuple-element.85), channel_id=1, source_target_pairs={{0,3},{1,2},{2,1},{3,0},{4,7},{5,6},{6,5},{7,4},{8,11},{9,10},{10,... | collective-permute-start | bytes 61448 | tf_op jit(solution)/shard_map/ppermute | solution.py:473
  30.0 5.8 %collective-permute-start.12 = (bf16[80,128]{1,0:T(8,128)(2,1)S(1)}, bf16[80,128]{1,0:T(8,128)(2,1)S(1)}, u32[]{:S(2)}, u32[]{:S(2)}) collective-permute-start(bf16[80,128]{1,0:T(8,128)(2,1)S(1)} %get-tuple-element.84.sent_col), channel_id=1, source_target_pairs={{0,1},{1,0},{2,3},{3,2},{4,5},{5,4},{6,7},{7,6},{8,9},{9,8},{10,11... | collective-permute-start | bytes 61448 | tf_op jit(solution)/shard_map/ppermute | solution.py:473
  30.6 3.7 %collective-permute-start.10 = (bf16[60,128]{1,0:T(8,128)(2,1)S(1)}, bf16[60,128]{1,0:T(8,128)(2,1)S(1)}, u32[]{:S(2)}, u32[]{:S(2)}) collective-permute-start(bf16[60,128]{1,0:T(8,128)(2,1)S(1)} %get-tuple-element.82), channel_id=1, source_target_pairs={{0,4},{1,5},{2,6},{3,7},{4,0},{5,1},{6,2},{7,3},{8,12},{9,13},{10,... | collective-permute-start | bytes 46088 | tf_op jit(solution)/shard_map/ppermute | solution.py:473
  32.1 3.7 %collective-permute-start.11 = (bf16[60,128]{1,0:T(8,128)(2,1)S(1)}, bf16[60,128]{1,0:T(8,128)(2,1)S(1)}, u32[]{:S(2)}, u32[]{:S(2)}) collective-permute-start(bf16[60,128]{1,0:T(8,128)(2,1)S(1)} %get-tuple-element.83), channel_id=1, source_target_pairs={{0,2},{1,3},{2,0},{3,1},{4,8},{5,9},{6,10},{7,11},{8,4},{9,5},{10,... | collective-permute-start | bytes 46088 | tf_op jit(solution)/shard_map/ppermute | solution.py:473
  36.2 6.1 %collective-permute-start.14 = (bf16[8,64]{1,0:T(8,128)(2,1)S(1)}, bf16[8,64]{1,0:T(8,128)(2,1)S(1)}, u32[]{:S(2)}, u32[]{:S(2)}) collective-permute-start(bf16[8,64]{1,0:T(8,128)(2,1)S(1)} %get-tuple-element.93), channel_id=1, source_target_pairs={{0,4},{1,5},{2,6},{3,7},{4,0},{5,1},{6,2},{7,3},{8,12},{9,13},{10,... | collective-permute-start | bytes 3080 | tf_op jit(solution)/shard_map/ppermute | solution.py:473
  38.7 3.7 %collective-permute-start.15 = (bf16[8,64]{1,0:T(8,128)(2,1)S(1)}, bf16[8,64]{1,0:T(8,128)(2,1)S(1)}, u32[]{:S(2)}, u32[]{:S(2)}) collective-permute-start(bf16[8,64]{1,0:T(8,128)(2,1)S(1)} %get-tuple-element.94), channel_id=1, source_target_pairs={{0,2},{1,3},{2,0},{3,1},{4,8},{5,9},{6,10},{7,11},{8,4},{9,5},{10,... | collective-permute-start | bytes 3080 | tf_op jit(solution)/shard_map/ppermute | solution.py:473
  (3 other events, 22.1 us)

commit v4 on v3

--- a/solution.py
+++ b/solution.py
@@ -47,67 +47,70 @@
     return lax.rem(index, 2) == 0
 
 
-def stress_rows(smap, rate_ref, nfreq):
+GROUP = 8
+
+
+def field_weights(smap, kmap, rate_ref, gain_ref, nfreq):
     spec = smap.shape[1]
     col = lax.broadcasted_iota(jnp.int32, (1, spec), 1)
     band = jnp.zeros((1, spec), jnp.int32)
     rate = jnp.full((1, spec), rate_ref[0], f32)
+    gain = jnp.full((1, spec), gain_ref[0], f32)
     for f in range(1, nfreq):
         past = col >= NDIR * f
         band = band + jnp.where(past, 1, 0)
         rate = jnp.where(past, rate_ref[f], rate)
-    direction = col - NDIR * band
-    row = lax.broadcasted_iota(jnp.int32, (NDIR, spec), 0)
-    keep = row == direction
-    weights = [jnp.where(keep, smap[i : i + 1] * rate, 0.0) for i in range(2)]
-    weights = jnp.concatenate(weights, axis=0)
-    high, low = split2(weights)
-    return jnp.concatenate([high.astype(f32), low.astype(f32)], axis=0).astype(bf16)
-
-
-def transfer(inter, weights, eb, t_ref, q_ref):
-    t_ref[...] = dot(inter, eb)
-    q = dot(weights, eb)
-    half = 2 * NDIR
-    q_ref[...] = q[:half] + q[half:]
-
-
-def wave_finish(
-    e_of, t_ref, q_ref, wind_ref, current_of, wet_ref, rate_of, gain_of, kmap, upd_ref, nfreq
-):
+        gain = jnp.where(past, gain_ref[f], gain)
+    keep = lax.broadcasted_iota(jnp.int32, (NDIR, spec), 0) == col - NDIR * band
+    maps = [smap[i : i + 1] for i in range(2)] + [kmap[i : i + 1] for i in range(2 * NBAND)]
+    rows = jnp.concatenate([jnp.where(keep, m * rate, 0.0) for m in maps], axis=0)
+    return rows, jnp.concatenate([jnp.zeros((2, spec), f32), kmap], axis=0), gain
+
+
+def rest_weights(stokes, gain, inter):
+    high, low = split2(stokes)
+    moved = dot(jnp.concatenate([high.astype(f32), low.astype(f32)], axis=0).astype(bf16), inter)
+    return jnp.concatenate([stokes * gain, stokes + moved[:GROUP] + moved[GROUP:]], axis=0)
+
+
+def joined(parts):
+    direct = GROUP * NDIR
+    rest = parts[direct : direct + 2 * GROUP] + parts[direct + 2 * GROUP :]
+    return jnp.concatenate([parts[:direct], rest], axis=0)
+
+
+def soft_growth(dx, dy):
+    heading = lax.broadcasted_iota(jnp.int32, (NDIR, dx.shape[1]), 0).astype(f32)
+    heading = (heading + 0.5) * (2.0 * math.pi / NDIR)
+    relative = dx * jnp.cos(heading) + dy * jnp.sin(heading)
+    return jnp.maximum(relative, 0.0) + jnp.log1p(jnp.exp(-jnp.abs(relative)))
+
+
+def fields_of(soft, level, wet, parts):
+    sums = [
+        jnp.sum(soft * parts[i * NDIR : (i + 1) * NDIR], axis=0, keepdims=True) for i in range(GROUP)
+    ]
+    rest = GROUP * NDIR
+    total = jnp.concatenate(sums, axis=0) + level * parts[rest : rest + GROUP] + parts[rest + GROUP :]
+    row = lax.broadcasted_iota(jnp.int32, total.shape, 0)
+    return jnp.where(row < 2, total, wet * total)
+
+
+def flat(ref, *first):
+    rows = ref.shape[-2]
+    return jnp.concatenate([ref[(*first, slice(y, y + 1), slice(None))] for y in range(rows)], axis=1)
+
+
+def update(old_of, moved_of, soft_ref, wet_ref, coef_ref, nfreq, store):
     rows, lanes = wet_ref.shape
-    heading = lax.broadcasted_iota(jnp.int32, (NDIR, lanes), 0).astype(f32)
-    heading = (heading + 0.5) * (2.0 * math.pi / NDIR)
-    cosine, sine = jnp.cos(heading), jnp.sin(heading)
-    stress = []
+    rate, gain = row_of(coef_ref, RATE), row_of(coef_ref, GAIN)
     for y in range(rows):
         cells = slice(y * lanes, (y + 1) * lanes)
-        dx = wind_ref[0, y : y + 1, :] - current_of(0, y)
-        dy = wind_ref[1, y : y + 1, :] - current_of(1, y)
-        level = current_of(2, y)
+        soft, level = soft_ref[:NDIR, cells], soft_ref[NDIR : NDIR + 1, cells]
         wet = wet_ref[y : y + 1, :].astype(f32)
-        relative = dx * cosine + dy * sine
-        soft = jnp.maximum(relative, 0.0) + jnp.log1p(jnp.exp(-jnp.abs(relative)))
-        stress.append(
-            [
-                jnp.sum(soft * q_ref[i * NDIR : (i + 1) * NDIR, cells], axis=0, keepdims=True)
-                for i in range(2)
-            ]
-        )
-        rate = jnp.concatenate(
-            [rate_of(f) * soft + gain_of(f) * level for f in range(nfreq)], axis=0
-        )
-        e = e_of(y)
-        upd_ref[:, cells] = (wet * (e + rate * e + t_ref[:, cells])).astype(bf16)
-    high, low = split2(kmap)
-    pair = jnp.concatenate([high.astype(f32), low.astype(f32)], axis=0).astype(bf16)
-    stokes = dot(pair, upd_ref[...])
-    bands = 2 * NBAND
-    stokes = stokes[:bands] + stokes[bands:]
-    stress = jnp.concatenate(
-        [jnp.concatenate([stress[y][i] for y in range(rows)], axis=1) for i in range(2)], axis=0
-    )
-    return jnp.concatenate([stress, stokes], axis=0)
+        growth = jnp.concatenate([rate(f) * soft + gain(f) * level for f in range(nfreq)], axis=0)
+        old = old_of(cells)
+        store(y, cells, wet * (old + growth * old + moved_of(cells)))
 
 
 def pick(fields, send, outs):
@@ -135,62 +138,96 @@
 
 def k_wave_first(
     nfreq,
-    spec_hbm, inter_hbm, smap_hbm, rate_hbm, wind_hbm, cur_hbm, wet_hbm, gain_hbm, kmap_hbm, send_hbm,
-    upd_ref, to_even, to_odd, own, weight_ref,
-    spec_ref, inter_ref, smap_ref, rate_ref, wind_ref, cur_ref, wet_ref, gain_ref, kmap_ref, send_ref,
-    ef, eb, t, q, sems,
+    smap_hbm, kmap_hbm, rate_hbm, gain_hbm, wind_hbm, cur_hbm, wet_hbm, send_hbm, spec_hbm, inter_hbm,
+    to_even, to_odd, own, old_ref, soft_ref, weight_ref,
+    smap_ref, kmap_ref, rate_ref, gain_ref, wind_ref, cur_ref, wet_ref, send_ref, spec_ref, inter_ref,
+    wide, sems,
 ):
-    sources = (spec_hbm, inter_hbm, smap_hbm, rate_hbm, wind_hbm, cur_hbm, wet_hbm, gain_hbm, kmap_hbm, send_hbm)
-    held = (spec_ref, inter_ref, smap_ref, rate_ref, wind_ref, cur_ref, wet_ref, gain_ref, kmap_ref, send_ref)
-    copies = [pltpu.make_async_copy(a, b, sems.at[i]) for i, (a, b) in enumerate(zip(sources, held))]
+    rows, lanes = wet_ref.shape
+    spec = inter_ref.shape[0]
+    cut = spec // 32 * 16
+    small = (
+        (smap_hbm, smap_ref), (kmap_hbm, kmap_ref), (rate_hbm, rate_ref), (gain_hbm, gain_ref),
+        (wind_hbm, wind_ref), (cur_hbm, cur_ref), (wet_hbm, wet_ref), (send_hbm, send_ref),
+    )
+    large = []
+    for first, size in ((0, cut), (cut, spec - cut)):
+        part = pl.ds(first * rows, size * rows)
+        large.append((spec_hbm.at[part], spec_ref.at[part]))
+    for first, size in ((0, cut), (cut, spec - cut)):
+        part = pl.ds(first, size)
+        large.append((inter_hbm.at[part], inter_ref.at[part]))
+    copies = [pltpu.make_async_copy(a, b, sems.at[i]) for i, (a, b) in enumerate((*small, *large))]
     for copy in copies:
         copy.start()
-    rows, lanes = wet_ref.shape
-    spec = inter_ref.shape[0]
-    copies[0].wait()
-    ef[...] = spec_ref[...].astype(f32)
-    for y in range(rows):
-        eb[:, y * lanes : (y + 1) * lanes] = ef[pl.ds(y, spec, stride=rows), :].astype(bf16)
-    for copy in copies[1:]:
+    for copy in copies[: len(small)]:
         copy.wait()
-    weight_ref[...] = stress_rows(smap_ref[...], rate_ref, nfreq)
-    transfer(inter_ref[...], weight_ref[...], eb[...], t, q)
-    fields = wave_finish(
-        lambda y: ef[pl.ds(y, spec, stride=rows), :],
-        t, q, wind_ref,
-        lambda i, y: cur_ref[i, y : y + 1, :],
-        wet_ref, lambda f: rate_ref[f], lambda f: gain_ref[f], kmap_ref[...], upd_ref, nfreq,
+    level = flat(cur_ref, 2)
+    soft = soft_growth(flat(wind_ref, 0) - flat(cur_ref, 0), flat(wind_ref, 1) - flat(cur_ref, 1))
+    soft_ref[:NDIR, :] = soft
+    soft_ref[NDIR:, :] = jnp.concatenate([level] * (soft_ref.shape[0] - NDIR), axis=0)
+    direct = GROUP * NDIR
+    weights, stokes, gain = field_weights(smap_ref[...], kmap_ref[...], rate_ref, gain_ref, nfreq)
+    weight_ref[:direct, :] = weights.astype(bf16)
+    for n, (first, size) in enumerate(((0, cut), (cut, spec - cut))):
+        copies[len(small) + n].wait()
+        part = slice(first * rows, (first + size) * rows)
+        wide[part, :] = spec_ref[part, :].astype(f32)
+        for y in range(rows):
+            taken = wide[pl.ds(first * rows + y, size, stride=rows), :]
+            old_ref[first : first + size, y * lanes : (y + 1) * lanes] = taken.astype(bf16)
+    for copy in copies[len(small) + 2 :]:
+        copy.wait()
+    half = direct + 2 * GROUP
+    rest = rest_weights(stokes, gain, inter_ref[...])
+    weight_ref[direct:half, :], weight_ref[half:, :] = split2(rest)
+    parts = joined(dot(weight_ref[...], old_ref[...]))
+    fields = fields_of(soft, level, flat(wet_ref).astype(f32), parts)
+    pick(fields, send_ref, (to_even, to_odd, own))
+
+
+def k_update(nfreq, old_ref, inter_ref, soft_ref, wet_ref, coef_ref, new_ref, moved):
+    moved[...] = dot(inter_ref[...], old_ref[...])
+
+    def store(y, cells, value):
+        new_ref[:, cells] = value.astype(bf16)
+
+    update(
+        lambda cells: old_ref[:, cells].astype(f32), lambda cells: moved[:, cells],
+        soft_ref, wet_ref, coef_ref, nfreq, store,
     )
+
+
+def k_transfer(old_ref, inter_ref, weight_ref, moved_ref, parts_ref):
+    parts_ref[...] = joined(dot(weight_ref[...], old_ref[...]))
+    moved_ref[...] = dot(inter_ref[...], old_ref[...])
+
+
+def k_wave_next(
+    n_row,
+    got_even, got_odd, got_own, recv_ref, parts_ref, wind_ref, wet_ref, send_ref,
+    to_even, to_odd, own, soft_ref,
+    cur_ref,
+):
+    cur_ref[...] = dot(gather_slots(got_even, got_odd, got_own, n_row), recv_ref[...])
+    level = cur_ref[2:3, :]
+    soft = soft_growth(flat(wind_ref, 0) - cur_ref[0:1, :], flat(wind_ref, 1) - cur_ref[1:2, :])
+    soft_ref[:NDIR, :] = soft
+    soft_ref[NDIR:, :] = jnp.concatenate([level] * (soft_ref.shape[0] - NDIR), axis=0)
+    fields = fields_of(soft, level, flat(wet_ref).astype(f32), parts_ref[...])
     pick(fields, send_ref, (to_even, to_odd, own))
 
 
-def k_transfer(upd_ref, inter_ref, weight_ref, t_ref, q_ref):
-    transfer(inter_ref[...], weight_ref[...], upd_ref[...], t_ref, q_ref)
-
-
-def k_wave_next(
-    nfreq, n_row,
-    got_even, got_odd, got_own, recv_ref, old_ref, t_ref, q_ref, wind_ref, wet_ref, coef_ref, kmap_ref, send_ref,
-    upd_ref, to_even, to_odd, own,
-    cur,
-):
-    lanes = wet_ref.shape[1]
-    slots = gather_slots(got_even, got_odd, got_own, n_row)
-    cur[...] = dot(slots, recv_ref[...])
-    fields = wave_finish(
-        lambda y: old_ref[:, y * lanes : (y + 1) * lanes].astype(f32),
-        t_ref, q_ref, wind_ref,
-        lambda i, y: cur[i : i + 1, y * lanes : (y + 1) * lanes],
-        wet_ref, row_of(coef_ref, RATE), row_of(coef_ref, GAIN), kmap_ref[...], upd_ref, nfreq,
+def k_update_last(nfreq, old_ref, moved_ref, soft_ref, wet_ref, coef_ref, out_ref, wide):
+    rows, spec = wet_ref.shape[0], old_ref.shape[0]
+
+    def store(y, cells, value):
+        wide[pl.ds(y, spec, stride=rows), :] = value
+
+    update(
+        lambda cells: old_ref[:, cells].astype(f32), lambda cells: moved_ref[:, cells],
+        soft_ref, wet_ref, coef_ref, nfreq, store,
     )
-    pick(fields, send_ref, (to_even, to_odd, own))
-
-
-def k_spectra_out(rows, upd_ref, out_ref, wide):
-    spec = upd_ref.shape[0]
-    lanes = out_ref.shape[1]
-    for y in range(rows):
-        wide[pl.ds(y, spec, stride=rows), :] = upd_ref[:, y * lanes : (y + 1) * lanes].astype(f32)
     out_ref[...] = wide[...].astype(bf16)
 
 
@@ -323,30 +360,35 @@
     row, col = lax.axis_index("row"), lax.axis_index("col")
     even = is_even(row)
     a, b = got_row_even[...].astype(f32), got_row_odd[...].astype(f32)
-    if whole:
-        pieces = [(line_ref[t * planes : (t + 1) * planes, :], t) for t in range(n_col)]
-    else:
-        pair_even = jnp.where(is_even(col), col + 1, col - 1)
-        pair_odd = lax.rem(jnp.where(is_even(col), col - 1, col + 1) + n_col, n_col)
-        pieces = [
-            (sent_col[:planes, :], col),
-            (got_col_even[:planes, :], pair_even),
-            (got_col_odd[:planes, :], pair_odd),
-            (got_row_odd[...], lax.rem(col + n_col // 2, n_col)),
-        ]
-    cell = lax.broadcasted_iota(jnp.int32, (ox, ox), 0)
-    across = None
-    for piece, tile in pieces:
-        hot = jnp.where(cell == fold_ref[...] - tile * ox, 1.0, 0.0).astype(bf16)
-        part = dot(piece, hot)
-        across = part if across is None else across + part
-    north = jnp.where(row == n_row - 1, -across, jnp.where(even, a, b))
+    north_ref[...] = jnp.where(even, a, b)
+
+    @pl.when(row == n_row - 1)
+    def _():
+        if whole:
+            pieces = [(line_ref[t * planes : (t + 1) * planes, :], t) for t in range(n_col)]
+        else:
+            pair_even = jnp.where(is_even(col), col + 1, col - 1)
+            pair_odd = lax.rem(jnp.where(is_even(col), col - 1, col + 1) + n_col, n_col)
+            pieces = [
+                (sent_col[:planes, :], col),
+                (got_col_even[:planes, :], pair_even),
+                (got_col_odd[:planes, :], pair_odd),
+                (got_row_odd[...], lax.rem(col + n_col // 2, n_col)),
+            ]
+        cell = lax.broadcasted_iota(jnp.int32, (ox, ox), 0)
+        across = None
+        for piece, tile in pieces:
+            hot = jnp.where(cell == fold_ref[...] - tile * ox, 1.0, 0.0).astype(bf16)
+            part = dot(piece, hot)
+            across = part if across is None else across + part
+        north_ref[...] = -across
+
+    north = north_ref[...]
     south = jnp.where(row == 0, 0.0, jnp.where(even, b, a))
     even = is_even(col)
     a = got_col_even[pad:, :].astype(f32)[:oy]
     b = got_col_odd[pad:, :].astype(f32)[:oy]
     east, west = jnp.where(even, a, b), jnp.where(even, b, a)
-    north_ref[...] = north
     south_ref[...] = south
     ends_ref[:oy, :] = east
     ends_ref[oy:, :] = west
@@ -473,36 +515,27 @@
         return lax.ppermute(array, axis, pairs[label])
 
     slots_out = [((8, slot), bf16)] * 3
-    wave_outs = [((spec, cells), bf16)] + slots_out
+    soft_out = ((32, cells), f32)
+    half = GROUP * (NDIR + 2)
     full = (planes * oy, ox)
     for step in range(STEPS):
         last = step + 1 == STEPS
         if step == 0:
             inputs = (
-                spectra.reshape(spec * rows, lanes), interaction, stress_map, input_rate, wind, wave_current,
-                wave_wet, eta_gain, stokes_map, wsend,
+                stress_map, stokes_map, input_rate, eta_gain, wind, wave_current, wave_wet, wsend,
+                spectra.reshape(spec * rows, lanes), interaction,
             )
             held = [(pltpu.SMEM if x.ndim == 1 else pltpu.VMEM)(x.shape, x.dtype) for x in inputs]
-            updated, to_even, to_odd, own, weights = call(
+            to_even, to_odd, own, energy, soft, weights = call(
                 functools.partial(k_wave_first, nfreq),
-                wave_outs + [((4 * NDIR, spec), bf16)],
+                slots_out + [((spec, cells), bf16), soft_out, ((half + 2 * GROUP, spec), bf16)],
                 [HBM] * len(inputs),
-                held
-                + [
-                    pltpu.VMEM((spec * rows, lanes), f32),
-                    pltpu.VMEM((spec, cells), bf16),
-                    pltpu.VMEM((spec, cells), f32),
-                    pltpu.VMEM((2 * NDIR, cells), f32),
-                    pltpu.SemaphoreType.DMA((len(inputs),)),
-                ],
+                held + [pltpu.VMEM((spec * rows, lanes), f32), pltpu.SemaphoreType.DMA((len(inputs) + 2,))],
             )(*(pltpu.with_memory_space_constraint(x, pltpu.HBM) for x in inputs))
         else:
-            updated, to_even, to_odd, own = call(
-                functools.partial(k_wave_next, nfreq, n_row), wave_outs, [VMEM] * 12, [pltpu.VMEM((8, cells), f32)]
-            )(
-                got_even, got_odd, own, wave_w, updated, moved, q, wind, wave_wet,
-                coef, stokes_map, wsend,
-            )
+            to_even, to_odd, own, soft = call(
+                functools.partial(k_wave_next, n_row), slots_out + [soft_out], [VMEM] * 8, [pltpu.VMEM((8, cells), f32)]
+            )(got_even, got_odd, own, wave_w, parts, wind, wave_wet, wsend)
         got_odd, got_even = trade("row_odd", to_odd), trade("row_even", to_even)
         if step == 0:
             coef, side, lane_rows = call(
@@ -515,11 +548,18 @@
             )
         if last:
             (spectra_out,) = call(
-                functools.partial(k_spectra_out, rows),
+                functools.partial(k_update_last, nfreq),
                 [((spec * rows, lanes), bf16)],
-                [VMEM],
+                [VMEM] * 5,
                 [pltpu.VMEM((spec * rows, lanes), f32)],
-            )(updated)
+            )(energy, moved, soft, wave_wet, coef)
+        else:
+            (energy,) = call(
+                functools.partial(k_update, nfreq),
+                [((spec, cells), bf16)],
+                [VMEM] * 5,
+                [pltpu.VMEM((spec, cells), f32)],
+            )(energy, interaction, soft, wave_wet, coef)
         forced, row_even, row_odd, col_even, col_odd = call(
             functools.partial(k_force, n_row, lev, pad),
             [(full, f32)] + [((planes, ox), bf16)] * 2 + [((pad + 16, ox), bf16)] * 2,
@@ -546,9 +586,9 @@
         )
         got_odd, got_even = trade("row_odd", to_odd), trade("row_even", to_even)
         if not last:
-            moved, q = call(
-                k_transfer, [((spec, cells), f32), ((2 * NDIR, cells), f32)], [VMEM] * 3
-            )(updated, interaction, weights)
+            moved, parts = call(
+                k_transfer, [((spec, cells), f32), ((half, cells), f32)], [VMEM] * 3
+            )(energy, interaction, weights)
         velocity, eta = call(
             functools.partial(k_mix, lev),
             [(full, f32), ((oy, ox), f32)],

time: 43.3 us -> 42.5 us (0.982)
  waiting for transfers between devices: 12.2 us -> 11.3 us
    ppermute x16, waiting for transfers between devices: 12.2 us -> 11.3 us  [trade(): return lax.ppermute(array, axis, pairs[label])]
    pallas_call x4 -> x5, Pallas kernels: 5.47 us -> 5.84 us  [the longest x1 2.19 us: shards(): call(functools.partial(k_wave_first, nfreq), slots_out + [((spec, cells),...]
  transfers between devices with their start and end apart: 16 -> 16, of which waited for: 9 -> 8; matrix products, arithmetic and copies ran while one was open for 0% -> 0% of each run, Pallas kernels for 9% -> 12%
where the time goes in v4:
time: 42.5 us; the launch traced here: 42.3 us
  starting transfers between devices  19.8 us (47%)
  waiting for transfers between devices  11.3 us (27%)
  Pallas kernels  10.2 us (24%)
  between operations  0.93 us (2%)
    ppermute x16, starting transfers between devices, trade(): return lax.ppermute(array, axis, pairs[label])  19.8 us
    ppermute x16, waiting for transfers between devices, trade(): return lax.ppermute(array, axis, pairs[label])  11.3 us
    pallas_call x1, Pallas kernels, shards(): call(functools.partial(k_wave_first, nfreq), slots_out + [((spec, cells),...  2.19 us
    pallas_call x1, Pallas kernels, shards(): call(functools.partial(k_update_last, nfreq), [((spec * rows, lanes), bf1...  1.58 us
    pallas_call x2, Pallas kernels, shards(): call(functools.partial(k_mix, lev), [(full, f32), ((oy, ox), f32)], [VMEM...  1.53 us
  transfers between devices with their start and end apart: 16, of which 8 were waited for; matrix products, arithmetic and copies ran while one was open for 0% of the time, Pallas kernels for 12%

profile of v4, /device:TPU:0, one launch (start us, length us, event | category | flops | bytes accessed | tf_op | source)
XLA Modules:
  0.0 42.3 jit_solution(12367890916564470857)
XLA Ops:
  0.8 2.2 %shard_map.237 = (bf16[8,64]{1,0:T(8,128)(2,1)S(1)}, bf16[8,64]{1,0:T(8,128)(2,1)S(1)}, bf16[8,64]{1,0:T(8,128)(2,1)S(1)}, bf16[600,512]{1,0:T(8,128)(2,1)S(1)},...) custom-call(f32[2,600]{1,0:T(2,128)} %smap_hbm.1, f32[6,600]{1,0:T(8,128)} %kmap_hbm.1, f32[25]{0:T(128)} %rate_hbm.1, ...), custom_call_target="tpu_custom_call" | custom-call | tf_op jit(solution)/shard_map/pallas_call | solution.py:529
  3.0 3.1 %collective-permute-start = (bf16[8,64]{1,0:T(8,128)(2,1)S(1)}, bf16[8,64]{1,0:T(8,128)(2,1)S(1)}, u32[]{:S(2)}, u32[]{:S(2)}) collective-permute-start(bf16[8,64]{1,0:T(8,128)(2,1)S(1)} %get-tuple-element.56), channel_id=1, source_target_pairs={{0,4},{1,5},{2,6},{3,7},{4,0},{5,1},{6,2},{7,3},{8,12},{9,13},{10,... | collective-permute-start | bytes 3080 | tf_op jit(solution)/shard_map/ppermute | solution.py:515
  6.0 1.5 %collective-permute-start.1 = (bf16[8,64]{1,0:T(8,128)(2,1)S(1)}, bf16[8,64]{1,0:T(8,128)(2,1)S(1)}, u32[]{:S(2)}, u32[]{:S(2)}) collective-permute-start(bf16[8,64]{1,0:T(8,128)(2,1)S(1)} %get-tuple-element.57), channel_id=1, source_target_pairs={{0,2},{1,3},{2,0},{3,1},{4,8},{5,9},{6,10},{7,11},{8,4},{9,5},{10,... | collective-permute-start | bytes 3080 | tf_op jit(solution)/shard_map/ppermute | solution.py:515
  7.7 1.9 %collective-permute-done.1.got_odd = bf16[8,64]{1,0:T(8,128)(2,1)S(1)} collective-permute-done((bf16[8,64]{1,0:T(8,128)(2,1)S(1)}, bf16[8,64]{1,0:T(8,128)(2,1)S(1)}, u32[]{:S(2)}, u32[]{:S(2)}) %collective-permute-start.1) | collective-permute-done | bytes 1056 | tf_op jit(solution)/shard_map/ppermute | solution.py:515
  9.7 0.4 shard_map.241
  10.1 1.6 %collective-permute-start.4 = (bf16[80,128]{1,0:T(8,128)(2,1)S(1)}, bf16[80,128]{1,0:T(8,128)(2,1)S(1)}, u32[]{:S(2)}, u32[]{:S(2)}) collective-permute-start(bf16[80,128]{1,0:T(8,128)(2,1)S(1)} %get-tuple-element.61.sent_col), channel_id=1, source_target_pairs={{0,1},{1,0},{2,3},{3,2},{4,5},{5,4},{6,7},{7,6},{8,9},{9,8},{10,11... | collective-permute-start | bytes 61448 | tf_op jit(solution)/shard_map/ppermute | solution.py:515
  11.7 1.4 %collective-permute-start.2 = (bf16[60,128]{1,0:T(8,128)(2,1)S(1)}, bf16[60,128]{1,0:T(8,128)(2,1)S(1)}, u32[]{:S(2)}, u32[]{:S(2)}) collective-permute-start(bf16[60,128]{1,0:T(8,128)(2,1)S(1)} %get-tuple-element.59), channel_id=1, source_target_pairs={{0,4},{1,5},{2,6},{3,7},{4,0},{5,1},{6,2},{7,3},{8,12},{9,13},{10,... | collective-permute-start | bytes 46088 | tf_op jit(solution)/shard_map/ppermute | solution.py:515
  13.5 2.0 %collective-permute-done.2.got_row_even = bf16[60,128]{1,0:T(8,128)(2,1)S(1)} collective-permute-done((bf16[60,128]{1,0:T(8,128)(2,1)S(1)}, bf16[60,128]{1,0:T(8,128)(2,1)S(1)}, u32[]{:S(2)}, u32[]{:S(2)}) %collective-permute-start.2) | collective-permute-done | bytes 15392 | tf_op jit(solution)/shard_map/ppermute | solution.py:515
  15.4 1.4 %collective-permute-done.3.got_row_odd = bf16[60,128]{1,0:T(8,128)(2,1)S(1)} collective-permute-done((bf16[60,128]{1,0:T(8,128)(2,1)S(1)}, bf16[60,128]{1,0:T(8,128)(2,1)S(1)}, u32[]{:S(2)}, u32[]{:S(2)}) %collective-permute-start.3) | collective-permute-done | bytes 15392 | tf_op jit(solution)/shard_map/ppermute | solution.py:515
  16.9 0.4 shard_map.243
  17.2 1.5 %collective-permute-start.6 = (bf16[8,64]{1,0:T(8,128)(2,1)S(1)}, bf16[8,64]{1,0:T(8,128)(2,1)S(1)}, u32[]{:S(2)}, u32[]{:S(2)}) collective-permute-start(bf16[8,64]{1,0:T(8,128)(2,1)S(1)} %get-tuple-element.67), channel_id=1, source_target_pairs={{0,4},{1,5},{2,6},{3,7},{4,0},{5,1},{6,2},{7,3},{8,12},{9,13},{10,... | collective-permute-start | bytes 3080 | tf_op jit(solution)/shard_map/ppermute | solution.py:515
  18.8 0.5 %collective-permute-start.7 = (bf16[8,64]{1,0:T(8,128)(2,1)S(1)}, bf16[8,64]{1,0:T(8,128)(2,1)S(1)}, u32[]{:S(2)}, u32[]{:S(2)}) collective-permute-start(bf16[8,64]{1,0:T(8,128)(2,1)S(1)} %get-tuple-element.68), channel_id=1, source_target_pairs={{0,2},{1,3},{2,0},{3,1},{4,8},{5,9},{6,10},{7,11},{8,4},{9,5},{10,... | collective-permute-start | bytes 3080 | tf_op jit(solution)/shard_map/ppermute | solution.py:515
  19.3 0.8 %shard_map.239.old_ref = bf16[600,512]{1,0:T(8,128)(2,1)S(1)} custom-call(bf16[600,512]{1,0:T(8,128)(2,1)S(1)} %get-tuple-element.51.old_ref, bf16[600,600]{1,0:T(8,128)(2,1)S(1)} %copy-done, f32[32,512]{1,0:T(8,128)S(1)} %get-tuple-element.52.soft_ref, s32[4,128]{1,0:T(4,128)S(1)} %copy-done.6, f32[256,128]{1,0:T(8,128)S(1)} %get-tuple-element.53.coef_ref), custom_call_target="tpu_custom_call" | custom-call | tf_op jit(solution)/shard_map/pallas_call | solution.py:557
  20.1 0.8 %shard_map.240 = (f32[600,512]{1,0:T(8,128)S(1)}, f32[208,512]{1,0:T(8,128)S(1)}) custom-call(bf16[600,512]{1,0:T(8,128)(2,1)S(1)} %shard_map.239.old_ref, bf16[600,600]{1,0:T(8,128)(2,1)S(1)} %copy-done, bf16[224,600]{1,0:T(8,128)(2,1)S(1)} %get-tuple-element.54.weight_ref), custom_call_target="tpu_custom_call" | custom-call | tf_op jit(solution)/shard_map/pallas_call | solution.py:589
  21.0 1.4 %collective-permute-done.7.got_odd = bf16[8,64]{1,0:T(8,128)(2,1)S(1)} collective-permute-done((bf16[8,64]{1,0:T(8,128)(2,1)S(1)}, bf16[8,64]{1,0:T(8,128)(2,1)S(1)}, u32[]{:S(2)}, u32[]{:S(2)}) %collective-permute-start.7) | collective-permute-done | bytes 1056 | tf_op jit(solution)/shard_map/ppermute | solution.py:515
  22.3 0.5 %shard_map.244 = (bf16[8,64]{1,0:T(8,128)(2,1)S(1)}, bf16[8,64]{1,0:T(8,128)(2,1)S(1)}, bf16[8,64]{1,0:T(8,128)(2,1)S(1)}, f32[32,512]{1,0:T(8,128)S(1)}) custom-call(bf16[8,64]{1,0:T(8,128)(2,1)S(1)} %collective-permute-done.6.got_even, bf16[8,64]{1,0:T(8,128)(2,1)S(1)} %collective-permute-done.7.got_odd, bf16[8,64]{1,0:T(8,128)(2,1)S(1)} %get-tuple-element.69.got_own, ...), custom_call_target="tpu_custom_call" | custom-call | tf_op jit(solution)/shard_map/pallas_call | solution.py:536
  22.8 2.1 %collective-permute-start.8 = (bf16[8,64]{1,0:T(8,128)(2,1)S(1)}, bf16[8,64]{1,0:T(8,128)(2,1)S(1)}, u32[]{:S(2)}, u32[]{:S(2)}) collective-permute-start(bf16[8,64]{1,0:T(8,128)(2,1)S(1)} %get-tuple-element.72), channel_id=1, source_target_pairs={{0,4},{1,5},{2,6},{3,7},{4,0},{5,1},{6,2},{7,3},{8,12},{9,13},{10,... | collective-permute-start | bytes 3080 | tf_op jit(solution)/shard_map/ppermute | solution.py:515
  24.9 0.5 %collective-permute-start.9 = (bf16[8,64]{1,0:T(8,128)(2,1)S(1)}, bf16[8,64]{1,0:T(8,128)(2,1)S(1)}, u32[]{:S(2)}, u32[]{:S(2)}) collective-permute-start(bf16[8,64]{1,0:T(8,128)(2,1)S(1)} %get-tuple-element.73), channel_id=1, source_target_pairs={{0,2},{1,3},{2,0},{3,1},{4,8},{5,9},{6,10},{7,11},{8,4},{9,5},{10,... | collective-permute-start | bytes 3080 | tf_op jit(solution)/shard_map/ppermute | solution.py:515
  25.4 0.4 shard_map.246
  25.9 0.6 %collective-permute-done.8.got_even = bf16[8,64]{1,0:T(8,128)(2,1)S(1)} collective-permute-done((bf16[8,64]{1,0:T(8,128)(2,1)S(1)}, bf16[8,64]{1,0:T(8,128)(2,1)S(1)}, u32[]{:S(2)}, u32[]{:S(2)}) %collective-permute-start.8) | collective-permute-done | bytes 1056 | tf_op jit(solution)/shard_map/ppermute | solution.py:515
  26.5 2.0 %collective-permute-done.9.got_odd = bf16[8,64]{1,0:T(8,128)(2,1)S(1)} collective-permute-done((bf16[8,64]{1,0:T(8,128)(2,1)S(1)}, bf16[8,64]{1,0:T(8,128)(2,1)S(1)}, u32[]{:S(2)}, u32[]{:S(2)}) %collective-permute-start.9) | collective-permute-done | bytes 1056 | tf_op jit(solution)/shard_map/ppermute | solution.py:515
  28.5 0.4 shard_map.247
  28.9 0.6 %collective-permute-start.12 = (bf16[80,128]{1,0:T(8,128)(2,1)S(1)}, bf16[80,128]{1,0:T(8,128)(2,1)S(1)}, u32[]{:S(2)}, u32[]{:S(2)}) collective-permute-start(bf16[80,128]{1,0:T(8,128)(2,1)S(1)} %get-tuple-element.86.sent_col), channel_id=1, source_target_pairs={{0,1},{1,0},{2,3},{3,2},{4,5},{5,4},{6,7},{7,6},{8,9},{9,8},{10,11... | collective-permute-start | bytes 61448 | tf_op jit(solution)/shard_map/ppermute | solution.py:515
  29.6 1.2 %collective-permute-start.10 = (bf16[60,128]{1,0:T(8,128)(2,1)S(1)}, bf16[60,128]{1,0:T(8,128)(2,1)S(1)}, u32[]{:S(2)}, u32[]{:S(2)}) collective-permute-start(bf16[60,128]{1,0:T(8,128)(2,1)S(1)} %get-tuple-element.84), channel_id=1, source_target_pairs={{0,4},{1,5},{2,6},{3,7},{4,0},{5,1},{6,2},{7,3},{8,12},{9,13},{10,... | collective-permute-start | bytes 46088 | tf_op jit(solution)/shard_map/ppermute | solution.py:515
  30.8 1.5 %collective-permute-start.11 = (bf16[60,128]{1,0:T(8,128)(2,1)S(1)}, bf16[60,128]{1,0:T(8,128)(2,1)S(1)}, u32[]{:S(2)}, u32[]{:S(2)}) collective-permute-start(bf16[60,128]{1,0:T(8,128)(2,1)S(1)} %get-tuple-element.85), channel_id=1, source_target_pairs={{0,2},{1,3},{2,0},{3,1},{4,8},{5,9},{6,10},{7,11},{8,4},{9,5},{10,... | collective-permute-start | bytes 46088 | tf_op jit(solution)/shard_map/ppermute | solution.py:515
  32.5 0.8 %collective-permute-done.10.got_row_even = bf16[60,128]{1,0:T(8,128)(2,1)S(1)} collective-permute-done((bf16[60,128]{1,0:T(8,128)(2,1)S(1)}, bf16[60,128]{1,0:T(8,128)(2,1)S(1)}, u32[]{:S(2)}, u32[]{:S(2)}) %collective-permute-start.10) | collective-permute-done | bytes 15392 | tf_op jit(solution)/shard_map/ppermute | solution.py:515
  33.3 1.2 %collective-permute-done.11.got_row_odd = bf16[60,128]{1,0:T(8,128)(2,1)S(1)} collective-permute-done((bf16[60,128]{1,0:T(8,128)(2,1)S(1)}, bf16[60,128]{1,0:T(8,128)(2,1)S(1)}, u32[]{:S(2)}, u32[]{:S(2)}) %collective-permute-start.11) | collective-permute-done | bytes 15392 | tf_op jit(solution)/shard_map/ppermute | solution.py:515
  34.9 2.4 %collective-permute-start.14 = (bf16[8,64]{1,0:T(8,128)(2,1)S(1)}, bf16[8,64]{1,0:T(8,128)(2,1)S(1)}, u32[]{:S(2)}, u32[]{:S(2)}) collective-permute-start(bf16[8,64]{1,0:T(8,128)(2,1)S(1)} %get-tuple-element.95), channel_id=1, source_target_pairs={{0,4},{1,5},{2,6},{3,7},{4,0},{5,1},{6,2},{7,3},{8,12},{9,13},{10,... | collective-permute-start | bytes 3080 | tf_op jit(solution)/shard_map/ppermute | solution.py:515
  37.3 1.5 %collective-permute-start.15 = (bf16[8,64]{1,0:T(8,128)(2,1)S(1)}, bf16[8,64]{1,0:T(8,128)(2,1)S(1)}, u32[]{:S(2)}, u32[]{:S(2)}) collective-permute-start(bf16[8,64]{1,0:T(8,128)(2,1)S(1)} %get-tuple-element.96), channel_id=1, source_target_pairs={{0,2},{1,3},{2,0},{3,1},{4,8},{5,9},{6,10},{7,11},{8,4},{9,5},{10,... | collective-permute-start | bytes 3080 | tf_op jit(solution)/shard_map/ppermute | solution.py:515
  38.8 1.6 %shard_map.245 = bf16[2400,128]{1,0:T(8,128)(2,1)} custom-call(bf16[600,512]{1,0:T(8,128)(2,1)S(1)} %shard_map.239.old_ref, f32[600,512]{1,0:T(8,128)S(1)} %get-tuple-element.55.moved_ref, f32[32,512]{1,0:T(8,128)S(1)} %get-tuple-element.71.soft_ref, s32[4,128]{1,0:T(4,128)S(1)} %copy-done.6, f32[256,128]{1,0:T(8,128)S(1)} %get-tuple-element.53.coef_ref), custom_call_target="tpu_custom_call" | custom-call | tf_op jit(solution)/shard_map/pallas_call | solution.py:550
  40.4 1.1 %shard_map.250 = (f32[480,128]{1,0:T(8,128)}, f32[8,128]{1,0:T(8,128)}) custom-call(f32[480,128]{1,0:T(8,128)S(1)} %get-tuple-element.83.part_ref, f32[60,128]{1,0:T(8,128)S(1)} %get-tuple-element.89.north_ref, f32[60,128]{1,0:T(8,128)S(1)} %get-tuple-element.90.south_ref, f32[16,128]{1,0:T(8,128)S(1)} %get-tuple-element.91.ends_ref, ...), custom_call_target="tpu_custom_call" | custom-call | tf_op jit(solution)/shard_map/pallas_call | solution.py:592
  41.5 0.8 %shard_map.251 = f32[3,4,128]{2,1,0:T(4,128)} custom-call(bf16[8,64]{1,0:T(8,128)(2,1)S(1)} %collective-permute-done.14.got_even, bf16[8,64]{1,0:T(8,128)(2,1)S(1)} %collective-permute-done.15.got_odd, bf16[8,64]{1,0:T(8,128)(2,1)S(1)} %get-tuple-element.97.own, bf16[192,512]{1,0:T(8,128)(2,1)S(1)} %bitcast.16), custom_call_target="tpu_custom_call" | custom-call | tf_op jit(solution)/shard_map/pallas_call | solution.py:598
  (51 shorter events, 1.3 us)
Async XLA Ops:
  0.6 6.9 %copy-start.14 = (f32[25]{0:T(128)S(1)}, f32[25]{0:T(128)}, u32[]{:S(2)}) copy-start(f32[25]{0:T(128)} %gain_hbm.1) | copy-start | bytes 304
  0.6 6.9 %copy-start.13 = (f32[25]{0:T(128)S(1)}, f32[25]{0:T(128)}, u32[]{:S(2)}) copy-start(f32[25]{0:T(128)} %rate_hbm.1) | copy-start | bytes 304
  0.7 6.9 %copy-start.5 = (f32[30,30]{1,0:T(8,128)S(1)}, f32[30,30]{1,0:T(8,128)}, u32[]{:S(2)}) copy-start(f32[30,30]{1,0:T(8,128)} %mix_ref.5) | copy-start | bytes 10804
  0.7 6.9 %copy-start.17 = (f32[30]{0:T(128)S(1)}, f32[30]{0:T(128)}, u32[]{:S(2)}) copy-start(f32[30]{0:T(128)} %param.37) | copy-start | bytes 364
  0.7 6.9 %copy-start.15 = (f32[3,30]{1,0:T(4,128)S(1)}, f32[3,30]{1,0:T(4,128)}, u32[]{:S(2)}) copy-start(f32[3,30]{1,0:T(4,128)} %prof_ref.1) | copy-start | bytes 1084
  0.7 6.9 %copy-start.16 = (f32[30]{0:T(128)S(1)}, f32[30]{0:T(128)}, u32[]{:S(2)}) copy-start(f32[30]{0:T(128)} %param.35) | copy-start | bytes 364
  0.7 8.9 %copy-start.3 = (s32[8,128]{1,0:T(8,128)S(1)}, s32[8,128]{1,0:T(8,128)}, u32[]{:S(2)}) copy-start(s32[8,128]{1,0:T(8,128)} %wet_ref.21) | copy-start | bytes 12292
  0.7 8.9 %copy-start.8 = (f32[8,128]{1,0:T(8,128)S(1)}, f32[8,128]{1,0:T(8,128)}, u32[]{:S(2)}) copy-start(f32[8,128]{1,0:T(8,128)} %cor_ref.3) | copy-start | bytes 12292
  0.7 8.9 %copy-start.1 = (bf16[1,1,3,64,1024]{4,3,2,1,0:T(8,128)(2,1)S(1)}, bf16[1,1,3,64,1024]{4,3,2,1,0:T(8,128)(2,1)}, u32[]{:S(2)}) copy-start(bf16[1,1,3,64,1024]{4,3,2,1,0:T(8,128)(2,1)} %param.41) | copy-start | bytes 1179652
  0.7 8.9 %copy-start.4 = (f32[2,30,8,128]{3,2,1,0:T(8,128)S(1)}, f32[2,30,8,128]{3,2,1,0:T(8,128)}, u32[]{:S(2)}) copy-start(f32[2,30,8,128]{3,2,1,0:T(8,128)} %param.31) | copy-start | bytes 737284
  0.7 12.5 %copy-start.12 = (f32[8,128]{1,0:T(8,128)S(1)}, f32[8,128]{1,0:T(8,128)}, u32[]{:S(2)}) copy-start(f32[8,128]{1,0:T(8,128)} %eta_ref.1) | copy-start | bytes 12292
  0.7 16.1 %copy-start.9 = (s32[128]{0:T(128)S(1)}, s32[128]{0:T(128)}, u32[]{:S(2)}) copy-start(s32[128]{0:T(128)} %param.39) | copy-start | bytes 1540
  0.8 16.1 %copy-start.10 = (s32[1,1,3,64]{3,1,2,0:T(1,128)S(1)}, s32[1,1,3,64]{3,1,2,0:T(1,128)}, u32[]{:S(2)}) copy-start(s32[1,1,3,64]{3,1,2,0:T(1,128)} %param.42) | copy-start | bytes 2308
  0.8 18.5 %copy-start = (bf16[600,600]{1,0:T(8,128)(2,1)S(1)}, bf16[600,600]{1,0:T(8,128)(2,1)}, u32[]{:S(2)}) copy-start(bf16[600,600]{1,0:T(8,128)(2,1)} %inter_ref.3) | copy-start | bytes 2160004
  0.8 18.5 %copy-start.6 = (s32[4,128]{1,0:T(4,128)S(1)}, s32[4,128]{1,0:T(4,128)}, u32[]{:S(2)}) copy-start(s32[4,128]{1,0:T(4,128)} %wet_ref.16) | copy-start | bytes 6148
  3.0 4.7 %collective-permute-start = (bf16[8,64]{1,0:T(8,128)(2,1)S(1)}, bf16[8,64]{1,0:T(8,128)(2,1)S(1)}, u32[]{:S(2)}, u32[]{:S(2)}) collective-permute-start(bf16[8,64]{1,0:T(8,128)(2,1)S(1)} %get-tuple-element.56), channel_id=1, source_target_pairs={{0,4},{1,5},{2,6},{3,7},{4,0},{5,1},{6,2},{7,3},{8,12},{9,13},{10,... | collective-permute-start | bytes 3080 | tf_op jit(solution)/shard_map/ppermute | solution.py:515
  6.0 3.6 %collective-permute-start.1 = (bf16[8,64]{1,0:T(8,128)(2,1)S(1)}, bf16[8,64]{1,0:T(8,128)(2,1)S(1)}, u32[]{:S(2)}, u32[]{:S(2)}) collective-permute-start(bf16[8,64]{1,0:T(8,128)(2,1)S(1)} %get-tuple-element.57), channel_id=1, source_target_pairs={{0,2},{1,3},{2,0},{3,1},{4,8},{5,9},{6,10},{7,11},{8,4},{9,5},{10,... | collective-permute-start | bytes 3080 | tf_op jit(solution)/shard_map/ppermute | solution.py:515
  10.0 6.8 %collective-permute-start.5 = (bf16[80,128]{1,0:T(8,128)(2,1)S(1)}, bf16[80,128]{1,0:T(8,128)(2,1)S(1)}, u32[]{:S(2)}, u32[]{:S(2)}) collective-permute-start(bf16[80,128]{1,0:T(8,128)(2,1)S(1)} %get-tuple-element.62), channel_id=1, source_target_pairs={{0,3},{1,2},{2,1},{3,0},{4,7},{5,6},{6,5},{7,4},{8,11},{9,10},{10,... | collective-permute-start | bytes 61448 | tf_op jit(solution)/shard_map/ppermute | solution.py:515
  10.1 6.7 %collective-permute-start.4 = (bf16[80,128]{1,0:T(8,128)(2,1)S(1)}, bf16[80,128]{1,0:T(8,128)(2,1)S(1)}, u32[]{:S(2)}, u32[]{:S(2)}) collective-permute-start(bf16[80,128]{1,0:T(8,128)(2,1)S(1)} %get-tuple-element.61.sent_col), channel_id=1, source_target_pairs={{0,1},{1,0},{2,3},{3,2},{4,5},{5,4},{6,7},{7,6},{8,9},{9,8},{10,11... | collective-permute-start | bytes 61448 | tf_op jit(solution)/shard_map/ppermute | solution.py:515
  11.7 3.7 %collective-permute-start.2 = (bf16[60,128]{1,0:T(8,128)(2,1)S(1)}, bf16[60,128]{1,0:T(8,128)(2,1)S(1)}, u32[]{:S(2)}, u32[]{:S(2)}) collective-permute-start(bf16[60,128]{1,0:T(8,128)(2,1)S(1)} %get-tuple-element.59), channel_id=1, source_target_pairs={{0,4},{1,5},{2,6},{3,7},{4,0},{5,1},{6,2},{7,3},{8,12},{9,13},{10,... | collective-permute-start | bytes 46088 | tf_op jit(solution)/shard_map/ppermute | solution.py:515
  13.1 3.7 %collective-permute-start.3 = (bf16[60,128]{1,0:T(8,128)(2,1)S(1)}, bf16[60,128]{1,0:T(8,128)(2,1)S(1)}, u32[]{:S(2)}, u32[]{:S(2)}) collective-permute-start(bf16[60,128]{1,0:T(8,128)(2,1)S(1)} %get-tuple-element.60), channel_id=1, source_target_pairs={{0,2},{1,3},{2,0},{3,1},{4,8},{5,9},{6,10},{7,11},{8,4},{9,5},{10,... | collective-permute-start | bytes 46088 | tf_op jit(solution)/shard_map/ppermute | solution.py:515
  17.2 3.7 %collective-permute-start.6 = (bf16[8,64]{1,0:T(8,128)(2,1)S(1)}, bf16[8,64]{1,0:T(8,128)(2,1)S(1)}, u32[]{:S(2)}, u32[]{:S(2)}) collective-permute-start(bf16[8,64]{1,0:T(8,128)(2,1)S(1)} %get-tuple-element.67), channel_id=1, source_target_pairs={{0,4},{1,5},{2,6},{3,7},{4,0},{5,1},{6,2},{7,3},{8,12},{9,13},{10,... | collective-permute-start | bytes 3080 | tf_op jit(solution)/shard_map/ppermute | solution.py:515
  18.8 3.6 %collective-permute-start.7 = (bf16[8,64]{1,0:T(8,128)(2,1)S(1)}, bf16[8,64]{1,0:T(8,128)(2,1)S(1)}, u32[]{:S(2)}, u32[]{:S(2)}) collective-permute-start(bf16[8,64]{1,0:T(8,128)(2,1)S(1)} %get-tuple-element.68), channel_id=1, source_target_pairs={{0,2},{1,3},{2,0},{3,1},{4,8},{5,9},{6,10},{7,11},{8,4},{9,5},{10,... | collective-permute-start | bytes 3080 | tf_op jit(solution)/shard_map/ppermute | solution.py:515
  20.1 2.3 %copy-start.2 = (bf16[1,1,3,64,512]{4,3,2,1,0:T(8,128)(2,1)S(1)}, bf16[1,1,3,64,512]{4,3,2,1,0:T(8,128)(2,1)}, u32[]{:S(2)}) copy-start(bf16[1,1,3,64,512]{4,3,2,1,0:T(8,128)(2,1)} %param.43) | copy-start | bytes 589828
  22.8 3.6 %collective-permute-start.8 = (bf16[8,64]{1,0:T(8,128)(2,1)S(1)}, bf16[8,64]{1,0:T(8,128)(2,1)S(1)}, u32[]{:S(2)}, u32[]{:S(2)}) collective-permute-start(bf16[8,64]{1,0:T(8,128)(2,1)S(1)} %get-tuple-element.72), channel_id=1, source_target_pairs={{0,4},{1,5},{2,6},{3,7},{4,0},{5,1},{6,2},{7,3},{8,12},{9,13},{10,... | collective-permute-start | bytes 3080 | tf_op jit(solution)/shard_map/ppermute | solution.py:515
  24.9 3.6 %collective-permute-start.9 = (bf16[8,64]{1,0:T(8,128)(2,1)S(1)}, bf16[8,64]{1,0:T(8,128)(2,1)S(1)}, u32[]{:S(2)}, u32[]{:S(2)}) collective-permute-start(bf16[8,64]{1,0:T(8,128)(2,1)S(1)} %get-tuple-element.73), channel_id=1, source_target_pairs={{0,2},{1,3},{2,0},{3,1},{4,8},{5,9},{6,10},{7,11},{8,4},{9,5},{10,... | collective-permute-start | bytes 3080 | tf_op jit(solution)/shard_map/ppermute | solution.py:515
  28.9 5.7 %collective-permute-start.13 = (bf16[80,128]{1,0:T(8,128)(2,1)S(1)}, bf16[80,128]{1,0:T(8,128)(2,1)S(1)}, u32[]{:S(2)}, u32[]{:S(2)}) collective-permute-start(bf16[80,128]{1,0:T(8,128)(2,1)S(1)} %get-tuple-element.87), channel_id=1, source_target_pairs={{0,3},{1,2},{2,1},{3,0},{4,7},{5,6},{6,5},{7,4},{8,11},{9,10},{10,... | collective-permute-start | bytes 61448 | tf_op jit(solution)/shard_map/ppermute | solution.py:515
  28.9 5.6 %collective-permute-start.12 = (bf16[80,128]{1,0:T(8,128)(2,1)S(1)}, bf16[80,128]{1,0:T(8,128)(2,1)S(1)}, u32[]{:S(2)}, u32[]{:S(2)}) collective-permute-start(bf16[80,128]{1,0:T(8,128)(2,1)S(1)} %get-tuple-element.86.sent_col), channel_id=1, source_target_pairs={{0,1},{1,0},{2,3},{3,2},{4,5},{5,4},{6,7},{7,6},{8,9},{9,8},{10,11... | collective-permute-start | bytes 61448 | tf_op jit(solution)/shard_map/ppermute | solution.py:515
  29.6 3.7 %collective-permute-start.10 = (bf16[60,128]{1,0:T(8,128)(2,1)S(1)}, bf16[60,128]{1,0:T(8,128)(2,1)S(1)}, u32[]{:S(2)}, u32[]{:S(2)}) collective-permute-start(bf16[60,128]{1,0:T(8,128)(2,1)S(1)} %get-tuple-element.84), channel_id=1, source_target_pairs={{0,4},{1,5},{2,6},{3,7},{4,0},{5,1},{6,2},{7,3},{8,12},{9,13},{10,... | collective-permute-start | bytes 46088 | tf_op jit(solution)/shard_map/ppermute | solution.py:515
  30.8 3.7 %collective-permute-start.11 = (bf16[60,128]{1,0:T(8,128)(2,1)S(1)}, bf16[60,128]{1,0:T(8,128)(2,1)S(1)}, u32[]{:S(2)}, u32[]{:S(2)}) collective-permute-start(bf16[60,128]{1,0:T(8,128)(2,1)S(1)} %get-tuple-element.85), channel_id=1, source_target_pairs={{0,2},{1,3},{2,0},{3,1},{4,8},{5,9},{6,10},{7,11},{8,4},{9,5},{10,... | collective-permute-start | bytes 46088 | tf_op jit(solution)/shard_map/ppermute | solution.py:515
  34.9 6.6 %collective-permute-start.14 = (bf16[8,64]{1,0:T(8,128)(2,1)S(1)}, bf16[8,64]{1,0:T(8,128)(2,1)S(1)}, u32[]{:S(2)}, u32[]{:S(2)}) collective-permute-start(bf16[8,64]{1,0:T(8,128)(2,1)S(1)} %get-tuple-element.95), channel_id=1, source_target_pairs={{0,4},{1,5},{2,6},{3,7},{4,0},{5,1},{6,2},{7,3},{8,12},{9,13},{10,... | collective-permute-start | bytes 3080 | tf_op jit(solution)/shard_map/ppermute | solution.py:515
  37.3 4.2 %collective-permute-start.15 = (bf16[8,64]{1,0:T(8,128)(2,1)S(1)}, bf16[8,64]{1,0:T(8,128)(2,1)S(1)}, u32[]{:S(2)}, u32[]{:S(2)}) collective-permute-start(bf16[8,64]{1,0:T(8,128)(2,1)S(1)} %get-tuple-element.96), channel_id=1, source_target_pairs={{0,2},{1,3},{2,0},{3,1},{4,8},{5,9},{6,10},{7,11},{8,4},{9,5},{10,... | collective-permute-start | bytes 3080 | tf_op jit(solution)/shard_map/ppermute | solution.py:515
  (2 other events, 4.5 us)

commit v5 on v4

--- a/solution.py
+++ b/solution.py
@@ -11,7 +11,6 @@
 
 NDIR = 24
 NBAND = 3
-STEPS = 2
 viscous = 0.2
 surface_rate = 0.5
 
@@ -21,13 +20,13 @@
 HBM = pl.BlockSpec(memory_space=pltpu.HBM)
 
 
-def call(kernel, outs, specs, scratch=()):
+def call(kernel, outs, specs, scratch=(), out_spec=VMEM):
     out_shape = tuple(jax.ShapeDtypeStruct(s, d) for s, d in outs)
     return pl.pallas_call(
         kernel,
         out_shape=out_shape,
         in_specs=list(specs),
-        out_specs=tuple(VMEM for _ in outs),
+        out_specs=tuple(out_spec for _ in outs),
         scratch_shapes=list(scratch),
         compiler_params=pltpu.CompilerParams(vmem_limit_bytes=12 << 20),
     )
@@ -113,18 +112,39 @@
         store(y, cells, wet * (old + growth * old + moved_of(cells)))
 
 
+def picked(fields, send):
+    index = jnp.concatenate([send[j] for j in range(3)], axis=1)
+    cell = lax.broadcasted_iota(jnp.int32, (fields.shape[1], index.shape[1]), 0)
+    return dot(fields.astype(bf16), jnp.where(cell == index, 1.0, 0.0).astype(bf16))
+
+
 def pick(fields, send, outs):
     to_even, to_odd, own = outs
     slot = send.shape[2]
-    index = jnp.concatenate([send[j] for j in range(3)], axis=1)
-    cell = lax.broadcasted_iota(jnp.int32, (fields.shape[1], 3 * slot), 0)
-    hot = jnp.where(cell == index, 1.0, 0.0).astype(bf16)
-    slots = dot(fields.astype(bf16), hot)
+    slots = picked(fields, send)
     even = is_even(lax.axis_index("row"))
     south, north = slots[:, :slot], slots[:, 2 * slot :]
     to_even[...] = jnp.where(even, north, south).astype(bf16)
     to_odd[...] = jnp.where(even, south, north).astype(bf16)
     own[...] = slots[:, slot : 2 * slot].astype(bf16)
+
+
+def in_first_half(row):
+    return lax.rem(row, 4) < 2
+
+
+def pick_far(fields, send, outs):
+    to_even, to_odd, own, far_even, far_odd = outs
+    slot = send.shape[2]
+    slots = picked(fields, send)
+    row = lax.axis_index("row")
+    even, first = is_even(row), in_first_half(row)
+    south, here, north = slots[:, :slot], slots[:, slot : 2 * slot], slots[:, 2 * slot :]
+    to_even[...] = jnp.concatenate([jnp.where(even, north, south), here], axis=1).astype(bf16)
+    to_odd[...] = jnp.concatenate([jnp.where(even, south, north), here], axis=1).astype(bf16)
+    own[...] = slots.astype(bf16)
+    far_even[...] = jnp.where(first, north, south).astype(bf16)
+    far_odd[...] = jnp.where(first, south, north).astype(bf16)
 
 
 def gather_slots(got_even, got_odd, own, rows):
@@ -198,28 +218,78 @@
     )
 
 
-def k_transfer(old_ref, inter_ref, weight_ref, moved_ref, parts_ref):
-    parts_ref[...] = joined(dot(weight_ref[...], old_ref[...]))
+def k_pack(energy_ref, weight_ref, recv_ref, wind_ref, wet_ref, send_ref, south_ref, own_ref, north_ref):
+    parts = joined(dot(weight_ref[...], energy_ref[...]))
+    slot = send_ref.shape[2]
+    rows = parts.shape[0]
+    extra = []
+    for i in range(2):
+        high, low = split2(flat(wind_ref, i))
+        extra += [high.astype(f32), low.astype(f32)]
+    extra.append(flat(wet_ref).astype(f32))
+    extra.append(jnp.zeros((rows - recv_ref.shape[0] - len(extra), parts.shape[1]), f32))
+    extra = jnp.concatenate(extra, axis=0).astype(bf16)
+    stack = jnp.concatenate([parts.astype(bf16), recv_ref[...], extra], axis=0)
+    cells = picked(stack, send_ref)
+    for j, ref in enumerate((south_ref, own_ref, north_ref)):
+        lanes = slice(j * slot, (j + 1) * slot)
+        ref[...] = jnp.concatenate([cells[:rows, lanes], cells[rows:, lanes]], axis=1).astype(bf16)
+
+
+def k_transfer(old_ref, inter_ref, moved_ref):
     moved_ref[...] = dot(inter_ref[...], old_ref[...])
 
 
 def k_wave_next(
-    n_row,
-    got_even, got_odd, got_own, recv_ref, parts_ref, wind_ref, wet_ref, send_ref,
-    to_even, to_odd, own, soft_ref,
-    cur_ref,
+    n_row, pad,
+    got_even, got_odd, far_even, far_odd, own_ref, row_even, row_odd, pack_ref,
+    slots_ref, mine_ref,
 ):
-    cur_ref[...] = dot(gather_slots(got_even, got_odd, got_own, n_row), recv_ref[...])
-    level = cur_ref[2:3, :]
-    soft = soft_growth(flat(wind_ref, 0) - cur_ref[0:1, :], flat(wind_ref, 1) - cur_ref[1:2, :])
-    soft_ref[:NDIR, :] = soft
-    soft_ref[NDIR:, :] = jnp.concatenate([level] * (soft_ref.shape[0] - NDIR), axis=0)
-    fields = fields_of(soft, level, flat(wet_ref).astype(f32), parts_ref[...])
-    pick(fields, send_ref, (to_even, to_odd, own))
-
-
-def k_update_last(nfreq, old_ref, moved_ref, soft_ref, wet_ref, coef_ref, out_ref, wide):
+    slot = far_even.shape[1]
+    row = lax.axis_index("row")
+    even, first = is_even(row), in_first_half(row)
+    a, b = got_even[...].astype(f32), got_odd[...].astype(f32)
+    north = jnp.where(row == n_row - 1, 0.0, jnp.where(even, a, b))
+    south = jnp.where(row == 0, 0.0, jnp.where(even, b, a))
+    a, b = far_even[...].astype(f32), far_odd[...].astype(f32)
+    far_north = jnp.where(row >= n_row - 2, 0.0, jnp.where(first, a, b))
+    far_south = jnp.where(row < 2, 0.0, jnp.where(first, b, a))
+    own = own_ref[...].astype(f32)
+    down, here, up = own[:, :slot], own[:, slot : 2 * slot], own[:, 2 * slot :]
+    mine = jnp.concatenate([north[:, :slot], here, south[:, :slot]], axis=1).astype(bf16)
+    mine_ref[...] = mine
+    slots = [
+        jnp.concatenate([far_north, north[:, slot:], up], axis=1).astype(bf16),
+        mine,
+        jnp.concatenate([down, south[:, slot:], far_south], axis=1).astype(bf16),
+    ]
+    a, b = row_even[pad:, :].astype(f32), row_odd[pad:, :].astype(f32)
+    packs = [jnp.where(even, a, b), pack_ref[...].astype(f32), jnp.where(even, b, a)]
+    recv = 3 * slot
+    current = jnp.concatenate(
+        [dot(x, p[:recv, slot:].astype(bf16)) for x, p in zip(slots, packs)], axis=1
+    )
+    extra = jnp.concatenate([p[recv : recv + 8, slot:] for p in packs], axis=1)
+    parts = jnp.concatenate([p[:, :slot] for p in packs], axis=1)
+    soft = soft_growth(
+        extra[0:1] + extra[1:2] - current[0:1], extra[2:3] + extra[3:4] - current[1:2]
+    )
+    fields = fields_of(soft, current[2:3], extra[4:5], parts)
+    lane = lax.broadcasted_iota(jnp.int32, fields.shape, 1)
+    fields = jnp.where((row == n_row - 1) & (lane < slot), 0.0, fields)
+    fields = jnp.where((row == 0) & (lane >= 2 * slot), 0.0, fields)
+    slots_ref[...] = fields.astype(bf16)
+
+
+def k_update_last(
+    nfreq, old_ref, moved_ref, mine_ref, recv_ref, wind_ref, wet_ref, coef_ref, out_ref, cur, soft_ref, wide
+):
     rows, spec = wet_ref.shape[0], old_ref.shape[0]
+    cur[...] = dot(mine_ref[...], recv_ref[...])
+    soft_ref[:NDIR, :] = soft_growth(
+        flat(wind_ref, 0) - cur[0:1, :], flat(wind_ref, 1) - cur[1:2, :]
+    )
+    soft_ref[NDIR:, :] = jnp.concatenate([cur[2:3, :]] * (soft_ref.shape[0] - NDIR), axis=0)
 
     def store(y, cells, value):
         wide[pl.ds(y, spec, stride=rows), :] = value
@@ -229,6 +299,25 @@
         soft_ref, wet_ref, coef_ref, nfreq, store,
     )
     out_ref[...] = wide[...].astype(bf16)
+
+
+def k_last(
+    lev,
+    spectra_ref, eta_ref, part_ref, north_ref, south_ref, ends_ref, sea_ref, mix_ref,
+    spectra_out, eta_out, vel_out,
+    vel_ref, smooth, pieces, sems,
+):
+    copies = [
+        pltpu.make_async_copy(spectra_ref, spectra_out, sems.at[0]),
+        pltpu.make_async_copy(eta_ref, eta_out, sems.at[1]),
+        pltpu.make_async_copy(vel_ref, vel_out, sems.at[2]),
+    ]
+    copies[0].start()
+    copies[1].start()
+    k_mix(lev, part_ref, north_ref, south_ref, ends_ref, sea_ref, mix_ref, vel_ref, smooth, pieces)
+    copies[2].start()
+    for copy in copies:
+        copy.wait()
 
 
 def k_current_out(n_row, got_even, got_odd, own, recv_ref, out_ref):
@@ -276,14 +365,19 @@
 
 
 def k_force(
-    n_row, lev, pad,
-    got_even, got_odd, own, recv_ref, vel_ref, wet_ref, cor_ref, coef_ref,
-    forced_ref, row_even, row_odd, col_even, col_odd,
-    fs,
+    n_row, lev, pad, first,
+    *refs,
 ):
+    if first:
+        got_even, got_odd, own, pack_south, pack_north, *refs = refs
+        slots = gather_slots(got_even, got_odd, own, n_row)
+    else:
+        slot_ref, *refs = refs
+        slots = slot_ref[...]
+    recv_ref, vel_ref, wet_ref, cor_ref, coef_ref, forced_ref, row_even, row_odd, col_even, col_odd, fs = refs
     oy, ox = wet_ref.shape
     planes = 2 * lev
-    forcing = dot(gather_slots(got_even, got_odd, own, n_row), recv_ref[...])
+    forcing = dot(slots, recv_ref[...])
     nf = forcing.shape[0]
     for y in range(oy):
         fs[y * nf : (y + 1) * nf, :] = forcing[:, y * ox : (y + 1) * ox]
@@ -310,8 +404,12 @@
     bottom = forced_ref[pl.ds(0, planes, stride=oy), :]
     top = forced_ref[pl.ds(oy - 1, planes, stride=oy), :]
     even = is_even(lax.axis_index("row"))
-    row_even[...] = jnp.where(even, top, bottom).astype(bf16)
-    row_odd[...] = jnp.where(even, bottom, top).astype(bf16)
+    row_even[:planes, :] = jnp.where(even, top, bottom).astype(bf16)
+    row_odd[:planes, :] = jnp.where(even, bottom, top).astype(bf16)
+    if first:
+        a, b = pack_south[...].astype(f32), pack_north[...].astype(f32)
+        row_even[pad:, :] = jnp.where(even, b, a).astype(bf16)
+        row_odd[pad:, :] = jnp.where(even, a, b).astype(bf16)
     even = is_even(lax.axis_index("col"))
     col_even[:planes, :] = top.astype(bf16)
     col_odd[:planes, :] = top.astype(bf16)
@@ -350,16 +448,16 @@
 
 
 def k_back(
-    n_row, n_col, pad, whole,
+    n_row, n_col, pad, whole, choose,
     got_row_even, got_row_odd, got_col_even, got_col_odd, sent_col, line_ref, fold_ref, sums_ref, wet_ref, side_ref, lane_ref, send_ref,
-    eta_out, to_even, to_odd, own, north_ref, south_ref, ends_ref,
-    bs,
+    eta_out, north_ref, south_ref, ends_ref, *outs,
 ):
+    *outs, bs = outs
     oy, ox = wet_ref.shape
-    planes = got_row_even.shape[0]
+    planes = north_ref.shape[0]
     row, col = lax.axis_index("row"), lax.axis_index("col")
     even = is_even(row)
-    a, b = got_row_even[...].astype(f32), got_row_odd[...].astype(f32)
+    a, b = got_row_even[:planes, :].astype(f32), got_row_odd[:planes, :].astype(f32)
     north_ref[...] = jnp.where(even, a, b)
 
     @pl.when(row == n_row - 1)
@@ -373,7 +471,7 @@
                 (sent_col[:planes, :], col),
                 (got_col_even[:planes, :], pair_even),
                 (got_col_odd[:planes, :], pair_odd),
-                (got_row_odd[...], lax.rem(col + n_col // 2, n_col)),
+                (got_row_odd[:planes, :], lax.rem(col + n_col // 2, n_col)),
             ]
         cell = lax.broadcasted_iota(jnp.int32, (ox, ox), 0)
         across = None
@@ -413,13 +511,12 @@
     bs[2 * oy : 3 * oy, :] = eta
     bs[3 * oy :, :] = jnp.zeros((5 * oy, ox), f32)
     back = jnp.concatenate([bs[pl.ds(y, 8, stride=oy), :] for y in range(oy)], axis=1)
-    pick(back, send_ref, (to_even, to_odd, own))
-
-
-def k_mix(lev, part_ref, north_ref, south_ref, ends_ref, wet_ref, mix_ref, eta_ref, vel_ref, eta_out, smooth, wide):
+    choose(back, send_ref, outs)
+
+
+def k_mix(lev, part_ref, north_ref, south_ref, ends_ref, wet_ref, mix_ref, vel_ref, smooth, wide):
     oy, ox = wet_ref.shape
     planes = 2 * lev
-    eta_out[...] = eta_ref[...]
     wet = viscous * wet_ref[...].astype(f32)
     is_top, is_bottom, is_east, is_west = borders(oy, ox)
     east, west = ends_ref[:oy, :], ends_ref[oy:, :]
@@ -461,9 +558,20 @@
                 row_odd.append((place(r, c), place(other, c)))
             else:
                 row_odd.append((place(r, c), place(r, (c + n_col // 2) % n_col)))
+    far_even = [(place(r, c), place(r ^ 2, c)) for r in range(n_row) for c in range(n_col)]
+    far_odd = []
+    for r in range(n_row):
+        other = r - 2 if r % 4 < 2 else r + 2
+        for c in range(n_col):
+            if 0 <= other < n_row:
+                far_odd.append((place(r, c), place(other, c)))
+            else:
+                far_odd.append((place(r, c), place(r, (c + n_col // 2) % n_col)))
     col_even = [(c, c ^ 1) for c in range(n_col)]
     col_odd = [(c, (c + 1 if c % 2 else c - 1) % n_col) for c in range(n_col)]
-    return dict(row_even=row_even, row_odd=row_odd, col_even=col_even, col_odd=col_odd)
+    return dict(
+        row_even=row_even, row_odd=row_odd, col_even=col_even, col_odd=col_odd, far_even=far_even, far_odd=far_odd
+    )
 
 
 def shards(
@@ -511,61 +619,24 @@
     whole = n_col != 4
 
     def trade(label, array):
-        axis = both if label.startswith("row") else "col"
+        axis = "col" if label.startswith("col") else both
         return lax.ppermute(array, axis, pairs[label])
 
     slots_out = [((8, slot), bf16)] * 3
     soft_out = ((32, cells), f32)
     half = GROUP * (NDIR + 2)
     full = (planes * oy, ox)
-    for step in range(STEPS):
-        last = step + 1 == STEPS
-        if step == 0:
-            inputs = (
-                stress_map, stokes_map, input_rate, eta_gain, wind, wave_current, wave_wet, wsend,
-                spectra.reshape(spec * rows, lanes), interaction,
-            )
-            held = [(pltpu.SMEM if x.ndim == 1 else pltpu.VMEM)(x.shape, x.dtype) for x in inputs]
-            to_even, to_odd, own, energy, soft, weights = call(
-                functools.partial(k_wave_first, nfreq),
-                slots_out + [((spec, cells), bf16), soft_out, ((half + 2 * GROUP, spec), bf16)],
-                [HBM] * len(inputs),
-                held + [pltpu.VMEM((spec * rows, lanes), f32), pltpu.SemaphoreType.DMA((len(inputs) + 2,))],
-            )(*(pltpu.with_memory_space_constraint(x, pltpu.HBM) for x in inputs))
-        else:
-            to_even, to_odd, own, soft = call(
-                functools.partial(k_wave_next, n_row), slots_out + [soft_out], [VMEM] * 8, [pltpu.VMEM((8, cells), f32)]
-            )(got_even, got_odd, own, wave_w, parts, wind, wave_wet, wsend)
-        got_odd, got_even = trade("row_odd", to_odd), trade("row_even", to_even)
-        if step == 0:
-            coef, side, lane_rows = call(
-                functools.partial(k_prepare, lev),
-                [((8 * 32, 128), f32), ((3, planes, 128), f32), ((8, 128), f32)],
-                [VMEM] * 6,
-            )(
-                tau_profile.reshape(1, lev), stokes_profile, thickness.reshape(1, lev), mix_inverse,
-                input_rate.reshape(1, nfreq), eta_gain.reshape(1, nfreq),
-            )
-        if last:
-            (spectra_out,) = call(
-                functools.partial(k_update_last, nfreq),
-                [((spec * rows, lanes), bf16)],
-                [VMEM] * 5,
-                [pltpu.VMEM((spec * rows, lanes), f32)],
-            )(energy, moved, soft, wave_wet, coef)
-        else:
-            (energy,) = call(
-                functools.partial(k_update, nfreq),
-                [((spec, cells), bf16)],
-                [VMEM] * 5,
-                [pltpu.VMEM((spec, cells), f32)],
-            )(energy, interaction, soft, wave_wet, coef)
+    mixer = [pltpu.VMEM(full, f32), pltpu.VMEM((96, 2 * oy * ox), bf16)]
+
+    def edges(step, lists, send_of):
+        first = step == 0
+        tall = pad + half if first else planes
         forced, row_even, row_odd, col_even, col_odd = call(
-            functools.partial(k_force, n_row, lev, pad),
-            [(full, f32)] + [((planes, ox), bf16)] * 2 + [((pad + 16, ox), bf16)] * 2,
-            [VMEM] * 8,
+            functools.partial(k_force, n_row, lev, pad, first),
+            [(full, f32)] + [((tall, ox), bf16)] * 2 + [((pad + 16, ox), bf16)] * 2,
+            [VMEM] * (len(lists) + 5),
             [pltpu.VMEM((8 * oy, ox), f32)],
-        )(got_even, got_odd, own, ocean_w, velocity, ocean_wet, coriolis, coef)
+        )(*lists, ocean_w, velocity, ocean_wet, coriolis, coef)
         got_row_odd, got_row_even = trade("row_odd", row_odd), trade("row_even", row_even)
         got_col_odd, got_col_even = trade("col_odd", col_odd), trade("col_even", col_even)
         part, sums = call(
@@ -575,26 +646,76 @@
             top_line = lax.all_gather(col_even[:planes], "col", axis=0, tiled=True)
         else:
             top_line = fold
-        eta, to_even, to_odd, own, north, south, ends = call(
-            functools.partial(k_back, n_row, n_col, pad, whole),
-            [((oy, ox), f32)] + slots_out + [((planes, ox), f32)] * 2 + [((2 * oy, ox), f32)],
+        choose, slots = send_of
+        eta_next, north, south, ends, *sent = call(
+            functools.partial(k_back, n_row, n_col, pad, whole, choose),
+            [((oy, ox), f32)] + [((planes, ox), f32)] * 2 + [((2 * oy, ox), f32)] + slots,
             [VMEM] * 12,
             [pltpu.VMEM((8 * oy, ox), f32)],
         )(
             got_row_even, got_row_odd, got_col_even, got_col_odd, col_even, top_line, fold, sums, ocean_wet,
             side, lane_rows, osend,
         )
-        got_odd, got_even = trade("row_odd", to_odd), trade("row_even", to_even)
-        if not last:
-            moved, parts = call(
-                k_transfer, [((spec, cells), f32), ((half, cells), f32)], [VMEM] * 3
-            )(energy, interaction, weights)
-        velocity, eta = call(
-            functools.partial(k_mix, lev),
-            [(full, f32), ((oy, ox), f32)],
-            [VMEM] * 7,
-            [pltpu.VMEM(full, f32), pltpu.VMEM((96, 2 * oy * ox), bf16)],
-        )(part, north, south, ends, ocean_wet, mix_inverse, eta)
+        return (part, north, south, ends), eta_next, sent, (got_row_even, got_row_odd)
+
+    inputs = (
+        stress_map, stokes_map, input_rate, eta_gain, wind, wave_current, wave_wet, wsend,
+        spectra.reshape(spec * rows, lanes), interaction,
+    )
+    held = [(pltpu.SMEM if x.ndim == 1 else pltpu.VMEM)(x.shape, x.dtype) for x in inputs]
+    to_even, to_odd, own, energy, soft, weights = call(
+        functools.partial(k_wave_first, nfreq),
+        slots_out + [((spec, cells), bf16), soft_out, ((half + 2 * GROUP, spec), bf16)],
+        [HBM] * len(inputs),
+        held + [pltpu.VMEM((spec * rows, lanes), f32), pltpu.SemaphoreType.DMA((len(inputs) + 2,))],
+    )(*(pltpu.with_memory_space_constraint(x, pltpu.HBM) for x in inputs))
+    got_odd, got_even = trade("row_odd", to_odd), trade("row_even", to_even)
+    coef, side, lane_rows = call(
+        functools.partial(k_prepare, lev), [((8 * 32, 128), f32), ((3, planes, 128), f32), ((8, 128), f32)], [VMEM] * 6
+    )(
+        tau_profile.reshape(1, lev), stokes_profile, thickness.reshape(1, lev), mix_inverse,
+        input_rate.reshape(1, nfreq), eta_gain.reshape(1, nfreq),
+    )
+    (energy,) = call(
+        functools.partial(k_update, nfreq), [((spec, cells), bf16)], [VMEM] * 5, [pltpu.VMEM((spec, cells), f32)]
+    )(energy, interaction, soft, wave_wet, coef)
+    pack_south, pack_own, pack_north = call(
+        k_pack, [((half, 2 * slot), bf16)] * 3, [VMEM] * 6
+    )(energy, weights, wave_w, wind, wave_wet, wsend)
+    far_slots = [((8, 2 * slot), bf16)] * 2 + [((8, 3 * slot), bf16)] + [((8, slot), bf16)] * 2
+    smooth, eta, sent, got_rows = edges(
+        0, (got_even, got_odd, own, pack_south, pack_north), (pick_far, far_slots)
+    )
+    to_even, to_odd, own, far_even, far_odd = sent
+    got_odd, got_even = trade("row_odd", to_odd), trade("row_even", to_even)
+    got_far_odd, got_far_even = trade("far_odd", far_odd), trade("far_even", far_even)
+    (moved,) = call(k_transfer, [((spec, cells), f32)], [VMEM] * 2)(
+        energy, interaction
+    )
+    (velocity,) = call(functools.partial(k_mix, lev), [(full, f32)], [VMEM] * 6, mixer)(*smooth, ocean_wet, mix_inverse)
+    fields, mine = call(
+        functools.partial(k_wave_next, n_row, pad), [((8, 3 * slot), bf16)] * 2, [VMEM] * 8
+    )(got_even, got_odd, got_far_even, got_far_odd, own, *got_rows, pack_own)
+    (spectra_new,) = call(
+        functools.partial(k_update_last, nfreq),
+        [((spec * rows, lanes), bf16)],
+        [VMEM] * 7,
+        [
+            pltpu.VMEM((8, cells), f32),
+            pltpu.VMEM(soft_out[0], f32),
+            pltpu.VMEM((spec * rows, lanes), f32),
+        ],
+    )(energy, moved, mine, wave_w, wind, wave_wet, coef)
+    smooth, eta, sent, _ = edges(1, (fields,), (pick, slots_out))
+    to_even, to_odd, own = sent
+    got_odd, got_even = trade("row_odd", to_odd), trade("row_even", to_even)
+    spectra_out, eta, velocity = call(
+        functools.partial(k_last, lev),
+        [((spec * rows, lanes), bf16), ((oy, ox), f32), (full, f32)],
+        [VMEM] * 8,
+        [pltpu.VMEM(full, f32), *mixer, pltpu.SemaphoreType.DMA((3,))],
+        HBM,
+    )(spectra_new, eta, *smooth, ocean_wet, mix_inverse)
     (current,) = call(
         functools.partial(k_current_out, n_row), [((3, rows, lanes), f32)], [VMEM] * 4
     )(got_even, got_odd, own, wave_w)

time: 42.5 us -> 38.6 us (0.908)
  waiting for transfers between devices: 11.3 us -> 7.84 us
  Pallas kernels: 10.2 us -> 9.77 us
    ppermute x16, waiting for transfers between devices: 11.3 us -> 7.84 us  [trade(): return lax.ppermute(array, axis, pairs[label])]
    pallas_call x1, Pallas kernels: 1.58 us -> 0.93 us  [shards(): call(functools.partial(k_update_last, nfreq), [((spec * rows, lanes), bf1...]
    pallas_call x10 -> x11, Pallas kernels: 4.7 us -> 4.95 us  [the longest x1 1.15 us: shards(): call(functools.partial(k_last, lev), [((spec * rows, lanes), bf16), ((oy,...]
  transfers between devices with their start and end apart: 16 -> 16, of which waited for: 8 -> 7; matrix products, arithmetic and copies ran while one was open for 0% -> 0% of each run, Pallas kernels for 12% -> 13%
where the time goes in v5:
time: 38.6 us; the launch traced here: 38.4 us
  starting transfers between devices  19.7 us (51%)
  Pallas kernels  9.77 us (25%)
  waiting for transfers between devices  7.84 us (20%)
  between operations  0.99 us (3%)
    ppermute x16, starting transfers between devices, trade(): return lax.ppermute(array, axis, pairs[label])  19.7 us
    ppermute x16, waiting for transfers between devices, trade(): return lax.ppermute(array, axis, pairs[label])  7.84 us
    pallas_call x1, Pallas kernels, shards(): call(functools.partial(k_wave_first, nfreq), slots_out + [((spec, cells),...  2.19 us
    pallas_call x1, Pallas kernels, shards(): call(functools.partial(k_last, lev), [((spec * rows, lanes), bf16), ((oy,...  1.15 us
    pallas_call x1, Pallas kernels, shards(): call(functools.partial(k_update_last, nfreq), [((spec * rows, lanes), bf1...  0.93 us
    pallas_call x1, Pallas kernels, shards(): call(functools.partial(k_update, nfreq), [((spec, cells), bf16)], [VMEM]...  0.78 us
    pallas_call x1, Pallas kernels, shards(): call(functools.partial(k_current_out, n_row), [((3, rows, lanes), f32)],...  0.78 us
  transfers between devices with their start and end apart: 16, of which 7 were waited for; matrix products, arithmetic and copies ran while one was open for 0% of the time, Pallas kernels for 13%

profile of v5, /device:TPU:0, one launch (start us, length us, event | category | flops | bytes accessed | tf_op | source)
XLA Modules:
  0.0 38.4 jit_solution(2556205484801237839)
XLA Ops:
  0.7 2.2 %shard_map.237 = (bf16[8,64]{1,0:T(8,128)(2,1)S(1)}, bf16[8,64]{1,0:T(8,128)(2,1)S(1)}, bf16[8,64]{1,0:T(8,128)(2,1)S(1)}, bf16[600,512]{1,0:T(8,128)(2,1)S(1)},...) custom-call(f32[2,600]{1,0:T(2,128)} %smap_hbm.1, f32[6,600]{1,0:T(8,128)} %kmap_hbm.1, f32[25]{0:T(128)} %rate_hbm.1, ...), custom_call_target="tpu_custom_call" | custom-call | tf_op jit(solution)/shard_map/pallas_call | solution.py:666
  2.9 3.1 %collective-permute-start = (bf16[8,64]{1,0:T(8,128)(2,1)S(1)}, bf16[8,64]{1,0:T(8,128)(2,1)S(1)}, u32[]{:S(2)}, u32[]{:S(2)}) collective-permute-start(bf16[8,64]{1,0:T(8,128)(2,1)S(1)} %get-tuple-element.54), channel_id=1, source_target_pairs={{0,4},{1,5},{2,6},{3,7},{4,0},{5,1},{6,2},{7,3},{8,12},{9,13},{10,... | collective-permute-start | bytes 3080 | tf_op jit(solution)/shard_map/ppermute | solution.py:623
  6.0 1.5 %collective-permute-start.1 = (bf16[8,64]{1,0:T(8,128)(2,1)S(1)}, bf16[8,64]{1,0:T(8,128)(2,1)S(1)}, u32[]{:S(2)}, u32[]{:S(2)}) collective-permute-start(bf16[8,64]{1,0:T(8,128)(2,1)S(1)} %get-tuple-element.55), channel_id=1, source_target_pairs={{0,2},{1,3},{2,0},{3,1},{4,8},{5,9},{6,10},{7,11},{8,4},{9,5},{10,... | collective-permute-start | bytes 3080 | tf_op jit(solution)/shard_map/ppermute | solution.py:623
  7.7 0.8 %shard_map.239.old_ref.energy_ref = bf16[600,512]{1,0:T(8,128)(2,1)S(1)} custom-call(bf16[600,512]{1,0:T(8,128)(2,1)S(1)} %get-tuple-element.51.old_ref, bf16[600,600]{1,0:T(8,128)(2,1)S(1)} %copy-done, f32[32,512]{1,0:T(8,128)S(1)} %get-tuple-element.52.soft_ref, s32[4,128]{1,0:T(4,128)S(1)} %copy-done.7, ...), custom_call_target="tpu_custom_call" | custom-call | tf_op jit(solution)/shard_map/pallas_call | solution.py:679
  8.6 0.6 %shard_map.241 = (bf16[208,128]{1,0:T(8,128)(2,1)S(1)}, bf16[208,128]{1,0:T(8,128)(2,1)S(1)}, bf16[208,128]{1,0:T(8,128)(2,1)S(1)}) custom-call(bf16[600,512]{1,0:T(8,128)(2,1)S(1)} %shard_map.239.old_ref.energy_ref, bf16[224,600]{1,0:T(8,128)(2,1)S(1)} %get-tuple-element.57.weight_ref, bf16[192,512]{1,0:T(8,128)(2,1)S(1)} %bitcast.13, ...), custom_call_target="tpu_custom_call" | custom-call | tf_op jit(solution)/shard_map/pallas_call | solution.py:682
  9.2 0.4 collective-permute-done.1.refs_1_
  9.6 0.4 %shard_map.242 = (f32[480,128]{1,0:T(8,128)S(1)}, bf16[272,128]{1,0:T(8,128)(2,1)S(1)}, bf16[272,128]{1,0:T(8,128)(2,1)S(1)}, bf16[80,128]{1,0:T(8,128)(2,1)S(1)}, bf16[80,128]{1,0:T(8,128)(2,1)S(1)}) custom-call(bf16[8,64]{1,0:T(8,128)(2,1)S(1)} %collective-permute-done.refs_0_, bf16[8,64]{1,0:T(8,128)(2,1)S(1)} %collective-permute-done.1.refs_1_, ...), custom_call_target="tpu_custom_call" | custom-call | tf_op jit(solution)/shard_map/pallas_call | solution.py:634
  10.0 1.3 %collective-permute-start.2 = (bf16[272,128]{1,0:T(8,128)(2,1)S(1)}, bf16[272,128]{1,0:T(8,128)(2,1)S(1)}, u32[]{:S(2)}, u32[]{:S(2)}) collective-permute-start(bf16[272,128]{1,0:T(8,128)(2,1)S(1)} %get-tuple-element.60), channel_id=1, source_target_pairs={{0,4},{1,5},{2,6},{3,7},{4,0},{5,1},{6,2},{7,3},{8,12},{9,13},{10,... | collective-permute-start | bytes 208904 | tf_op jit(solution)/shard_map/ppermute | solution.py:623
  11.3 1.7 %collective-permute-start.3 = (bf16[272,128]{1,0:T(8,128)(2,1)S(1)}, bf16[272,128]{1,0:T(8,128)(2,1)S(1)}, u32[]{:S(2)}, u32[]{:S(2)}) collective-permute-start(bf16[272,128]{1,0:T(8,128)(2,1)S(1)} %get-tuple-element.61), channel_id=1, source_target_pairs={{0,2},{1,3},{2,0},{3,1},{4,8},{5,9},{6,10},{7,11},{8,4},{9,5},{10,... | collective-permute-start | bytes 208904 | tf_op jit(solution)/shard_map/ppermute | solution.py:623
  13.0 0.5 %collective-permute-start.4 = (bf16[80,128]{1,0:T(8,128)(2,1)S(1)}, bf16[80,128]{1,0:T(8,128)(2,1)S(1)}, u32[]{:S(2)}, u32[]{:S(2)}) collective-permute-start(bf16[80,128]{1,0:T(8,128)(2,1)S(1)} %get-tuple-element.62.sent_col), channel_id=1, source_target_pairs={{0,1},{1,0},{2,3},{3,2},{4,5},{5,4},{6,7},{7,6},{8,9},{9,8},{10,11... | collective-permute-start | bytes 61448 | tf_op jit(solution)/shard_map/ppermute | solution.py:623
  13.7 2.5 %collective-permute-done.5.got_col_odd = bf16[80,128]{1,0:T(8,128)(2,1)S(1)} collective-permute-done((bf16[80,128]{1,0:T(8,128)(2,1)S(1)}, bf16[80,128]{1,0:T(8,128)(2,1)S(1)}, u32[]{:S(2)}, u32[]{:S(2)}) %collective-permute-start.5) | collective-permute-done | bytes 20512 | tf_op jit(solution)/shard_map/ppermute | solution.py:623
  16.5 1.7 %collective-permute-start.6 = (bf16[8,128]{1,0:T(8,128)(2,1)S(1)}, bf16[8,128]{1,0:T(8,128)(2,1)S(1)}, u32[]{:S(2)}, u32[]{:S(2)}) collective-permute-start(bf16[8,128]{1,0:T(8,128)(2,1)S(1)} %get-tuple-element.68), channel_id=1, source_target_pairs={{0,4},{1,5},{2,6},{3,7},{4,0},{5,1},{6,2},{7,3},{8,12},{9,13},{10,... | collective-permute-start | bytes 6152 | tf_op jit(solution)/shard_map/ppermute | solution.py:623
  18.2 1.3 %collective-permute-start.7 = (bf16[8,128]{1,0:T(8,128)(2,1)S(1)}, bf16[8,128]{1,0:T(8,128)(2,1)S(1)}, u32[]{:S(2)}, u32[]{:S(2)}) collective-permute-start(bf16[8,128]{1,0:T(8,128)(2,1)S(1)} %get-tuple-element.69), channel_id=1, source_target_pairs={{0,2},{1,3},{2,0},{3,1},{4,8},{5,9},{6,10},{7,11},{8,4},{9,5},{10,... | collective-permute-start | bytes 6152 | tf_op jit(solution)/shard_map/ppermute | solution.py:623
  19.5 0.5 %collective-permute-start.8 = (bf16[8,64]{1,0:T(8,128)(2,1)S(1)}, bf16[8,64]{1,0:T(8,128)(2,1)S(1)}, u32[]{:S(2)}, u32[]{:S(2)}) collective-permute-start(bf16[8,64]{1,0:T(8,128)(2,1)S(1)} %get-tuple-element.70), channel_id=1, source_target_pairs={{0,8},{1,9},{2,10},{3,11},{4,12},{5,13},{6,14},{7,15},{8,0},{9,1},... | collective-permute-start | bytes 3080 | tf_op jit(solution)/shard_map/ppermute | solution.py:623
  20.1 1.5 %collective-permute-start.9 = (bf16[8,64]{1,0:T(8,128)(2,1)S(1)}, bf16[8,64]{1,0:T(8,128)(2,1)S(1)}, u32[]{:S(2)}, u32[]{:S(2)}) collective-permute-start(bf16[8,64]{1,0:T(8,128)(2,1)S(1)} %get-tuple-element.71), channel_id=1, source_target_pairs={{0,2},{1,3},{2,0},{3,1},{4,6},{5,7},{6,4},{7,5},{8,16},{9,17},{10,... | collective-permute-start | bytes 3080 | tf_op jit(solution)/shard_map/ppermute | solution.py:623
  21.6 0.4 %shard_map.247.refs_2_ = f32[480,128]{1,0:T(8,128)S(1)} custom-call(f32[480,128]{1,0:T(8,128)S(1)} %get-tuple-element.76.part_ref, f32[60,128]{1,0:T(8,128)S(1)} %get-tuple-element.77.north_ref, f32[60,128]{1,0:T(8,128)S(1)} %get-tuple-element.78.south_ref, f32[16,128]{1,0:T(8,128)S(1)} %get-tuple-element.79.ends_ref, s32[8,128]{1,0:T(8,128)S(1)} %copy-done.3, ...), custom_call_target="tpu_custom_call" | custom-call | tf_op jit(solution)/shard_map/pallas_call | solution.py:695
  22.0 1.1 %collective-permute-done.8.far_even = bf16[8,64]{1,0:T(8,128)(2,1)S(1)} collective-permute-done((bf16[8,64]{1,0:T(8,128)(2,1)S(1)}, bf16[8,64]{1,0:T(8,128)(2,1)S(1)}, u32[]{:S(2)}, u32[]{:S(2)}) %collective-permute-start.8) | collective-permute-done | bytes 1056 | tf_op jit(solution)/shard_map/ppermute | solution.py:623
  23.1 0.5 %collective-permute-done.9.far_odd = bf16[8,64]{1,0:T(8,128)(2,1)S(1)} collective-permute-done((bf16[8,64]{1,0:T(8,128)(2,1)S(1)}, bf16[8,64]{1,0:T(8,128)(2,1)S(1)}, u32[]{:S(2)}, u32[]{:S(2)}) %collective-permute-start.9) | collective-permute-done | bytes 1056 | tf_op jit(solution)/shard_map/ppermute | solution.py:623
  23.7 0.3 shard_map.245
  24.0 0.3 shard_map.248
  24.4 1.6 %collective-permute-start.12 = (bf16[80,128]{1,0:T(8,128)(2,1)S(1)}, bf16[80,128]{1,0:T(8,128)(2,1)S(1)}, u32[]{:S(2)}, u32[]{:S(2)}) collective-permute-start(bf16[80,128]{1,0:T(8,128)(2,1)S(1)} %get-tuple-element.82.sent_col), channel_id=1, source_target_pairs={{0,1},{1,0},{2,3},{3,2},{4,5},{5,4},{6,7},{7,6},{8,9},{9,8},{10,11... | collective-permute-start | bytes 61448 | tf_op jit(solution)/shard_map/ppermute | solution.py:623
  26.0 3.0 %collective-permute-start.10 = (bf16[60,128]{1,0:T(8,128)(2,1)S(1)}, bf16[60,128]{1,0:T(8,128)(2,1)S(1)}, u32[]{:S(2)}, u32[]{:S(2)}) collective-permute-start(bf16[60,128]{1,0:T(8,128)(2,1)S(1)} %get-tuple-element.80), channel_id=1, source_target_pairs={{0,4},{1,5},{2,6},{3,7},{4,0},{5,1},{6,2},{7,3},{8,12},{9,13},{10,... | collective-permute-start | bytes 46088 | tf_op jit(solution)/shard_map/ppermute | solution.py:623
  29.1 0.5 %collective-permute-start.11 = (bf16[60,128]{1,0:T(8,128)(2,1)S(1)}, bf16[60,128]{1,0:T(8,128)(2,1)S(1)}, u32[]{:S(2)}, u32[]{:S(2)}) collective-permute-start(bf16[60,128]{1,0:T(8,128)(2,1)S(1)} %get-tuple-element.81), channel_id=1, source_target_pairs={{0,2},{1,3},{2,0},{3,1},{4,8},{5,9},{6,10},{7,11},{8,4},{9,5},{10,... | collective-permute-start | bytes 46088 | tf_op jit(solution)/shard_map/ppermute | solution.py:623
  29.8 1.0 %collective-permute-done.10.got_row_even = bf16[60,128]{1,0:T(8,128)(2,1)S(1)} collective-permute-done((bf16[60,128]{1,0:T(8,128)(2,1)S(1)}, bf16[60,128]{1,0:T(8,128)(2,1)S(1)}, u32[]{:S(2)}, u32[]{:S(2)}) %collective-permute-start.10) | collective-permute-done | bytes 15392 | tf_op jit(solution)/shard_map/ppermute | solution.py:623
  30.8 2.0 %collective-permute-done.11.got_row_odd = bf16[60,128]{1,0:T(8,128)(2,1)S(1)} collective-permute-done((bf16[60,128]{1,0:T(8,128)(2,1)S(1)}, bf16[60,128]{1,0:T(8,128)(2,1)S(1)}, u32[]{:S(2)}, u32[]{:S(2)}) %collective-permute-start.11) | collective-permute-done | bytes 15392 | tf_op jit(solution)/shard_map/ppermute | solution.py:623
  32.8 0.3 shard_map.250
  33.1 0.9 %collective-permute-start.14 = (bf16[8,64]{1,0:T(8,128)(2,1)S(1)}, bf16[8,64]{1,0:T(8,128)(2,1)S(1)}, u32[]{:S(2)}, u32[]{:S(2)}) collective-permute-start(bf16[8,64]{1,0:T(8,128)(2,1)S(1)} %get-tuple-element.95), channel_id=1, source_target_pairs={{0,4},{1,5},{2,6},{3,7},{4,0},{5,1},{6,2},{7,3},{8,12},{9,13},{10,... | collective-permute-start | bytes 3080 | tf_op jit(solution)/shard_map/ppermute | solution.py:623
  34.1 0.5 %collective-permute-start.15 = (bf16[8,64]{1,0:T(8,128)(2,1)S(1)}, bf16[8,64]{1,0:T(8,128)(2,1)S(1)}, u32[]{:S(2)}, u32[]{:S(2)}) collective-permute-start(bf16[8,64]{1,0:T(8,128)(2,1)S(1)} %get-tuple-element.96), channel_id=1, source_target_pairs={{0,2},{1,3},{2,0},{3,1},{4,8},{5,9},{6,10},{7,11},{8,4},{9,5},{10,... | collective-permute-start | bytes 3080 | tf_op jit(solution)/shard_map/ppermute | solution.py:623
  34.6 0.6 %shard_map.240.moved_ref = f32[600,512]{1,0:T(8,128)S(1)} custom-call(bf16[600,512]{1,0:T(8,128)(2,1)S(1)} %shard_map.239.old_ref.energy_ref, bf16[600,600]{1,0:T(8,128)(2,1)S(1)} %copy-done), custom_call_target="tpu_custom_call" | custom-call | tf_op jit(solution)/shard_map/pallas_call | solution.py:692
  35.2 0.9 %shard_map.246.spectra_ref = bf16[2400,128]{1,0:T(8,128)(2,1)S(1)} custom-call(bf16[600,512]{1,0:T(8,128)(2,1)S(1)} %shard_map.239.old_ref.energy_ref, f32[600,512]{1,0:T(8,128)S(1)} %shard_map.240.moved_ref, bf16[8,192]{1,0:T(8,128)(2,1)S(1)} %get-tuple-element.74.mine_ref, bf16[192,512]{1,0:T(8,128)(2,1)S(1)} %bitcast.14, f32[2,4,128]{2,1,0:T(4,128)S(1)} %copy-done.6, ...), custom_call_target="tpu_custom_call" | custom-call | tf_op jit(solution)/shard_map/pallas_call | solution.py:699
  36.2 1.1 %shard_map.251 = (bf16[2400,128]{1,0:T(8,128)(2,1)}, f32[8,128]{1,0:T(8,128)}, f32[480,128]{1,0:T(8,128)}) custom-call(bf16[2400,128]{1,0:T(8,128)(2,1)S(1)} %shard_map.246.spectra_ref, f32[8,128]{1,0:T(8,128)S(1)} %get-tuple-element.87.eta_ref, f32[480,128]{1,0:T(8,128)S(1)} %get-tuple-element.88.part_ref, f32[60,128]{1,0:T(8,128)S(1)} %get-tuple-element.89.north_ref, ...), custom_call_target="tpu_custom_call" | custom-call | tf_op jit(solution)/shard_map/pallas_call | solution.py:712
  37.6 0.8 %shard_map.252 = f32[3,4,128]{2,1,0:T(4,128)} custom-call(bf16[8,64]{1,0:T(8,128)(2,1)S(1)} %collective-permute-done.14.got_even, bf16[8,64]{1,0:T(8,128)(2,1)S(1)} %collective-permute-done.15.got_odd, bf16[8,64]{1,0:T(8,128)(2,1)S(1)} %get-tuple-element.97.own, bf16[192,512]{1,0:T(8,128)(2,1)S(1)} %bitcast.15), custom_call_target="tpu_custom_call" | custom-call | tf_op jit(solution)/shard_map/pallas_call | solution.py:719
  (52 shorter events, 1.3 us)
Async XLA Ops:
  0.6 7.0 %copy-start.7 = (s32[4,128]{1,0:T(4,128)S(1)}, s32[4,128]{1,0:T(4,128)}, u32[]{:S(2)}) copy-start(s32[4,128]{1,0:T(4,128)} %wet_ref.12) | copy-start | bytes 6148
  0.6 7.0 %copy-start = (bf16[600,600]{1,0:T(8,128)(2,1)S(1)}, bf16[600,600]{1,0:T(8,128)(2,1)}, u32[]{:S(2)}) copy-start(bf16[600,600]{1,0:T(8,128)(2,1)} %inter_ref.3) | copy-start | bytes 2160004
  0.7 6.8 %copy-start.14 = (f32[25]{0:T(128)S(1)}, f32[25]{0:T(128)}, u32[]{:S(2)}) copy-start(f32[25]{0:T(128)} %gain_hbm.1) | copy-start | bytes 304
  0.7 6.8 %copy-start.13 = (f32[25]{0:T(128)S(1)}, f32[25]{0:T(128)}, u32[]{:S(2)}) copy-start(f32[25]{0:T(128)} %rate_hbm.1) | copy-start | bytes 304
  0.7 6.8 %copy-start.5 = (f32[30,30]{1,0:T(8,128)S(1)}, f32[30,30]{1,0:T(8,128)}, u32[]{:S(2)}) copy-start(f32[30,30]{1,0:T(8,128)} %mix_ref.5) | copy-start | bytes 10804
  0.7 6.8 %copy-start.17 = (f32[30]{0:T(128)S(1)}, f32[30]{0:T(128)}, u32[]{:S(2)}) copy-start(f32[30]{0:T(128)} %param.37) | copy-start | bytes 364
  0.7 6.8 %copy-start.15 = (f32[3,30]{1,0:T(4,128)S(1)}, f32[3,30]{1,0:T(4,128)}, u32[]{:S(2)}) copy-start(f32[3,30]{1,0:T(4,128)} %prof_ref.1) | copy-start | bytes 1084
  0.7 6.8 %copy-start.16 = (f32[30]{0:T(128)S(1)}, f32[30]{0:T(128)}, u32[]{:S(2)}) copy-start(f32[30]{0:T(128)} %param.35) | copy-start | bytes 364
  2.9 5.7 %copy-start.1 = (bf16[1,1,3,64,512]{4,3,2,1,0:T(8,128)(2,1)S(1)}, bf16[1,1,3,64,512]{4,3,2,1,0:T(8,128)(2,1)}, u32[]{:S(2)}) copy-start(bf16[1,1,3,64,512]{4,3,2,1,0:T(8,128)(2,1)} %param.43) | copy-start | bytes 589828
  2.9 5.7 %copy-start.6 = (f32[2,4,128]{2,1,0:T(4,128)S(1)}, f32[2,4,128]{2,1,0:T(4,128)}, u32[]{:S(2)}) copy-start(f32[2,4,128]{2,1,0:T(4,128)} %wind_ref.3) | copy-start | bytes 12292
  2.9 5.7 %copy-start.10 = (s32[1,1,3,64]{3,1,2,0:T(1,128)S(1)}, s32[1,1,3,64]{3,1,2,0:T(1,128)}, u32[]{:S(2)}) copy-start(s32[1,1,3,64]{3,1,2,0:T(1,128)} %param.40) | copy-start | bytes 2308
  2.9 6.3 %collective-permute-start = (bf16[8,64]{1,0:T(8,128)(2,1)S(1)}, bf16[8,64]{1,0:T(8,128)(2,1)S(1)}, u32[]{:S(2)}, u32[]{:S(2)}) collective-permute-start(bf16[8,64]{1,0:T(8,128)(2,1)S(1)} %get-tuple-element.54), channel_id=1, source_target_pairs={{0,4},{1,5},{2,6},{3,7},{4,0},{5,1},{6,2},{7,3},{8,12},{9,13},{10,... | collective-permute-start | bytes 3080 | tf_op jit(solution)/shard_map/ppermute | solution.py:623
  6.0 3.6 %collective-permute-start.1 = (bf16[8,64]{1,0:T(8,128)(2,1)S(1)}, bf16[8,64]{1,0:T(8,128)(2,1)S(1)}, u32[]{:S(2)}, u32[]{:S(2)}) collective-permute-start(bf16[8,64]{1,0:T(8,128)(2,1)S(1)} %get-tuple-element.55), channel_id=1, source_target_pairs={{0,2},{1,3},{2,0},{3,1},{4,8},{5,9},{6,10},{7,11},{8,4},{9,5},{10,... | collective-permute-start | bytes 3080 | tf_op jit(solution)/shard_map/ppermute | solution.py:623
  7.7 1.9 %copy-start.2 = (bf16[1,1,3,64,1024]{4,3,2,1,0:T(8,128)(2,1)S(1)}, bf16[1,1,3,64,1024]{4,3,2,1,0:T(8,128)(2,1)}, u32[]{:S(2)}) copy-start(bf16[1,1,3,64,1024]{4,3,2,1,0:T(8,128)(2,1)} %param.41) | copy-start | bytes 1179652
  7.7 1.9 %copy-start.3 = (s32[8,128]{1,0:T(8,128)S(1)}, s32[8,128]{1,0:T(8,128)}, u32[]{:S(2)}) copy-start(s32[8,128]{1,0:T(8,128)} %sea_ref.1) | copy-start | bytes 12292
  8.5 4.9 %copy-start.12 = (f32[8,128]{1,0:T(8,128)S(1)}, f32[8,128]{1,0:T(8,128)}, u32[]{:S(2)}) copy-start(f32[8,128]{1,0:T(8,128)} %eta_ref.1) | copy-start | bytes 12292
  8.5 7.7 %copy-start.9 = (s32[128]{0:T(128)S(1)}, s32[128]{0:T(128)}, u32[]{:S(2)}) copy-start(s32[128]{0:T(128)} %param.39) | copy-start | bytes 1540
  8.6 7.7 %copy-start.11 = (s32[1,1,3,64]{3,1,2,0:T(1,128)S(1)}, s32[1,1,3,64]{3,1,2,0:T(1,128)}, u32[]{:S(2)}) copy-start(s32[1,1,3,64]{3,1,2,0:T(1,128)} %param.42) | copy-start | bytes 2308
  10.0 6.2 %collective-permute-start.2 = (bf16[272,128]{1,0:T(8,128)(2,1)S(1)}, bf16[272,128]{1,0:T(8,128)(2,1)S(1)}, u32[]{:S(2)}, u32[]{:S(2)}) collective-permute-start(bf16[272,128]{1,0:T(8,128)(2,1)S(1)} %get-tuple-element.60), channel_id=1, source_target_pairs={{0,4},{1,5},{2,6},{3,7},{4,0},{5,1},{6,2},{7,3},{8,12},{9,13},{10,... | collective-permute-start | bytes 208904 | tf_op jit(solution)/shard_map/ppermute | solution.py:623
  11.3 4.9 %collective-permute-start.3 = (bf16[272,128]{1,0:T(8,128)(2,1)S(1)}, bf16[272,128]{1,0:T(8,128)(2,1)S(1)}, u32[]{:S(2)}, u32[]{:S(2)}) collective-permute-start(bf16[272,128]{1,0:T(8,128)(2,1)S(1)} %get-tuple-element.61), channel_id=1, source_target_pairs={{0,2},{1,3},{2,0},{3,1},{4,8},{5,9},{6,10},{7,11},{8,4},{9,5},{10,... | collective-permute-start | bytes 208904 | tf_op jit(solution)/shard_map/ppermute | solution.py:623
  13.0 3.2 %collective-permute-start.5 = (bf16[80,128]{1,0:T(8,128)(2,1)S(1)}, bf16[80,128]{1,0:T(8,128)(2,1)S(1)}, u32[]{:S(2)}, u32[]{:S(2)}) collective-permute-start(bf16[80,128]{1,0:T(8,128)(2,1)S(1)} %get-tuple-element.63), channel_id=1, source_target_pairs={{0,3},{1,2},{2,1},{3,0},{4,7},{5,6},{6,5},{7,4},{8,11},{9,10},{10,... | collective-permute-start | bytes 61448 | tf_op jit(solution)/shard_map/ppermute | solution.py:623
  13.0 3.2 %collective-permute-start.4 = (bf16[80,128]{1,0:T(8,128)(2,1)S(1)}, bf16[80,128]{1,0:T(8,128)(2,1)S(1)}, u32[]{:S(2)}, u32[]{:S(2)}) collective-permute-start(bf16[80,128]{1,0:T(8,128)(2,1)S(1)} %get-tuple-element.62.sent_col), channel_id=1, source_target_pairs={{0,1},{1,0},{2,3},{3,2},{4,5},{5,4},{6,7},{7,6},{8,9},{9,8},{10,11... | collective-permute-start | bytes 61448 | tf_op jit(solution)/shard_map/ppermute | solution.py:623
  16.5 7.2 %collective-permute-start.6 = (bf16[8,128]{1,0:T(8,128)(2,1)S(1)}, bf16[8,128]{1,0:T(8,128)(2,1)S(1)}, u32[]{:S(2)}, u32[]{:S(2)}) collective-permute-start(bf16[8,128]{1,0:T(8,128)(2,1)S(1)} %get-tuple-element.68), channel_id=1, source_target_pairs={{0,4},{1,5},{2,6},{3,7},{4,0},{5,1},{6,2},{7,3},{8,12},{9,13},{10,... | collective-permute-start | bytes 6152 | tf_op jit(solution)/shard_map/ppermute | solution.py:623
  18.2 5.4 %collective-permute-start.7 = (bf16[8,128]{1,0:T(8,128)(2,1)S(1)}, bf16[8,128]{1,0:T(8,128)(2,1)S(1)}, u32[]{:S(2)}, u32[]{:S(2)}) collective-permute-start(bf16[8,128]{1,0:T(8,128)(2,1)S(1)} %get-tuple-element.69), channel_id=1, source_target_pairs={{0,2},{1,3},{2,0},{3,1},{4,8},{5,9},{6,10},{7,11},{8,4},{9,5},{10,... | collective-permute-start | bytes 6152 | tf_op jit(solution)/shard_map/ppermute | solution.py:623
  19.5 3.6 %collective-permute-start.8 = (bf16[8,64]{1,0:T(8,128)(2,1)S(1)}, bf16[8,64]{1,0:T(8,128)(2,1)S(1)}, u32[]{:S(2)}, u32[]{:S(2)}) collective-permute-start(bf16[8,64]{1,0:T(8,128)(2,1)S(1)} %get-tuple-element.70), channel_id=1, source_target_pairs={{0,8},{1,9},{2,10},{3,11},{4,12},{5,13},{6,14},{7,15},{8,0},{9,1},... | collective-permute-start | bytes 3080 | tf_op jit(solution)/shard_map/ppermute | solution.py:623
  20.1 3.6 %collective-permute-start.9 = (bf16[8,64]{1,0:T(8,128)(2,1)S(1)}, bf16[8,64]{1,0:T(8,128)(2,1)S(1)}, u32[]{:S(2)}, u32[]{:S(2)}) collective-permute-start(bf16[8,64]{1,0:T(8,128)(2,1)S(1)} %get-tuple-element.71), channel_id=1, source_target_pairs={{0,2},{1,3},{2,0},{3,1},{4,6},{5,7},{6,4},{7,5},{8,16},{9,17},{10,... | collective-permute-start | bytes 3080 | tf_op jit(solution)/shard_map/ppermute | solution.py:623
  24.3 8.5 %collective-permute-start.13 = (bf16[80,128]{1,0:T(8,128)(2,1)S(1)}, bf16[80,128]{1,0:T(8,128)(2,1)S(1)}, u32[]{:S(2)}, u32[]{:S(2)}) collective-permute-start(bf16[80,128]{1,0:T(8,128)(2,1)S(1)} %get-tuple-element.83), channel_id=1, source_target_pairs={{0,3},{1,2},{2,1},{3,0},{4,7},{5,6},{6,5},{7,4},{8,11},{9,10},{10,... | collective-permute-start | bytes 61448 | tf_op jit(solution)/shard_map/ppermute | solution.py:623
  24.4 8.4 %collective-permute-start.12 = (bf16[80,128]{1,0:T(8,128)(2,1)S(1)}, bf16[80,128]{1,0:T(8,128)(2,1)S(1)}, u32[]{:S(2)}, u32[]{:S(2)}) collective-permute-start(bf16[80,128]{1,0:T(8,128)(2,1)S(1)} %get-tuple-element.82.sent_col), channel_id=1, source_target_pairs={{0,1},{1,0},{2,3},{3,2},{4,5},{5,4},{6,7},{7,6},{8,9},{9,8},{10,11... | collective-permute-start | bytes 61448 | tf_op jit(solution)/shard_map/ppermute | solution.py:623
  26.0 4.8 %collective-permute-start.10 = (bf16[60,128]{1,0:T(8,128)(2,1)S(1)}, bf16[60,128]{1,0:T(8,128)(2,1)S(1)}, u32[]{:S(2)}, u32[]{:S(2)}) collective-permute-start(bf16[60,128]{1,0:T(8,128)(2,1)S(1)} %get-tuple-element.80), channel_id=1, source_target_pairs={{0,4},{1,5},{2,6},{3,7},{4,0},{5,1},{6,2},{7,3},{8,12},{9,13},{10,... | collective-permute-start | bytes 46088 | tf_op jit(solution)/shard_map/ppermute | solution.py:623
  29.1 3.7 %collective-permute-start.11 = (bf16[60,128]{1,0:T(8,128)(2,1)S(1)}, bf16[60,128]{1,0:T(8,128)(2,1)S(1)}, u32[]{:S(2)}, u32[]{:S(2)}) collective-permute-start(bf16[60,128]{1,0:T(8,128)(2,1)S(1)} %get-tuple-element.81), channel_id=1, source_target_pairs={{0,2},{1,3},{2,0},{3,1},{4,8},{5,9},{6,10},{7,11},{8,4},{9,5},{10,... | collective-permute-start | bytes 46088 | tf_op jit(solution)/shard_map/ppermute | solution.py:623
  33.1 4.2 %collective-permute-start.14 = (bf16[8,64]{1,0:T(8,128)(2,1)S(1)}, bf16[8,64]{1,0:T(8,128)(2,1)S(1)}, u32[]{:S(2)}, u32[]{:S(2)}) collective-permute-start(bf16[8,64]{1,0:T(8,128)(2,1)S(1)} %get-tuple-element.95), channel_id=1, source_target_pairs={{0,4},{1,5},{2,6},{3,7},{4,0},{5,1},{6,2},{7,3},{8,12},{9,13},{10,... | collective-permute-start | bytes 3080 | tf_op jit(solution)/shard_map/ppermute | solution.py:623
  34.1 3.6 %collective-permute-start.15 = (bf16[8,64]{1,0:T(8,128)(2,1)S(1)}, bf16[8,64]{1,0:T(8,128)(2,1)S(1)}, u32[]{:S(2)}, u32[]{:S(2)}) collective-permute-start(bf16[8,64]{1,0:T(8,128)(2,1)S(1)} %get-tuple-element.96), channel_id=1, source_target_pairs={{0,2},{1,3},{2,0},{3,1},{4,8},{5,9},{6,10},{7,11},{8,4},{9,5},{10,... | collective-permute-start | bytes 3080 | tf_op jit(solution)/shard_map/ppermute | solution.py:623
  (2 other events, 3.8 us)

commit v6 on v5

--- a/solution.py
+++ b/solution.py
@@ -46,6 +46,7 @@
     return lax.rem(index, 2) == 0
 
 
+PACK = 16
 GROUP = 8
 
 
@@ -134,14 +135,18 @@
 
 
 def pick_far(fields, send, outs):
-    to_even, to_odd, own, far_even, far_odd = outs
+    to_even, to_odd, own, far_even, far_odd, pack_south, pack_north = outs
     slot = send.shape[2]
     slots = picked(fields, send)
     row = lax.axis_index("row")
     even, first = is_even(row), in_first_half(row)
     south, here, north = slots[:, :slot], slots[:, slot : 2 * slot], slots[:, 2 * slot :]
-    to_even[...] = jnp.concatenate([jnp.where(even, north, south), here], axis=1).astype(bf16)
-    to_odd[...] = jnp.concatenate([jnp.where(even, south, north), here], axis=1).astype(bf16)
+    rows = slots.shape[0]
+    to_even[:rows, :] = jnp.concatenate([jnp.where(even, north, south), here], axis=1).astype(bf16)
+    to_odd[:rows, :] = jnp.concatenate([jnp.where(even, south, north), here], axis=1).astype(bf16)
+    a, b = pack_south[...].astype(f32), pack_north[...].astype(f32)
+    to_even[PACK:, :] = jnp.where(even, b, a).astype(bf16)
+    to_odd[PACK:, :] = jnp.where(even, a, b).astype(bf16)
     own[...] = slots.astype(bf16)
     far_even[...] = jnp.where(first, north, south).astype(bf16)
     far_odd[...] = jnp.where(first, south, north).astype(bf16)
@@ -241,14 +246,15 @@
 
 
 def k_wave_next(
-    n_row, pad,
-    got_even, got_odd, far_even, far_odd, own_ref, row_even, row_odd, pack_ref,
+    n_row,
+    got_even, got_odd, far_even, far_odd, own_ref, pack_ref,
     slots_ref, mine_ref,
 ):
     slot = far_even.shape[1]
     row = lax.axis_index("row")
     even, first = is_even(row), in_first_half(row)
-    a, b = got_even[...].astype(f32), got_odd[...].astype(f32)
+    rows = own_ref.shape[0]
+    a, b = got_even[:rows, :].astype(f32), got_odd[:rows, :].astype(f32)
     north = jnp.where(row == n_row - 1, 0.0, jnp.where(even, a, b))
     south = jnp.where(row == 0, 0.0, jnp.where(even, b, a))
     a, b = far_even[...].astype(f32), far_odd[...].astype(f32)
@@ -263,7 +269,7 @@
         mine,
         jnp.concatenate([down, south[:, slot:], far_south], axis=1).astype(bf16),
     ]
-    a, b = row_even[pad:, :].astype(f32), row_odd[pad:, :].astype(f32)
+    a, b = got_even[PACK:, :].astype(f32), got_odd[PACK:, :].astype(f32)
     packs = [jnp.where(even, a, b), pack_ref[...].astype(f32), jnp.where(even, b, a)]
     recv = 3 * slot
     current = jnp.concatenate(
@@ -369,7 +375,7 @@
     *refs,
 ):
     if first:
-        got_even, got_odd, own, pack_south, pack_north, *refs = refs
+        got_even, got_odd, own, *refs = refs
         slots = gather_slots(got_even, got_odd, own, n_row)
     else:
         slot_ref, *refs = refs
@@ -404,12 +410,8 @@
     bottom = forced_ref[pl.ds(0, planes, stride=oy), :]
     top = forced_ref[pl.ds(oy - 1, planes, stride=oy), :]
     even = is_even(lax.axis_index("row"))
-    row_even[:planes, :] = jnp.where(even, top, bottom).astype(bf16)
-    row_odd[:planes, :] = jnp.where(even, bottom, top).astype(bf16)
-    if first:
-        a, b = pack_south[...].astype(f32), pack_north[...].astype(f32)
-        row_even[pad:, :] = jnp.where(even, b, a).astype(bf16)
-        row_odd[pad:, :] = jnp.where(even, a, b).astype(bf16)
+    row_even[...] = jnp.where(even, top, bottom).astype(bf16)
+    row_odd[...] = jnp.where(even, bottom, top).astype(bf16)
     even = is_even(lax.axis_index("col"))
     col_even[:planes, :] = top.astype(bf16)
     col_odd[:planes, :] = top.astype(bf16)
@@ -448,11 +450,12 @@
 
 
 def k_back(
-    n_row, n_col, pad, whole, choose,
+    n_row, n_col, pad, whole, choose, n_extra,
     got_row_even, got_row_odd, got_col_even, got_col_odd, sent_col, line_ref, fold_ref, sums_ref, wet_ref, side_ref, lane_ref, send_ref,
-    eta_out, north_ref, south_ref, ends_ref, *outs,
+    *refs,
 ):
-    *outs, bs = outs
+    extra = refs[:n_extra]
+    eta_out, north_ref, south_ref, ends_ref, *outs, bs = refs[n_extra:]
     oy, ox = wet_ref.shape
     planes = north_ref.shape[0]
     row, col = lax.axis_index("row"), lax.axis_index("col")
@@ -511,7 +514,7 @@
     bs[2 * oy : 3 * oy, :] = eta
     bs[3 * oy :, :] = jnp.zeros((5 * oy, ox), f32)
     back = jnp.concatenate([bs[pl.ds(y, 8, stride=oy), :] for y in range(oy)], axis=1)
-    choose(back, send_ref, outs)
+    choose(back, send_ref, (*outs, *extra))
 
 
 def k_mix(lev, part_ref, north_ref, south_ref, ends_ref, wet_ref, mix_ref, vel_ref, smooth, wide):
@@ -628,12 +631,11 @@
     full = (planes * oy, ox)
     mixer = [pltpu.VMEM(full, f32), pltpu.VMEM((96, 2 * oy * ox), bf16)]
 
-    def edges(step, lists, send_of):
+    def edges(step, lists, send_of, extra=()):
         first = step == 0
-        tall = pad + half if first else planes
         forced, row_even, row_odd, col_even, col_odd = call(
             functools.partial(k_force, n_row, lev, pad, first),
-            [(full, f32)] + [((tall, ox), bf16)] * 2 + [((pad + 16, ox), bf16)] * 2,
+            [(full, f32)] + [((planes, ox), bf16)] * 2 + [((pad + 16, ox), bf16)] * 2,
             [VMEM] * (len(lists) + 5),
             [pltpu.VMEM((8 * oy, ox), f32)],
         )(*lists, ocean_w, velocity, ocean_wet, coriolis, coef)
@@ -648,15 +650,15 @@
             top_line = fold
         choose, slots = send_of
         eta_next, north, south, ends, *sent = call(
-            functools.partial(k_back, n_row, n_col, pad, whole, choose),
+            functools.partial(k_back, n_row, n_col, pad, whole, choose, len(extra)),
             [((oy, ox), f32)] + [((planes, ox), f32)] * 2 + [((2 * oy, ox), f32)] + slots,
-            [VMEM] * 12,
+            [VMEM] * (12 + len(extra)),
             [pltpu.VMEM((8 * oy, ox), f32)],
         )(
             got_row_even, got_row_odd, got_col_even, got_col_odd, col_even, top_line, fold, sums, ocean_wet,
-            side, lane_rows, osend,
+            side, lane_rows, osend, *extra,
         )
-        return (part, north, south, ends), eta_next, sent, (got_row_even, got_row_odd)
+        return (part, north, south, ends), eta_next, sent
 
     inputs = (
         stress_map, stokes_map, input_rate, eta_gain, wind, wave_current, wave_wet, wsend,
@@ -682,9 +684,9 @@
     pack_south, pack_own, pack_north = call(
         k_pack, [((half, 2 * slot), bf16)] * 3, [VMEM] * 6
     )(energy, weights, wave_w, wind, wave_wet, wsend)
-    far_slots = [((8, 2 * slot), bf16)] * 2 + [((8, 3 * slot), bf16)] + [((8, slot), bf16)] * 2
-    smooth, eta, sent, got_rows = edges(
-        0, (got_even, got_odd, own, pack_south, pack_north), (pick_far, far_slots)
+    far_slots = [((PACK + half, 2 * slot), bf16)] * 2 + [((8, 3 * slot), bf16)] + [((8, slot), bf16)] * 2
+    smooth, eta, sent = edges(
+        0, (got_even, got_odd, own), (pick_far, far_slots), (pack_south, pack_north)
     )
     to_even, to_odd, own, far_even, far_odd = sent
     got_odd, got_even = trade("row_odd", to_odd), trade("row_even", to_even)
@@ -694,8 +696,8 @@
     )
     (velocity,) = call(functools.partial(k_mix, lev), [(full, f32)], [VMEM] * 6, mixer)(*smooth, ocean_wet, mix_inverse)
     fields, mine = call(
-        functools.partial(k_wave_next, n_row, pad), [((8, 3 * slot), bf16)] * 2, [VMEM] * 8
-    )(got_even, got_odd, got_far_even, got_far_odd, own, *got_rows, pack_own)
+        functools.partial(k_wave_next, n_row), [((8, 3 * slot), bf16)] * 2, [VMEM] * 6
+    )(got_even, got_odd, got_far_even, got_far_odd, own, pack_own)
     (spectra_new,) = call(
         functools.partial(k_update_last, nfreq),
         [((spec * rows, lanes), bf16)],
@@ -706,7 +708,7 @@
             pltpu.VMEM((spec * rows, lanes), f32),
         ],
     )(energy, moved, mine, wave_w, wind, wave_wet, coef)
-    smooth, eta, sent, _ = edges(1, (fields,), (pick, slots_out))
+    smooth, eta, sent = edges(1, (fields,), (pick, slots_out))
     to_even, to_odd, own = sent
     got_odd, got_even = trade("row_odd", to_odd), trade("row_even", to_even)
     spectra_out, eta, velocity = call(

time: 38.6 us -> 39.4 us (1.021)
  waiting for transfers between devices: 7.84 us -> 8.47 us
    ppermute x16, waiting for transfers between devices: 7.84 us -> 8.47 us  [trade(): return lax.ppermute(array, axis, pairs[label])]
  transfers between devices with their start and end apart: 16 -> 16, of which waited for: 7 -> 6; matrix products, arithmetic and copies ran while one was open for 0% -> 0% of each run, Pallas kernels for 13% -> 13%
where the time goes in v6:
time: 39.4 us; the launch traced here: 39.2 us
  starting transfers between devices  19.9 us (51%)
  Pallas kernels  9.76 us (25%)
  waiting for transfers between devices  8.47 us (21%)
  between operations  0.99 us (3%)
    ppermute x16, starting transfers between devices, trade(): return lax.ppermute(array, axis, pairs[label])  19.9 us
    ppermute x16, waiting for transfers between devices, trade(): return lax.ppermute(array, axis, pairs[label])  8.47 us
    pallas_call x1, Pallas kernels, shards(): call(functools.partial(k_wave_first, nfreq), slots_out + [((spec, cells),...  2.19 us
    pallas_call x1, Pallas kernels, shards(): call(functools.partial(k_last, lev), [((spec * rows, lanes), bf16), ((oy,...  1.15 us
    pallas_call x1, Pallas kernels, shards(): call(functools.partial(k_update_last, nfreq), [((spec * rows, lanes), bf1...  0.93 us
  transfers between devices with their start and end apart: 16, of which 6 were waited for; matrix products, arithmetic and copies ran while one was open for 0% of the time, Pallas kernels for 13%

profile of v6, /device:TPU:0, one launch (start us, length us, event | category | flops | bytes accessed | tf_op | source)
XLA Modules:
  0.0 39.2 jit_solution(4922845071881420769)
XLA Ops:
  0.8 2.2 %shard_map.237 = (bf16[8,64]{1,0:T(8,128)(2,1)S(1)}, bf16[8,64]{1,0:T(8,128)(2,1)S(1)}, bf16[8,64]{1,0:T(8,128)(2,1)S(1)}, bf16[600,512]{1,0:T(8,128)(2,1)S(1)},...) custom-call(f32[2,600]{1,0:T(2,128)} %smap_hbm.1, f32[6,600]{1,0:T(8,128)} %kmap_hbm.1, f32[25]{0:T(128)} %rate_hbm.1, ...), custom_call_target="tpu_custom_call" | custom-call | tf_op jit(solution)/shard_map/pallas_call | solution.py:668
  3.0 3.1 %collective-permute-start = (bf16[8,64]{1,0:T(8,128)(2,1)S(1)}, bf16[8,64]{1,0:T(8,128)(2,1)S(1)}, u32[]{:S(2)}, u32[]{:S(2)}) collective-permute-start(bf16[8,64]{1,0:T(8,128)(2,1)S(1)} %get-tuple-element.54), channel_id=1, source_target_pairs={{0,4},{1,5},{2,6},{3,7},{4,0},{5,1},{6,2},{7,3},{8,12},{9,13},{10,... | collective-permute-start | bytes 3080 | tf_op jit(solution)/shard_map/ppermute | solution.py:626
  6.0 1.5 %collective-permute-start.1 = (bf16[8,64]{1,0:T(8,128)(2,1)S(1)}, bf16[8,64]{1,0:T(8,128)(2,1)S(1)}, u32[]{:S(2)}, u32[]{:S(2)}) collective-permute-start(bf16[8,64]{1,0:T(8,128)(2,1)S(1)} %get-tuple-element.55), channel_id=1, source_target_pairs={{0,2},{1,3},{2,0},{3,1},{4,8},{5,9},{6,10},{7,11},{8,4},{9,5},{10,... | collective-permute-start | bytes 3080 | tf_op jit(solution)/shard_map/ppermute | solution.py:626
  7.7 1.9 %collective-permute-done.1.refs_1_ = bf16[8,64]{1,0:T(8,128)(2,1)S(1)} collective-permute-done((bf16[8,64]{1,0:T(8,128)(2,1)S(1)}, bf16[8,64]{1,0:T(8,128)(2,1)S(1)}, u32[]{:S(2)}, u32[]{:S(2)}) %collective-permute-start.1) | collective-permute-done | bytes 1056 | tf_op jit(solution)/shard_map/ppermute | solution.py:626
  9.6 0.4 shard_map.241
  10.1 1.6 %collective-permute-start.4 = (bf16[80,128]{1,0:T(8,128)(2,1)S(1)}, bf16[80,128]{1,0:T(8,128)(2,1)S(1)}, u32[]{:S(2)}, u32[]{:S(2)}) collective-permute-start(bf16[80,128]{1,0:T(8,128)(2,1)S(1)} %get-tuple-element.59.sent_col), channel_id=1, source_target_pairs={{0,1},{1,0},{2,3},{3,2},{4,5},{5,4},{6,7},{7,6},{8,9},{9,8},{10,11... | collective-permute-start | bytes 61448 | tf_op jit(solution)/shard_map/ppermute | solution.py:626
  11.7 1.4 %collective-permute-start.2 = (bf16[60,128]{1,0:T(8,128)(2,1)S(1)}, bf16[60,128]{1,0:T(8,128)(2,1)S(1)}, u32[]{:S(2)}, u32[]{:S(2)}) collective-permute-start(bf16[60,128]{1,0:T(8,128)(2,1)S(1)} %get-tuple-element.57), channel_id=1, source_target_pairs={{0,4},{1,5},{2,6},{3,7},{4,0},{5,1},{6,2},{7,3},{8,12},{9,13},{10,... | collective-permute-start | bytes 46088 | tf_op jit(solution)/shard_map/ppermute | solution.py:626
  13.3 0.8 %shard_map.239.old_ref.energy_ref = bf16[600,512]{1,0:T(8,128)(2,1)S(1)} custom-call(bf16[600,512]{1,0:T(8,128)(2,1)S(1)} %get-tuple-element.51.old_ref, bf16[600,600]{1,0:T(8,128)(2,1)S(1)} %copy-done, f32[32,512]{1,0:T(8,128)S(1)} %get-tuple-element.52.soft_ref, s32[4,128]{1,0:T(4,128)S(1)} %copy-done.7, ...), custom_call_target="tpu_custom_call" | custom-call | tf_op jit(solution)/shard_map/pallas_call | solution.py:681
  14.1 0.6 %shard_map.243 = (bf16[208,128]{1,0:T(8,128)(2,1)S(1)}, bf16[208,128]{1,0:T(8,128)(2,1)S(1)}, bf16[208,128]{1,0:T(8,128)(2,1)S(1)}) custom-call(bf16[600,512]{1,0:T(8,128)(2,1)S(1)} %shard_map.239.old_ref.energy_ref, bf16[224,600]{1,0:T(8,128)(2,1)S(1)} %get-tuple-element.65.weight_ref, bf16[192,512]{1,0:T(8,128)(2,1)S(1)} %bitcast.13, ...), custom_call_target="tpu_custom_call" | custom-call | tf_op jit(solution)/shard_map/pallas_call | solution.py:684
  15.0 0.5 %collective-permute-done.2.got_row_even = bf16[60,128]{1,0:T(8,128)(2,1)S(1)} collective-permute-done((bf16[60,128]{1,0:T(8,128)(2,1)S(1)}, bf16[60,128]{1,0:T(8,128)(2,1)S(1)}, u32[]{:S(2)}, u32[]{:S(2)}) %collective-permute-start.2) | collective-permute-done | bytes 15392 | tf_op jit(solution)/shard_map/ppermute | solution.py:626
  15.5 1.4 %collective-permute-done.3.got_row_odd = bf16[60,128]{1,0:T(8,128)(2,1)S(1)} collective-permute-done((bf16[60,128]{1,0:T(8,128)(2,1)S(1)}, bf16[60,128]{1,0:T(8,128)(2,1)S(1)}, u32[]{:S(2)}, u32[]{:S(2)}) %collective-permute-start.3) | collective-permute-done | bytes 15392 | tf_op jit(solution)/shard_map/ppermute | solution.py:626
  16.9 0.3 shard_map.244
  17.2 1.5 %collective-permute-start.6 = (bf16[224,128]{1,0:T(8,128)(2,1)S(1)}, bf16[224,128]{1,0:T(8,128)(2,1)S(1)}, u32[]{:S(2)}, u32[]{:S(2)}) collective-permute-start(bf16[224,128]{1,0:T(8,128)(2,1)S(1)} %get-tuple-element.68), channel_id=1, source_target_pairs={{0,4},{1,5},{2,6},{3,7},{4,0},{5,1},{6,2},{7,3},{8,12},{9,13},{10,... | collective-permute-start | bytes 172040 | tf_op jit(solution)/shard_map/ppermute | solution.py:626
  18.7 0.5 %collective-permute-start.7 = (bf16[224,128]{1,0:T(8,128)(2,1)S(1)}, bf16[224,128]{1,0:T(8,128)(2,1)S(1)}, u32[]{:S(2)}, u32[]{:S(2)}) collective-permute-start(bf16[224,128]{1,0:T(8,128)(2,1)S(1)} %get-tuple-element.69), channel_id=1, source_target_pairs={{0,2},{1,3},{2,0},{3,1},{4,8},{5,9},{6,10},{7,11},{8,4},{9,5},{10,... | collective-permute-start | bytes 172040 | tf_op jit(solution)/shard_map/ppermute | solution.py:626
  19.2 1.9 %collective-permute-start.8 = (bf16[8,64]{1,0:T(8,128)(2,1)S(1)}, bf16[8,64]{1,0:T(8,128)(2,1)S(1)}, u32[]{:S(2)}, u32[]{:S(2)}) collective-permute-start(bf16[8,64]{1,0:T(8,128)(2,1)S(1)} %get-tuple-element.70), channel_id=1, source_target_pairs={{0,8},{1,9},{2,10},{3,11},{4,12},{5,13},{6,14},{7,15},{8,0},{9,1},... | collective-permute-start | bytes 3080 | tf_op jit(solution)/shard_map/ppermute | solution.py:626
  21.2 0.5 %collective-permute-start.9 = (bf16[8,64]{1,0:T(8,128)(2,1)S(1)}, bf16[8,64]{1,0:T(8,128)(2,1)S(1)}, u32[]{:S(2)}, u32[]{:S(2)}) collective-permute-start(bf16[8,64]{1,0:T(8,128)(2,1)S(1)} %get-tuple-element.71), channel_id=1, source_target_pairs={{0,2},{1,3},{2,0},{3,1},{4,6},{5,7},{6,4},{7,5},{8,16},{9,17},{10,... | collective-permute-start | bytes 3080 | tf_op jit(solution)/shard_map/ppermute | solution.py:626
  21.7 0.4 %shard_map.247.refs_2_ = f32[480,128]{1,0:T(8,128)S(1)} custom-call(f32[480,128]{1,0:T(8,128)S(1)} %get-tuple-element.76.part_ref, f32[60,128]{1,0:T(8,128)S(1)} %get-tuple-element.77.north_ref, f32[60,128]{1,0:T(8,128)S(1)} %get-tuple-element.78.south_ref, f32[16,128]{1,0:T(8,128)S(1)} %get-tuple-element.79.ends_ref, s32[8,128]{1,0:T(8,128)S(1)} %copy-done.3, ...), custom_call_target="tpu_custom_call" | custom-call | tf_op jit(solution)/shard_map/pallas_call | solution.py:697
  22.1 1.2 %collective-permute-done.8.far_even = bf16[8,64]{1,0:T(8,128)(2,1)S(1)} collective-permute-done((bf16[8,64]{1,0:T(8,128)(2,1)S(1)}, bf16[8,64]{1,0:T(8,128)(2,1)S(1)}, u32[]{:S(2)}, u32[]{:S(2)}) %collective-permute-start.8) | collective-permute-done | bytes 1056 | tf_op jit(solution)/shard_map/ppermute | solution.py:626
  23.4 1.4 %collective-permute-done.9.far_odd = bf16[8,64]{1,0:T(8,128)(2,1)S(1)} collective-permute-done((bf16[8,64]{1,0:T(8,128)(2,1)S(1)}, bf16[8,64]{1,0:T(8,128)(2,1)S(1)}, u32[]{:S(2)}, u32[]{:S(2)}) %collective-permute-start.9) | collective-permute-done | bytes 1056 | tf_op jit(solution)/shard_map/ppermute | solution.py:626
  24.8 0.3 shard_map.245
  25.1 0.3 shard_map.248
  25.5 0.6 %collective-permute-start.12 = (bf16[80,128]{1,0:T(8,128)(2,1)S(1)}, bf16[80,128]{1,0:T(8,128)(2,1)S(1)}, u32[]{:S(2)}, u32[]{:S(2)}) collective-permute-start(bf16[80,128]{1,0:T(8,128)(2,1)S(1)} %get-tuple-element.82.sent_col), channel_id=1, source_target_pairs={{0,1},{1,0},{2,3},{3,2},{4,5},{5,4},{6,7},{7,6},{8,9},{9,8},{10,11... | collective-permute-start | bytes 61448 | tf_op jit(solution)/shard_map/ppermute | solution.py:626
  26.2 3.0 %collective-permute-start.10 = (bf16[60,128]{1,0:T(8,128)(2,1)S(1)}, bf16[60,128]{1,0:T(8,128)(2,1)S(1)}, u32[]{:S(2)}, u32[]{:S(2)}) collective-permute-start(bf16[60,128]{1,0:T(8,128)(2,1)S(1)} %get-tuple-element.80), channel_id=1, source_target_pairs={{0,4},{1,5},{2,6},{3,7},{4,0},{5,1},{6,2},{7,3},{8,12},{9,13},{10,... | collective-permute-start | bytes 46088 | tf_op jit(solution)/shard_map/ppermute | solution.py:626
  29.2 1.5 %collective-permute-start.11 = (bf16[60,128]{1,0:T(8,128)(2,1)S(1)}, bf16[60,128]{1,0:T(8,128)(2,1)S(1)}, u32[]{:S(2)}, u32[]{:S(2)}) collective-permute-start(bf16[60,128]{1,0:T(8,128)(2,1)S(1)} %get-tuple-element.81), channel_id=1, source_target_pairs={{0,2},{1,3},{2,0},{3,1},{4,8},{5,9},{6,10},{7,11},{8,4},{9,5},{10,... | collective-permute-start | bytes 46088 | tf_op jit(solution)/shard_map/ppermute | solution.py:626
  30.9 2.0 %collective-permute-done.11.got_row_odd = bf16[60,128]{1,0:T(8,128)(2,1)S(1)} collective-permute-done((bf16[60,128]{1,0:T(8,128)(2,1)S(1)}, bf16[60,128]{1,0:T(8,128)(2,1)S(1)}, u32[]{:S(2)}, u32[]{:S(2)}) %collective-permute-start.11) | collective-permute-done | bytes 15392 | tf_op jit(solution)/shard_map/ppermute | solution.py:626
  33.0 0.3 shard_map.250
  33.3 0.9 %collective-permute-start.14 = (bf16[8,64]{1,0:T(8,128)(2,1)S(1)}, bf16[8,64]{1,0:T(8,128)(2,1)S(1)}, u32[]{:S(2)}, u32[]{:S(2)}) collective-permute-start(bf16[8,64]{1,0:T(8,128)(2,1)S(1)} %get-tuple-element.95), channel_id=1, source_target_pairs={{0,4},{1,5},{2,6},{3,7},{4,0},{5,1},{6,2},{7,3},{8,12},{9,13},{10,... | collective-permute-start | bytes 3080 | tf_op jit(solution)/shard_map/ppermute | solution.py:626
  34.2 1.5 %collective-permute-start.15 = (bf16[8,64]{1,0:T(8,128)(2,1)S(1)}, bf16[8,64]{1,0:T(8,128)(2,1)S(1)}, u32[]{:S(2)}, u32[]{:S(2)}) collective-permute-start(bf16[8,64]{1,0:T(8,128)(2,1)S(1)} %get-tuple-element.96), channel_id=1, source_target_pairs={{0,2},{1,3},{2,0},{3,1},{4,8},{5,9},{6,10},{7,11},{8,4},{9,5},{10,... | collective-permute-start | bytes 3080 | tf_op jit(solution)/shard_map/ppermute | solution.py:626
  35.7 0.6 %shard_map.240.moved_ref = f32[600,512]{1,0:T(8,128)S(1)} custom-call(bf16[600,512]{1,0:T(8,128)(2,1)S(1)} %shard_map.239.old_ref.energy_ref, bf16[600,600]{1,0:T(8,128)(2,1)S(1)} %copy-done), custom_call_target="tpu_custom_call" | custom-call | tf_op jit(solution)/shard_map/pallas_call | solution.py:694
  36.3 0.9 %shard_map.246.spectra_ref = bf16[2400,128]{1,0:T(8,128)(2,1)S(1)} custom-call(bf16[600,512]{1,0:T(8,128)(2,1)S(1)} %shard_map.239.old_ref.energy_ref, f32[600,512]{1,0:T(8,128)S(1)} %shard_map.240.moved_ref, bf16[8,192]{1,0:T(8,128)(2,1)S(1)} %get-tuple-element.74.mine_ref, bf16[192,512]{1,0:T(8,128)(2,1)S(1)} %bitcast.14, f32[2,4,128]{2,1,0:T(4,128)S(1)} %copy-done.6, ...), custom_call_target="tpu_custom_call" | custom-call | tf_op jit(solution)/shard_map/pallas_call | solution.py:701
  37.3 1.1 %shard_map.251 = (bf16[2400,128]{1,0:T(8,128)(2,1)}, f32[8,128]{1,0:T(8,128)}, f32[480,128]{1,0:T(8,128)}) custom-call(bf16[2400,128]{1,0:T(8,128)(2,1)S(1)} %shard_map.246.spectra_ref, f32[8,128]{1,0:T(8,128)S(1)} %get-tuple-element.87.eta_ref, f32[480,128]{1,0:T(8,128)S(1)} %get-tuple-element.88.part_ref, f32[60,128]{1,0:T(8,128)S(1)} %get-tuple-element.89.north_ref, ...), custom_call_target="tpu_custom_call" | custom-call | tf_op jit(solution)/shard_map/pallas_call | solution.py:714
  38.5 0.8 %shard_map.252 = f32[3,4,128]{2,1,0:T(4,128)} custom-call(bf16[8,64]{1,0:T(8,128)(2,1)S(1)} %collective-permute-done.14.got_even, bf16[8,64]{1,0:T(8,128)(2,1)S(1)} %collective-permute-done.15.got_odd, bf16[8,64]{1,0:T(8,128)(2,1)S(1)} %get-tuple-element.97.own, bf16[192,512]{1,0:T(8,128)(2,1)S(1)} %bitcast.15), custom_call_target="tpu_custom_call" | custom-call | tf_op jit(solution)/shard_map/pallas_call | solution.py:721
  (52 shorter events, 1.0 us)
Async XLA Ops:
  0.6 12.6 %copy-start.7 = (s32[4,128]{1,0:T(4,128)S(1)}, s32[4,128]{1,0:T(4,128)}, u32[]{:S(2)}) copy-start(s32[4,128]{1,0:T(4,128)} %wet_ref.12) | copy-start | bytes 6148
  0.6 12.6 %copy-start = (bf16[600,600]{1,0:T(8,128)(2,1)S(1)}, bf16[600,600]{1,0:T(8,128)(2,1)}, u32[]{:S(2)}) copy-start(bf16[600,600]{1,0:T(8,128)(2,1)} %inter_ref.3) | copy-start | bytes 2160004
  0.7 6.8 %copy-start.14 = (f32[25]{0:T(128)S(1)}, f32[25]{0:T(128)}, u32[]{:S(2)}) copy-start(f32[25]{0:T(128)} %gain_hbm.1) | copy-start | bytes 304
  0.7 6.8 %copy-start.13 = (f32[25]{0:T(128)S(1)}, f32[25]{0:T(128)}, u32[]{:S(2)}) copy-start(f32[25]{0:T(128)} %rate_hbm.1) | copy-start | bytes 304
  0.7 6.8 %copy-start.5 = (f32[30,30]{1,0:T(8,128)S(1)}, f32[30,30]{1,0:T(8,128)}, u32[]{:S(2)}) copy-start(f32[30,30]{1,0:T(8,128)} %mix_ref.5) | copy-start | bytes 10804
  0.7 6.8 %copy-start.17 = (f32[30]{0:T(128)S(1)}, f32[30]{0:T(128)}, u32[]{:S(2)}) copy-start(f32[30]{0:T(128)} %param.37) | copy-start | bytes 364
  0.7 6.8 %copy-start.15 = (f32[3,30]{1,0:T(4,128)S(1)}, f32[3,30]{1,0:T(4,128)}, u32[]{:S(2)}) copy-start(f32[3,30]{1,0:T(4,128)} %prof_ref.1) | copy-start | bytes 1084
  0.7 6.8 %copy-start.16 = (f32[30]{0:T(128)S(1)}, f32[30]{0:T(128)}, u32[]{:S(2)}) copy-start(f32[30]{0:T(128)} %param.35) | copy-start | bytes 364
  0.7 8.9 %copy-start.3 = (s32[8,128]{1,0:T(8,128)S(1)}, s32[8,128]{1,0:T(8,128)}, u32[]{:S(2)}) copy-start(s32[8,128]{1,0:T(8,128)} %sea_ref.1) | copy-start | bytes 12292
  0.7 8.9 %copy-start.8 = (f32[8,128]{1,0:T(8,128)S(1)}, f32[8,128]{1,0:T(8,128)}, u32[]{:S(2)}) copy-start(f32[8,128]{1,0:T(8,128)} %refs_4_.1) | copy-start | bytes 12292
  0.7 8.9 %copy-start.2 = (bf16[1,1,3,64,1024]{4,3,2,1,0:T(8,128)(2,1)S(1)}, bf16[1,1,3,64,1024]{4,3,2,1,0:T(8,128)(2,1)}, u32[]{:S(2)}) copy-start(bf16[1,1,3,64,1024]{4,3,2,1,0:T(8,128)(2,1)} %param.41) | copy-start | bytes 1179652
  0.7 8.9 %copy-start.4 = (f32[2,30,8,128]{3,2,1,0:T(8,128)S(1)}, f32[2,30,8,128]{3,2,1,0:T(8,128)}, u32[]{:S(2)}) copy-start(f32[2,30,8,128]{3,2,1,0:T(8,128)} %param.31) | copy-start | bytes 737284
  3.0 4.7 %collective-permute-start = (bf16[8,64]{1,0:T(8,128)(2,1)S(1)}, bf16[8,64]{1,0:T(8,128)(2,1)S(1)}, u32[]{:S(2)}, u32[]{:S(2)}) collective-permute-start(bf16[8,64]{1,0:T(8,128)(2,1)S(1)} %get-tuple-element.54), channel_id=1, source_target_pairs={{0,4},{1,5},{2,6},{3,7},{4,0},{5,1},{6,2},{7,3},{8,12},{9,13},{10,... | collective-permute-start | bytes 3080 | tf_op jit(solution)/shard_map/ppermute | solution.py:626
  6.0 3.6 %collective-permute-start.1 = (bf16[8,64]{1,0:T(8,128)(2,1)S(1)}, bf16[8,64]{1,0:T(8,128)(2,1)S(1)}, u32[]{:S(2)}, u32[]{:S(2)}) collective-permute-start(bf16[8,64]{1,0:T(8,128)(2,1)S(1)} %get-tuple-element.55), channel_id=1, source_target_pairs={{0,2},{1,3},{2,0},{3,1},{4,8},{5,9},{6,10},{7,11},{8,4},{9,5},{10,... | collective-permute-start | bytes 3080 | tf_op jit(solution)/shard_map/ppermute | solution.py:626
  10.0 4.1 %copy-start.1 = (bf16[1,1,3,64,512]{4,3,2,1,0:T(8,128)(2,1)S(1)}, bf16[1,1,3,64,512]{4,3,2,1,0:T(8,128)(2,1)}, u32[]{:S(2)}) copy-start(bf16[1,1,3,64,512]{4,3,2,1,0:T(8,128)(2,1)} %param.43) | copy-start | bytes 589828
  10.0 4.1 %copy-start.6 = (f32[2,4,128]{2,1,0:T(4,128)S(1)}, f32[2,4,128]{2,1,0:T(4,128)}, u32[]{:S(2)}) copy-start(f32[2,4,128]{2,1,0:T(4,128)} %wind_ref.3) | copy-start | bytes 12292
  10.0 4.1 %copy-start.10 = (s32[1,1,3,64]{3,1,2,0:T(1,128)S(1)}, s32[1,1,3,64]{3,1,2,0:T(1,128)}, u32[]{:S(2)}) copy-start(s32[1,1,3,64]{3,1,2,0:T(1,128)} %param.40) | copy-start | bytes 2308
  10.0 6.8 %collective-permute-start.5 = (bf16[80,128]{1,0:T(8,128)(2,1)S(1)}, bf16[80,128]{1,0:T(8,128)(2,1)S(1)}, u32[]{:S(2)}, u32[]{:S(2)}) collective-permute-start(bf16[80,128]{1,0:T(8,128)(2,1)S(1)} %get-tuple-element.60), channel_id=1, source_target_pairs={{0,3},{1,2},{2,1},{3,0},{4,7},{5,6},{6,5},{7,4},{8,11},{9,10},{10,... | collective-permute-start | bytes 61448 | tf_op jit(solution)/shard_map/ppermute | solution.py:626
  10.1 6.7 %collective-permute-start.4 = (bf16[80,128]{1,0:T(8,128)(2,1)S(1)}, bf16[80,128]{1,0:T(8,128)(2,1)S(1)}, u32[]{:S(2)}, u32[]{:S(2)}) collective-permute-start(bf16[80,128]{1,0:T(8,128)(2,1)S(1)} %get-tuple-element.59.sent_col), channel_id=1, source_target_pairs={{0,1},{1,0},{2,3},{3,2},{4,5},{5,4},{6,7},{7,6},{8,9},{9,8},{10,11... | collective-permute-start | bytes 61448 | tf_op jit(solution)/shard_map/ppermute | solution.py:626
  11.7 3.7 %collective-permute-start.2 = (bf16[60,128]{1,0:T(8,128)(2,1)S(1)}, bf16[60,128]{1,0:T(8,128)(2,1)S(1)}, u32[]{:S(2)}, u32[]{:S(2)}) collective-permute-start(bf16[60,128]{1,0:T(8,128)(2,1)S(1)} %get-tuple-element.57), channel_id=1, source_target_pairs={{0,4},{1,5},{2,6},{3,7},{4,0},{5,1},{6,2},{7,3},{8,12},{9,13},{10,... | collective-permute-start | bytes 46088 | tf_op jit(solution)/shard_map/ppermute | solution.py:626
  13.1 3.7 %collective-permute-start.3 = (bf16[60,128]{1,0:T(8,128)(2,1)S(1)}, bf16[60,128]{1,0:T(8,128)(2,1)S(1)}, u32[]{:S(2)}, u32[]{:S(2)}) collective-permute-start(bf16[60,128]{1,0:T(8,128)(2,1)S(1)} %get-tuple-element.58), channel_id=1, source_target_pairs={{0,2},{1,3},{2,0},{3,1},{4,8},{5,9},{6,10},{7,11},{8,4},{9,5},{10,... | collective-permute-start | bytes 46088 | tf_op jit(solution)/shard_map/ppermute | solution.py:626
  14.1 2.8 %copy-start.9 = (s32[128]{0:T(128)S(1)}, s32[128]{0:T(128)}, u32[]{:S(2)}) copy-start(s32[128]{0:T(128)} %param.39) | copy-start | bytes 1540
  17.2 7.6 %collective-permute-start.6 = (bf16[224,128]{1,0:T(8,128)(2,1)S(1)}, bf16[224,128]{1,0:T(8,128)(2,1)S(1)}, u32[]{:S(2)}, u32[]{:S(2)}) collective-permute-start(bf16[224,128]{1,0:T(8,128)(2,1)S(1)} %get-tuple-element.68), channel_id=1, source_target_pairs={{0,4},{1,5},{2,6},{3,7},{4,0},{5,1},{6,2},{7,3},{8,12},{9,13},{10,... | collective-permute-start | bytes 172040 | tf_op jit(solution)/shard_map/ppermute | solution.py:626
  18.7 6.1 %collective-permute-start.7 = (bf16[224,128]{1,0:T(8,128)(2,1)S(1)}, bf16[224,128]{1,0:T(8,128)(2,1)S(1)}, u32[]{:S(2)}, u32[]{:S(2)}) collective-permute-start(bf16[224,128]{1,0:T(8,128)(2,1)S(1)} %get-tuple-element.69), channel_id=1, source_target_pairs={{0,2},{1,3},{2,0},{3,1},{4,8},{5,9},{6,10},{7,11},{8,4},{9,5},{10,... | collective-permute-start | bytes 172040 | tf_op jit(solution)/shard_map/ppermute | solution.py:626
  19.2 4.1 %collective-permute-start.8 = (bf16[8,64]{1,0:T(8,128)(2,1)S(1)}, bf16[8,64]{1,0:T(8,128)(2,1)S(1)}, u32[]{:S(2)}, u32[]{:S(2)}) collective-permute-start(bf16[8,64]{1,0:T(8,128)(2,1)S(1)} %get-tuple-element.70), channel_id=1, source_target_pairs={{0,8},{1,9},{2,10},{3,11},{4,12},{5,13},{6,14},{7,15},{8,0},{9,1},... | collective-permute-start | bytes 3080 | tf_op jit(solution)/shard_map/ppermute | solution.py:626
  21.2 3.6 %collective-permute-start.9 = (bf16[8,64]{1,0:T(8,128)(2,1)S(1)}, bf16[8,64]{1,0:T(8,128)(2,1)S(1)}, u32[]{:S(2)}, u32[]{:S(2)}) collective-permute-start(bf16[8,64]{1,0:T(8,128)(2,1)S(1)} %get-tuple-element.71), channel_id=1, source_target_pairs={{0,2},{1,3},{2,0},{3,1},{4,6},{5,7},{6,4},{7,5},{8,16},{9,17},{10,... | collective-permute-start | bytes 3080 | tf_op jit(solution)/shard_map/ppermute | solution.py:626
  25.4 7.5 %collective-permute-start.13 = (bf16[80,128]{1,0:T(8,128)(2,1)S(1)}, bf16[80,128]{1,0:T(8,128)(2,1)S(1)}, u32[]{:S(2)}, u32[]{:S(2)}) collective-permute-start(bf16[80,128]{1,0:T(8,128)(2,1)S(1)} %get-tuple-element.83), channel_id=1, source_target_pairs={{0,3},{1,2},{2,1},{3,0},{4,7},{5,6},{6,5},{7,4},{8,11},{9,10},{10,... | collective-permute-start | bytes 61448 | tf_op jit(solution)/shard_map/ppermute | solution.py:626
  25.5 7.4 %collective-permute-start.12 = (bf16[80,128]{1,0:T(8,128)(2,1)S(1)}, bf16[80,128]{1,0:T(8,128)(2,1)S(1)}, u32[]{:S(2)}, u32[]{:S(2)}) collective-permute-start(bf16[80,128]{1,0:T(8,128)(2,1)S(1)} %get-tuple-element.82.sent_col), channel_id=1, source_target_pairs={{0,1},{1,0},{2,3},{3,2},{4,5},{5,4},{6,7},{7,6},{8,9},{9,8},{10,11... | collective-permute-start | bytes 61448 | tf_op jit(solution)/shard_map/ppermute | solution.py:626
  26.2 4.8 %collective-permute-start.10 = (bf16[60,128]{1,0:T(8,128)(2,1)S(1)}, bf16[60,128]{1,0:T(8,128)(2,1)S(1)}, u32[]{:S(2)}, u32[]{:S(2)}) collective-permute-start(bf16[60,128]{1,0:T(8,128)(2,1)S(1)} %get-tuple-element.80), channel_id=1, source_target_pairs={{0,4},{1,5},{2,6},{3,7},{4,0},{5,1},{6,2},{7,3},{8,12},{9,13},{10,... | collective-permute-start | bytes 46088 | tf_op jit(solution)/shard_map/ppermute | solution.py:626
  29.2 3.7 %collective-permute-start.11 = (bf16[60,128]{1,0:T(8,128)(2,1)S(1)}, bf16[60,128]{1,0:T(8,128)(2,1)S(1)}, u32[]{:S(2)}, u32[]{:S(2)}) collective-permute-start(bf16[60,128]{1,0:T(8,128)(2,1)S(1)} %get-tuple-element.81), channel_id=1, source_target_pairs={{0,2},{1,3},{2,0},{3,1},{4,8},{5,9},{6,10},{7,11},{8,4},{9,5},{10,... | collective-permute-start | bytes 46088 | tf_op jit(solution)/shard_map/ppermute | solution.py:626
  33.3 5.1 %collective-permute-start.14 = (bf16[8,64]{1,0:T(8,128)(2,1)S(1)}, bf16[8,64]{1,0:T(8,128)(2,1)S(1)}, u32[]{:S(2)}, u32[]{:S(2)}) collective-permute-start(bf16[8,64]{1,0:T(8,128)(2,1)S(1)} %get-tuple-element.95), channel_id=1, source_target_pairs={{0,4},{1,5},{2,6},{3,7},{4,0},{5,1},{6,2},{7,3},{8,12},{9,13},{10,... | collective-permute-start | bytes 3080 | tf_op jit(solution)/shard_map/ppermute | solution.py:626
  34.2 4.2 %collective-permute-start.15 = (bf16[8,64]{1,0:T(8,128)(2,1)S(1)}, bf16[8,64]{1,0:T(8,128)(2,1)S(1)}, u32[]{:S(2)}, u32[]{:S(2)}) collective-permute-start(bf16[8,64]{1,0:T(8,128)(2,1)S(1)} %get-tuple-element.96), channel_id=1, source_target_pairs={{0,2},{1,3},{2,0},{3,1},{4,8},{5,9},{6,10},{7,11},{8,4},{9,5},{10,... | collective-permute-start | bytes 3080 | tf_op jit(solution)/shard_map/ppermute | solution.py:626
  (2 other events, 4.3 us)

commit v7 on v6

--- a/solution.py
+++ b/solution.py
@@ -135,7 +135,7 @@
 
 
 def pick_far(fields, send, outs):
-    to_even, to_odd, own, far_even, far_odd, pack_south, pack_north = outs
+    to_even, to_odd, own, far_even, far_odd, pack_even, pack_odd = outs
     slot = send.shape[2]
     slots = picked(fields, send)
     row = lax.axis_index("row")
@@ -144,9 +144,8 @@
     rows = slots.shape[0]
     to_even[:rows, :] = jnp.concatenate([jnp.where(even, north, south), here], axis=1).astype(bf16)
     to_odd[:rows, :] = jnp.concatenate([jnp.where(even, south, north), here], axis=1).astype(bf16)
-    a, b = pack_south[...].astype(f32), pack_north[...].astype(f32)
-    to_even[PACK:, :] = jnp.where(even, b, a).astype(bf16)
-    to_odd[PACK:, :] = jnp.where(even, a, b).astype(bf16)
+    to_even[PACK:, :] = pack_even[...]
+    to_odd[PACK:, :] = pack_odd[...]
     own[...] = slots.astype(bf16)
     far_even[...] = jnp.where(first, north, south).astype(bf16)
     far_odd[...] = jnp.where(first, south, north).astype(bf16)
@@ -223,7 +222,7 @@
     )
 
 
-def k_pack(energy_ref, weight_ref, recv_ref, wind_ref, wet_ref, send_ref, south_ref, own_ref, north_ref):
+def k_pack(energy_ref, weight_ref, recv_ref, wind_ref, wet_ref, send_ref, even_ref, own_ref, odd_ref):
     parts = joined(dot(weight_ref[...], energy_ref[...]))
     slot = send_ref.shape[2]
     rows = parts.shape[0]
@@ -236,9 +235,12 @@
     extra = jnp.concatenate(extra, axis=0).astype(bf16)
     stack = jnp.concatenate([parts.astype(bf16), recv_ref[...], extra], axis=0)
     cells = picked(stack, send_ref)
-    for j, ref in enumerate((south_ref, own_ref, north_ref)):
-        lanes = slice(j * slot, (j + 1) * slot)
-        ref[...] = jnp.concatenate([cells[:rows, lanes], cells[rows:, lanes]], axis=1).astype(bf16)
+    lanes = [slice(j * slot, (j + 1) * slot) for j in range(3)]
+    south, own, north = [jnp.concatenate([cells[:rows, x], cells[rows:, x]], axis=1) for x in lanes]
+    even = is_even(lax.axis_index("row"))
+    even_ref[...] = jnp.where(even, north, south).astype(bf16)
+    own_ref[...] = own.astype(bf16)
+    odd_ref[...] = jnp.where(even, south, north).astype(bf16)
 
 
 def k_transfer(old_ref, inter_ref, moved_ref):
@@ -681,12 +683,12 @@
     (energy,) = call(
         functools.partial(k_update, nfreq), [((spec, cells), bf16)], [VMEM] * 5, [pltpu.VMEM((spec, cells), f32)]
     )(energy, interaction, soft, wave_wet, coef)
-    pack_south, pack_own, pack_north = call(
+    pack_even, pack_own, pack_odd = call(
         k_pack, [((half, 2 * slot), bf16)] * 3, [VMEM] * 6
     )(energy, weights, wave_w, wind, wave_wet, wsend)
     far_slots = [((PACK + half, 2 * slot), bf16)] * 2 + [((8, 3 * slot), bf16)] + [((8, slot), bf16)] * 2
     smooth, eta, sent = edges(
-        0, (got_even, got_odd, own), (pick_far, far_slots), (pack_south, pack_north)
+        0, (got_even, got_odd, own), (pick_far, far_slots), (pack_even, pack_odd)
     )
     to_even, to_odd, own, far_even, far_odd = sent
     got_odd, got_even = trade("row_odd", to_odd), trade("row_even", to_even)

time: 39.4 us -> 39.4 us (level)
  no operation moved by 1% of the time
where the time goes in v7:
time: 39.4 us; the launch traced here: 39.2 us
  starting transfers between devices  19.9 us (51%)
  Pallas kernels  9.76 us (25%)
  waiting for transfers between devices  8.47 us (21%)
  between operations  0.99 us (3%)
    ppermute x16, starting transfers between devices, trade(): return lax.ppermute(array, axis, pairs[label])  19.9 us
    ppermute x16, waiting for transfers between devices, trade(): return lax.ppermute(array, axis, pairs[label])  8.47 us
    pallas_call x1, Pallas kernels, shards(): call(functools.partial(k_wave_first, nfreq), slots_out + [((spec, cells),...  2.19 us
    pallas_call x1, Pallas kernels, shards(): call(functools.partial(k_last, lev), [((spec * rows, lanes), bf16), ((oy,...  1.15 us
    pallas_call x1, Pallas kernels, shards(): call(functools.partial(k_update_last, nfreq), [((spec * rows, lanes), bf1...  0.93 us
  transfers between devices with their start and end apart: 16, of which 6 were waited for; matrix products, arithmetic and copies ran while one was open for 0% of the time, Pallas kernels for 13%

profile of v7, /device:TPU:0, one launch (start us, length us, event | category | flops | bytes accessed | tf_op | source)
XLA Modules:
  0.0 39.2 jit_solution(6567705012877638107)
XLA Ops:
  0.8 2.2 %shard_map.237 = (bf16[8,64]{1,0:T(8,128)(2,1)S(1)}, bf16[8,64]{1,0:T(8,128)(2,1)S(1)}, bf16[8,64]{1,0:T(8,128)(2,1)S(1)}, bf16[600,512]{1,0:T(8,128)(2,1)S(1)},...) custom-call(f32[2,600]{1,0:T(2,128)} %smap_hbm.1, f32[6,600]{1,0:T(8,128)} %kmap_hbm.1, f32[25]{0:T(128)} %rate_hbm.1, ...), custom_call_target="tpu_custom_call" | custom-call | tf_op jit(solution)/shard_map/pallas_call | solution.py:670
  3.0 3.1 %collective-permute-start = (bf16[8,64]{1,0:T(8,128)(2,1)S(1)}, bf16[8,64]{1,0:T(8,128)(2,1)S(1)}, u32[]{:S(2)}, u32[]{:S(2)}) collective-permute-start(bf16[8,64]{1,0:T(8,128)(2,1)S(1)} %get-tuple-element.54), channel_id=1, source_target_pairs={{0,4},{1,5},{2,6},{3,7},{4,0},{5,1},{6,2},{7,3},{8,12},{9,13},{10,... | collective-permute-start | bytes 3080 | tf_op jit(solution)/shard_map/ppermute | solution.py:628
  6.0 1.5 %collective-permute-start.1 = (bf16[8,64]{1,0:T(8,128)(2,1)S(1)}, bf16[8,64]{1,0:T(8,128)(2,1)S(1)}, u32[]{:S(2)}, u32[]{:S(2)}) collective-permute-start(bf16[8,64]{1,0:T(8,128)(2,1)S(1)} %get-tuple-element.55), channel_id=1, source_target_pairs={{0,2},{1,3},{2,0},{3,1},{4,8},{5,9},{6,10},{7,11},{8,4},{9,5},{10,... | collective-permute-start | bytes 3080 | tf_op jit(solution)/shard_map/ppermute | solution.py:628
  7.7 1.9 %collective-permute-done.1.refs_1_ = bf16[8,64]{1,0:T(8,128)(2,1)S(1)} collective-permute-done((bf16[8,64]{1,0:T(8,128)(2,1)S(1)}, bf16[8,64]{1,0:T(8,128)(2,1)S(1)}, u32[]{:S(2)}, u32[]{:S(2)}) %collective-permute-start.1) | collective-permute-done | bytes 1056 | tf_op jit(solution)/shard_map/ppermute | solution.py:628
  9.6 0.4 shard_map.241
  10.1 1.6 %collective-permute-start.4 = (bf16[80,128]{1,0:T(8,128)(2,1)S(1)}, bf16[80,128]{1,0:T(8,128)(2,1)S(1)}, u32[]{:S(2)}, u32[]{:S(2)}) collective-permute-start(bf16[80,128]{1,0:T(8,128)(2,1)S(1)} %get-tuple-element.59.sent_col), channel_id=1, source_target_pairs={{0,1},{1,0},{2,3},{3,2},{4,5},{5,4},{6,7},{7,6},{8,9},{9,8},{10,11... | collective-permute-start | bytes 61448 | tf_op jit(solution)/shard_map/ppermute | solution.py:628
  11.7 1.4 %collective-permute-start.2 = (bf16[60,128]{1,0:T(8,128)(2,1)S(1)}, bf16[60,128]{1,0:T(8,128)(2,1)S(1)}, u32[]{:S(2)}, u32[]{:S(2)}) collective-permute-start(bf16[60,128]{1,0:T(8,128)(2,1)S(1)} %get-tuple-element.57), channel_id=1, source_target_pairs={{0,4},{1,5},{2,6},{3,7},{4,0},{5,1},{6,2},{7,3},{8,12},{9,13},{10,... | collective-permute-start | bytes 46088 | tf_op jit(solution)/shard_map/ppermute | solution.py:628
  13.3 0.8 %shard_map.239.old_ref.energy_ref = bf16[600,512]{1,0:T(8,128)(2,1)S(1)} custom-call(bf16[600,512]{1,0:T(8,128)(2,1)S(1)} %get-tuple-element.51.old_ref, bf16[600,600]{1,0:T(8,128)(2,1)S(1)} %copy-done, f32[32,512]{1,0:T(8,128)S(1)} %get-tuple-element.52.soft_ref, s32[4,128]{1,0:T(4,128)S(1)} %copy-done.7, ...), custom_call_target="tpu_custom_call" | custom-call | tf_op jit(solution)/shard_map/pallas_call | solution.py:683
  14.1 0.6 %shard_map.243 = (bf16[208,128]{1,0:T(8,128)(2,1)S(1)}, bf16[208,128]{1,0:T(8,128)(2,1)S(1)}, bf16[208,128]{1,0:T(8,128)(2,1)S(1)}) custom-call(bf16[600,512]{1,0:T(8,128)(2,1)S(1)} %shard_map.239.old_ref.energy_ref, bf16[224,600]{1,0:T(8,128)(2,1)S(1)} %get-tuple-element.65.weight_ref, bf16[192,512]{1,0:T(8,128)(2,1)S(1)} %bitcast.13, ...), custom_call_target="tpu_custom_call" | custom-call | tf_op jit(solution)/shard_map/pallas_call | solution.py:686
  15.0 0.5 %collective-permute-done.2.got_row_even = bf16[60,128]{1,0:T(8,128)(2,1)S(1)} collective-permute-done((bf16[60,128]{1,0:T(8,128)(2,1)S(1)}, bf16[60,128]{1,0:T(8,128)(2,1)S(1)}, u32[]{:S(2)}, u32[]{:S(2)}) %collective-permute-start.2) | collective-permute-done | bytes 15392 | tf_op jit(solution)/shard_map/ppermute | solution.py:628
  15.5 1.4 %collective-permute-done.3.got_row_odd = bf16[60,128]{1,0:T(8,128)(2,1)S(1)} collective-permute-done((bf16[60,128]{1,0:T(8,128)(2,1)S(1)}, bf16[60,128]{1,0:T(8,128)(2,1)S(1)}, u32[]{:S(2)}, u32[]{:S(2)}) %collective-permute-start.3) | collective-permute-done | bytes 15392 | tf_op jit(solution)/shard_map/ppermute | solution.py:628
  16.9 0.3 shard_map.244
  17.2 1.5 %collective-permute-start.6 = (bf16[224,128]{1,0:T(8,128)(2,1)S(1)}, bf16[224,128]{1,0:T(8,128)(2,1)S(1)}, u32[]{:S(2)}, u32[]{:S(2)}) collective-permute-start(bf16[224,128]{1,0:T(8,128)(2,1)S(1)} %get-tuple-element.68), channel_id=1, source_target_pairs={{0,4},{1,5},{2,6},{3,7},{4,0},{5,1},{6,2},{7,3},{8,12},{9,13},{10,... | collective-permute-start | bytes 172040 | tf_op jit(solution)/shard_map/ppermute | solution.py:628
  18.7 0.5 %collective-permute-start.7 = (bf16[224,128]{1,0:T(8,128)(2,1)S(1)}, bf16[224,128]{1,0:T(8,128)(2,1)S(1)}, u32[]{:S(2)}, u32[]{:S(2)}) collective-permute-start(bf16[224,128]{1,0:T(8,128)(2,1)S(1)} %get-tuple-element.69), channel_id=1, source_target_pairs={{0,2},{1,3},{2,0},{3,1},{4,8},{5,9},{6,10},{7,11},{8,4},{9,5},{10,... | collective-permute-start | bytes 172040 | tf_op jit(solution)/shard_map/ppermute | solution.py:628
  19.2 1.9 %collective-permute-start.8 = (bf16[8,64]{1,0:T(8,128)(2,1)S(1)}, bf16[8,64]{1,0:T(8,128)(2,1)S(1)}, u32[]{:S(2)}, u32[]{:S(2)}) collective-permute-start(bf16[8,64]{1,0:T(8,128)(2,1)S(1)} %get-tuple-element.70), channel_id=1, source_target_pairs={{0,8},{1,9},{2,10},{3,11},{4,12},{5,13},{6,14},{7,15},{8,0},{9,1},... | collective-permute-start | bytes 3080 | tf_op jit(solution)/shard_map/ppermute | solution.py:628
  21.2 0.5 %collective-permute-start.9 = (bf16[8,64]{1,0:T(8,128)(2,1)S(1)}, bf16[8,64]{1,0:T(8,128)(2,1)S(1)}, u32[]{:S(2)}, u32[]{:S(2)}) collective-permute-start(bf16[8,64]{1,0:T(8,128)(2,1)S(1)} %get-tuple-element.71), channel_id=1, source_target_pairs={{0,2},{1,3},{2,0},{3,1},{4,6},{5,7},{6,4},{7,5},{8,16},{9,17},{10,... | collective-permute-start | bytes 3080 | tf_op jit(solution)/shard_map/ppermute | solution.py:628
  21.7 0.4 %shard_map.247.refs_2_ = f32[480,128]{1,0:T(8,128)S(1)} custom-call(f32[480,128]{1,0:T(8,128)S(1)} %get-tuple-element.76.part_ref, f32[60,128]{1,0:T(8,128)S(1)} %get-tuple-element.77.north_ref, f32[60,128]{1,0:T(8,128)S(1)} %get-tuple-element.78.south_ref, f32[16,128]{1,0:T(8,128)S(1)} %get-tuple-element.79.ends_ref, s32[8,128]{1,0:T(8,128)S(1)} %copy-done.3, ...), custom_call_target="tpu_custom_call" | custom-call | tf_op jit(solution)/shard_map/pallas_call | solution.py:699
  22.1 1.2 %collective-permute-done.8.far_even = bf16[8,64]{1,0:T(8,128)(2,1)S(1)} collective-permute-done((bf16[8,64]{1,0:T(8,128)(2,1)S(1)}, bf16[8,64]{1,0:T(8,128)(2,1)S(1)}, u32[]{:S(2)}, u32[]{:S(2)}) %collective-permute-start.8) | collective-permute-done | bytes 1056 | tf_op jit(solution)/shard_map/ppermute | solution.py:628
  23.4 1.4 %collective-permute-done.9.far_odd = bf16[8,64]{1,0:T(8,128)(2,1)S(1)} collective-permute-done((bf16[8,64]{1,0:T(8,128)(2,1)S(1)}, bf16[8,64]{1,0:T(8,128)(2,1)S(1)}, u32[]{:S(2)}, u32[]{:S(2)}) %collective-permute-start.9) | collective-permute-done | bytes 1056 | tf_op jit(solution)/shard_map/ppermute | solution.py:628
  24.8 0.3 shard_map.245
  25.1 0.3 shard_map.248
  25.5 0.6 %collective-permute-start.12 = (bf16[80,128]{1,0:T(8,128)(2,1)S(1)}, bf16[80,128]{1,0:T(8,128)(2,1)S(1)}, u32[]{:S(2)}, u32[]{:S(2)}) collective-permute-start(bf16[80,128]{1,0:T(8,128)(2,1)S(1)} %get-tuple-element.82.sent_col), channel_id=1, source_target_pairs={{0,1},{1,0},{2,3},{3,2},{4,5},{5,4},{6,7},{7,6},{8,9},{9,8},{10,11... | collective-permute-start | bytes 61448 | tf_op jit(solution)/shard_map/ppermute | solution.py:628
  26.2 3.0 %collective-permute-start.10 = (bf16[60,128]{1,0:T(8,128)(2,1)S(1)}, bf16[60,128]{1,0:T(8,128)(2,1)S(1)}, u32[]{:S(2)}, u32[]{:S(2)}) collective-permute-start(bf16[60,128]{1,0:T(8,128)(2,1)S(1)} %get-tuple-element.80), channel_id=1, source_target_pairs={{0,4},{1,5},{2,6},{3,7},{4,0},{5,1},{6,2},{7,3},{8,12},{9,13},{10,... | collective-permute-start | bytes 46088 | tf_op jit(solution)/shard_map/ppermute | solution.py:628
  29.2 1.5 %collective-permute-start.11 = (bf16[60,128]{1,0:T(8,128)(2,1)S(1)}, bf16[60,128]{1,0:T(8,128)(2,1)S(1)}, u32[]{:S(2)}, u32[]{:S(2)}) collective-permute-start(bf16[60,128]{1,0:T(8,128)(2,1)S(1)} %get-tuple-element.81), channel_id=1, source_target_pairs={{0,2},{1,3},{2,0},{3,1},{4,8},{5,9},{6,10},{7,11},{8,4},{9,5},{10,... | collective-permute-start | bytes 46088 | tf_op jit(solution)/shard_map/ppermute | solution.py:628
  30.9 2.0 %collective-permute-done.11.got_row_odd = bf16[60,128]{1,0:T(8,128)(2,1)S(1)} collective-permute-done((bf16[60,128]{1,0:T(8,128)(2,1)S(1)}, bf16[60,128]{1,0:T(8,128)(2,1)S(1)}, u32[]{:S(2)}, u32[]{:S(2)}) %collective-permute-start.11) | collective-permute-done | bytes 15392 | tf_op jit(solution)/shard_map/ppermute | solution.py:628
  33.0 0.3 shard_map.250
  33.3 0.9 %collective-permute-start.14 = (bf16[8,64]{1,0:T(8,128)(2,1)S(1)}, bf16[8,64]{1,0:T(8,128)(2,1)S(1)}, u32[]{:S(2)}, u32[]{:S(2)}) collective-permute-start(bf16[8,64]{1,0:T(8,128)(2,1)S(1)} %get-tuple-element.95), channel_id=1, source_target_pairs={{0,4},{1,5},{2,6},{3,7},{4,0},{5,1},{6,2},{7,3},{8,12},{9,13},{10,... | collective-permute-start | bytes 3080 | tf_op jit(solution)/shard_map/ppermute | solution.py:628
  34.2 1.5 %collective-permute-start.15 = (bf16[8,64]{1,0:T(8,128)(2,1)S(1)}, bf16[8,64]{1,0:T(8,128)(2,1)S(1)}, u32[]{:S(2)}, u32[]{:S(2)}) collective-permute-start(bf16[8,64]{1,0:T(8,128)(2,1)S(1)} %get-tuple-element.96), channel_id=1, source_target_pairs={{0,2},{1,3},{2,0},{3,1},{4,8},{5,9},{6,10},{7,11},{8,4},{9,5},{10,... | collective-permute-start | bytes 3080 | tf_op jit(solution)/shard_map/ppermute | solution.py:628
  35.7 0.6 %shard_map.240.moved_ref = f32[600,512]{1,0:T(8,128)S(1)} custom-call(bf16[600,512]{1,0:T(8,128)(2,1)S(1)} %shard_map.239.old_ref.energy_ref, bf16[600,600]{1,0:T(8,128)(2,1)S(1)} %copy-done), custom_call_target="tpu_custom_call" | custom-call | tf_op jit(solution)/shard_map/pallas_call | solution.py:696
  36.3 0.9 %shard_map.246.spectra_ref = bf16[2400,128]{1,0:T(8,128)(2,1)S(1)} custom-call(bf16[600,512]{1,0:T(8,128)(2,1)S(1)} %shard_map.239.old_ref.energy_ref, f32[600,512]{1,0:T(8,128)S(1)} %shard_map.240.moved_ref, bf16[8,192]{1,0:T(8,128)(2,1)S(1)} %get-tuple-element.74.mine_ref, bf16[192,512]{1,0:T(8,128)(2,1)S(1)} %bitcast.14, f32[2,4,128]{2,1,0:T(4,128)S(1)} %copy-done.6, ...), custom_call_target="tpu_custom_call" | custom-call | tf_op jit(solution)/shard_map/pallas_call | solution.py:703
  37.3 1.1 %shard_map.251 = (bf16[2400,128]{1,0:T(8,128)(2,1)}, f32[8,128]{1,0:T(8,128)}, f32[480,128]{1,0:T(8,128)}) custom-call(bf16[2400,128]{1,0:T(8,128)(2,1)S(1)} %shard_map.246.spectra_ref, f32[8,128]{1,0:T(8,128)S(1)} %get-tuple-element.87.eta_ref, f32[480,128]{1,0:T(8,128)S(1)} %get-tuple-element.88.part_ref, f32[60,128]{1,0:T(8,128)S(1)} %get-tuple-element.89.north_ref, ...), custom_call_target="tpu_custom_call" | custom-call | tf_op jit(solution)/shard_map/pallas_call | solution.py:716
  38.5 0.8 %shard_map.252 = f32[3,4,128]{2,1,0:T(4,128)} custom-call(bf16[8,64]{1,0:T(8,128)(2,1)S(1)} %collective-permute-done.14.got_even, bf16[8,64]{1,0:T(8,128)(2,1)S(1)} %collective-permute-done.15.got_odd, bf16[8,64]{1,0:T(8,128)(2,1)S(1)} %get-tuple-element.97.own, bf16[192,512]{1,0:T(8,128)(2,1)S(1)} %bitcast.15), custom_call_target="tpu_custom_call" | custom-call | tf_op jit(solution)/shard_map/pallas_call | solution.py:723
  (52 shorter events, 1.0 us)
Async XLA Ops:
  0.6 12.6 %copy-start.7 = (s32[4,128]{1,0:T(4,128)S(1)}, s32[4,128]{1,0:T(4,128)}, u32[]{:S(2)}) copy-start(s32[4,128]{1,0:T(4,128)} %wet_ref.12) | copy-start | bytes 6148
  0.6 12.6 %copy-start = (bf16[600,600]{1,0:T(8,128)(2,1)S(1)}, bf16[600,600]{1,0:T(8,128)(2,1)}, u32[]{:S(2)}) copy-start(bf16[600,600]{1,0:T(8,128)(2,1)} %inter_ref.3) | copy-start | bytes 2160004
  0.7 6.8 %copy-start.14 = (f32[25]{0:T(128)S(1)}, f32[25]{0:T(128)}, u32[]{:S(2)}) copy-start(f32[25]{0:T(128)} %gain_hbm.1) | copy-start | bytes 304
  0.7 6.8 %copy-start.13 = (f32[25]{0:T(128)S(1)}, f32[25]{0:T(128)}, u32[]{:S(2)}) copy-start(f32[25]{0:T(128)} %rate_hbm.1) | copy-start | bytes 304
  0.7 6.8 %copy-start.5 = (f32[30,30]{1,0:T(8,128)S(1)}, f32[30,30]{1,0:T(8,128)}, u32[]{:S(2)}) copy-start(f32[30,30]{1,0:T(8,128)} %mix_ref.5) | copy-start | bytes 10804
  0.7 6.8 %copy-start.17 = (f32[30]{0:T(128)S(1)}, f32[30]{0:T(128)}, u32[]{:S(2)}) copy-start(f32[30]{0:T(128)} %param.37) | copy-start | bytes 364
  0.7 6.8 %copy-start.15 = (f32[3,30]{1,0:T(4,128)S(1)}, f32[3,30]{1,0:T(4,128)}, u32[]{:S(2)}) copy-start(f32[3,30]{1,0:T(4,128)} %prof_ref.1) | copy-start | bytes 1084
  0.7 6.8 %copy-start.16 = (f32[30]{0:T(128)S(1)}, f32[30]{0:T(128)}, u32[]{:S(2)}) copy-start(f32[30]{0:T(128)} %param.35) | copy-start | bytes 364
  0.7 8.9 %copy-start.3 = (s32[8,128]{1,0:T(8,128)S(1)}, s32[8,128]{1,0:T(8,128)}, u32[]{:S(2)}) copy-start(s32[8,128]{1,0:T(8,128)} %sea_ref.1) | copy-start | bytes 12292
  0.7 8.9 %copy-start.8 = (f32[8,128]{1,0:T(8,128)S(1)}, f32[8,128]{1,0:T(8,128)}, u32[]{:S(2)}) copy-start(f32[8,128]{1,0:T(8,128)} %refs_4_.1) | copy-start | bytes 12292
  0.7 8.9 %copy-start.2 = (bf16[1,1,3,64,1024]{4,3,2,1,0:T(8,128)(2,1)S(1)}, bf16[1,1,3,64,1024]{4,3,2,1,0:T(8,128)(2,1)}, u32[]{:S(2)}) copy-start(bf16[1,1,3,64,1024]{4,3,2,1,0:T(8,128)(2,1)} %param.41) | copy-start | bytes 1179652
  0.7 8.9 %copy-start.4 = (f32[2,30,8,128]{3,2,1,0:T(8,128)S(1)}, f32[2,30,8,128]{3,2,1,0:T(8,128)}, u32[]{:S(2)}) copy-start(f32[2,30,8,128]{3,2,1,0:T(8,128)} %param.31) | copy-start | bytes 737284
  3.0 4.7 %collective-permute-start = (bf16[8,64]{1,0:T(8,128)(2,1)S(1)}, bf16[8,64]{1,0:T(8,128)(2,1)S(1)}, u32[]{:S(2)}, u32[]{:S(2)}) collective-permute-start(bf16[8,64]{1,0:T(8,128)(2,1)S(1)} %get-tuple-element.54), channel_id=1, source_target_pairs={{0,4},{1,5},{2,6},{3,7},{4,0},{5,1},{6,2},{7,3},{8,12},{9,13},{10,... | collective-permute-start | bytes 3080 | tf_op jit(solution)/shard_map/ppermute | solution.py:628
  6.0 3.6 %collective-permute-start.1 = (bf16[8,64]{1,0:T(8,128)(2,1)S(1)}, bf16[8,64]{1,0:T(8,128)(2,1)S(1)}, u32[]{:S(2)}, u32[]{:S(2)}) collective-permute-start(bf16[8,64]{1,0:T(8,128)(2,1)S(1)} %get-tuple-element.55), channel_id=1, source_target_pairs={{0,2},{1,3},{2,0},{3,1},{4,8},{5,9},{6,10},{7,11},{8,4},{9,5},{10,... | collective-permute-start | bytes 3080 | tf_op jit(solution)/shard_map/ppermute | solution.py:628
  10.0 4.1 %copy-start.1 = (bf16[1,1,3,64,512]{4,3,2,1,0:T(8,128)(2,1)S(1)}, bf16[1,1,3,64,512]{4,3,2,1,0:T(8,128)(2,1)}, u32[]{:S(2)}) copy-start(bf16[1,1,3,64,512]{4,3,2,1,0:T(8,128)(2,1)} %param.43) | copy-start | bytes 589828
  10.0 4.1 %copy-start.6 = (f32[2,4,128]{2,1,0:T(4,128)S(1)}, f32[2,4,128]{2,1,0:T(4,128)}, u32[]{:S(2)}) copy-start(f32[2,4,128]{2,1,0:T(4,128)} %wind_ref.3) | copy-start | bytes 12292
  10.0 4.1 %copy-start.10 = (s32[1,1,3,64]{3,1,2,0:T(1,128)S(1)}, s32[1,1,3,64]{3,1,2,0:T(1,128)}, u32[]{:S(2)}) copy-start(s32[1,1,3,64]{3,1,2,0:T(1,128)} %param.40) | copy-start | bytes 2308
  10.0 6.8 %collective-permute-start.5 = (bf16[80,128]{1,0:T(8,128)(2,1)S(1)}, bf16[80,128]{1,0:T(8,128)(2,1)S(1)}, u32[]{:S(2)}, u32[]{:S(2)}) collective-permute-start(bf16[80,128]{1,0:T(8,128)(2,1)S(1)} %get-tuple-element.60), channel_id=1, source_target_pairs={{0,3},{1,2},{2,1},{3,0},{4,7},{5,6},{6,5},{7,4},{8,11},{9,10},{10,... | collective-permute-start | bytes 61448 | tf_op jit(solution)/shard_map/ppermute | solution.py:628
  10.1 6.7 %collective-permute-start.4 = (bf16[80,128]{1,0:T(8,128)(2,1)S(1)}, bf16[80,128]{1,0:T(8,128)(2,1)S(1)}, u32[]{:S(2)}, u32[]{:S(2)}) collective-permute-start(bf16[80,128]{1,0:T(8,128)(2,1)S(1)} %get-tuple-element.59.sent_col), channel_id=1, source_target_pairs={{0,1},{1,0},{2,3},{3,2},{4,5},{5,4},{6,7},{7,6},{8,9},{9,8},{10,11... | collective-permute-start | bytes 61448 | tf_op jit(solution)/shard_map/ppermute | solution.py:628
  11.7 3.7 %collective-permute-start.2 = (bf16[60,128]{1,0:T(8,128)(2,1)S(1)}, bf16[60,128]{1,0:T(8,128)(2,1)S(1)}, u32[]{:S(2)}, u32[]{:S(2)}) collective-permute-start(bf16[60,128]{1,0:T(8,128)(2,1)S(1)} %get-tuple-element.57), channel_id=1, source_target_pairs={{0,4},{1,5},{2,6},{3,7},{4,0},{5,1},{6,2},{7,3},{8,12},{9,13},{10,... | collective-permute-start | bytes 46088 | tf_op jit(solution)/shard_map/ppermute | solution.py:628
  13.1 3.7 %collective-permute-start.3 = (bf16[60,128]{1,0:T(8,128)(2,1)S(1)}, bf16[60,128]{1,0:T(8,128)(2,1)S(1)}, u32[]{:S(2)}, u32[]{:S(2)}) collective-permute-start(bf16[60,128]{1,0:T(8,128)(2,1)S(1)} %get-tuple-element.58), channel_id=1, source_target_pairs={{0,2},{1,3},{2,0},{3,1},{4,8},{5,9},{6,10},{7,11},{8,4},{9,5},{10,... | collective-permute-start | bytes 46088 | tf_op jit(solution)/shard_map/ppermute | solution.py:628
  14.1 2.8 %copy-start.9 = (s32[128]{0:T(128)S(1)}, s32[128]{0:T(128)}, u32[]{:S(2)}) copy-start(s32[128]{0:T(128)} %param.39) | copy-start | bytes 1540
  17.2 7.6 %collective-permute-start.6 = (bf16[224,128]{1,0:T(8,128)(2,1)S(1)}, bf16[224,128]{1,0:T(8,128)(2,1)S(1)}, u32[]{:S(2)}, u32[]{:S(2)}) collective-permute-start(bf16[224,128]{1,0:T(8,128)(2,1)S(1)} %get-tuple-element.68), channel_id=1, source_target_pairs={{0,4},{1,5},{2,6},{3,7},{4,0},{5,1},{6,2},{7,3},{8,12},{9,13},{10,... | collective-permute-start | bytes 172040 | tf_op jit(solution)/shard_map/ppermute | solution.py:628
  18.7 6.1 %collective-permute-start.7 = (bf16[224,128]{1,0:T(8,128)(2,1)S(1)}, bf16[224,128]{1,0:T(8,128)(2,1)S(1)}, u32[]{:S(2)}, u32[]{:S(2)}) collective-permute-start(bf16[224,128]{1,0:T(8,128)(2,1)S(1)} %get-tuple-element.69), channel_id=1, source_target_pairs={{0,2},{1,3},{2,0},{3,1},{4,8},{5,9},{6,10},{7,11},{8,4},{9,5},{10,... | collective-permute-start | bytes 172040 | tf_op jit(solution)/shard_map/ppermute | solution.py:628
  19.2 4.1 %collective-permute-start.8 = (bf16[8,64]{1,0:T(8,128)(2,1)S(1)}, bf16[8,64]{1,0:T(8,128)(2,1)S(1)}, u32[]{:S(2)}, u32[]{:S(2)}) collective-permute-start(bf16[8,64]{1,0:T(8,128)(2,1)S(1)} %get-tuple-element.70), channel_id=1, source_target_pairs={{0,8},{1,9},{2,10},{3,11},{4,12},{5,13},{6,14},{7,15},{8,0},{9,1},... | collective-permute-start | bytes 3080 | tf_op jit(solution)/shard_map/ppermute | solution.py:628
  21.2 3.6 %collective-permute-start.9 = (bf16[8,64]{1,0:T(8,128)(2,1)S(1)}, bf16[8,64]{1,0:T(8,128)(2,1)S(1)}, u32[]{:S(2)}, u32[]{:S(2)}) collective-permute-start(bf16[8,64]{1,0:T(8,128)(2,1)S(1)} %get-tuple-element.71), channel_id=1, source_target_pairs={{0,2},{1,3},{2,0},{3,1},{4,6},{5,7},{6,4},{7,5},{8,16},{9,17},{10,... | collective-permute-start | bytes 3080 | tf_op jit(solution)/shard_map/ppermute | solution.py:628
  25.4 7.5 %collective-permute-start.13 = (bf16[80,128]{1,0:T(8,128)(2,1)S(1)}, bf16[80,128]{1,0:T(8,128)(2,1)S(1)}, u32[]{:S(2)}, u32[]{:S(2)}) collective-permute-start(bf16[80,128]{1,0:T(8,128)(2,1)S(1)} %get-tuple-element.83), channel_id=1, source_target_pairs={{0,3},{1,2},{2,1},{3,0},{4,7},{5,6},{6,5},{7,4},{8,11},{9,10},{10,... | collective-permute-start | bytes 61448 | tf_op jit(solution)/shard_map/ppermute | solution.py:628
  25.5 7.4 %collective-permute-start.12 = (bf16[80,128]{1,0:T(8,128)(2,1)S(1)}, bf16[80,128]{1,0:T(8,128)(2,1)S(1)}, u32[]{:S(2)}, u32[]{:S(2)}) collective-permute-start(bf16[80,128]{1,0:T(8,128)(2,1)S(1)} %get-tuple-element.82.sent_col), channel_id=1, source_target_pairs={{0,1},{1,0},{2,3},{3,2},{4,5},{5,4},{6,7},{7,6},{8,9},{9,8},{10,11... | collective-permute-start | bytes 61448 | tf_op jit(solution)/shard_map/ppermute | solution.py:628
  26.2 4.8 %collective-permute-start.10 = (bf16[60,128]{1,0:T(8,128)(2,1)S(1)}, bf16[60,128]{1,0:T(8,128)(2,1)S(1)}, u32[]{:S(2)}, u32[]{:S(2)}) collective-permute-start(bf16[60,128]{1,0:T(8,128)(2,1)S(1)} %get-tuple-element.80), channel_id=1, source_target_pairs={{0,4},{1,5},{2,6},{3,7},{4,0},{5,1},{6,2},{7,3},{8,12},{9,13},{10,... | collective-permute-start | bytes 46088 | tf_op jit(solution)/shard_map/ppermute | solution.py:628
  29.2 3.7 %collective-permute-start.11 = (bf16[60,128]{1,0:T(8,128)(2,1)S(1)}, bf16[60,128]{1,0:T(8,128)(2,1)S(1)}, u32[]{:S(2)}, u32[]{:S(2)}) collective-permute-start(bf16[60,128]{1,0:T(8,128)(2,1)S(1)} %get-tuple-element.81), channel_id=1, source_target_pairs={{0,2},{1,3},{2,0},{3,1},{4,8},{5,9},{6,10},{7,11},{8,4},{9,5},{10,... | collective-permute-start | bytes 46088 | tf_op jit(solution)/shard_map/ppermute | solution.py:628
  33.3 5.1 %collective-permute-start.14 = (bf16[8,64]{1,0:T(8,128)(2,1)S(1)}, bf16[8,64]{1,0:T(8,128)(2,1)S(1)}, u32[]{:S(2)}, u32[]{:S(2)}) collective-permute-start(bf16[8,64]{1,0:T(8,128)(2,1)S(1)} %get-tuple-element.95), channel_id=1, source_target_pairs={{0,4},{1,5},{2,6},{3,7},{4,0},{5,1},{6,2},{7,3},{8,12},{9,13},{10,... | collective-permute-start | bytes 3080 | tf_op jit(solution)/shard_map/ppermute | solution.py:628
  34.2 4.2 %collective-permute-start.15 = (bf16[8,64]{1,0:T(8,128)(2,1)S(1)}, bf16[8,64]{1,0:T(8,128)(2,1)S(1)}, u32[]{:S(2)}, u32[]{:S(2)}) collective-permute-start(bf16[8,64]{1,0:T(8,128)(2,1)S(1)} %get-tuple-element.96), channel_id=1, source_target_pairs={{0,2},{1,3},{2,0},{3,1},{4,8},{5,9},{6,10},{7,11},{8,4},{9,5},{10,... | collective-permute-start | bytes 3080 | tf_op jit(solution)/shard_map/ppermute | solution.py:628
  (2 other events, 4.3 us)
